TPU v7x, 32 devices: a whole 2x2x4 slice. The times are simulated.
32 devices in a mesh: fsdp: 8 (over z, core), seq: 4 (over y, x).
Axes of the slice: x: 2, y: 2, z: 4, core: 2. Of those that a mesh axis runs over, the one named last changes fastest.
Arguments:
- hidden: float32 [8, 1024, 2048], P('fsdp', 'seq'), may hold values from -6 to 6
- positions: int32 [8, 1024], P('fsdp', 'seq'), may hold values from 0 to 1023, as said below
- gains: float32 [1, 2, 2048], replicated, may hold values from 0.5 to 1.5
- w_qkv: bfloat16 [1, 2560, 2048], P(None, 'fsdp')
- w_out: bfloat16 [1, 2048, 2048], P(None, 'fsdp'), may hold values from -0.5 to 0.5
- w_gate_up: bfloat16 [1, 11264, 2048], P(None, 'fsdp'), may hold values from -0.125 to 0.125
- w_down: bfloat16 [1, 2048, 5632], P(None, 'fsdp'), may hold values from -0.078125 to 0.078125
- cotangent: float32 [8, 1024, 2048], P('fsdp', 'seq'), may hold values from -6 to 6
Outputs:
- hidden_out: float32 [8, 1024, 2048], P('fsdp', 'seq')
- grad_hidden: float32 [8, 1024, 2048], P('fsdp', 'seq')
- grad_gains: float32 [1, 2, 2048], replicated
- grad_w_qkv: float32 [1, 2560, 2048], P(None, 'fsdp')
- grad_w_out: float32 [1, 2048, 2048], P(None, 'fsdp')
- grad_w_gate_up: float32 [1, 11264, 2048], P(None, 'fsdp')
- grad_w_down: float32 [1, 2048, 5632], P(None, 'fsdp')
Inputs may be any that keep to these rules, and one draw needn't show every extreme that they name: `positions`: within a sequence, a position is 0 where a document starts (always at the sequence's first token) and one more than the position before it elsewhere. Sequence 0 is a single document.
All inputs are finite; a program needn't handle non-finite values.
Results may differ from a plain program's by a relative error of at most 0.02.
Values may be sent and summed in bfloat16 or wider, within the bound.
A program may use at most 448 MiB of HBM per device.

v0:
```python
import math

import jax
import jax.numpy as jnp
import numpy as np
from jax import lax
from jax.sharding import PartitionSpec as P

H = 32
KVH = 4
HD = 64
FF = 5632
LAYERS = 1


EPS = 1e-05


def rope_tables(position_ids):
    halfway = HD // 2
    frequency = jnp.exp(jnp.arange(halfway, dtype=jnp.float32) * (-2.0 * math.log(10000.0) / HD))
    angles = position_ids.astype(jnp.float32)[..., None] * frequency
    cosines = jnp.cos(angles)
    sines = jnp.sin(angles)
    return (
        jnp.concatenate([cosines, cosines], -1)[..., None, :],
        jnp.concatenate([sines, sines], -1)[..., None, :],
    )


def rotate(values, cosines, sines):
    halfway = values.shape[-1] // 2
    turned = jnp.concatenate([-values[..., halfway:], values[..., :halfway]], -1)
    return values * cosines + turned * sines


def unrotate(grads, cosines, sines):
    halfway = grads.shape[-1] // 2
    scaled = grads * sines
    return grads * cosines + jnp.concatenate([scaled[..., halfway:], -scaled[..., :halfway]], -1)


def normalize(values, gain):
    scale = lax.rsqrt(jnp.mean(values * values, -1, keepdims=True) + EPS)
    return ((values * scale * gain).astype(jnp.bfloat16), scale)


def normalize_back(grads, values, scale, gain):
    unit = values * scale
    gain_grad = jnp.sum((grads * unit).reshape(-1, unit.shape[-1]), 0)
    inner = grads * gain
    return (scale * (inner - unit * jnp.mean(inner * unit, -1, keepdims=True)), gain_grad)


def masked_scores(queries, keys_wide):
    scores = jnp.einsum(
        "qhd,khd->hqk", queries, keys_wide, preferred_element_type=jnp.float32
    ) * queries.shape[-1] ** (-0.5)
    length = queries.shape[0]
    causal = jnp.arange(length)[:, None] >= jnp.arange(length)[None, :]
    return jnp.where(causal[None], scores, -1e30)


def local_attend(operands):
    queries, keys_in, values_in = operands
    repeat_by = queries.shape[1] // keys_in.shape[1]
    keys_wide = jnp.repeat(keys_in, repeat_by, axis=1)
    values_wide = jnp.repeat(values_in, repeat_by, axis=1)
    scores = masked_scores(queries, keys_wide)
    peak = jnp.max(scores, -1, keepdims=True)
    log_total = peak[..., 0] + jnp.log(jnp.sum(jnp.exp(scores - peak), -1))
    weights = jnp.exp(scores - log_total[..., None]).astype(jnp.bfloat16)
    output = jnp.einsum("hqk,khd->qhd", weights, values_wide, preferred_element_type=jnp.float32)
    return (output.astype(jnp.bfloat16), log_total)


def local_attend_back(operands):
    queries, keys_in, values_in, output, log_total, dattn = operands
    length, kv_dev, head_dim = keys_in.shape
    repeat_by = queries.shape[1] // kv_dev
    keys_wide = jnp.repeat(keys_in, repeat_by, axis=1)
    values_wide = jnp.repeat(values_in, repeat_by, axis=1)
    scores = masked_scores(queries, keys_wide)
    probs = jnp.exp(scores - log_total[..., None])
    delta = jnp.sum(output.astype(jnp.float32) * dattn.astype(jnp.float32), -1).T
    dprob = jnp.einsum("qhd,khd->hqk", dattn, values_wide, preferred_element_type=jnp.float32)
    dscore = (probs * (dprob - delta[..., None])).astype(jnp.bfloat16)
    dqueries = jnp.einsum(
        "hqk,khd->qhd", dscore, keys_wide, preferred_element_type=jnp.float32
    ) * head_dim ** (-0.5)
    dkeys = jnp.einsum(
        "hqk,qhd->khd", dscore, queries, preferred_element_type=jnp.float32
    ) * head_dim ** (-0.5)
    dvalues = jnp.einsum(
        "hqk,qhd->khd", probs.astype(jnp.bfloat16), dattn, preferred_element_type=jnp.float32
    )

    def fold_heads(per_head):
        return jnp.sum(per_head.reshape(length, kv_dev, repeat_by, head_dim), 2).astype(
            jnp.bfloat16
        )

    return (dqueries.astype(jnp.bfloat16), fold_heads(dkeys), fold_heads(dvalues))


def project(inputs, weight):
    return lax.dot_general(
        inputs,
        lax.all_gather(weight, "fsdp", axis=0, tiled=True),
        (((1,), (1,)), ((), ())),
        preferred_element_type=jnp.float32,
    )


def project_back(grads, weight):
    shard_rows = lax.all_gather(weight, "fsdp", axis=0, tiled=True)
    picked = lax.slice_in_dim(grads, 0, shard_rows.shape[0], axis=1)
    return jnp.dot(picked, shard_rows, preferred_element_type=jnp.float32)


def weight_grad(grads, inputs, shard_size):
    picked = lax.slice_in_dim(grads, 0, shard_size * lax.axis_size("fsdp"), axis=1)
    summed = lax.psum_scatter(
        lax.dot_general(
            picked, inputs, (((0,), (0,)), ((), ())), preferred_element_type=jnp.float32
        ).astype(jnp.bfloat16),
        "fsdp",
        scatter_dimension=0,
        tiled=True,
    )
    return lax.psum(summed, "seq").astype(jnp.float32)


def backward_pair(grads, inputs, weight):
    wgrad = weight_grad(grads, inputs, weight.shape[0])
    return (project_back(grads, weight), wgrad)


def body(hidden, positions, gains, w_qkv, w_out, w_gate_up, w_down, cotangent):
    seq_count, part_len, model_width = hidden.shape
    row_count = seq_count * part_len
    group_count = lax.axis_size("seq")
    full_len = part_len * group_count
    heads_dev = H // group_count
    share = H // KVH
    kv_dev = max(1, heads_dev // share)
    first_kv = np.arange(group_count) * heads_dev // share
    slot_table = np.concatenate(
        [
            first_kv[:, None] + np.arange(kv_dev)[None, :],
            KVH + first_kv[:, None] + np.arange(kv_dev)[None, :],
        ],
        1,
    ).reshape(-1)
    slot_onehot = jnp.asarray(
        (slot_table[:, None] == np.arange(2 * KVH)[None, :]).astype(np.float32), jnp.bfloat16
    )
    cosines, sines = rope_tables(positions)
    layer_index = 0
    gain = gains[layer_index]
    normed, scale_one = normalize(hidden, gain[0])
    normed_flat = normed.reshape(row_count, model_width)
    joint = project(normed_flat, w_qkv[layer_index]).reshape(seq_count, part_len, -1)
    queries = joint[..., : H * HD].reshape(seq_count, part_len, H, HD)
    keys_in = joint[..., H * HD : (H + KVH) * HD].reshape(seq_count, part_len, KVH, HD)
    values_in = joint[..., (H + KVH) * HD :].reshape(seq_count, part_len, KVH, HD)
    q_rot = rotate(queries, cosines, sines).astype(jnp.bfloat16)
    kv_all = jnp.concatenate(
        [rotate(keys_in, cosines, sines).astype(jnp.bfloat16), values_in.astype(jnp.bfloat16)], 2
    )
    q_send = q_rot.reshape(seq_count, part_len, group_count, heads_dev * HD)
    kv_send = jnp.take(kv_all, slot_table, axis=2).reshape(
        seq_count, part_len, group_count, 2 * kv_dev * HD
    )
    q_heads = lax.all_to_all(q_send, "seq", split_axis=2, concat_axis=1, tiled=True)
    kv_heads = lax.all_to_all(kv_send, "seq", split_axis=2, concat_axis=1, tiled=True)
    q_heads = q_heads.reshape(seq_count, full_len, heads_dev, HD)
    kv_heads = kv_heads.reshape(seq_count, full_len, 2 * kv_dev, HD)
    k_heads = kv_heads[:, :, :kv_dev]
    v_heads = kv_heads[:, :, kv_dev:]
    o_heads, log_total = lax.map(local_attend, (q_heads, k_heads, v_heads))
    o_back = lax.all_to_all(
        o_heads.reshape(seq_count, full_len, 1, heads_dev * HD),
        "seq",
        split_axis=1,
        concat_axis=2,
        tiled=True,
    )
    attn_flat = o_back.reshape(row_count, model_width)
    middle = hidden + project(attn_flat, w_out[layer_index]).reshape(
        seq_count, part_len, model_width
    )
    normed_two, scale_two = normalize(middle, gain[1])
    normed_two_flat = normed_two.reshape(row_count, model_width)
    both = project(normed_two_flat, w_gate_up[layer_index])
    gate_part = both[:, :FF]
    up_part = both[:, FF:]
    activated = (jax.nn.silu(gate_part) * up_part).astype(jnp.bfloat16)
    result = middle + project(activated, w_down[layer_index]).reshape(
        seq_count, part_len, model_width
    )
    saved = [
        (
            hidden,
            normed_flat,
            scale_one,
            q_heads,
            k_heads,
            v_heads,
            o_heads,
            log_total,
            attn_flat,
            middle,
            normed_two_flat,
            scale_two,
            gate_part,
            up_part,
            activated,
        )
    ]
    flowing = cotangent
    grads_qkv = [None] * LAYERS
    grads_out = [None] * LAYERS
    grads_gate_up = [None] * LAYERS
    grads_down = [None] * LAYERS
    gain_terms = [None] * LAYERS
    for layer_index in reversed(range(LAYERS)):
        (
            layer_in,
            normed_flat,
            scale_one,
            q_heads,
            k_heads,
            v_heads,
            o_heads,
            log_total,
            attn_flat,
            middle,
            normed_two_flat,
            scale_two,
            gate_part,
            up_part,
            activated,
        ) = saved[layer_index]
        gain = gains[layer_index]
        dm_cast = flowing.reshape(row_count, model_width).astype(jnp.bfloat16)
        dact, grads_down[layer_index] = backward_pair(dm_cast, activated, w_down[layer_index])
        sigma = jax.nn.sigmoid(gate_part)
        dgate = dact * up_part * sigma * (1.0 + gate_part * (1.0 - sigma))
        dup = dact * gate_part * sigma
        dgu = jnp.concatenate([dgate, dup], 1).astype(jnp.bfloat16)
        dnormed_two, grads_gate_up[layer_index] = backward_pair(
            dgu, normed_two_flat, w_gate_up[layer_index]
        )
        dnormed_two = dnormed_two.reshape(seq_count, part_len, model_width)
        dmid_norm, gain_two = normalize_back(dnormed_two, middle, scale_two, gain[1])
        dmiddle = flowing + dmid_norm
        dy_cast = dmiddle.reshape(row_count, model_width).astype(jnp.bfloat16)
        dattn_wide, grads_out[layer_index] = backward_pair(dy_cast, attn_flat, w_out[layer_index])
        dattn = dattn_wide.astype(jnp.bfloat16)
        dattn_heads = lax.all_to_all(
            dattn.reshape(seq_count, part_len, group_count, heads_dev * HD),
            "seq",
            split_axis=2,
            concat_axis=1,
            tiled=True,
        )
        dattn_heads = dattn_heads.reshape(seq_count, full_len, heads_dev, HD)
        dq_heads, dk_heads, dv_heads = lax.map(
            local_attend_back, (q_heads, k_heads, v_heads, o_heads, log_total, dattn_heads)
        )
        dkv_heads = jnp.concatenate([dk_heads, dv_heads], 2).reshape(
            seq_count, full_len, 1, 2 * kv_dev * HD
        )
        dq_tok, dkv_tok = (
            lax.all_to_all(
                dq_heads.reshape(seq_count, full_len, 1, heads_dev * HD),
                "seq",
                split_axis=1,
                concat_axis=2,
                tiled=True,
            ),
            lax.all_to_all(dkv_heads, "seq", split_axis=1, concat_axis=2, tiled=True),
        )
        dqueries = dq_tok.reshape(seq_count, part_len, H, HD)
        dkv_sum = jnp.einsum(
            "stnd,nm->stmd",
            dkv_tok.reshape(seq_count, part_len, group_count * 2 * kv_dev, HD),
            slot_onehot,
            preferred_element_type=jnp.float32,
        )
        dq_pre = unrotate(dqueries, cosines, sines)
        dk_pre = unrotate(dkv_sum[:, :, :KVH], cosines, sines)
        dvalues = dkv_sum[:, :, KVH:]
        djoint = jnp.concatenate(
            [
                dq_pre.reshape(row_count, -1),
                dk_pre.reshape(row_count, -1),
                dvalues.reshape(row_count, -1),
            ],
            1,
        ).astype(jnp.bfloat16)
        dnormed, grads_qkv[layer_index] = backward_pair(djoint, normed_flat, w_qkv[layer_index])
        dnormed = dnormed.reshape(seq_count, part_len, model_width)
        dcur_norm, gain_one = normalize_back(dnormed, layer_in, scale_one, gain[0])
        gain_terms[layer_index] = jnp.stack([gain_one, gain_two])
        flowing = dmiddle + dcur_norm
    gain_total = lax.psum(jnp.stack(gain_terms), ("fsdp", "seq"))
    return (
        result,
        flowing,
        gain_total,
        jnp.stack(grads_qkv),
        jnp.stack(grads_out),
        jnp.stack(grads_gate_up),
        jnp.stack(grads_down),
    )


def solution(mesh):
    placed = (
        P("fsdp", "seq", None),
        P("fsdp", "seq"),
        P(),
        P(None, "fsdp", None),
        P(None, "fsdp", None),
        P(None, "fsdp", None),
        P(None, "fsdp", None),
        P("fsdp", "seq", None),
    )
    return jax.shard_map(
        body,
        mesh=mesh,
        in_specs=placed,
        out_specs=(
            P("fsdp", "seq", None),
            P("fsdp", "seq", None),
            P(),
            P(None, "fsdp", None),
            P(None, "fsdp", None),
            P(None, "fsdp", None),
            P(None, "fsdp", None),
        ),
        check_vma=False,
    )
```

profile of v0, /device:TPU:0, one launch (start us, length us, event | category | flops | bytes accessed | tf_op | source)
XLA Modules:
  0.0 2009.0 jit_solution(14080543616072539957)
XLA Ops:
  11.3 100.5 %all-gather.9.cloned.1.call-done = bf16[1,2560,2048]{2,1,0:T(8,128)(2,1)} async-done(((bf16[1,320,2048]{2,1,0:T(8,128)(2,1)}), bf16[1,2560,2048]{2,1,0:T(8,128)(2,1)}) %all-gather.9.cloned.1.call-update) | async-done | bytes 10485776 | tf_op jit(solution)/shard_map/all_gather | solution.py:109
  137.4 12.1 all-to-all-done.1
  151.1 13.7 fusion.9
  164.8 14.4 exponential_reduce_fusion
  179.3 16.1 convolution_convert_fusion.3
  200.8 8.1 reduce.12
  211.5 16.6 all_to_all.84
  235.7 7.5 multiply_reduce_fusion.2
  243.1 344.0 %all-gather.13.cloned.1.call-done = bf16[1,11264,2048]{2,1,0:T(8,128)(2,1)} async-done(((bf16[1,1408,2048]{2,1,0:T(8,128)(2,1)}), bf16[1,11264,2048]{2,1,0:T(8,128)(2,1)}) %all-gather.13.cloned.1.call-update) | async-done | bytes 46137360 | tf_op jit(solution)/shard_map/all_gather | solution.py:109
  587.1 24.6 %fusion.2 = f32[256,11264]{1,0:T(8,128)} fusion(bf16[1,11264,2048]{2,1,0:T(8,128)(2,1)} %all-gather.13.cloned.1.call-done, f32[1,256,2048]{2,1,0:T(8,128)} %get-tuple-element.111, f32[2048]{0:T(1024)S(1)} %bitcast.271, f32[256]{0:T(256)S(1)} %add_rsqrt_fusion), kind=kOutput, calls=%fused_computation.3 | convolution fusion | flops 11812732928 | bytes 59778048 | tf_op jit(solution)/shard_map/dot_general | solution.py:107
  611.7 177.9 %all-gather.15.cloned.1.call-done = bf16[1,2048,5632]{2,1,0:T(8,128)(2,1)} async-done(((bf16[1,256,5632]{2,1,0:T(8,128)(2,1)}), bf16[1,2048,5632]{2,1,0:T(8,128)(2,1)}) %all-gather.15.cloned.1.call-update) | async-done | bytes 23068688 | tf_op jit(solution)/shard_map/all_gather | solution.py:109
  789.6 19.7 multiply_convert_fusion.2
  809.3 21.8 %fusion.36 = (f32[2048]{0:T(1024)}, f32[256]{0:T(256)S(1)}, f32[256,2048]{1,0:T(8,128)S(1)}) fusion(f32[1,256,2048]{2,1,0:T(8,128)} %get-tuple-element.111, f32[256]{0:T(256)S(1)} %add_rsqrt_fusion, f32[2048]{0:T(1024)S(1)} %bitcast.272, bf16[1,11264,2048]{2,1,0:T(8,128)(2,1)} %all-gather.13.cloned.1.call-done, bf16[256,5632]{1,0:T(8,128)(2,1)} %get-tuple-element.92, ...), kind=kOutput, calls=%fused_computation.42 | convolution fusion | flops 11825838080 | bytes 56117248 | tf_op jit(solution)/shard_map/dot_general | solution.py:118
  838.1 6.7 fusion.33
  847.0 18.3 all_to_all.85
  871.6 20.9 %multiply_convert_fusion = bf16[8,1024,1024]{1,2,0:T(8,128)(2,1)} fusion(f32[8,1024,1024]{1,2,0:T(8,128)} %get-tuple-element.109, f32[8,1024]{1,0:T(8,128)S(1)} %bitcast.275, f32[8,1024]{1,0:T(8,128)S(1)} %log_add_fusion, pred[1024,1024]{0,1:T(8,128)(4,1)S(1)} %iota_compare_fusion, bf16[1024,8,64]{0,2,1:T(8,128)(2,1)} %squeeze.54, ...), kind=kOutput, calls=%fused_computation.6 | convolution fusion | flops 1124073472 | bytes 52625408 | tf_op jit(solution)/shard_map/while/body/eval_jaxpr/qhd,khd->hqk/dot_general | solution.py:86
  892.6 11.5 multiply_reduce_fusion
  904.1 15.5 fusion.48
  926.9 8.8 multiply_convert_fusion.4
  939.6 8.1 reduce.14
  958.6 7.8 all-to-all-done.4
  980.2 7.5 convolution_convert_fusion.1
  987.8 13.2 convert_bitcast_fusion
  1001.1 21.8 %convolution_convert_fusion = bf16[11264,2048]{1,0:T(8,128)(2,1)} fusion(bf16[256,5632]{1,0:T(8,128)(2,1)} %get-tuple-element.92, bf16[256,5632]{1,0:T(8,128)(2,1)} %get-tuple-element.91, f32[1,256,2048]{2,1,0:T(8,128)} %get-tuple-element.111, f32[2048]{0:T(1024)S(1)} %bitcast.274, f32[256]{0:T(256)S(1)} %add_rsqrt_fusion), kind=kOutput, calls=%fused_computation.5 | convolution fusion | flops 11847335936 | bytes 54010880 | tf_op jit(solution)/shard_map/dot_general | solution.py:124
  1023.0 71.6 %reduce-scatter.7.cloned.1.call-done = bf16[320,2048]{1,0:T(8,128)(2,1)} async-done(((bf16[2560,2048]{1,0:T(8,128)(2,1)}), bf16[320,2048]{1,0:T(8,128)(2,1)}) %reduce-scatter.7.cloned.1.call-update) | async-done | bytes 1310736 | tf_op jit(solution)/shard_map/reduce_scatter | solution.py:123
  1094.6 228.2 %reduce-scatter.11.cloned.1.call-done = bf16[256,5632]{0,1:T(8,128)(2,1)} async-done(((bf16[2048,5632]{0,1:T(8,128)(2,1)}), bf16[256,5632]{0,1:T(8,128)(2,1)}) %reduce-scatter.11.cloned.1.call-update) | async-done | bytes 2883600 | tf_op jit(solution)/shard_map/reduce_scatter | solution.py:123
  1322.7 444.5 %reduce-scatter.13.cloned.1.call-done = bf16[1408,2048]{1,0:T(8,128)(2,1)} async-done(((bf16[11264,2048]{1,0:T(8,128)(2,1)}), bf16[1408,2048]{1,0:T(8,128)(2,1)}) %reduce-scatter.13.cloned.1.call-update) | async-done | bytes 5767184
  1767.3 14.7 fusion.30
  1781.9 9.1 fusion.37
  1791.0 39.0 %psum.35 = f32[1,2,2048]{2,1,0:T(2,128)} all-reduce(f32[1,2,2048]{2,1,0:T(2,128)S(1)} %maximum_bitcast_fusion.3), channel_id=1, replica_groups=mesh['fsdp'=8,'seq'=4] {'fsdp','seq'}, use_global_device_ids=true, to_apply=%region_10.11 | all-reduce | flops 4096 | bytes 32768 | tf_op jit(solution)/shard_map/psum | solution.py:308
  1834.1 151.1 %all-reduce.4.cloned.1.call-done = (bf16[1,256,5632]{1,2,0:T(8,128)(2,1)}, bf16[1,320,2048]{2,1,0:T(8,128)(2,1)}, bf16[1,256,2048]{2,1,0:T(8,128)(2,1)}, bf16[1,1408,2048]{2,1,0:T(8,128)(2,1)}) async-done(((bf16[1,256,5632]{1,2,0:T(8,128)(2,1)}, bf16[1,320,2048]{2,1,0:T(8,128)(2,1)}, bf16[1,256,2048]{2,1,0:T(8,128)(2,1)}, bf16[1,1408,2048]{2,1,0:T(8,128)(2,1)}), (bf16[1,256,5632]{1,2,0:T(8,128)(2,1)}, ...) | async-done | bytes 11010064 | tf_op jit(solution)/shard_map/psum | solution.py:131
  1993.6 8.7 stack.45
  (157 shorter events, 110.6 us)
Async XLA Ops:
  7.2 104.6 %all-gather.9.cloned.1.call-start = ((), (), s32[]{:S(2)}) async-start(), calls=%async_computation.13 | async-start | bytes 11796480 | tf_op jit(solution)/shard_map/all_gather | solution.py:109
  7.9 227.8 %all-gather.11.cloned.1.call-start = ((), (), s32[]{:S(2)}) async-start(), calls=%async_computation.14 | async-start | bytes 9437184 | tf_op jit(solution)/shard_map/all_gather | solution.py:109
  8.7 578.5 %all-gather.13.cloned.1.call-start = ((), (), s32[]{:S(2)}) async-start(), calls=%async_computation.15 | async-start | bytes 51904512 | tf_op jit(solution)/shard_map/all_gather | solution.py:109
  9.4 1.6 copy-start.1
  9.4 1.8 copy-start.19
  9.4 780.2 %all-gather.15.cloned.1.call-start = ((), (), s32[]{:S(2)}) async-start(), calls=%async_computation.16 | async-start | bytes 25952256 | tf_op jit(solution)/shard_map/all_gather | solution.py:109
  10.3 117.4 %copy-start.14 = (f32[256,64]{0,1:T(8,128)}, f32[256,64]{0,1:T(8,128)S(1)}, u32[]{:S(2)}) copy-start(f32[256,64]{0,1:T(8,128)S(1)} %maximum_bitcast_fusion.1) | copy-start | bytes 196612
  11.0 116.4 %copy-start.12 = (f32[256,64]{0,1:T(8,128)}, f32[256,64]{0,1:T(8,128)S(1)}, u32[]{:S(2)}) copy-start(f32[256,64]{0,1:T(8,128)S(1)} %maximum_bitcast_fusion.2) | copy-start | bytes 196612
  11.2 106.2 %copy-start.20 = (f32[256]{0:T(256)}, f32[256]{0:T(256)S(1)}, u32[]{:S(2)}) copy-start(f32[256]{0:T(256)S(1)} %add_rsqrt_fusion.1) | copy-start | bytes 3076
  11.3 106.2 %copy-start.17 = (f32[1,1,2048]{2,1,0:T(1,128)}, f32[1,1,2048]{2,1,0:T(1,128)S(1)}, u32[]{:S(2)}) copy-start(f32[1,1,2048]{2,1,0:T(1,128)S(1)} %get-tuple-element.105) | copy-start | bytes 24580
  123.4 9.4 all-to-all-start
  132.9 16.6 all-to-all-start.1
  136.4 886.6 %reduce-scatter.9.cloned.1.call-start = ((), (), s32[]{:S(2)}) async-start(), calls=%async_computation.11 | async-start | bytes 9437184 | tf_op jit(solution)/shard_map/reduce_scatter | solution.py:123
  137.4 27.4 %copy-start.9 = (bf16[1024,64]{0,1:T(8,128)(2,1)}, bf16[1024,64]{0,1:T(8,128)(2,1)S(1)}, u32[]{:S(2)}) copy-start(bf16[1024,64]{0,1:T(8,128)(2,1)S(1)} %get-tuple-element.100) | copy-start | bytes 393220
  151.0 13.7 copy-start.4
  230.4 5.3 copy-start.2
  587.1 202.5 %copy-start.5 = (f32[1,256,2048]{2,1,0:T(8,128)S(1)}, f32[1,256,2048]{2,1,0:T(8,128)}, u32[]{:S(2)}) copy-start(f32[1,256,2048]{2,1,0:T(8,128)} %param.17) | copy-start | bytes 6291460
  809.3 21.8 %copy-start.6 = (f32[1,256,2048]{2,1,0:T(8,128)S(1)}, f32[1,256,2048]{2,1,0:T(8,128)}, u32[]{:S(2)}) copy-start(f32[1,256,2048]{2,1,0:T(8,128)} %param.17) | copy-start | bytes 6291460
  809.3 21.8 %copy-start.7 = (f32[1,256,2048]{2,1,0:T(8,128)S(1)}, f32[1,256,2048]{2,1,0:T(8,128)}, u32[]{:S(2)}) copy-start(f32[1,256,2048]{2,1,0:T(8,128)} %get-tuple-element.111) | copy-start | bytes 6291460
  919.6 7.3 copy-start.10
  923.0 26.6 %all-to-all-start.5 = ((bf16[4,2,16384]{2,1,0:T(2,128)(2,1)}), bf16[4,2,16384]{2,1,0:T(2,128)(2,1)S(1)}, u32[]{:S(2)}, u32[]{:S(2)}) async-start(bf16[4,2,16384]{2,1,0:T(2,128)(2,1)} %reshape.568), calls=%async_computation.5 | async-start | bytes 524288 | tf_op jit(solution)/shard_map/all_to_all | solution.py:283
  947.6 10.3 copy-start.23
  949.6 8.7 copy-start.13
  949.7 8.8 copy-start.15
  949.7 16.7 all-to-all-start.4
  954.0 140.6 %reduce-scatter.7.cloned.1.call-start = ((), (), s32[]{:S(2)}) async-start(), calls=%async_computation.10 | async-start | bytes 11796480 | tf_op jit(solution)/shard_map/reduce_scatter | solution.py:123
  987.8 334.9 %reduce-scatter.11.cloned.1.call-start = ((), (), s32[]{:S(2)}) async-start(), calls=%async_computation.12 | async-start | bytes 25952256 | tf_op jit(solution)/shard_map/reduce_scatter | solution.py:123
  1001.1 766.2 %reduce-scatter.13.cloned.1.call-start = ((), (), s32[]{:S(2)}) async-start(), calls=%async_computation.17 | async-start | bytes 51904512
  1022.9 962.3 %all-reduce.4.cloned.1.call-start = ((), (), s32[]{:S(2)}) async-start(), calls=%async_computation.18 | async-start | bytes 22020096 | tf_op jit(solution)/shard_map/psum | solution.py:131
  1781.9 9.1 copy-start.22
  1985.2 2.9 copy-start.16
  1985.2 4.7 copy-start.11
  (7 other events, 9.0 us)
Sparse Core Ops, SparseCore 0:
  9.6 102.0 all-gather.8
  113.3 80.3 all-gather.10
  195.4 391.6 all-gather.12
  588.6 200.9 all-gather.14
  838.2 87.6 reduce-scatter.8
  987.9 106.5 reduce-scatter.6
  1096.9 225.7 reduce-scatter.10
  1325.1 442.1 reduce-scatter.12
  1771.2 213.9 all-reduce.3
where the time goes:
time: 2010 us
  waiting for transfers between devices  1540 us (77%)
  matrix products  245 us (12%)
  blocking collectives  73.9 us (4%)
  other arithmetic  60.3 us (3%)
  local copies, waits for them, and re-layouts  56.1 us (3%)
    all_gather x4, waiting for transfers between devices, project(): lax.all_gather(weight, 'fsdp', axis=0, tiled=True)  622 us
    unnamed x10, waiting for transfers between devices  447 us
    reduce_scatter x3, waiting for transfers between devices, weight_grad(): lax.psum_scatter(lax.dot_general(picked, inputs, (((0,), (0,)), ((), ()))...  300 us
    psum x1, waiting for transfers between devices, weight_grad(): return lax.psum(summed, 'seq').astype(jnp.float32)  151 us
    dot_general x4, matrix products, project_back(): return jnp.dot(picked, shard_rows, preferred_element_type=jnp.float32)  57.3 us
    dot_general x4, matrix products, project(): lax.dot_general(inputs, lax.all_gather(weight, 'fsdp', axis=0, tiled=True...  52.4 us
    dot_general x4, matrix products, weight_grad(): lax.dot_general(picked, inputs, (((0,), (0,)), ((), ())), preferred_eleme...  48.1 us
  transfers between devices with their start and end apart: 13, of which 10 were waited for; matrix products, arithmetic and copies ran while one was open for 15% of the time, Pallas kernels for 0%

commit v1 on v0

--- a/solution.py
+++ b/solution.py
@@ -4,7 +4,10 @@
 import jax.numpy as jnp
 import numpy as np
 from jax import lax
+from jax.experimental import pallas as pl
+from jax.experimental.pallas import tpu as pltpu
 from jax.sharding import PartitionSpec as P
+
 
 H = 32
 KVH = 4
@@ -317,6 +320,459 @@
     )
 
 
+def neighbour(values, step):
+    count = lax.axis_size("seq")
+    return lax.ppermute(values, "seq", [(i, i ^ step) for i in range(count)])
+
+
+def gather_tokens(block):
+    half = block.shape[0] // 2
+    side = neighbour(block, 1)
+    below = neighbour(block, 2)
+    far_top = neighbour(side[:half], 2)
+    far_bottom = neighbour(below[half:], 1)
+    return jnp.concatenate([block, side, below, far_top, far_bottom], 0)
+
+
+def scatter_tokens(partial):
+    count = lax.axis_size("seq")
+    blocks = partial.reshape(count, 2, -1, partial.shape[-1])
+    top, bottom = blocks[:, 0], blocks[:, 1]
+    from_side = neighbour(jnp.stack([top[1], top[3]]), 1)
+    from_below = neighbour(jnp.stack([bottom[2], bottom[3]]), 2)
+    wide = jnp.float32
+    second_top = neighbour((top[2].astype(wide) + from_side[1].astype(wide)).astype(partial.dtype), 2)
+    second_bottom = neighbour((bottom[1].astype(wide) + from_below[1].astype(wide)).astype(partial.dtype), 1)
+    return jnp.concatenate(
+        [
+            top[0].astype(wide) + from_side[0].astype(wide) + second_top.astype(wide),
+            bottom[0].astype(wide) + from_below[0].astype(wide) + second_bottom.astype(wide),
+        ],
+        0,
+    )
+
+
+def gather_shards(block, axis):
+    count = lax.axis_size("seq")
+    index = lax.axis_index("seq")
+    half = block.shape[0] // 2
+    side = neighbour(block, 1)
+    below = neighbour(block, 2)
+    far = jnp.concatenate([neighbour(side[:half], 2), neighbour(below[half:], 1)], 0)
+    shape = list(block.shape)
+    shape.insert(axis, count)
+    whole = jnp.zeros(shape, jnp.float32)
+    for step, part in enumerate((block, side, below, far)):
+        whole = lax.dynamic_update_index_in_dim(whole, part.astype(jnp.float32), index ^ step, axis)
+    return whole
+
+
+def matmul(left, right, left_dim, right_dim):
+    return lax.dot_general(
+        left, right, (((left_dim,), (right_dim,)), ((), ())), preferred_element_type=jnp.float32
+    )
+
+
+ROOT = HD ** (-0.5)
+LIMIT = 60 * 1024 * 1024
+
+
+def swap_halves(values):
+    width = values.shape[1]
+    half = HD // 2
+    column = lax.broadcasted_iota(jnp.int32, values.shape, 1)
+    return jnp.where(
+        column % HD < half, pltpu.roll(values, width - half, 1), pltpu.roll(values, half, 1)
+    )
+
+
+def spread_tables(table, pairs, last):
+    half = HD // 2
+    cosines, sines = table[:, :half], table[:, half:]
+    ones, zeros = jnp.ones_like(table), jnp.zeros_like(table)
+    tail = [[cosines, cosines, ones], [-sines, sines, zeros]] if last else [[], []]
+    if not pairs:
+        return jnp.concatenate(tail[0], 1), jnp.concatenate(tail[1], 1)
+    cosines = [jnp.concatenate([cosines] * 4, 1)] * pairs
+    sines = [jnp.concatenate([-sines, sines] * 2, 1)] * pairs
+    if last:
+        cosines.append(jnp.concatenate(tail[0], 1))
+        sines.append(jnp.concatenate(tail[1], 1))
+    return jnp.concatenate(cosines, 1), jnp.concatenate(sines, 1)
+
+
+def qkv_kernel(index_ref, normed_ref, weight_ref, table_ref, q_ref, k_ref, v_ref):
+    heads = q_ref.shape[0]
+    joint = matmul(normed_ref[...], weight_ref[...], 1, 1)
+    cosines, sines = spread_tables(table_ref[...], heads // 2, True)
+    turned = joint * cosines + swap_halves(joint) * sines
+    for head in range(heads):
+        q_ref[head] = (turned[:, head * HD : (head + 1) * HD].astype(jnp.bfloat16).astype(jnp.float32) * ROOT).astype(
+            jnp.bfloat16
+        )
+    k_ref[...] = turned[:, heads * HD : (heads + 1) * HD].astype(jnp.bfloat16)
+    v_ref[...] = turned[:, (heads + 1) * HD :].astype(jnp.bfloat16)
+
+
+def project_qkv(index, normed, weight, table, count):
+    length, width = normed.shape
+    part = length // count
+    heads = weight.shape[0] // HD - 2
+    return pl.pallas_call(
+        qkv_kernel,
+        out_shape=(
+            jax.ShapeDtypeStruct((heads, length, HD), jnp.bfloat16),
+            jax.ShapeDtypeStruct((length, HD), jnp.bfloat16),
+            jax.ShapeDtypeStruct((length, HD), jnp.bfloat16),
+        ),
+        grid_spec=pltpu.PrefetchScalarGridSpec(
+            num_scalar_prefetch=1,
+            grid=(count,),
+            in_specs=[
+                pl.BlockSpec((part, width), lambda i, s: (i, 0)),
+                pl.BlockSpec(weight.shape, lambda i, s: (0, 0)),
+                pl.BlockSpec((part, table.shape[1]), lambda i, s: (i, 0)),
+            ],
+            out_specs=[
+                pl.BlockSpec((heads, part, HD), lambda i, s: (0, i ^ s[0], 0)),
+                pl.BlockSpec((part, HD), lambda i, s: (i ^ s[0], 0)),
+                pl.BlockSpec((part, HD), lambda i, s: (i ^ s[0], 0)),
+            ],
+        ),
+        compiler_params=pltpu.CompilerParams(vmem_limit_bytes=LIMIT),
+        name="project_qkv",
+    )(index, normed, weight, table)
+
+
+def attend_kernel(count, index_ref, q_ref, k_ref, v_ref, weight_ref, sent_ref, attn_ref, lse_ref, held_ref):
+    heads, part, _ = q_ref.shape
+    here = pl.program_id(0)
+    row = lax.broadcasted_iota(jnp.int32, (part, part), 0)
+    column = lax.broadcasted_iota(jnp.int32, (part, part), 1)
+    for block in range(count):
+
+        @pl.when(here == block)
+        def _():
+            before = block * part
+            seen = before + part
+            keys_in, values_in = k_ref[:seen], v_ref[:seen]
+
+            def one_head(head, carry):
+                scores = matmul(q_ref[head], keys_in, 1, 1)
+                last = jnp.where(row >= column, scores[:, before:], -1e30)
+                scores = jnp.concatenate([scores[:, :before], last], 1) if block else last
+                peak = jnp.max(scores, 1, keepdims=True)
+                weights = jnp.exp(scores - peak)
+                total = jnp.sum(weights, 1, keepdims=True)
+                output = matmul(weights.astype(jnp.bfloat16), values_in, 1, 0) / total
+                held_ref[head] = output.astype(jnp.bfloat16)
+                log_total = jnp.broadcast_to(peak + jnp.log(total), (part, 128))
+                lse_ref[pl.ds(head, 1), :] = jnp.transpose(log_total)[:1]
+                return carry
+
+            lax.fori_loop(0, heads, one_head, 0, unroll=2)
+
+    attn = jnp.concatenate([held_ref[head] for head in range(heads)], 1)
+    attn_ref[...] = attn
+    sent_ref[...] = matmul(attn, weight_ref[...], 1, 1).astype(jnp.bfloat16)
+
+
+def attend(index, queries, keys_in, values_in, weight, count):
+    heads, length, _ = queries.shape
+    part = length // count
+    width = weight.shape[0]
+    return pl.pallas_call(
+        lambda *refs: attend_kernel(count, *refs),
+        out_shape=(
+            jax.ShapeDtypeStruct((length, width), jnp.bfloat16),
+            jax.ShapeDtypeStruct((length, heads * HD), jnp.bfloat16),
+            jax.ShapeDtypeStruct((heads, length), jnp.float32),
+        ),
+        grid_spec=pltpu.PrefetchScalarGridSpec(
+            num_scalar_prefetch=1,
+            grid=(count,),
+            in_specs=[
+                pl.BlockSpec((heads, part, HD), lambda i, s: (0, i, 0)),
+                pl.BlockSpec((length, HD), lambda i, s: (0, 0)),
+                pl.BlockSpec((length, HD), lambda i, s: (0, 0)),
+                pl.BlockSpec(weight.shape, lambda i, s: (0, 0)),
+            ],
+            out_specs=[
+                pl.BlockSpec((part, width), lambda i, s: (i ^ s[0], 0)),
+                pl.BlockSpec((part, heads * HD), lambda i, s: (i ^ s[0], 0)),
+                pl.BlockSpec((heads, part), lambda i, s: (0, i)),
+            ],
+            scratch_shapes=[pltpu.VMEM((heads, part, HD), jnp.bfloat16)],
+        ),
+        compiler_params=pltpu.CompilerParams(vmem_limit_bytes=LIMIT),
+        name="attend",
+    )(index, queries, keys_in, values_in, weight)
+
+
+def attend_back_kernel(
+    count, index_ref, q_ref, k_ref, v_ref, attn_ref, lse_ref, dy_ref, weight_ref, table_ref, pick_ref,
+    out_ref, turned_ref, do_ref, delta_ref, dq_ref, dk_ref, dv_ref,
+):
+    heads, part, _ = q_ref.shape
+    wide = jnp.float32
+    here = pl.program_id(0)
+    index = index_ref[0]
+    spot = here ^ index
+
+    @pl.when(here == 0)
+    def _():
+        dk_ref[...] = jnp.zeros_like(dk_ref)
+        dv_ref[...] = jnp.zeros_like(dv_ref)
+
+    dattn = matmul(dy_ref[...], weight_ref[...], 1, 0).astype(jnp.bfloat16)
+    product = dattn.astype(wide) * attn_ref[...].astype(wide)
+    owner = lax.broadcasted_iota(jnp.int32, (heads, heads * HD), 1) // HD
+    same = owner == lax.broadcasted_iota(jnp.int32, (heads, heads * HD), 0)
+    delta_ref[...] = lax.dot_general(
+        same.astype(wide), product, (((1,), (1,)), ((), ())),
+        precision=lax.Precision.HIGHEST, preferred_element_type=wide,
+    )
+    for head in range(heads):
+        do_ref[head] = dattn[:, head * HD : (head + 1) * HD]
+    row = lax.broadcasted_iota(jnp.int32, (part, part), 0)
+    column = lax.broadcasted_iota(jnp.int32, (part, part), 1)
+    for block in range(count):
+
+        @pl.when(here == block)
+        def _():
+            before = block * part
+            seen = before + part
+            keys_in, values_in = k_ref[:seen], v_ref[:seen]
+
+            def one_head(head, carry):
+                query, dout = q_ref[head], do_ref[head]
+                scores = matmul(keys_in, query, 1, 1)
+                last = jnp.where(row <= column, scores[before:], -1e30)
+                scores = jnp.concatenate([scores[:before], last], 0) if block else last
+                probs = jnp.exp(scores - lse_ref[pl.ds(head, 1), :])
+                dprob = matmul(values_in, dout, 1, 1)
+                dscore = (probs * (dprob - delta_ref[pl.ds(head, 1), :])).astype(jnp.bfloat16)
+                dv_ref[:seen] += matmul(probs.astype(jnp.bfloat16), dout, 1, 0)
+                dk_ref[:seen] += matmul(dscore, query, 1, 0)
+                dq_ref[head] = (matmul(dscore, keys_in, 0, 0) * ROOT).astype(jnp.bfloat16)
+                return carry
+
+            lax.fori_loop(0, heads, one_head, 0, unroll=2)
+
+    def unturn(grads, cosines, sines):
+        return grads * cosines + swap_halves(grads * sines)
+
+    rows_here = pl.ds(pl.multiple_of(spot * part, part), part)
+    dq = jnp.concatenate([dq_ref[head] for head in range(heads)], 1).astype(wide)
+    dq = unturn(dq, *spread_tables(table_ref[rows_here, :], heads // 2, False))
+    out_ref[rows_here, : heads * HD] = dq.astype(jnp.bfloat16)
+
+    @pl.when(here == count - 1)
+    def _():
+        for block in range(count):
+            rows_there = pl.ds(pl.multiple_of((block ^ index) * part, part), part)
+            rows_block = slice(block * part, (block + 1) * part)
+            both = jnp.concatenate([dk_ref[rows_block], dv_ref[rows_block]], 1).astype(jnp.bfloat16).astype(wide)
+            both = unturn(both, *spread_tables(table_ref[rows_there, :], 0, True))
+            out_ref[rows_there, heads * HD :] = both.astype(jnp.bfloat16)
+        chosen = matmul(pick_ref[...], out_ref[...], 1, 1).astype(jnp.bfloat16)
+        size = turned_ref.shape[1]
+        for block in range(count):
+            turned_ref[block] = chosen[block * size : (block + 1) * size]
+
+
+def attend_back(index, queries, keys_in, values_in, attn, lse, dy, weight, table, pick, count):
+    heads, length, _ = queries.shape
+    part = length // count
+    width = weight.shape[0]
+    columns = (heads + 2) * HD
+    return pl.pallas_call(
+        lambda *refs: attend_back_kernel(count, *refs),
+        out_shape=(
+            jax.ShapeDtypeStruct((length, columns), jnp.bfloat16),
+            jax.ShapeDtypeStruct((count, columns // count, length), jnp.bfloat16),
+        ),
+        grid_spec=pltpu.PrefetchScalarGridSpec(
+            num_scalar_prefetch=1,
+            grid=(count,),
+            in_specs=[
+                pl.BlockSpec((heads, part, HD), lambda i, s: (0, i, 0)),
+                pl.BlockSpec((length, HD), lambda i, s: (0, 0)),
+                pl.BlockSpec((length, HD), lambda i, s: (0, 0)),
+                pl.BlockSpec((part, heads * HD), lambda i, s: (i ^ s[0], 0)),
+                pl.BlockSpec((heads, part), lambda i, s: (0, i)),
+                pl.BlockSpec((part, width), lambda i, s: (i ^ s[0], 0)),
+                pl.BlockSpec(weight.shape, lambda i, s: (0, 0)),
+                pl.BlockSpec(table.shape, lambda i, s: (0, 0)),
+                pl.BlockSpec(pick.shape, lambda i, s: (0, 0)),
+            ],
+            out_specs=[
+                pl.BlockSpec((length, columns), lambda i, s: (0, 0)),
+                pl.BlockSpec((count, columns // count, length), lambda i, s: (0, 0, 0)),
+            ],
+            scratch_shapes=[
+                pltpu.VMEM((heads, part, HD), jnp.bfloat16),
+                pltpu.VMEM((heads, part), jnp.float32),
+                pltpu.VMEM((heads, part, HD), jnp.bfloat16),
+                pltpu.VMEM((length, HD), jnp.float32),
+                pltpu.VMEM((length, HD), jnp.float32),
+            ],
+        ),
+        compiler_params=pltpu.CompilerParams(vmem_limit_bytes=LIMIT),
+        name="attend_back",
+    )(index, queries, keys_in, values_in, attn, lse, dy, weight, table, pick)
+
+
+def fast_body(hidden, positions, gains, w_qkv, w_out, w_gate_up, w_down, cotangent):
+    count = lax.axis_size("seq")
+    fsdp = lax.axis_size("fsdp")
+    index = lax.axis_index("seq")
+    place = index.astype(jnp.int32).reshape(1)
+    current = hidden[0]
+    part_len, width = current.shape
+    length = part_len * count
+    heads = H // count
+    gain = gains[0]
+    after = lax.optimization_barrier
+
+    rows = w_qkv.shape[1]
+    group = math.gcd(rows, HD)
+    chunk = group // count
+    per_head = HD // group
+    qkv_part = lax.dynamic_index_in_dim(
+        w_qkv[0].reshape(rows // group, count, chunk, width), index, 1, keepdims=False
+    ).reshape(rows // count, width)
+    qkv_part = lax.all_gather(qkv_part, "fsdp", axis=0, tiled=True)
+
+    def by_owner(values):
+        values = values.reshape(H + 2 * KVH, per_head, chunk, width)
+        return jnp.concatenate(
+            [
+                values[:H].reshape(count, H // count, per_head, chunk, width),
+                values[H : H + KVH].reshape(count, KVH // count, per_head, chunk, width),
+                values[H + KVH :].reshape(count, KVH // count, per_head, chunk, width),
+            ],
+            1,
+        )
+
+    qkv_rows = lax.all_to_all(by_owner(qkv_part), "seq", 0, 0, tiled=True)
+    qkv_rows = jnp.transpose(qkv_rows, (1, 2, 0, 3, 4)).reshape(-1, width)
+    out_cols = lax.all_gather(
+        lax.dynamic_slice_in_dim(w_out[0], index * heads * HD, heads * HD, 1), "fsdp", axis=0, tiled=True
+    )
+    gu_rows = w_gate_up.shape[1] // count
+    gate_up = lax.all_gather(
+        lax.dynamic_slice_in_dim(w_gate_up[0], index * gu_rows, gu_rows, 0), "fsdp", axis=0, tiled=True
+    )
+    units = FF // count
+    down_rows = w_down.shape[1]
+    down_cols = lax.all_gather(
+        lax.dynamic_index_in_dim(
+            w_down[0].reshape(down_rows, fsdp // 2, count, gu_rows), index, 2, keepdims=False
+        ).reshape(down_rows, units),
+        "fsdp",
+        axis=0,
+        tiled=True,
+    )
+
+    normed, scale_one = normalize(current, gain[0])
+    normed_all = gather_tokens(normed)
+    spots = positions[0]
+    spots = jnp.concatenate([spots] + [neighbour(spots, step) for step in range(1, count)])
+    frequency = jnp.exp(jnp.arange(HD // 2, dtype=jnp.float32) * (-2.0 * math.log(10000.0) / HD))
+    angles = spots.astype(jnp.float32)[:, None] * frequency
+    table = jnp.concatenate([jnp.cos(angles), jnp.sin(angles)], 1)
+    flowing = cotangent[0]
+    normed_all, qkv_rows, dm_sent = after((normed_all, qkv_rows, flowing.astype(jnp.bfloat16)))
+    dm_all = gather_tokens(dm_sent)
+    queries, keys_in, values_in = project_qkv(place, normed_all, qkv_rows, table, count)
+    sent, attn_flat, log_total = attend(place, queries, keys_in, values_in, out_cols, count)
+    middle = current + scatter_tokens(sent)
+    normed_two, scale_two = normalize(middle, gain[1])
+    normed_two_all = gather_tokens(normed_two)
+    both = matmul(normed_two_all, gate_up, 1, 1)
+    gate_part, up_part = both[:, :units], both[:, units:]
+    activated = (jax.nn.silu(gate_part) * up_part).astype(jnp.bfloat16)
+    down_sent = matmul(activated, down_cols, 1, 1).astype(jnp.bfloat16)
+
+
+    def owned(grad):
+        return lax.psum_scatter(grad.astype(jnp.bfloat16), "fsdp", scatter_dimension=0, tiled=True)
+
+    term_down = matmul(dm_all, activated, 0, 0).astype(jnp.bfloat16)
+    dm_all, term_down = after((dm_all, term_down))
+    grad_down = owned(term_down)
+    dact = matmul(dm_all, down_cols, 1, 0)
+    sigma = jax.nn.sigmoid(gate_part)
+    dgate = dact * up_part * sigma * (1.0 + gate_part * (1.0 - sigma))
+    dup = dact * gate_part * sigma
+    dgu = jnp.concatenate([dgate, dup], 1).astype(jnp.bfloat16)
+    term_gate_up = matmul(dgu, normed_two_all, 0, 0).astype(jnp.bfloat16)
+    dnormed_two = scatter_tokens(matmul(dgu, gate_up, 1, 0).astype(jnp.bfloat16))
+    dnormed_two, term_gate_up = after((dnormed_two, term_gate_up))
+    grad_gate_up = owned(term_gate_up)
+    dmid_norm, gain_two = normalize_back(dnormed_two, middle, scale_two, gain[1])
+    dmiddle = flowing + dmid_norm
+    dy_all = gather_tokens(dmiddle.astype(jnp.bfloat16))
+    dy_all, down_sent, grad_down = after((dy_all, down_sent, grad_down))
+    result = middle + scatter_tokens(down_sent)
+    grad_out = owned(matmul(dy_all, attn_flat, 0, 0))
+    share = KVH // count
+    pieces = heads + 2 * share
+    picked = np.arange(pieces * HD).reshape(pieces * per_head, count, chunk).transpose(1, 0, 2).reshape(-1)
+    pick = jnp.asarray(picked[:, None] == np.arange(pieces * HD)[None, :], jnp.bfloat16)
+    djoint, djoint_turned = attend_back(
+        place, queries, keys_in, values_in, attn_flat, log_total, dy_all, out_cols, table, pick, count
+    )
+    dnormed = scatter_tokens(matmul(djoint, qkv_rows, 1, 0).astype(jnp.bfloat16))
+
+    whole = jnp.zeros((count,) + djoint_turned.shape[1:], jnp.bfloat16)
+    for step in range(count):
+        part = lax.dynamic_index_in_dim(djoint_turned, index ^ step, 0, keepdims=False)
+        if step:
+            part = neighbour(part, step).reshape(-1, count, part_len)
+            part = jnp.concatenate([part[:, step ^ block] for block in range(count)], 1)
+        whole = lax.dynamic_update_index_in_dim(whole, part, index ^ step, 0)
+    whole = whole.reshape(count, pieces, per_head, chunk, length)
+    whole = jnp.concatenate(
+        [
+            whole[:, :heads].reshape(-1, length),
+            whole[:, heads : heads + share].reshape(-1, length),
+            whole[:, heads + share :].reshape(-1, length),
+        ],
+        0,
+    )
+    term_qkv = matmul(whole, normed_all, 1, 0)
+    grad_qkv = owned(term_qkv)
+    gain_one = jnp.sum(term_qkv * qkv_part.astype(jnp.float32), 0) / gain[0]
+    gain_total = jnp.stack([gain_one, gain_two])[None]
+    for axis in ("seq", "fsdp"):
+        step = 1
+        while step < lax.axis_size(axis):
+            pairs = [(i, i ^ step) for i in range(lax.axis_size(axis))]
+            gain_total = gain_total + lax.ppermute(gain_total, axis, pairs)
+            step *= 2
+    unit = current * scale_one
+    inner = dnormed * gain[0]
+    dcur_norm = scale_one * (inner - unit * jnp.mean(inner * unit, -1, keepdims=True))
+    qkv_shard = gather_shards(grad_qkv.reshape(rows // group, chunk, width), 1)
+    down_shard = gather_shards(grad_down.reshape(down_rows, fsdp // 2, gu_rows), 2)
+    return (
+        result[None],
+        (dmiddle + dcur_norm)[None],
+        gain_total,
+        qkv_shard.reshape(1, rows, width),
+        gather_shards(grad_out, 1).reshape(1, down_rows, width),
+        gather_shards(grad_gate_up, 0).reshape(1, -1, width),
+        down_shard.reshape(1, down_rows, FF),
+    )
+
+
+def fits(mesh):
+    count, fsdp = mesh.shape["seq"], mesh.shape["fsdp"]
+    return count == KVH == 4 and fsdp % 2 == 0 and fsdp & (fsdp - 1) == 0
+
+
 def solution(mesh):
     placed = (
         P("fsdp", "seq", None),
@@ -328,8 +784,9 @@
         P(None, "fsdp", None),
         P("fsdp", "seq", None),
     )
+    fast = fits(mesh)
     return jax.shard_map(
-        body,
+        fast_body if fast else body,
         mesh=mesh,
         in_specs=placed,
         out_specs=(

time: 2010 us -> 734 us (0.37)
  waiting for transfers between devices: 1540 us -> 323 us
  matrix products: 245 us -> 102 us
  blocking collectives: 73.9 us -> 0 us
  Pallas kernels: 0 us -> 65.7 us
  starting transfers between devices: 15.8 us -> 72.9 us
  local copies, waits for them, and re-layouts: 56.1 us -> 82.7 us
    all_gather x4, waiting for transfers between devices: 622 us -> 22.8 us  [the longest x1 22.8 us: fast_body(): qkv_part = lax.all_gather(qkv_part, 'fsdp', axis=0, tiled=True)]
    unnamed x10 -> x8, waiting for transfers between devices: 447 us -> 0.81 us
    reduce_scatter x3 -> x4, waiting for transfers between devices: 300 us -> 0.03 us  [owned(): lax.psum_scatter(grad.astype(jnp.bfloat16), 'fsdp', scatter_dimension=0,...]
    ppermute x0 -> x59, waiting for transfers between devices: none -> 299 us  [the longest x54 277 us: neighbour(): return lax.ppermute(values, 'seq', [(i, i ^ step) for i in range(count)])]
    psum x1 -> x0, waiting for transfers between devices: 151 us -> none  [weight_grad(): return lax.psum(summed, 'seq').astype(jnp.float32)]
    dot_general x19 -> x9, matrix products: 245 us -> 102 us  [matmul(): lax.dot_general(left, right, (((left_dim,), (right_dim,)), ((), ())), pre...]
    ppermute x0 -> x59, starting transfers between devices: none -> 67.8 us  [the longest x54 64.1 us: neighbour(): return lax.ppermute(values, 'seq', [(i, i ^ step) for i in range(count)])]
    pallas_call x0 -> x3, Pallas kernels: none -> 65.7 us  [the longest x1 33.6 us: attend_back(): pl.pallas_call(lambda *refs: attend_back_kernel(count, *refs), out_shape=...]
  transfers between devices with their start and end apart: 13 -> 68, of which waited for: 10 -> 37; matrix products, arithmetic and copies ran while one was open for 15% -> 26% of each run, Pallas kernels for 0% -> 9%
where the time goes in v1:
time: 734 us; the launch traced here: 724 us
  waiting for transfers between devices  323 us (44%)
  matrix products  102 us (14%)
  local copies, waits for them, and re-layouts  82.7 us (11%)
  starting transfers between devices  72.9 us (10%)
  Pallas kernels  65.7 us (9%)
  other arithmetic  62.1 us (8%)
  between operations  15.7 us (2%)
    ppermute x54, waiting for transfers between devices, neighbour(): return lax.ppermute(values, 'seq', [(i, i ^ step) for i in range(count)])  277 us
    dot_general x9, matrix products, matmul(): lax.dot_general(left, right, (((left_dim,), (right_dim,)), ((), ())), pre...  102 us
    ppermute x54, starting transfers between devices, neighbour(): return lax.ppermute(values, 'seq', [(i, i ^ step) for i in range(count)])  64.1 us
    unnamed x111, local copies, waits for them, and re-layouts  41.4 us
    pallas_call x1, Pallas kernels, attend_back(): pl.pallas_call(lambda *refs: attend_back_kernel(count, *refs), out_shape=...  33.6 us
    pallas_call x1, Pallas kernels, attend(): pl.pallas_call(lambda *refs: attend_kernel(count, *refs), out_shape=(jax....  23 us
    all_gather x1, waiting for transfers between devices, fast_body(): qkv_part = lax.all_gather(qkv_part, 'fsdp', axis=0, tiled=True)  22.8 us
    ppermute x5, waiting for transfers between devices, fast_body(): gain_total = gain_total + lax.ppermute(gain_total, axis, pairs)  22.4 us
  transfers between devices with their start and end apart: 68, of which 37 were waited for; matrix products, arithmetic and copies ran while one was open for 26% of the time, Pallas kernels for 9%

profile of v1, /device:TPU:0, one launch (start us, length us, event | category | flops | bytes accessed | tf_op | source)
XLA Modules:
  0.0 724.1 jit_solution(17741381148886265865)
XLA Ops:
  23.9 22.8 %all-gather.7.cloned.1.call-done = bf16[640,2048]{1,0:T(8,128)(2,1)} async-done(((bf16[80,2048]{1,0:T(8,128)(2,1)}), bf16[640,2048]{1,0:T(8,128)(2,1)}) %all-gather.7.cloned.1.call-update) | async-done | bytes 2621456 | tf_op jit(solution)/shard_map/all_gather | solution.py:645
  69.4 28.3 %collective-permute-done.2 = bf16[128,2048]{1,0:T(8,128)(2,1)S(1)} collective-permute-done((bf16[128,2048]{1,0:T(8,128)(2,1)S(1)}, bf16[128,2048]{1,0:T(8,128)(2,1)S(1)}, u32[]{:S(2)}, u32[]{:S(2)}) %collective-permute-start.2) | collective-permute-done | bytes 524320 | tf_op jit(solution)/shard_map/ppermute | solution.py:325
  103.0 9.1 %project_qkv.1 = (bf16[8,1024,64]{2,1,0:T(8,128)(2,1)}, bf16[1024,64]{1,0:T(8,128)(2,1)}, bf16[1024,64]{1,0:T(8,128)(2,1)}) custom-call(s32[1]{0:T(128)} %bitcast.index_ref.refs_0_, bf16[1024,2048]{1,0:T(8,128)(2,1)} %constant_dynamic-update-slice_fusion.normed_ref, bf16[640,2048]{1,0:T(8,128)(2,1)} %bitcast.395, f32[1024,64]{1,0:T(8,128)} %pad_maximum_fusion.13.table_ref.refs_8_), custom_call_target="tpu_custom_call" | custom-call | tf_op jit(solution)/shard_map/project_qkv/pallas_call | solution.py:421
  112.1 23.0 %attend.1 = (bf16[1024,2048]{1,0:T(8,128)(2,1)}, bf16[1024,512]{1,0:T(8,128)(2,1)}, f32[8,1024]{1,0:T(8,128)}) custom-call(s32[1]{0:T(128)} %bitcast.index_ref.refs_0_, bf16[8,1024,64]{2,1,0:T(8,128)(2,1)} %get-tuple-element.27.refs_1_, bf16[1024,64]{1,0:T(8,128)(2,1)} %get-tuple-element.28.refs_2_, bf16[1024,64]{1,0:T(8,128)(2,1)} %get-tuple-element.29.refs_3_, ...), custom_call_target="tpu_custom_call" | custom-call | tf_op jit(solution)/shard_map/attend/pallas_call | solution.py:484
  139.3 22.2 %collective-permute-done.7 = bf16[2,128,2048]{2,1,0:T(8,128)(2,1)S(1)} collective-permute-done((bf16[2,128,2048]{2,1,0:T(8,128)(2,1)S(1)}, bf16[2,128,2048]{2,1,0:T(8,128)(2,1)S(1)}, u32[]{:S(2)}, u32[]{:S(2)}) %collective-permute-start.7) | collective-permute-done | bytes 1048608 | tf_op jit(solution)/shard_map/ppermute | solution.py:325
  163.6 11.7 %collective-permute-done.8 = bf16[128,2048]{1,0:T(8,128)(2,1)S(1)} collective-permute-done((bf16[128,2048]{1,0:T(8,128)(2,1)S(1)}, bf16[128,2048]{1,0:T(8,128)(2,1)S(1)}, u32[]{:S(2)}, u32[]{:S(2)}) %collective-permute-start.8) | collective-permute-done | bytes 524320 | tf_op jit(solution)/shard_map/ppermute | solution.py:325
  200.0 15.7 %collective-permute-done.11 = bf16[256,2048]{1,0:T(8,128)(2,1)S(1)} collective-permute-done((bf16[256,2048]{1,0:T(8,128)(2,1)}, bf16[256,2048]{1,0:T(8,128)(2,1)S(1)}, u32[]{:S(2)}, u32[]{:S(2)}) %collective-permute-start.11) | collective-permute-done | bytes 1048608 | tf_op jit(solution)/shard_map/ppermute | solution.py:325
  220.9 9.6 %collective-permute-done.13 = bf16[128,2048]{1,0:T(8,128)(2,1)S(1)} collective-permute-done((bf16[128,2048]{1,0:T(8,128)(2,1)S(1)}, bf16[128,2048]{1,0:T(8,128)(2,1)S(1)}, u32[]{:S(2)}, u32[]{:S(2)}) %collective-permute-start.13) | collective-permute-done | bytes 524320 | tf_op jit(solution)/shard_map/ppermute | solution.py:325
  230.6 7.5 %collective-permute-done.15 = bf16[256,2048]{1,0:T(8,128)(2,1)S(1)} collective-permute-done((bf16[256,2048]{1,0:T(8,128)(2,1)S(1)}, bf16[256,2048]{1,0:T(8,128)(2,1)S(1)}, u32[]{:S(2)}, u32[]{:S(2)}) %collective-permute-start.15) | collective-permute-done | bytes 1048608 | tf_op jit(solution)/shard_map/ppermute | solution.py:325
  239.0 7.3 %collective-permute-done.14 = bf16[128,2048]{1,0:T(8,128)(2,1)S(1)} collective-permute-done((bf16[128,2048]{1,0:T(8,128)(2,1)S(1)}, bf16[128,2048]{1,0:T(8,128)(2,1)S(1)}, u32[]{:S(2)}, u32[]{:S(2)}) %collective-permute-start.14) | collective-permute-done | bytes 524320 | tf_op jit(solution)/shard_map/ppermute | solution.py:325
  262.0 17.3 %fusion.2 = f32[1024,2816]{1,0:T(8,128)S(1)} fusion(bf16[1024,2048]{1,0:T(8,128)(2,1)} %constant_dynamic-update-slice_fusion.10, bf16[1,2816,2048]{2,1,0:T(8,128)(2,1)} %all-gather.13.cloned.1.call-done), kind=kOutput, calls=%fused_computation.2 | convolution fusion | flops 11811160064 | bytes 27262976 | tf_op jit(solution)/shard_map/dot_general | solution.py:371
  286.2 8.7 %convolution_convert_fusion.1 = bf16[2048,1408]{1,0:T(8,128)(2,1)} fusion(bf16[1024,2048]{1,0:T(8,128)(2,1)S(1)} %copy-done.29, bf16[1024,1408]{1,0:T(8,128)(2,1)S(1)} %multiply_convert_fusion.2), kind=kOutput, calls=%fused_computation.5 | convolution fusion | flops 5908463616 | bytes 12845056 | tf_op jit(solution)/shard_map/dot_general | solution.py:371
  294.9 14.3 %multiply_convert_fusion.1 = (bf16[1024,1408]{1,0:T(8,128)(2,1)S(1)}, bf16[1024,1408]{1,0:T(8,128)(2,1)S(1)}) fusion(f32[1024,2816]{1,0:T(8,128)} %copy-done.6, bf16[1024,2048]{1,0:T(8,128)(2,1)} %copy-done.28, bf16[2048,1408]{0,1:T(8,128)(2,1)} %all-gather.9.cloned.1.call-done), kind=kOutput, calls=%fused_computation.8 | convolution fusion | flops 5924323328 | bytes 27262976 | tf_op jit(solution)/shard_map/dot_general | solution.py:371
  309.2 17.0 %fusion.4 = bf16[1024,2048]{1,0:T(8,128)(2,1)S(1)} fusion(bf16[1,2816,2048]{2,1,0:T(8,128)(2,1)} %all-gather.13.cloned.1.call-done, bf16[1024,1408]{1,0:T(8,128)(2,1)S(1)} %get-tuple-element.104, bf16[1024,1408]{1,0:T(8,128)(2,1)S(1)} %get-tuple-element.103), kind=kOutput, calls=%fused_computation.12 | convolution fusion | flops 11824791552 | bytes 21495808 | tf_op jit(solution)/shard_map/dot_general | solution.py:371
  330.9 13.6 %collective-permute-done.19 = bf16[2,128,2048]{2,1,0:T(8,128)(2,1)S(1)} collective-permute-done((bf16[2,128,2048]{2,1,0:T(8,128)(2,1)S(1)}, bf16[2,128,2048]{2,1,0:T(8,128)(2,1)S(1)}, u32[]{:S(2)}, u32[]{:S(2)}) %collective-permute-start.19) | collective-permute-done | bytes 1048608 | tf_op jit(solution)/shard_map/ppermute | solution.py:325
  351.6 5.6 collective-permute-done.20
  359.4 17.8 %convolution_convert_fusion = bf16[2816,2048]{1,0:T(8,128)(2,1)} fusion(bf16[1024,2048]{1,0:T(8,128)(2,1)} %constant_dynamic-update-slice_fusion.10, bf16[1024,1408]{1,0:T(8,128)(2,1)S(1)} %copy-done.42, bf16[1024,1408]{1,0:T(8,128)(2,1)S(1)} %copy-done.40), kind=kOutput, calls=%fused_computation.4 | convolution fusion | flops 11828461568 | bytes 21495808 | tf_op jit(solution)/shard_map/dot_general | solution.py:371
  385.2 16.3 %collective-permute-done.23 = bf16[256,2048]{1,0:T(8,128)(2,1)S(1)} collective-permute-done((bf16[256,2048]{1,0:T(8,128)(2,1)S(1)}, bf16[256,2048]{1,0:T(8,128)(2,1)S(1)}, u32[]{:S(2)}, u32[]{:S(2)}) %collective-permute-start.23) | collective-permute-done | bytes 1048608 | tf_op jit(solution)/shard_map/ppermute | solution.py:325
  402.4 8.2 %convolution_convert_fusion.3 = bf16[1024,2048]{1,0:T(8,128)(2,1)} fusion(bf16[1024,1408]{1,0:T(8,128)(2,1)S(1)} %copy-done.18, bf16[2048,1408]{0,1:T(8,128)(2,1)S(1)} %bitcast.455), kind=kOutput, calls=%fused_computation.14 | convolution fusion | flops 5907677184 | bytes 12845056 | tf_op jit(solution)/shard_map/dot_general | solution.py:371
  414.3 5.6 collective-permute-done.26
  420.7 5.9 convolution_convert_fusion.4
  426.7 33.6 %attend_back.1 = (bf16[1024,640]{1,0:T(8,128)(2,1)}, bf16[4,160,1024]{2,1,0:T(8,128)(2,1)}) custom-call(s32[1]{0:T(128)} %bitcast.index_ref.refs_0_, bf16[8,1024,64]{2,1,0:T(8,128)(2,1)} %get-tuple-element.27.refs_1_, bf16[1024,64]{1,0:T(8,128)(2,1)} %get-tuple-element.28.refs_2_, bf16[1024,64]{1,0:T(8,128)(2,1)} %get-tuple-element.29.refs_3_, ...), custom_call_target="tpu_custom_call" | custom-call | tf_op jit(solution)/shard_map/attend_back/pallas_call | solution.py:589
  476.8 7.5 %fusion.40 = (bf16[640,2048]{1,0:T(8,128)(2,1)}, f32[2048]{0:T(1024)S(1)}) fusion(bf16[640,2048]{1,0:T(8,128)(2,1)S(1)} %copy-done.13, bf16[1024,2048]{1,0:T(8,128)(2,1)} %constant_dynamic-update-slice_fusion.normed_ref, bf16[64,1024]{1,0:T(8,128)(2,1)S(1)} %bitcast.445, bf16[64,1024]{1,0:T(8,128)(2,1)S(1)} %bitcast.444, bf16[512,1024]{1,0:T(8,128)(2,1)S(1)} %bitcast.424), kind=kOutput, calls=%fused_computation.209 | convolution fusion | flops 2693527552 | bytes 10756096 | tf_op jit(solution)/shard_map/dot_general | solution.py:371
  498.8 20.4 %collective-permute-done.38 = f32[1,2,2048]{2,1,0:T(2,128)S(1)} collective-permute-done((f32[1,2,2048]{2,1,0:T(2,128)S(1)}, f32[1,2,2048]{2,1,0:T(2,128)S(1)}, u32[]{:S(2)}, u32[]{:S(2)}) %collective-permute-start.38) | collective-permute-done | bytes 16416 | tf_op jit(solution)/shard_map/ppermute | solution.py:753
  544.9 8.0 %collective-permute-done.27 = bf16[2,128,2048]{2,1,0:T(8,128)(2,1)S(1)} collective-permute-done((bf16[2,128,2048]{2,1,0:T(8,128)(2,1)}, bf16[2,128,2048]{2,1,0:T(8,128)(2,1)S(1)}, u32[]{:S(2)}, u32[]{:S(2)}) %collective-permute-start.27) | collective-permute-done | bytes 1048608 | tf_op jit(solution)/shard_map/ppermute | solution.py:325
  556.3 34.0 %collective-permute-done.57 = bf16[128,4,352]{0,2,1:T(8,128)(2,1)S(1)} collective-permute-done((bf16[128,4,352]{0,2,1:T(8,128)(2,1)S(1)}, bf16[128,4,352]{0,2,1:T(8,128)(2,1)S(1)}, u32[]{:S(2)}, u32[]{:S(2)}) %collective-permute-start.57) | collective-permute-done | bytes 360480 | tf_op jit(solution)/shard_map/ppermute | solution.py:325
  592.5 6.2 copy.176
  604.7 6.7 collective-permute-done.28
  617.0 9.9 %collective-permute-done.30 = bf16[128,2048]{1,0:T(8,128)(2,1)S(1)} collective-permute-done((bf16[128,2048]{1,0:T(8,128)(2,1)S(1)}, bf16[128,2048]{1,0:T(8,128)(2,1)S(1)}, u32[]{:S(2)}, u32[]{:S(2)}) %collective-permute-start.30) | collective-permute-done | bytes 524320 | tf_op jit(solution)/shard_map/ppermute | solution.py:325
  658.6 6.7 collective-permute-done.44
  675.9 22.8 %collective-permute-done.51 = bf16[352,2048]{1,0:T(8,128)(2,1)S(1)} collective-permute-done((bf16[352,2048]{1,0:T(8,128)(2,1)}, bf16[352,2048]{1,0:T(8,128)(2,1)S(1)}, u32[]{:S(2)}, u32[]{:S(2)}) %collective-permute-start.51) | collective-permute-done | bytes 1441824 | tf_op jit(solution)/shard_map/ppermute | solution.py:325
  702.0 8.9 %collective-permute-done.53 = bf16[176,2048]{1,0:T(8,128)(2,1)S(1)} collective-permute-done((bf16[176,2048]{1,0:T(8,128)(2,1)S(1)}, bf16[176,2048]{1,0:T(8,128)(2,1)S(1)}, u32[]{:S(2)}, u32[]{:S(2)}) %collective-permute-start.53) | collective-permute-done | bytes 720928 | tf_op jit(solution)/shard_map/ppermute | solution.py:325
  (356 shorter events, 256.1 us)
Async XLA Ops:
  7.2 39.5 %all-gather.7.cloned.1.call-start = ((), (), s32[]{:S(2)}) async-start(), calls=%async_computation.5 | async-start | bytes 2949120 | tf_op jit(solution)/shard_map/all_gather | solution.py:645
  9.3 102.8 %all-gather.11.cloned.1.call-start = ((), (), s32[]{:S(2)}) async-start(), calls=%async_computation.11 | async-start | bytes 2359296 | tf_op jit(solution)/shard_map/all_gather | solution.py:660
  11.2 250.9 %all-gather.13.cloned.1.call-start = ((), (), s32[]{:S(2)}) async-start(), calls=%async_computation.12 | async-start | bytes 12976128 | tf_op jit(solution)/shard_map/all_gather | solution.py:664
  15.9 44.4 %collective-permute-start = (bf16[256,2048]{1,0:T(8,128)(2,1)}, bf16[256,2048]{1,0:T(8,128)(2,1)S(1)}, u32[]{:S(2)}, u32[]{:S(2)}) collective-permute-start(bf16[256,2048]{1,0:T(8,128)(2,1)} %get-tuple-element.102), channel_id=1, source_target_pairs={{0,1},{1,0},{2,3},{3,2},{4,5},{5,4},{6,7},{7,6},{8,9},{9,8},{10,11... | collective-permute-start | bytes 3145736 | tf_op jit(solution)/shard_map/ppermute | solution.py:325
  18.8 44.4 %collective-permute-start.1 = (bf16[256,2048]{1,0:T(8,128)(2,1)}, bf16[256,2048]{1,0:T(8,128)(2,1)}, u32[]{:S(2)}, u32[]{:S(2)}) collective-permute-start(bf16[256,2048]{1,0:T(8,128)(2,1)} %get-tuple-element.102), channel_id=1, source_target_pairs={{0,2},{1,3},{2,0},{3,1},{4,6},{5,7},{6,4},{7,5},{8,10},{9,11},{10,... | collective-permute-start | bytes 3145736 | tf_op jit(solution)/shard_map/ppermute | solution.py:325
  20.4 38.0 %collective-permute-start.4 = (s32[256]{0:T(256)S(1)}, s32[256]{0:T(256)S(1)}, u32[]{:S(2)}, u32[]{:S(2)}) collective-permute-start(s32[256]{0:T(256)S(1)} %bitcast.450), channel_id=1, source_target_pairs={{0,1},{1,0},{2,3},{3,2},{4,5},{5,4},{6,7},{7,6},{8,9},{9,8},{10,11... | collective-permute-start | bytes 3080 | tf_op jit(solution)/shard_map/ppermute | solution.py:325
  20.9 37.4 %collective-permute-start.5 = (s32[256]{0:T(256)S(1)}, s32[256]{0:T(256)S(1)}, u32[]{:S(2)}, u32[]{:S(2)}) collective-permute-start(s32[256]{0:T(256)S(1)} %bitcast.451), channel_id=1, source_target_pairs={{0,2},{1,3},{2,0},{3,1},{4,6},{5,7},{6,4},{7,5},{8,10},{9,11},{10,... | collective-permute-start | bytes 3080 | tf_op jit(solution)/shard_map/ppermute | solution.py:325
  20.9 37.4 %collective-permute-start.6 = (s32[256]{0:T(256)S(1)}, s32[256]{0:T(256)S(1)}, u32[]{:S(2)}, u32[]{:S(2)}) collective-permute-start(s32[256]{0:T(256)S(1)} %bitcast.452), channel_id=1, source_target_pairs={{0,3},{1,2},{2,1},{3,0},{4,7},{5,6},{6,5},{7,4},{8,11},{9,10},{10,... | collective-permute-start | bytes 3080 | tf_op jit(solution)/shard_map/ppermute | solution.py:325
  50.9 48.6 %all-to-all-start = ((bf16[4,10,1,16,2048]{4,3,1,2,0:T(8,128)(2,1)}), bf16[4,10,1,16,2048]{4,3,1,2,0:T(8,128)(2,1)}, u32[]{:S(2)}, u32[]{:S(2)}) async-start(bf16[4,10,1,16,2048]{4,3,1,2,0:T(8,128)(2,1)} %pad_maximum_fusion.3), calls=%async_computation | async-start | bytes 5242880 | tf_op jit(solution)/shard_map/all_to_all | solution.py:658
  55.4 239.5 %all-gather.9.cloned.1.call-start = ((), (), s32[]{:S(2)}) async-start(), calls=%async_computation.6 | async-start | bytes 6488064 | tf_op jit(solution)/shard_map/all_gather | solution.py:669
  60.3 37.4 %collective-permute-start.2 = (bf16[128,2048]{1,0:T(8,128)(2,1)S(1)}, bf16[128,2048]{1,0:T(8,128)(2,1)S(1)}, u32[]{:S(2)}, u32[]{:S(2)}) collective-permute-start(bf16[128,2048]{1,0:T(8,128)(2,1)S(1)} %slice.472), channel_id=1, source_target_pairs={{0,2},{1,3},{2,0},{3,1},{4,6},{5,7},{6,4},{7,5},{8,10},{9,11},{10,... | collective-permute-start | bytes 1572872 | tf_op jit(solution)/shard_map/ppermute | solution.py:325
  64.3 34.2 %collective-permute-start.3 = (bf16[128,2048]{1,0:T(8,128)(2,1)S(1)}, bf16[128,2048]{1,0:T(8,128)(2,1)S(1)}, u32[]{:S(2)}, u32[]{:S(2)}) collective-permute-start(bf16[128,2048]{1,0:T(8,128)(2,1)S(1)} %slice.473), channel_id=1, source_target_pairs={{0,1},{1,0},{2,3},{3,2},{4,5},{5,4},{6,7},{7,6},{8,9},{9,8},{10,11... | collective-permute-start | bytes 1572872 | tf_op jit(solution)/shard_map/ppermute | solution.py:325
  186.3 234.4 %reduce-scatter.5.cloned.1.call-start = ((), (), s32[]{:S(2)}) async-start(), calls=%async_computation.7 | async-start | bytes 6488064 | tf_op jit(solution)/shard_map/reduce_scatter | solution.py:700
  186.5 29.1 %collective-permute-start.11 = (bf16[256,2048]{1,0:T(8,128)(2,1)}, bf16[256,2048]{1,0:T(8,128)(2,1)S(1)}, u32[]{:S(2)}, u32[]{:S(2)}) collective-permute-start(bf16[256,2048]{1,0:T(8,128)(2,1)} %bitcast_convert_fusion), channel_id=1, source_target_pairs={{0,1},{1,0},{2,3},{3,2},{4,5},{5,4},{6,7},{7,6},{8,9},{9,8},{10,11... | collective-permute-start | bytes 3145736 | tf_op jit(solution)/shard_map/ppermute | solution.py:325
  187.1 32.0 %collective-permute-start.12 = (bf16[256,2048]{1,0:T(8,128)(2,1)}, bf16[256,2048]{1,0:T(8,128)(2,1)S(1)}, u32[]{:S(2)}, u32[]{:S(2)}) collective-permute-start(bf16[256,2048]{1,0:T(8,128)(2,1)} %bitcast_convert_fusion), channel_id=1, source_target_pairs={{0,2},{1,3},{2,0},{3,1},{4,6},{5,7},{6,4},{7,5},{8,10},{9,11},{10,... | collective-permute-start | bytes 3145736 | tf_op jit(solution)/shard_map/ppermute | solution.py:325
  198.5 39.6 %collective-permute-start.15 = (bf16[256,2048]{1,0:T(8,128)(2,1)S(1)}, bf16[256,2048]{1,0:T(8,128)(2,1)S(1)}, u32[]{:S(2)}, u32[]{:S(2)}) collective-permute-start(bf16[256,2048]{1,0:T(8,128)(2,1)S(1)} %get-tuple-element.98), channel_id=1, source_target_pairs={{0,1},{1,0},{2,3},{3,2},{4,5},{5,4},{6,7},{7,6},{8,9},{9,8},{10,11... | collective-permute-start | bytes 3145736 | tf_op jit(solution)/shard_map/ppermute | solution.py:325
  216.6 35.3 %collective-permute-start.16 = (bf16[256,2048]{1,0:T(8,128)(2,1)S(1)}, bf16[256,2048]{1,0:T(8,128)(2,1)S(1)}, u32[]{:S(2)}, u32[]{:S(2)}) collective-permute-start(bf16[256,2048]{1,0:T(8,128)(2,1)S(1)} %get-tuple-element.98), channel_id=1, source_target_pairs={{0,2},{1,3},{2,0},{3,1},{4,6},{5,7},{6,4},{7,5},{8,10},{9,11},{10,... | collective-permute-start | bytes 3145736 | tf_op jit(solution)/shard_map/ppermute | solution.py:325
  219.2 27.2 %collective-permute-start.14 = (bf16[128,2048]{1,0:T(8,128)(2,1)S(1)}, bf16[128,2048]{1,0:T(8,128)(2,1)S(1)}, u32[]{:S(2)}, u32[]{:S(2)}) collective-permute-start(bf16[128,2048]{1,0:T(8,128)(2,1)S(1)} %slice.490), channel_id=1, source_target_pairs={{0,1},{1,0},{2,3},{3,2},{4,5},{5,4},{6,7},{7,6},{8,9},{9,8},{10,11... | collective-permute-start | bytes 1572872 | tf_op jit(solution)/shard_map/ppermute | solution.py:325
  328.4 302.9 %reduce-scatter.9.cloned.1.call-start = ((), (), s32[]{:S(2)}) async-start(), calls=%async_computation.9 | async-start | bytes 2359296 | tf_op jit(solution)/shard_map/reduce_scatter | solution.py:700
  426.7 225.8 %reduce-scatter.7.cloned.1.call-start = ((), (), s32[]{:S(2)}) async-start(), calls=%async_computation.8 | async-start | bytes 2949120 | tf_op jit(solution)/shard_map/reduce_scatter | solution.py:700
  484.4 181.8 %reduce-scatter.11.cloned.1.call-start = ((), (), s32[]{:S(2)}) async-start(), calls=%async_computation.10 | async-start | bytes 12976128 | tf_op jit(solution)/shard_map/reduce_scatter | solution.py:700
  486.6 48.9 %collective-permute-start.55 = (bf16[256,4,352]{0,2,1:T(8,128)(2,1)}, bf16[256,4,352]{0,2,1:T(8,128)(2,1)S(1)}, u32[]{:S(2)}, u32[]{:S(2)}) collective-permute-start(bf16[256,4,352]{0,2,1:T(8,128)(2,1)} %bitcast.115), channel_id=1, source_target_pairs={{0,1},{1,0},{2,3},{3,2},{4,5},{5,4},{6,7},{7,6},{8,9},{9,8},{10,11... | collective-permute-start | bytes 2162696 | tf_op jit(solution)/shard_map/ppermute | solution.py:325
  487.2 49.4 %collective-permute-start.56 = (bf16[256,4,352]{0,2,1:T(8,128)(2,1)}, bf16[256,4,352]{0,2,1:T(8,128)(2,1)}, u32[]{:S(2)}, u32[]{:S(2)}) collective-permute-start(bf16[256,4,352]{0,2,1:T(8,128)(2,1)} %bitcast.115), channel_id=1, source_target_pairs={{0,2},{1,3},{2,0},{3,1},{4,6},{5,7},{6,4},{7,5},{8,10},{9,11},{10,... | collective-permute-start | bytes 2162696 | tf_op jit(solution)/shard_map/ppermute | solution.py:325
  496.4 45.9 %collective-permute-start.31 = (bf16[2,128,2048]{2,1,0:T(8,128)(2,1)}, bf16[2,128,2048]{2,1,0:T(8,128)(2,1)}, u32[]{:S(2)}, u32[]{:S(2)}) collective-permute-start(bf16[2,128,2048]{2,1,0:T(8,128)(2,1)} %pad_maximum_fusion.11), channel_id=1, source_target_pairs={{0,1},{1,0},{2,3},{3,2},{4,5},{5,4},{6,7},{7,6},{8,9},{9,8},{10,11... | collective-permute-start | bytes 3145736 | tf_op jit(solution)/shard_map/ppermute | solution.py:325
  526.6 26.3 %collective-permute-start.27 = (bf16[2,128,2048]{2,1,0:T(8,128)(2,1)}, bf16[2,128,2048]{2,1,0:T(8,128)(2,1)S(1)}, u32[]{:S(2)}, u32[]{:S(2)}) collective-permute-start(bf16[2,128,2048]{2,1,0:T(8,128)(2,1)} %pad_maximum_fusion.9), channel_id=1, source_target_pairs={{0,1},{1,0},{2,3},{3,2},{4,5},{5,4},{6,7},{7,6},{8,9},{9,8},{10,11... | collective-permute-start | bytes 3145736 | tf_op jit(solution)/shard_map/ppermute | solution.py:325
  533.9 64.9 %collective-permute-start.33 = (bf16[2,128,2048]{2,1,0:T(8,128)(2,1)}, bf16[2,128,2048]{2,1,0:T(8,128)(2,1)S(1)}, u32[]{:S(2)}, u32[]{:S(2)}) collective-permute-start(bf16[2,128,2048]{2,1,0:T(8,128)(2,1)} %pad_maximum_fusion.12), channel_id=1, source_target_pairs={{0,2},{1,3},{2,0},{3,1},{4,6},{5,7},{6,4},{7,5},{8,10},{9,11},{10,... | collective-permute-start | bytes 3145736 | tf_op jit(solution)/shard_map/ppermute | solution.py:325
  535.5 69.2 %collective-permute-start.29 = (bf16[2,128,2048]{2,1,0:T(8,128)(2,1)S(1)}, bf16[2,128,2048]{2,1,0:T(8,128)(2,1)}, u32[]{:S(2)}, u32[]{:S(2)}) collective-permute-start(bf16[2,128,2048]{2,1,0:T(8,128)(2,1)S(1)} %copy-done.21), channel_id=1, source_target_pairs={{0,2},{1,3},{2,0},{3,1},{4,6},{5,7},{6,4},{7,5},{8,10},{9,11},{10,... | collective-permute-start | bytes 3145736 | tf_op jit(solution)/shard_map/ppermute | solution.py:325
  536.6 53.7 %collective-permute-start.57 = (bf16[128,4,352]{0,2,1:T(8,128)(2,1)S(1)}, bf16[128,4,352]{0,2,1:T(8,128)(2,1)S(1)}, u32[]{:S(2)}, u32[]{:S(2)}) collective-permute-start(bf16[128,4,352]{0,2,1:T(8,128)(2,1)S(1)} %slice.554), channel_id=1, source_target_pairs={{0,2},{1,3},{2,0},{3,1},{4,6},{5,7},{6,4},{7,5},{8,10},{9,11},{10,... | collective-permute-start | bytes 1081352 | tf_op jit(solution)/shard_map/ppermute | solution.py:325
  542.3 49.0 %collective-permute-start.58 = (bf16[128,4,352]{0,2,1:T(8,128)(2,1)S(1)}, bf16[128,4,352]{0,2,1:T(8,128)(2,1)S(1)}, u32[]{:S(2)}, u32[]{:S(2)}) collective-permute-start(bf16[128,4,352]{0,2,1:T(8,128)(2,1)S(1)} %slice.555), channel_id=1, source_target_pairs={{0,1},{1,0},{2,3},{3,2},{4,5},{5,4},{6,7},{7,6},{8,9},{9,8},{10,11... | collective-permute-start | bytes 1081352 | tf_op jit(solution)/shard_map/ppermute | solution.py:325
  552.9 48.7 %collective-permute-start.32 = (bf16[128,2048]{1,0:T(8,128)(2,1)S(1)}, bf16[128,2048]{1,0:T(8,128)(2,1)S(1)}, u32[]{:S(2)}, u32[]{:S(2)}) collective-permute-start(bf16[128,2048]{1,0:T(8,128)(2,1)S(1)} %fusion.17), channel_id=1, source_target_pairs={{0,2},{1,3},{2,0},{3,1},{4,6},{5,7},{6,4},{7,5},{8,10},{9,11},{10,... | collective-permute-start | bytes 1572872 | tf_op jit(solution)/shard_map/ppermute | solution.py:325
  666.2 32.5 %collective-permute-start.51 = (bf16[352,2048]{1,0:T(8,128)(2,1)}, bf16[352,2048]{1,0:T(8,128)(2,1)S(1)}, u32[]{:S(2)}, u32[]{:S(2)}) collective-permute-start(bf16[352,2048]{1,0:T(8,128)(2,1)} %reduce-scatter.11.cloned.1.call-done), channel_id=1, source_target_pairs={{0,1},{1,0},{2,3},{3,2},{4,5},{5,4},{6,7},{7,6},{8,9},{9,8},{10,11... | collective-permute-start | bytes 4325384 | tf_op jit(solution)/shard_map/ppermute | solution.py:325
  667.6 33.0 %collective-permute-start.52 = (bf16[352,2048]{1,0:T(8,128)(2,1)}, bf16[352,2048]{1,0:T(8,128)(2,1)S(1)}, u32[]{:S(2)}, u32[]{:S(2)}) collective-permute-start(bf16[352,2048]{1,0:T(8,128)(2,1)} %reduce-scatter.11.cloned.1.call-done), channel_id=1, source_target_pairs={{0,2},{1,3},{2,0},{3,1},{4,6},{5,7},{6,4},{7,5},{8,10},{9,11},{10,... | collective-permute-start | bytes 4325384 | tf_op jit(solution)/shard_map/ppermute | solution.py:325
  (82 other events, 849.4 us)
Sparse Core Ops, SparseCore 0:
  10.2 36.4 all-gather.6
  48.8 28.2 all-gather.10
  79.4 107.4 all-gather.12
  188.3 59.0 all-gather.8
  328.5 63.7 reduce-scatter.4
  426.8 34.3 reduce-scatter.8
  484.5 36.1 reduce-scatter.6
  523.5 118.5 reduce-scatter.10

commit v2 on v0

--- a/solution.py
+++ b/solution.py
@@ -4,7 +4,10 @@
 import jax.numpy as jnp
 import numpy as np
 from jax import lax
+from jax.experimental import pallas as pl
+from jax.experimental.pallas import tpu as pltpu
 from jax.sharding import PartitionSpec as P
+
 
 H = 32
 KVH = 4
@@ -317,6 +320,1067 @@
     )
 
 
+def neighbour(values, step):
+    count = lax.axis_size("seq")
+    return lax.ppermute(values, "seq", [(i, i ^ step) for i in range(count)])
+
+
+def matmul(left, right, left_dim, right_dim):
+    return lax.dot_general(
+        left, right, (((left_dim,), (right_dim,)), ((), ())), preferred_element_type=jnp.float32
+    )
+
+
+ROOT = HD ** (-0.5)
+LIMIT = 60 * 1024 * 1024
+
+
+def swap_halves(values):
+    width = values.shape[1]
+    half = HD // 2
+    column = lax.broadcasted_iota(jnp.int32, values.shape, 1)
+    return jnp.where(
+        column % HD < half, pltpu.roll(values, width - half, 1), pltpu.roll(values, half, 1)
+    )
+
+
+def spread_tables(table, pairs, last):
+    half = HD // 2
+    cosines, sines = table[:, :half], table[:, half:]
+    ones, zeros = jnp.ones_like(table), jnp.zeros_like(table)
+    tail = [[cosines, cosines, ones], [-sines, sines, zeros]] if last else [[], []]
+    if not pairs:
+        return jnp.concatenate(tail[0], 1), jnp.concatenate(tail[1], 1)
+    cosines = [jnp.concatenate([cosines] * 4, 1)] * pairs
+    sines = [jnp.concatenate([-sines, sines] * 2, 1)] * pairs
+    if last:
+        cosines.append(jnp.concatenate(tail[0], 1))
+        sines.append(jnp.concatenate(tail[1], 1))
+    return jnp.concatenate(cosines, 1), jnp.concatenate(sines, 1)
+
+
+MESH = pl.DeviceIdType.MESH
+
+
+def seq_peer(step):
+    return {"seq": lax.axis_index("seq") ^ step}
+
+
+def fsdp_peer(place):
+    return {"fsdp": place}
+
+
+def remote(source, target, sems, slot, peer):
+    return pltpu.make_async_remote_copy(
+        src_ref=source,
+        dst_ref=target,
+        send_sem=sems[0].at[slot],
+        recv_sem=sems[1].at[slot],
+        device_id=peer,
+        device_id_type=MESH,
+    )
+
+
+def gather_copies(own, slots, half, sems, base=0):
+    top, bottom = pl.ds(0, half), pl.ds(half, own.shape[0] - half)
+
+    def slot(step, rows):
+        return slots.at[step].at[rows]
+
+    return [
+        remote(own.at[top], slot(1, top), sems, base, seq_peer(1)),
+        remote(own.at[bottom], slot(2, bottom), sems, base + 1, seq_peer(2)),
+        remote(own.at[bottom], slot(1, bottom), sems, base + 2, seq_peer(1)),
+        remote(own.at[top], slot(2, top), sems, base + 3, seq_peer(2)),
+        remote(slot(1, top), slot(3, top), sems, base + 4, seq_peer(2)),
+        remote(slot(2, bottom), slot(3, bottom), sems, base + 5, seq_peer(1)),
+    ]
+
+
+def greet(peers):
+    barrier = pltpu.get_barrier_semaphore()
+    for peer in peers:
+        pl.semaphore_signal(barrier, inc=1, device_id=peer, device_id_type=MESH)
+    pl.semaphore_wait(barrier, len(peers))
+
+
+def sum_copies(sent, side, below, far, half, sems, passed=None):
+    top, bottom = pl.ds(0, half), pl.ds(half, half)
+    return [
+        remote(sent.at[3].at[top], side.at[1], sems, 0, seq_peer(1)),
+        remote(sent.at[3].at[bottom], below.at[1], sems, 1, seq_peer(2)),
+        remote(sent.at[2].at[bottom], below.at[0], sems, 2, seq_peer(2)),
+        remote(sent.at[1].at[top], side.at[0], sems, 3, seq_peer(1)),
+        remote(passed.at[0] if passed is not None else sent.at[2].at[top], far.at[0], sems, 4, seq_peer(2)),
+        remote(passed.at[1] if passed is not None else sent.at[1].at[bottom], far.at[1], sems, 5, seq_peer(1)),
+    ]
+
+
+def pass_sums(turn, step, partial, sums, sent_ref, side_ref, below_ref, own_ref, half):
+    wide, narrow = jnp.float32, jnp.bfloat16
+    last = len(sums) // 2
+
+    @pl.when(turn == last)
+    def _():
+        own_ref[...] = partial
+
+    @pl.when(turn < last)
+    def _():
+        sent_ref[step] = partial.astype(narrow)
+
+    @pl.when(turn == 0)
+    def _():
+        sums[0].start()
+        sums[1].start()
+
+    @pl.when(turn == 1)
+    def _():
+        sums[2].start()
+
+    @pl.when(turn == 2)
+    def _():
+        sums[3].start()
+        sums[0].wait_recv()
+        sent_ref[2, :half] = (sent_ref[2, :half].astype(wide) + side_ref[1].astype(wide)).astype(narrow)
+        sums[4].start()
+        sums[1].wait_recv()
+        sent_ref[1, half:] = (sent_ref[1, half:].astype(wide) + below_ref[1].astype(wide)).astype(narrow)
+        sums[5].start()
+
+
+def end_sums(sums, side_ref, below_ref, far_ref, own_ref, half):
+    wide = jnp.float32
+    sums[2].wait_recv()
+    sums[3].wait_recv()
+    own_ref[:half] += side_ref[0].astype(wide)
+    own_ref[half:] += below_ref[0].astype(wide)
+    sums[4].wait_recv()
+    own_ref[:half] += far_ref[0].astype(wide)
+    sums[5].wait_recv()
+    own_ref[half:] += far_ref[1].astype(wide)
+
+
+def share_own(all_ref, half, sems, before):
+    copies = gather_copies(all_ref.at[0], all_ref, half, sems, len(before))
+    for copy in copies[:4]:
+        copy.start()
+    copies[0].wait_recv()
+    copies[4].start()
+    copies[1].wait_recv()
+    copies[5].start()
+    for copy in copies[2:]:
+        copy.wait_recv()
+    for copy in before + copies:
+        copy.wait_send()
+
+
+def enter_kernel(
+    count, normed_ref, spots_ref, shard_ref, out_shard_ref,
+    all_ref, rows_ref, out_ref, table_ref,
+    held_ref, send_sems, recv_sems, spot_send, spot_recv, item_up, item_down, item_side, item_recv, local_sem,
+):
+    part, _ = normed_ref.shape
+    heads = H // count
+    pieces = heads + 2
+    items = pieces + lax.axis_size("fsdp")
+    per_shard = shard_ref.shape[0] // HD
+    out_rows, columns = out_shard_ref.shape[0], heads * HD
+    chips = lax.axis_size("fsdp") // 2
+    index = lax.axis_index("seq")
+    place = lax.axis_index("fsdp")
+    chip, core = place // 2, place % 2
+    sems = (send_sems, recv_sems)
+
+    barrier = pltpu.get_barrier_semaphore()
+    for peer in [seq_peer(step) for step in range(1, count)] + [fsdp_peer(place ^ 1)]:
+        pl.semaphore_signal(barrier, inc=1, device_id=peer, device_id_type=MESH)
+
+    @pl.when(chip > 0)
+    def _():
+        pl.semaphore_signal(barrier, inc=1, device_id=fsdp_peer(place - 2), device_id_type=MESH)
+
+    @pl.when(chip < chips - 1)
+    def _():
+        pl.semaphore_signal(barrier, inc=1, device_id=fsdp_peer(place + 2), device_id_type=MESH)
+
+    greetings = count + (chip > 0).astype(jnp.int32) + (chip < chips - 1).astype(jnp.int32)
+    pl.semaphore_wait(barrier, greetings)
+
+    copies = gather_copies(normed_ref, all_ref, part // 2, sems)
+    for copy in copies[:4]:
+        copy.start()
+    held_ref[0] = spots_ref[...]
+    spot_copies = [
+        remote(spots_ref, held_ref.at[step], (spot_send, spot_recv), step - 1, seq_peer(step))
+        for step in range(1, count)
+    ]
+    for copy in spot_copies:
+        copy.start()
+    own = pltpu.make_async_copy(normed_ref, all_ref.at[0], local_sem.at[items])
+    own.start()
+
+    def qkv_item(item):
+        block = jnp.where(
+            item < heads, index * heads + item, jnp.where(item == heads, H + index, H + KVH + index)
+        )
+        source = shard_ref.at[pl.ds(pl.multiple_of(block % per_shard * HD, HD), HD)]
+        return block // per_shard, source, rows_ref.at[pl.ds(pl.multiple_of(item * HD, HD), HD)], item
+
+    def out_item(item):
+        source = out_shard_ref.at[:, pl.ds(pl.multiple_of(index * columns, columns), columns)]
+        target = out_ref.at[pl.ds(pl.multiple_of(item * out_rows, out_rows), out_rows)]
+        return item, source, target, item + pieces
+
+    kinds = ((qkv_item, pieces), (out_item, items - pieces))
+
+    def item_copy(source, target, slot, sem, peer):
+        return pltpu.make_async_remote_copy(
+            src_ref=source,
+            dst_ref=target,
+            send_sem=sem.at[slot],
+            recv_sem=item_recv.at[slot],
+            device_id=fsdp_peer(peer),
+            device_id_type=MESH,
+        )
+
+    def pass_on(source, target, slot, owner_chip, act):
+        @pl.when((chip >= owner_chip) & (chip < chips - 1))
+        def _():
+            act(item_copy(source, target, slot, item_up, place + 2))
+
+        @pl.when((chip <= owner_chip) & (chip > 0))
+        def _():
+            act(item_copy(source, target, slot, item_down, place - 2))
+
+        act(item_copy(source, target, slot, item_side, place ^ 1))
+
+    def send_own(item_of):
+        def body(item, carry):
+            owner, source, target, slot = item_of(item)
+
+            @pl.when(place == owner)
+            def _():
+                pass_on(source, target, slot, owner // 2, lambda copy: copy.start())
+                pltpu.make_async_copy(source, target, local_sem.at[slot]).start()
+
+            return carry
+
+        return body
+
+    def pass_far(item_of, distance):
+        def body(item, carry):
+            owner, _, target, slot = item_of(item)
+            owner_chip = owner // 2
+            apart = jnp.where(chip > owner_chip, chip - owner_chip, owner_chip - chip)
+
+            @pl.when((apart == distance) & (core == owner % 2))
+            def _():
+                item_copy(target, target, slot, item_side, place ^ 1).wait_recv()
+                pass_on(target, target, slot, owner_chip, lambda copy: copy.start())
+
+            return carry
+
+        return body
+
+    for item_of, number in kinds:
+        lax.fori_loop(0, number, send_own(item_of), 0)
+    for distance in range(1, chips):
+        for item_of, number in kinds:
+            lax.fori_loop(0, number, pass_far(item_of, distance), 0)
+            if distance == 1 and item_of is qkv_item:
+                copies[0].wait_recv()
+                copies[4].start()
+                copies[1].wait_recv()
+                copies[5].start()
+
+    for copy in spot_copies:
+        copy.wait()
+    half = HD // 2
+    for step in range(count):
+        spots = held_ref[step][:1]
+        frequency = jnp.exp(
+            lax.broadcasted_iota(jnp.int32, (half, 1), 0).astype(jnp.float32) * (-2.0 * math.log(10000.0) / HD)
+        )
+        angles = frequency * spots
+        turned = jnp.concatenate([jnp.cos(angles), jnp.sin(angles)], 0)
+        table_ref[pl.ds(step * part, part), :] = jnp.transpose(turned)
+
+    def finish(item_of):
+        def body(item, carry):
+            owner, source, target, slot = item_of(item)
+
+            @pl.when(core != owner % 2)
+            def _():
+                item_copy(target, target, slot, item_side, place ^ 1).wait_recv()
+
+            @pl.when(place == owner)
+            def _():
+                pltpu.make_async_copy(source, target, local_sem.at[slot]).wait()
+
+            @pl.when(core == owner % 2)
+            def _():
+                pass_on(target, target, slot, owner // 2, lambda copy: copy.wait_send())
+
+            return carry
+
+        return body
+
+    for item_of, number in kinds:
+        lax.fori_loop(0, number, finish(item_of), 0)
+    own.wait()
+    for copy in copies[2:]:
+        copy.wait_recv()
+    for copy in copies:
+        copy.wait_send()
+
+
+def enter(normed, spots, shard, out_shard, count):
+    part, width = normed.shape
+    length = part * count
+    heads = H // count
+    pieces = heads + 2
+    items = pieces + lax.axis_size("fsdp")
+    vmem = pl.BlockSpec(memory_space=pltpu.VMEM)
+    spots = jnp.broadcast_to(spots.astype(jnp.float32)[None], (8, part))
+    gathered, rows, out_cols, table = pl.pallas_call(
+        lambda *refs: enter_kernel(count, *refs),
+        out_shape=(
+            jax.ShapeDtypeStruct((count, part, width), jnp.bfloat16),
+            jax.ShapeDtypeStruct((pieces * HD, width), jnp.bfloat16),
+            jax.ShapeDtypeStruct((out_shard.shape[0] * (items - pieces), heads * HD), jnp.bfloat16),
+            jax.ShapeDtypeStruct((length, HD), jnp.float32),
+        ),
+        in_specs=[vmem] * 4,
+        out_specs=[vmem] * 4,
+        scratch_shapes=[
+            pltpu.VMEM((count, 8, part), jnp.float32),
+            pltpu.SemaphoreType.DMA((6,)),
+            pltpu.SemaphoreType.DMA((6,)),
+            pltpu.SemaphoreType.DMA((count - 1,)),
+            pltpu.SemaphoreType.DMA((count - 1,)),
+            pltpu.SemaphoreType.DMA((items,)),
+            pltpu.SemaphoreType.DMA((items,)),
+            pltpu.SemaphoreType.DMA((items,)),
+            pltpu.SemaphoreType.DMA((items,)),
+            pltpu.SemaphoreType.DMA((items + 1,)),
+        ],
+        compiler_params=pltpu.CompilerParams(collective_id=1, has_side_effects=True, vmem_limit_bytes=LIMIT),
+        name="enter",
+    )(normed, spots, shard, out_shard)
+    return gathered.reshape(length, width), rows, out_cols, table
+
+
+def qkv_kernel(index_ref, normed_ref, weight_ref, table_ref, q_ref, k_ref, v_ref):
+    heads = q_ref.shape[0]
+    joint = matmul(normed_ref[...], weight_ref[...], 1, 1)
+    cosines, sines = spread_tables(table_ref[...], heads // 2, True)
+    turned = joint * cosines + swap_halves(joint) * sines
+    for head in range(heads):
+        rounded = turned[:, head * HD : (head + 1) * HD].astype(jnp.bfloat16).astype(jnp.float32)
+        q_ref[head] = (rounded * ROOT).astype(jnp.bfloat16)
+    k_ref[...] = turned[:, heads * HD : (heads + 1) * HD].astype(jnp.bfloat16)
+    v_ref[...] = turned[:, (heads + 1) * HD :].astype(jnp.bfloat16)
+
+
+def project_qkv(index, normed, weight, table, count):
+    length, width = normed.shape
+    part = length // count
+    heads = weight.shape[0] // HD - 2
+    return pl.pallas_call(
+        qkv_kernel,
+        out_shape=(
+            jax.ShapeDtypeStruct((heads, length, HD), jnp.bfloat16),
+            jax.ShapeDtypeStruct((length, HD), jnp.bfloat16),
+            jax.ShapeDtypeStruct((length, HD), jnp.bfloat16),
+        ),
+        grid_spec=pltpu.PrefetchScalarGridSpec(
+            num_scalar_prefetch=1,
+            grid=(count,),
+            in_specs=[
+                pl.BlockSpec((part, width), lambda i, s: (i, 0)),
+                pl.BlockSpec(weight.shape, lambda i, s: (0, 0)),
+                pl.BlockSpec((part, table.shape[1]), lambda i, s: (i, 0)),
+            ],
+            out_specs=[
+                pl.BlockSpec((heads, part, HD), lambda i, s: (0, i ^ s[0], 0)),
+                pl.BlockSpec((part, HD), lambda i, s: (i ^ s[0], 0)),
+                pl.BlockSpec((part, HD), lambda i, s: (i ^ s[0], 0)),
+            ],
+        ),
+        compiler_params=pltpu.CompilerParams(vmem_limit_bytes=LIMIT),
+        name="project_qkv",
+    )(index, normed, weight, table)
+
+
+def attend_kernel(
+    count, q_ref, k_ref, v_ref, weight_ref, current_ref, gain_ref,
+    attn_ref, lse_ref, middle_ref, scale_ref, all_ref,
+    held_ref, sent_ref, side_ref, below_ref, far_ref, send_sems, recv_sems,
+):
+    heads, _, _ = q_ref.shape
+    part, _ = current_ref.shape
+    half = part // 2
+    index = lax.axis_index("seq")
+    top, bottom = pl.ds(0, half), pl.ds(half, half)
+    sems = (send_sems, recv_sems)
+    greet([seq_peer(1), seq_peer(2)])
+    sums = sum_copies(sent_ref, side_ref, below_ref, far_ref, half, sems)
+    row = lax.broadcasted_iota(jnp.int32, (part, part), 0)
+    column = lax.broadcasted_iota(jnp.int32, (part, part), 1)
+
+    def one_part(turn, carry):
+        step = count - 1 - turn
+        here = step ^ index
+        rows_here = pl.ds(pl.multiple_of(here * part, part), part)
+        rows_step = pl.ds(pl.multiple_of(step * part, part), part)
+        for block in range(count):
+
+            @pl.when(here == block)
+            def _():
+                before = block * part
+                seen = before + part
+                keys_in, values_in = k_ref[:seen], v_ref[:seen]
+
+                def one_head(head, carry):
+                    scores = matmul(q_ref[head, before:seen, :], keys_in, 1, 1)
+                    last = jnp.where(row >= column, scores[:, before:], -1e30)
+                    scores = jnp.concatenate([scores[:, :before], last], 1) if block else last
+                    peak = jnp.max(scores, 1, keepdims=True)
+                    weights = jnp.exp(scores - peak)
+                    total = jnp.sum(weights, 1, keepdims=True)
+                    output = matmul(weights.astype(jnp.bfloat16), values_in, 1, 0) / total
+                    held_ref[head] = output.astype(jnp.bfloat16)
+                    log_total = jnp.broadcast_to(peak + jnp.log(total), (part, 128))
+                    lse_ref[pl.ds(head, 1), before:seen] = jnp.transpose(log_total)[:1]
+                    return carry
+
+                lax.fori_loop(0, heads, one_head, 0, unroll=2)
+
+        attn = jnp.concatenate([held_ref[head] for head in range(heads)], 1)
+        attn_ref[rows_step, :] = attn
+        partial = matmul(attn, weight_ref[...], 1, 1)
+
+        pass_sums(turn, step, partial, sums, sent_ref, side_ref, below_ref, middle_ref, half)
+        return carry
+
+    lax.fori_loop(0, count, one_part, 0)
+    end_sums(sums, side_ref, below_ref, far_ref, middle_ref, half)
+    middle_ref[...] += current_ref[...]
+    middle = middle_ref[...]
+    scale = lax.rsqrt(jnp.mean(middle * middle, 1, keepdims=True) + EPS)
+    scale_ref[...] = jnp.broadcast_to(scale, scale_ref.shape)
+    all_ref[0] = (middle * scale * gain_ref[...]).astype(jnp.bfloat16)
+    share_own(all_ref, half, sems, sums)
+
+
+def attend(queries, keys_in, values_in, weight, current, gain, count):
+    heads, length, _ = queries.shape
+    part, width = current.shape
+    vmem = pl.BlockSpec(memory_space=pltpu.VMEM)
+    attn, lse, middle, scale, gathered = pl.pallas_call(
+        lambda *refs: attend_kernel(count, *refs),
+        out_shape=(
+            jax.ShapeDtypeStruct((length, heads * HD), jnp.bfloat16),
+            jax.ShapeDtypeStruct((heads, length), jnp.float32),
+            jax.ShapeDtypeStruct((part, width), jnp.float32),
+            jax.ShapeDtypeStruct((part, 128), jnp.float32),
+            jax.ShapeDtypeStruct((count, part, width), jnp.bfloat16),
+        ),
+        in_specs=[vmem] * 6,
+        out_specs=[vmem] * 5,
+        scratch_shapes=[
+            pltpu.VMEM((heads, part, HD), jnp.bfloat16),
+            pltpu.VMEM((count, part, width), jnp.bfloat16),
+            pltpu.VMEM((2, part // 2, width), jnp.bfloat16),
+            pltpu.VMEM((2, part // 2, width), jnp.bfloat16),
+            pltpu.VMEM((2, part // 2, width), jnp.bfloat16),
+            pltpu.SemaphoreType.DMA((12,)),
+            pltpu.SemaphoreType.DMA((12,)),
+        ],
+        compiler_params=pltpu.CompilerParams(collective_id=2, has_side_effects=True, vmem_limit_bytes=LIMIT),
+        name="attend",
+    )(queries, keys_in, values_in, weight, current, gain)
+    return attn, lse, middle, scale, gathered.reshape(length, width)
+
+
+def share_start(copies):
+    for group in copies:
+        group[0].start()
+        group[1].start()
+    for group in copies:
+        group[2].start()
+        group[3].start()
+
+
+def share_on(group):
+    group[0].wait_recv()
+    group[4].start()
+    group[1].wait_recv()
+    group[5].start()
+
+
+def share_end(copies):
+    for group in copies:
+        for copy in group[2:]:
+            copy.wait_recv()
+    for group in copies:
+        for copy in group:
+            copy.wait_send()
+
+
+def upper_half(rows):
+    return -(-(rows // 2) // 16) * 16
+
+
+def attend_back_kernel(
+    count, q_ref, k_ref, v_ref, attn_ref, lse_ref, dy_ref, weight_ref, table_ref, pick_ref, down_ref, middle_ref,
+    out_ref, turned_ref, term_ref, result_ref,
+    do_ref, delta_ref, dq_ref, dk_ref, dv_ref, side_ref, below_ref, far_ref, passed_ref, send_sems, recv_sems,
+):
+    heads, length, _ = q_ref.shape
+    part = length // count
+    wide = jnp.float32
+    index = lax.axis_index("seq")
+    greet([seq_peer(1), seq_peer(2)])
+    half = part // 2
+    sums = sum_copies(down_ref, side_ref, below_ref, far_ref, half, (send_sems, recv_sems), passed_ref)
+    for copy in sums[:4]:
+        copy.start()
+    result_ref[...] = middle_ref[...] + down_ref[0].astype(wide)
+    dk_ref[...] = jnp.zeros_like(dk_ref)
+    dv_ref[...] = jnp.zeros_like(dv_ref)
+    owner = lax.broadcasted_iota(jnp.int32, (heads, heads * HD), 1) // HD
+    same = (owner == lax.broadcasted_iota(jnp.int32, (heads, heads * HD), 0)).astype(wide)
+    row = lax.broadcasted_iota(jnp.int32, (part, part), 0)
+    column = lax.broadcasted_iota(jnp.int32, (part, part), 1)
+
+    def unturn(grads, cosines, sines):
+        return grads * cosines + swap_halves(grads * sines)
+
+    def one_part(here, carry):
+        spot = here ^ index
+        rows_here = pl.ds(pl.multiple_of(spot * part, part), part)
+        dattn = matmul(dy_ref[rows_here, :], weight_ref[...], 1, 0).astype(jnp.bfloat16)
+        product = dattn.astype(wide) * attn_ref[rows_here, :].astype(wide)
+        delta_ref[...] = lax.dot_general(
+            same, product, (((1,), (1,)), ((), ())), precision=lax.Precision.HIGHEST, preferred_element_type=wide
+        )
+        for head in range(heads):
+            do_ref[head] = dattn[:, head * HD : (head + 1) * HD]
+        for block in range(count):
+
+            @pl.when(here == block)
+            def _():
+                before = block * part
+                seen = before + part
+                keys_in, values_in = k_ref[:seen], v_ref[:seen]
+
+                def one_head(head, carry):
+                    query, dout = q_ref[head, before:seen, :], do_ref[head]
+                    scores = matmul(keys_in, query, 1, 1)
+                    last = jnp.where(row <= column, scores[before:], -1e30)
+                    scores = jnp.concatenate([scores[:before], last], 0) if block else last
+                    probs = jnp.exp(scores - lse_ref[pl.ds(head, 1), before:seen])
+                    dprob = matmul(values_in, dout, 1, 1)
+                    dscore = (probs * (dprob - delta_ref[pl.ds(head, 1), :])).astype(jnp.bfloat16)
+                    dv_ref[:seen] += matmul(probs.astype(jnp.bfloat16), dout, 1, 0)
+                    dk_ref[:seen] += matmul(dscore, query, 1, 0)
+                    dq_ref[head] = (matmul(dscore, keys_in, 0, 0) * ROOT).astype(jnp.bfloat16)
+                    return carry
+
+                lax.fori_loop(0, heads, one_head, 0, unroll=2)
+
+        dq = jnp.concatenate([dq_ref[head] for head in range(heads)], 1).astype(wide)
+        dq = unturn(dq, *spread_tables(table_ref[rows_here, :], heads // 2, False))
+        out_ref[rows_here, : heads * HD] = dq.astype(jnp.bfloat16)
+
+        @pl.when(here == 1)
+        def _():
+            sums[0].wait_recv()
+            passed_ref[0] = (down_ref[2, :half].astype(wide) + side_ref[1].astype(wide)).astype(jnp.bfloat16)
+            sums[4].start()
+            sums[1].wait_recv()
+            passed_ref[1] = (down_ref[1, half:].astype(wide) + below_ref[1].astype(wide)).astype(jnp.bfloat16)
+            sums[5].start()
+
+        return carry
+
+    lax.fori_loop(0, count, one_part, 0)
+    for block in range(count):
+        rows_there = pl.ds(pl.multiple_of((block ^ index) * part, part), part)
+        rows_block = slice(block * part, (block + 1) * part)
+        both = jnp.concatenate([dk_ref[rows_block], dv_ref[rows_block]], 1).astype(jnp.bfloat16).astype(wide)
+        both = unturn(both, *spread_tables(table_ref[rows_there, :], 0, True))
+        out_ref[rows_there, heads * HD :] = both.astype(jnp.bfloat16)
+    chosen = matmul(pick_ref[...], out_ref[...], 1, 1).astype(jnp.bfloat16)
+    size = turned_ref.shape[1]
+    for block in range(count):
+        turned_ref[block] = chosen[block * size : (block + 1) * size]
+    tile = 2 * 128
+
+    def one_tile(number, carry):
+        columns = pl.ds(pl.multiple_of(number * tile, tile), tile)
+        term_ref[columns, :] = matmul(dy_ref[:, columns], attn_ref[...], 0, 0).astype(jnp.bfloat16)
+        return carry
+
+    lax.fori_loop(0, dy_ref.shape[1] // tile, one_tile, 0)
+    end_sums(sums, side_ref, below_ref, far_ref, result_ref, half)
+    for copy in sums:
+        copy.wait_send()
+
+
+def attend_back(queries, keys_in, values_in, attn, lse, dy, weight, table, pick, down, middle, count):
+    heads, length, _ = queries.shape
+    part, width = middle.shape
+    columns = (heads + 2) * HD
+    vmem = pl.BlockSpec(memory_space=pltpu.VMEM)
+    return pl.pallas_call(
+        lambda *refs: attend_back_kernel(count, *refs),
+        out_shape=[
+            jax.ShapeDtypeStruct((length, columns), jnp.bfloat16),
+            jax.ShapeDtypeStruct((count, columns // count, length), jnp.bfloat16),
+            jax.ShapeDtypeStruct((width, heads * HD), jnp.bfloat16),
+            jax.ShapeDtypeStruct((part, width), jnp.float32),
+        ],
+        in_specs=[vmem] * 11,
+        out_specs=[vmem] * 4,
+        scratch_shapes=[
+            pltpu.VMEM((heads, part, HD), jnp.bfloat16),
+            pltpu.VMEM((heads, part), jnp.float32),
+            pltpu.VMEM((heads, part, HD), jnp.bfloat16),
+            pltpu.VMEM((length, HD), jnp.float32),
+            pltpu.VMEM((length, HD), jnp.float32),
+        ]
+        + [pltpu.VMEM((2, part // 2, width), jnp.bfloat16)] * 4
+        + [pltpu.SemaphoreType.DMA((6,)), pltpu.SemaphoreType.DMA((6,))],
+        compiler_params=pltpu.CompilerParams(collective_id=4, has_side_effects=True, vmem_limit_bytes=LIMIT),
+        name="attend_back",
+    )(queries, keys_in, values_in, attn, lse, dy, weight, table, pick, down, middle)
+
+
+def leave_kernel(
+    count, grads_ref, weight_ref, flowing_ref, first_ref, scale_ref, gain_ref, turned_ref, normed_ref,
+    own_ref, gain_out_ref, term_ref,
+    sent_ref, side_ref, below_ref, far_ref, slot_ref, whole_ref, send_sems, recv_sems, swap_send, swap_recv,
+):
+    part, _ = flowing_ref.shape
+    half = part // 2
+    size = turned_ref.shape[1]
+    heads = H // count
+    chunk = size // (heads + 2)
+    index = lax.axis_index("seq")
+    greet([seq_peer(step) for step in range(1, count)])
+    swaps = [
+        remote(turned_ref.at[index ^ step], slot_ref.at[step], (swap_send, swap_recv), step - 1, seq_peer(step))
+        for step in range(1, count)
+    ]
+    for copy in swaps:
+        copy.start()
+    slot_ref[0] = turned_ref[index]
+    sums = sum_copies(sent_ref, side_ref, below_ref, far_ref, half, (send_sems, recv_sems))
+
+    def one_part(turn, carry):
+        step = count - 1 - turn
+        rows_step = pl.ds(pl.multiple_of(step * part, part), part)
+        partial = matmul(grads_ref[rows_step, :], weight_ref[...], 1, 0)
+        pass_sums(turn, step, partial, sums, sent_ref, side_ref, below_ref, own_ref, half)
+        return carry
+
+    lax.fori_loop(0, count, one_part, 0)
+    for step in range(count):
+        if step:
+            swaps[step - 1].wait_recv()
+        peer = index ^ step
+        for block in range(count):
+            piece = slot_ref[step, :, (step ^ block) * part : ((step ^ block) + 1) * part]
+            tokens = slice(block * part, (block + 1) * part)
+            for start, rows in ((0, heads * chunk), (H * chunk, chunk), ((H + KVH) * chunk, chunk)):
+                begin = 0 if start == 0 else heads * chunk + (0 if start == H * chunk else chunk)
+                spot = pl.multiple_of(start + peer * rows, chunk)
+                whole_ref[pl.ds(spot, rows), tokens] = piece[begin : begin + rows]
+    term_ref[...] = matmul(whole_ref[...], normed_ref[...], 1, 0).astype(jnp.bfloat16)
+    end_sums(sums, side_ref, below_ref, far_ref, own_ref, half)
+    unit = first_ref[...] * scale_ref[:, :1]
+    grads = own_ref[...]
+    gain_out_ref[...] = jnp.sum(grads * unit, 0, keepdims=True)
+    inner = grads * gain_ref[...]
+    own_ref[...] = flowing_ref[...] + scale_ref[:, :1] * (inner - unit * jnp.mean(inner * unit, 1, keepdims=True))
+    for copy in sums + swaps:
+        copy.wait_send()
+
+
+def leave(grads, weight, flowing, first, scale, gain, turned, normed, count):
+    part, width = flowing.shape
+    vmem = pl.BlockSpec(memory_space=pltpu.VMEM)
+    size, length = turned.shape[1:]
+    own, gain_term, term = pl.pallas_call(
+        lambda *refs: leave_kernel(count, *refs),
+        out_shape=(
+            jax.ShapeDtypeStruct((part, width), jnp.float32),
+            jax.ShapeDtypeStruct((1, width), jnp.float32),
+            jax.ShapeDtypeStruct((size * count, width), jnp.bfloat16),
+        ),
+        in_specs=[vmem] * 8,
+        out_specs=[vmem] * 3,
+        scratch_shapes=[
+            pltpu.VMEM((count, part, width), jnp.bfloat16),
+            pltpu.VMEM((2, part // 2, width), jnp.bfloat16),
+            pltpu.VMEM((2, part // 2, width), jnp.bfloat16),
+            pltpu.VMEM((2, part // 2, width), jnp.bfloat16),
+            pltpu.VMEM((count, size, length), jnp.bfloat16),
+            pltpu.VMEM((count * size, length), jnp.bfloat16),
+            pltpu.SemaphoreType.DMA((6,)),
+            pltpu.SemaphoreType.DMA((6,)),
+            pltpu.SemaphoreType.DMA((count - 1,)),
+            pltpu.SemaphoreType.DMA((count - 1,)),
+        ],
+        compiler_params=pltpu.CompilerParams(collective_id=5, has_side_effects=True, vmem_limit_bytes=LIMIT),
+        name="leave",
+    )(grads, weight, flowing, first, scale, gain, turned, normed)
+    return own, gain_term[0], term
+
+
+def share_kernel(number, fsdp, *refs):
+    extra = 1 if fsdp else 0
+    shards, slots = refs[:number], refs[number + extra : 2 * number + extra]
+    send_sems, recv_sems = refs[2 * number + 2 * extra : 2 * number + 2 * extra + 2]
+    peers = [seq_peer(1), seq_peer(2)]
+    steps = []
+    if fsdp:
+        term_ref, total_ref = refs[number], refs[2 * number + 1]
+        heard_ref, told_ref, sum_send, sum_recv = refs[2 * number + 4 :]
+        place = lax.axis_index("fsdp")
+        steps = [seq_peer(1), seq_peer(2)] + [fsdp_peer(place ^ (1 << bit)) for bit in range(fsdp.bit_length() - 1)]
+        peers += steps[2:]
+    greet(peers)
+    copies = [
+        gather_copies(shard, slot, upper_half(shard.shape[0]), (send_sems, recv_sems), 6 * spot)
+        for spot, (shard, slot) in enumerate(zip(shards, slots))
+    ]
+    share_start(copies)
+    if fsdp:
+        total_ref[...] = term_ref[...]
+    tells = []
+    for step, peer in enumerate(steps):
+        told_ref[step] = total_ref[...]
+        tell = remote(told_ref.at[step], heard_ref.at[step], (sum_send, sum_recv), step, peer)
+        tell.start()
+        tell.wait_recv()
+        total_ref[...] += heard_ref[step]
+        tells.append(tell)
+    for shard, slot in zip(shards, slots):
+        slot[0] = shard[...]
+    for group in copies:
+        share_on(group)
+    share_end(copies)
+    for tell in tells:
+        tell.wait_send()
+
+
+def share(name, shards, count, term=None):
+    vmem = pl.BlockSpec(memory_space=pltpu.VMEM)
+    fsdp = lax.axis_size("fsdp") if term is not None else 0
+    extra = [] if term is None else [term]
+    scratch = [pltpu.SemaphoreType.DMA((6 * len(shards),)) for _ in range(2)]
+    if fsdp:
+        steps = fsdp.bit_length() + 1
+        scratch += [pltpu.VMEM((steps,) + term.shape, term.dtype) for _ in range(2)]
+        scratch += [pltpu.SemaphoreType.DMA((steps,)) for _ in range(2)]
+    return pl.pallas_call(
+        lambda *refs: share_kernel(len(shards), fsdp, *refs),
+        out_shape=[jax.ShapeDtypeStruct((count,) + shard.shape, shard.dtype) for shard in shards]
+        + [jax.ShapeDtypeStruct(value.shape, value.dtype) for value in extra],
+        in_specs=[vmem] * (len(shards) + len(extra)),
+        out_specs=[vmem] * (len(shards) + len(extra)),
+        scratch_shapes=scratch,
+        compiler_params=pltpu.CompilerParams(
+            collective_id=name, has_side_effects=True, vmem_limit_bytes=LIMIT
+        ),
+        name="share",
+    )(*shards, *extra)
+
+
+def join_rows_kernel(index_ref, *refs):
+    out_ref = refs[-1]
+    out_ref[...] = jnp.concatenate([ref[0] for ref in refs[:-1]], 1).astype(jnp.float32)
+
+
+def join_rows(index, slots, count):
+    rows = slots[0].shape[1]
+    width = sum(slot.shape[2] for slot in slots)
+    return pl.pallas_call(
+        join_rows_kernel,
+        out_shape=jax.ShapeDtypeStruct((rows * count, width), jnp.float32),
+        grid_spec=pltpu.PrefetchScalarGridSpec(
+            num_scalar_prefetch=1,
+            grid=(count,),
+            in_specs=[pl.BlockSpec((1,) + slot.shape[1:], lambda i, s: (i ^ s[0], 0, 0)) for slot in slots],
+            out_specs=pl.BlockSpec((rows, width), lambda i, s: (i, 0)),
+        ),
+        compiler_params=pltpu.CompilerParams(vmem_limit_bytes=LIMIT),
+        name="join_rows",
+    )(index, *slots)
+
+
+def join_pieces_kernel(count, row_piece, column_piece, index_ref, slot_ref, out_ref):
+    index = index_ref[0]
+    _, rows, columns = slot_ref.shape
+    for device in range(count):
+        values = slot_ref[device ^ index].astype(jnp.float32)
+        for top in range(0, rows, row_piece):
+            for left in range(0, columns, column_piece):
+                down = top * count + device * row_piece if row_piece < rows else top
+                across = left * count + device * column_piece if row_piece == rows else left
+                out_ref[down : down + row_piece, across : across + column_piece] = values[
+                    top : top + row_piece, left : left + column_piece
+                ]
+
+
+def join_pieces(index, slots, row_piece, column_piece):
+    count, rows, columns = slots.shape
+    shape = (rows * count, columns) if row_piece < rows else (rows, columns * count)
+    return pl.pallas_call(
+        lambda *refs: join_pieces_kernel(count, row_piece, column_piece, *refs),
+        out_shape=jax.ShapeDtypeStruct(shape, jnp.float32),
+        grid_spec=pltpu.PrefetchScalarGridSpec(
+            num_scalar_prefetch=1,
+            grid=(1,),
+            in_specs=[pl.BlockSpec(slots.shape, lambda i, s: (0, 0, 0))],
+            out_specs=pl.BlockSpec(shape, lambda i, s: (0, 0)),
+        ),
+        compiler_params=pltpu.CompilerParams(vmem_limit_bytes=LIMIT),
+        name="join_pieces",
+    )(index, slots)
+
+
+def norm_back_kernel(
+    count, grads_ref, weight_ref, flowing_ref, middle_ref, scale_ref, gain_ref, inputs_ref,
+    own_ref, gain_out_ref, dy_ref, left_ref, right_ref,
+    sent_ref, side_ref, below_ref, far_ref, stage_ref, send_sems, recv_sems, store_sems,
+):
+    part, width = flowing_ref.shape
+    half = part // 2
+    sems = (send_sems, recv_sems)
+    greet([seq_peer(1), seq_peer(2)])
+    sums = sum_copies(sent_ref, side_ref, below_ref, far_ref, half, sems)
+
+    def one_part(turn, carry):
+        step = count - 1 - turn
+        rows_step = pl.ds(pl.multiple_of(step * part, part), part)
+        partial = matmul(grads_ref[rows_step, :], weight_ref[...], 1, 0)
+        pass_sums(turn, step, partial, sums, sent_ref, side_ref, below_ref, own_ref, half)
+        return carry
+
+    lax.fori_loop(0, count, one_part, 0)
+
+    tile = stage_ref.shape[1]
+    tiles = grads_ref.shape[1] // tile
+
+    def stores(number):
+        slot = number % 2
+        rows = pl.ds(pl.multiple_of(number * tile, tile), tile)
+        return [
+            pltpu.make_async_copy(
+                stage_ref.at[slot, :, pl.ds(place * (width // 2), width // 2)],
+                target.at[rows],
+                store_sems.at[place, slot],
+            )
+            for place, target in enumerate((left_ref, right_ref))
+        ]
+
+    def one_tile(number, carry):
+        @pl.when(number >= 2)
+        def _():
+            for store in stores(number - 2):
+                store.wait()
+
+        columns = pl.ds(pl.multiple_of(number * tile, tile), tile)
+        stage_ref[number % 2] = matmul(grads_ref[:, columns], inputs_ref[...], 0, 0).astype(jnp.bfloat16)
+        for store in stores(number):
+            store.start()
+        return carry
+
+    lax.fori_loop(0, tiles, one_tile, 0)
+    end_sums(sums, side_ref, below_ref, far_ref, own_ref, half)
+    scale = scale_ref[:, :1]
+    unit = middle_ref[...] * scale
+    grads = own_ref[...]
+    gain_out_ref[...] = jnp.sum(grads * unit, 0, keepdims=True)
+    inner = grads * gain_ref[...]
+    own_ref[...] = flowing_ref[...] + scale * (inner - unit * jnp.mean(inner * unit, 1, keepdims=True))
+    dy_ref[...] = own_ref[...].astype(jnp.bfloat16)
+    for number in range(tiles - 2, tiles):
+        for store in stores(number):
+            store.wait()
+    for copy in sums:
+        copy.wait_send()
+
+
+def norm_back(grads, weight, flowing, middle, scale, gain, inputs, count):
+    part, width = flowing.shape
+    units = grads.shape[1]
+    tile = 2 * 128
+    vmem = pl.BlockSpec(memory_space=pltpu.VMEM)
+    own, gain_term, dy, left, right = pl.pallas_call(
+        lambda *refs: norm_back_kernel(count, *refs),
+        out_shape=(
+            jax.ShapeDtypeStruct((part, width), jnp.float32),
+            jax.ShapeDtypeStruct((1, width), jnp.float32),
+            jax.ShapeDtypeStruct((part, width), jnp.bfloat16),
+            jax.ShapeDtypeStruct((units, width // 2), jnp.bfloat16),
+            jax.ShapeDtypeStruct((units, width // 2), jnp.bfloat16),
+        ),
+        in_specs=[vmem] * 7,
+        out_specs=[vmem] * 3 + [pl.BlockSpec(memory_space=pl.ANY)] * 2,
+        scratch_shapes=[
+            pltpu.VMEM((count, part, width), jnp.bfloat16),
+            pltpu.VMEM((2, part // 2, width), jnp.bfloat16),
+            pltpu.VMEM((2, part // 2, width), jnp.bfloat16),
+            pltpu.VMEM((2, part // 2, width), jnp.bfloat16),
+            pltpu.VMEM((2, tile, width), jnp.bfloat16),
+            pltpu.SemaphoreType.DMA((6,)),
+            pltpu.SemaphoreType.DMA((6,)),
+            pltpu.SemaphoreType.DMA((2, 2)),
+        ],
+        compiler_params=pltpu.CompilerParams(collective_id=3, has_side_effects=True, vmem_limit_bytes=LIMIT),
+        name="norm_back",
+    )(grads, weight, flowing, middle, scale, gain, inputs)
+    return own, gain_term[0], dy, left, right
+
+
+def share_dy_kernel(count, dy_ref, act_ref, weight_ref, all_ref, down_ref, send_sems, recv_sems):
+    part = dy_ref.shape[0]
+    greet([seq_peer(1), seq_peer(2)])
+    group = gather_copies(dy_ref, all_ref, part // 2, (send_sems, recv_sems))
+    share_start([group])
+    all_ref[0] = dy_ref[...]
+
+    def one_part(step, carry):
+        rows = pl.ds(pl.multiple_of(step * part, part), part)
+        down_ref[step] = matmul(act_ref[rows, :], weight_ref[...], 1, 1).astype(jnp.bfloat16)
+        return carry
+
+    lax.fori_loop(0, count, one_part, 0)
+    share_on(group)
+    share_end([group])
+
+
+def share_dy(dy, act, weight, count):
+    part, width = dy.shape
+    vmem = pl.BlockSpec(memory_space=pltpu.VMEM)
+    gathered, down = pl.pallas_call(
+        lambda *refs: share_dy_kernel(count, *refs),
+        out_shape=[jax.ShapeDtypeStruct((count, part, width), jnp.bfloat16)] * 2,
+        in_specs=[vmem] * 3,
+        out_specs=[vmem] * 2,
+        scratch_shapes=[pltpu.SemaphoreType.DMA((6,)), pltpu.SemaphoreType.DMA((6,))],
+        compiler_params=pltpu.CompilerParams(collective_id=8, has_side_effects=True, vmem_limit_bytes=LIMIT),
+        name="share_dy",
+    )(dy, act, weight)
+    return gathered.reshape(part * count, width), down
+
+
+def fast_body(hidden, positions, gains, w_qkv, w_out, w_gate_up, w_down, cotangent):
+    count = lax.axis_size("seq")
+    fsdp = lax.axis_size("fsdp")
+    index = lax.axis_index("seq")
+    place = index.astype(jnp.int32).reshape(1)
+    current = hidden[0]
+    part_len, width = current.shape
+    heads = H // count
+    gain = gains[0]
+    after = lax.optimization_barrier
+
+    rows = w_qkv.shape[1]
+    group = math.gcd(rows, HD)
+    chunk = group // count
+    per_head = HD // group
+    normed, scale_one = normalize(current, gain[0])
+    scale_one = jnp.broadcast_to(scale_one, (part_len, 128))
+    normed_all, qkv_rows, out_cols, table = enter(normed, positions[0], w_qkv[0], w_out[0], count)
+    normed_all, gate_up_shard = after((normed_all, w_gate_up[0]))
+    gu_rows = w_gate_up.shape[1] // count
+    gate_up = lax.all_gather(
+        lax.dynamic_slice_in_dim(gate_up_shard, index * gu_rows, gu_rows, 0), "fsdp", axis=0, tiled=True
+    )
+    units = FF // count
+    down_rows = w_down.shape[1]
+    down_cols = lax.all_gather(
+        lax.dynamic_index_in_dim(
+            w_down[0].reshape(down_rows, fsdp // 2, count, gu_rows), index, 2, keepdims=False
+        ).reshape(down_rows, units),
+        "fsdp",
+        axis=0,
+        tiled=True,
+    )
+
+    queries, keys_in, values_in = project_qkv(place, normed_all, qkv_rows, table, count)
+    attn_flat, log_total, middle, scale_two, normed_two_all = attend(
+        queries, keys_in, values_in, out_cols, current, gain[1:], count
+    )
+    flowing = cotangent[0]
+    normed_two_all, dm_sent = after((normed_two_all, flowing.astype(jnp.bfloat16)))
+    dm_all = jnp.concatenate([dm_sent] + [neighbour(dm_sent, step) for step in range(1, count)], 0)
+    both = matmul(normed_two_all, gate_up, 1, 1)
+    gate_part, up_part = both[:, :units], both[:, units:]
+    activated = (jax.nn.silu(gate_part) * up_part).astype(jnp.bfloat16)
+
+    def owned(grad):
+        return lax.psum_scatter(grad.astype(jnp.bfloat16), "fsdp", scatter_dimension=0, tiled=True)
+
+    term_down = matmul(dm_all, activated, 0, 0).astype(jnp.bfloat16)
+    dm_all, term_down = after((dm_all, term_down))
+    grad_down = owned(term_down)
+    dact = matmul(dm_all, down_cols, 1, 0)
+    sigma = jax.nn.sigmoid(gate_part)
+    dgate = dact * up_part * sigma * (1.0 + gate_part * (1.0 - sigma))
+    dup = dact * gate_part * sigma
+    dgu = jnp.concatenate([dgate, dup], 1).astype(jnp.bfloat16)
+    dmiddle, gain_two, dy, *terms_gate_up = norm_back(
+        dgu, gate_up, flowing, middle, scale_two, gain[1:], normed_two_all, count
+    )
+    grads_gate_up = [owned(terms_gate_up[0]), owned(terms_gate_up[1])]
+    dy_all, down_sent = share_dy(dy, activated, down_cols, count)
+    pieces = heads + 2
+    picked = np.arange(pieces * HD).reshape(pieces * per_head, count, chunk).transpose(1, 0, 2).reshape(-1)
+    pick = jnp.asarray(picked[:, None] == np.arange(pieces * HD)[None, :], jnp.bfloat16)
+    djoint, djoint_turned, term_out, result = attend_back(
+        queries, keys_in, values_in, attn_flat, log_total, dy_all, out_cols, table, pick, down_sent, middle, count
+    )
+    grad_out = owned(term_out)
+    grad_hidden, gain_one, term_qkv = leave(
+        djoint, qkv_rows, dmiddle, current, scale_one, gain[:1], djoint_turned, normed_all, count
+    )
+    grad_qkv = owned(term_qkv)
+    down_slots, gate_up_slots, gain_total = share(
+        6, (grad_down, grads_gate_up[0]), count, jnp.stack([gain_one, gain_two])
+    )
+    grad_gate_up_b, gate_up_slots = after((grads_gate_up[1], gate_up_slots))
+    gate_up_slots_b, out_slots = share(7, (grad_gate_up_b, grad_out), count)
+    gate_up_slots_b, grad_qkv = after((gate_up_slots_b, grad_qkv))
+    (qkv_slots,) = share(9, (grad_qkv,), count)
+    gain_total = gain_total[None]
+    down_shard = join_pieces(place, down_slots, down_rows, gu_rows)
+    gate_up_shard = join_rows(place, (gate_up_slots, gate_up_slots_b), count)
+    out_shard = join_pieces(place, out_slots, down_rows, heads * HD)
+    qkv_shard = join_pieces(place, qkv_slots, chunk, width)
+    return (
+        result[None],
+        grad_hidden[None],
+        gain_total,
+        qkv_shard[None],
+        out_shard[None],
+        gate_up_shard[None],
+        down_shard[None],
+    )
+
+
+def fits(mesh):
+    count, fsdp = mesh.shape["seq"], mesh.shape["fsdp"]
+    rows = (H + 2 * KVH) * HD // fsdp
+    return count == KVH == 4 and fsdp % 2 == 0 and fsdp & (fsdp - 1) == 0 and rows % HD == 0
+
+
 def solution(mesh):
     placed = (
         P("fsdp", "seq", None),
@@ -328,8 +1392,9 @@
         P(None, "fsdp", None),
         P("fsdp", "seq", None),
     )
+    fast = fits(mesh)
     return jax.shard_map(
-        body,
+        fast_body if fast else body,
         mesh=mesh,
         in_specs=placed,
         out_specs=(

time: 2010 us -> 650 us (0.32)
  waiting for transfers between devices: 1540 us -> 69.8 us
  Pallas kernels: 0 us -> 476 us
  matrix products: 245 us -> 43.6 us
  blocking collectives: 73.9 us -> 0 us
  other arithmetic: 60.3 us -> 11.5 us
  local copies, waits for them, and re-layouts: 56.1 us -> 22.7 us
    all_gather x4 -> x2, waiting for transfers between devices: 622 us -> 0.01 us  [the longest x1 0.01 us: fast_body(): lax.all_gather(lax.dynamic_slice_in_dim(gate_up_shard, index * gu_rows, g...]
    pallas_call x0 -> x14, Pallas kernels: none -> 476 us  [the longest x3 118 us: share(): pl.pallas_call(lambda *refs: share_kernel(len(shards), fsdp, *refs), out_...]
    unnamed x10 -> x7, waiting for transfers between devices: 447 us -> 1.14 us
    reduce_scatter x3 -> x5, waiting for transfers between devices: 300 us -> 26.4 us  [owned(): lax.psum_scatter(grad.astype(jnp.bfloat16), 'fsdp', scatter_dimension=0,...]
    dot_general x19 -> x3, matrix products: 245 us -> 43.6 us  [matmul(): lax.dot_general(left, right, (((left_dim,), (right_dim,)), ((), ())), pre...]
    psum x1 -> x0, waiting for transfers between devices: 151 us -> none  [weight_grad(): return lax.psum(summed, 'seq').astype(jnp.float32)]
    ppermute x0 -> x3, waiting for transfers between devices: none -> 42.3 us  [neighbour(): return lax.ppermute(values, 'seq', [(i, i ^ step) for i in range(count)])]
    psum x1 -> x0, blocking collectives: 39 us -> none  [body(): gain_total = lax.psum(jnp.stack(gain_terms), ('fsdp', 'seq'))]
  transfers between devices with their start and end apart: 13 -> 10, of which waited for: 10 -> 4; matrix products, arithmetic and copies ran while one was open for 15% -> 7% of each run, Pallas kernels for 0% -> 53%
where the time goes in v2:
time: 650 us; the launch traced here: 642 us
  Pallas kernels  476 us (73%)
  waiting for transfers between devices  69.8 us (11%)
  matrix products  43.6 us (7%)
  local copies, waits for them, and re-layouts  22.7 us (3%)
  between operations  14.8 us (2%)
  other arithmetic  11.5 us (2%)
    pallas_call x3, Pallas kernels, share(): pl.pallas_call(lambda *refs: share_kernel(len(shards), fsdp, *refs), out_...  118 us
    pallas_call x1, Pallas kernels, attend(): pl.pallas_call(lambda *refs: attend_kernel(count, *refs), out_shape=(jax....  90.2 us
    pallas_call x1, Pallas kernels, enter(): pl.pallas_call(lambda *refs: enter_kernel(count, *refs), out_shape=(jax.S...  53.6 us
    pallas_call x1, Pallas kernels, leave(): pl.pallas_call(lambda *refs: leave_kernel(count, *refs), out_shape=(jax.S...  52.2 us
    pallas_call x1, Pallas kernels, norm_back(): pl.pallas_call(lambda *refs: norm_back_kernel(count, *refs), out_shape=(j...  48.1 us
    pallas_call x1, Pallas kernels, attend_back(): pl.pallas_call(lambda *refs: attend_back_kernel(count, *refs), out_shape=...  46.1 us
    dot_general x3, matrix products, matmul(): lax.dot_general(left, right, (((left_dim,), (right_dim,)), ((), ())), pre...  43.6 us
    ppermute x3, waiting for transfers between devices, neighbour(): return lax.ppermute(values, 'seq', [(i, i ^ step) for i in range(count)])  42.3 us
  transfers between devices with their start and end apart: 10, of which 4 were waited for; matrix products, arithmetic and copies ran while one was open for 7% of the time, Pallas kernels for 53%

profile of v2, /device:TPU:0, one launch (start us, length us, event | category | flops | bytes accessed | tf_op | source)
XLA Modules:
  0.0 641.8 jit_solution(16679835180638078815)
XLA Ops:
  7.2 1.4 slice_bitcast_fusion.1
  8.6 1.8 multiply_reduce_fusion
  11.1 2.8 multiply_convert_fusion.3.refs_0_
  14.5 53.6 %enter.1 = (bf16[4,256,2048]{2,1,0:T(8,128)(2,1)}, bf16[640,2048]{1,0:T(8,128)(2,1)}, bf16[2048,512]{1,0:T(8,128)(2,1)}, f32[1024,64]{1,0:T(8,128)}) custom-call(bf16[256,2048]{1,0:T(8,128)(2,1)} %multiply_convert_fusion.3.refs_0_, f32[8,256]{1,0:T(8,128)} %broadcast_in_dim.36.refs_1_, bf16[320,2048]{1,0:T(8,128)(2,1)} %bitcast.49, bf16[256,2048]{1,0:T(8,128)(2,1)} %bitcast.50), custom_call_target="tpu_custom_call" | custom-call | tf_op jit(solution)/shard_map/enter/pallas_call | solution.py:645
  68.1 2.6 constant_dynamic-slice_fusion.1
  70.8 3.1 copy.17
  74.9 2.2 copy.18
  77.2 9.2 %project_qkv.1 = (bf16[8,1024,64]{2,1,0:T(8,128)(2,1)}, bf16[1024,64]{1,0:T(8,128)(2,1)}, bf16[1024,64]{1,0:T(8,128)(2,1)}) custom-call(s32[1]{0:T(128)} %bitcast.index_ref.refs_0_, bf16[1024,2048]{1,0:T(8,128)(2,1)} %bitcast.35, bf16[640,2048]{1,0:T(8,128)(2,1)} %get-tuple-element.50.weight_ref.refs_1_, f32[1024,64]{1,0:T(8,128)} %get-tuple-element.51.table_ref.refs_7_), custom_call_target="tpu_custom_call" | custom-call | tf_op jit(solution)/shard_map/project_qkv/pallas_call | solution.py:689
  86.4 90.2 %attend.1 = (bf16[1024,512]{1,0:T(8,128)(2,1)}, f32[8,1024]{1,0:T(8,128)}, f32[256,2048]{1,0:T(8,128)}, f32[256,128]{1,0:T(8,128)}, bf16[4,256,2048]{2,1,0:T(8,128)(2,1)}) custom-call(bf16[8,1024,64]{2,1,0:T(8,128)(2,1)} %get-tuple-element.52.refs_0_, bf16[1024,64]{1,0:T(8,128)(2,1)} %get-tuple-element.53.refs_1_, ...), custom_call_target="tpu_custom_call" | custom-call | tf_op jit(solution)/shard_map/attend/pallas_call | solution.py:780
  176.8 1.8 collective-permute-start
  178.8 1.5 collective-permute-start.2
  181.4 21.5 %collective-permute-done = bf16[256,2048]{1,0:T(8,128)(2,1)S(1)} collective-permute-done((bf16[256,2048]{1,0:T(8,128)(2,1)S(1)}, bf16[256,2048]{1,0:T(8,128)(2,1)S(1)}, u32[]{:S(2)}, u32[]{:S(2)}) %collective-permute-start) | collective-permute-done | bytes 1048608 | tf_op jit(solution)/shard_map/ppermute | solution.py:325
  203.9 20.8 %collective-permute-done.1 = bf16[256,2048]{1,0:T(8,128)(2,1)S(1)} collective-permute-done((bf16[256,2048]{1,0:T(8,128)(2,1)S(1)}, bf16[256,2048]{1,0:T(8,128)(2,1)S(1)}, u32[]{:S(2)}, u32[]{:S(2)}) %collective-permute-start.1) | collective-permute-done | bytes 1048608 | tf_op jit(solution)/shard_map/ppermute | solution.py:325
  226.8 17.5 %fusion = f32[1024,2816]{1,0:T(8,128)S(1)} fusion(bf16[1024,2048]{1,0:T(8,128)(2,1)} %bitcast.41, bf16[2816,2048]{1,0:T(8,128)(2,1)} %all-gather.3.cloned.1.call-done.refs_1_), kind=kOutput, calls=%fused_computation.19 | convolution fusion | flops 11811160064 | bytes 27262976 | tf_op jit(solution)/shard_map/dot_general | solution.py:329
  244.4 1.8 multiply_convert_fusion.2.refs_1_
  246.2 2.6 copy-done.1
  248.8 11.9 %convolution_convert_fusion = bf16[2048,1408]{1,0:T(8,128)(2,1)} fusion(bf16[1024,2048]{1,0:T(8,128)(2,1)} %constant_dynamic-update-slice_fusion, bf16[1024,1408]{1,0:T(8,128)(2,1)S(1)} %multiply_convert_fusion.2.refs_1_), kind=kOutput, calls=%fused_computation | convolution fusion | flops 5908463616 | bytes 12845056 | tf_op jit(solution)/shard_map/dot_general | solution.py:329
  260.7 14.1 %multiply_convert_fusion.1 = (bf16[1024,1408]{1,0:T(8,128)(2,1)S(1)}, bf16[1024,1408]{1,0:T(8,128)(2,1)S(1)}) fusion(f32[1024,2816]{1,0:T(8,128)} %copy-done.1, bf16[1024,2048]{1,0:T(8,128)(2,1)} %constant_dynamic-update-slice_fusion, bf16[2048,1408]{1,0:T(8,128)(2,1)} %all-gather.5.cloned.1.call-done.refs_2_), kind=kOutput, calls=%fused_computation.3 | convolution fusion | flops 5924323328 | bytes 27262976 | tf_op jit(solution)/shard_map/dot_general | solution.py:329
  274.8 2.9 pad_maximum_fusion.refs_0_
  277.8 48.1 %norm_back.1 = (f32[256,2048]{1,0:T(8,128)}, f32[1,2048]{1,0:T(1,128)}, bf16[256,2048]{1,0:T(8,128)(2,1)}, bf16[2816,1024]{1,0:T(8,128)(2,1)}, bf16[2816,1024]{1,0:T(8,128)(2,1)}) custom-call(bf16[1024,2816]{1,0:T(8,128)(2,1)} %pad_maximum_fusion.refs_0_, bf16[2816,2048]{1,0:T(8,128)(2,1)} %all-gather.3.cloned.1.call-done.refs_1_, f32[256,2048]{1,0:T(8,128)} %bitcast.38, ...), custom_call_target="tpu_custom_call" | custom-call | tf_op jit(solution)/shard_map/norm_back/pallas_call | solution.py:1224
  327.1 39.6 %share_dy.1 = (bf16[4,256,2048]{2,1,0:T(8,128)(2,1)}, bf16[4,256,2048]{2,1,0:T(8,128)(2,1)}) custom-call(bf16[256,2048]{1,0:T(8,128)(2,1)} %get-tuple-element.65.refs_0_, bf16[1024,1408]{1,0:T(8,128)(2,1)} %copy-done, bf16[2048,1408]{1,0:T(8,128)(2,1)} %all-gather.5.cloned.1.call-done.refs_2_), custom_call_target="tpu_custom_call" | custom-call | tf_op jit(solution)/shard_map/share_dy/pallas_call | solution.py:1271
  366.7 46.1 %attend_back.1 = (bf16[1024,640]{1,0:T(8,128)(2,1)}, bf16[4,160,1024]{2,1,0:T(8,128)(2,1)}, bf16[2048,512]{1,0:T(8,128)(2,1)}, f32[256,2048]{1,0:T(8,128)}) custom-call(bf16[8,1024,64]{2,1,0:T(8,128)(2,1)} %get-tuple-element.52.refs_0_, bf16[1024,64]{1,0:T(8,128)(2,1)} %get-tuple-element.53.refs_1_, bf16[1024,64]{1,0:T(8,128)(2,1)} %get-tuple-element.54.refs_2_, ...), custom_call_target="tpu_custom_call" | custom-call | tf_op jit(solution)/shard_map/attend_back/pallas_call | solution.py:937
  413.7 52.2 %leave.1 = (f32[256,2048]{1,0:T(8,128)}, f32[1,2048]{1,0:T(1,128)}, bf16[640,2048]{1,0:T(8,128)(2,1)}) custom-call(bf16[1024,640]{1,0:T(8,128)(2,1)} %get-tuple-element.69.refs_0_, bf16[640,2048]{1,0:T(8,128)(2,1)} %get-tuple-element.50.weight_ref.refs_1_, f32[256,2048]{1,0:T(8,128)} %get-tuple-element.70.refs_2_, f32[256,2048]{1,0:T(8,128)} %bitcast.34, ...), custom_call_target="tpu_custom_call" | custom-call | tf_op jit(solution)/shard_map/leave/pallas_call | solution.py:1016
  467.2 68.3 %share.3 = (bf16[4,256,1408]{2,1,0:T(8,128)(2,1)}, bf16[4,352,1024]{2,1,0:T(8,128)(2,1)}, f32[2,2048]{1,0:T(2,128)}) custom-call(bf16[256,1408]{1,0:T(8,128)(2,1)} %reduce-scatter.6.cloned.1.call-done.refs_0_, bf16[352,1024]{1,0:T(8,128)(2,1)} %reduce-scatter.8.cloned.1.call-done.refs_1_, f32[2,2048]{1,0:T(2,128)} %pad_maximum_fusion.1.refs_2_), custom_call_target="tpu_custom_call" | custom-call | tf_op jit(solution)/shard_map/share/pallas_call | solution.py:1089
  535.6 23.1 %reduce-scatter.12.cloned.1.call-done.refs_1_ = bf16[256,512]{1,0:T(8,128)(2,1)} async-done(((bf16[2048,512]{1,0:T(8,128)(2,1)}), bf16[256,512]{1,0:T(8,128)(2,1)}) %reduce-scatter.12.cloned.1.call-update) | async-done | bytes 262160 | tf_op jit(solution)/shard_map/reduce_scatter | solution.py:1329
  558.6 35.5 %share.4 = (bf16[4,352,1024]{2,1,0:T(8,128)(2,1)}, bf16[4,256,512]{2,1,0:T(8,128)(2,1)}) custom-call(bf16[352,1024]{1,0:T(8,128)(2,1)} %reduce-scatter.10.cloned.1.call-done.refs_0_, bf16[256,512]{1,0:T(8,128)(2,1)} %reduce-scatter.12.cloned.1.call-done.refs_1_), custom_call_target="tpu_custom_call" | custom-call | tf_op jit(solution)/shard_map/share/pallas_call | solution.py:1089
  594.2 3.3 reduce-scatter.14.cloned.1.call-done.refs_0_
  597.5 14.4 %share.5.refs_1_ = bf16[4,80,2048]{2,1,0:T(8,128)(2,1)} custom-call(bf16[80,2048]{1,0:T(8,128)(2,1)} %reduce-scatter.14.cloned.1.call-done.refs_0_), custom_call_target="tpu_custom_call" | custom-call | tf_op jit(solution)/shard_map/share/pallas_call | solution.py:1089
  611.9 3.0 join_pieces.3
  614.8 2.7 join_pieces.4
  617.5 5.1 join_pieces.5
  622.7 7.5 %join_rows.1 = f32[1408,2048]{1,0:T(8,128)} custom-call(s32[1]{0:T(128)} %bitcast.index_ref.refs_0_, bf16[4,352,1024]{2,1,0:T(8,128)(2,1)} %get-tuple-element.86.refs_0_, bf16[4,352,1024]{2,1,0:T(8,128)(2,1)} %get-tuple-element.87.refs_1_), custom_call_target="tpu_custom_call" | custom-call | tf_op jit(solution)/shard_map/join_rows/pallas_call | solution.py:1111
  (48 shorter events, 14.5 us)
Async XLA Ops:
  7.2 219.7 %all-gather.3.cloned.1.call-start = ((), (), s32[]{:S(2)}) async-start(), calls=%async_computation.5 | async-start | bytes 12976128 | tf_op jit(solution)/shard_map/all_gather | solution.py:1303
  70.8 190.0 %all-gather.5.cloned.1.call-start = ((), (), s32[]{:S(2)}) async-start(), calls=%async_computation.6 | async-start | bytes 6488064 | tf_op jit(solution)/shard_map/all_gather | solution.py:1308
  77.1 390.1 %reduce-scatter.8.cloned.1.call-start = ((), (), s32[]{:S(2)}) async-start(), calls=%async_computation.8 | async-start | bytes 6488064 | tf_op jit(solution)/shard_map/reduce_scatter | solution.py:1329
  86.4 90.2 %copy-start.2 = (f32[1,256,2048]{2,1,0:T(8,128)S(1)}, f32[1,256,2048]{2,1,0:T(8,128)}, u32[]{:S(2)}) copy-start(f32[1,256,2048]{2,1,0:T(8,128)} %param.16) | copy-start | bytes 6291460
  176.8 26.1 %collective-permute-start = (bf16[256,2048]{1,0:T(8,128)(2,1)S(1)}, bf16[256,2048]{1,0:T(8,128)(2,1)S(1)}, u32[]{:S(2)}, u32[]{:S(2)}) collective-permute-start(bf16[256,2048]{1,0:T(8,128)(2,1)S(1)} %bitcast_convert_fusion), channel_id=1, source_target_pairs={{0,1},{1,0},{2,3},{3,2},{4,5},{5,4},{6,7},{7,6},{8,9},{9,8},{10,11... | collective-permute-start | bytes 3145736 | tf_op jit(solution)/shard_map/ppermute | solution.py:325
  178.6 46.1 %collective-permute-start.1 = (bf16[256,2048]{1,0:T(8,128)(2,1)S(1)}, bf16[256,2048]{1,0:T(8,128)(2,1)S(1)}, u32[]{:S(2)}, u32[]{:S(2)}) collective-permute-start(bf16[256,2048]{1,0:T(8,128)(2,1)S(1)} %bitcast_convert_fusion), channel_id=1, source_target_pairs={{0,2},{1,3},{2,0},{3,1},{4,6},{5,7},{6,4},{7,5},{8,10},{9,11},{10,... | collective-permute-start | bytes 3145736 | tf_op jit(solution)/shard_map/ppermute | solution.py:325
  178.8 47.0 %collective-permute-start.2 = (bf16[256,2048]{1,0:T(8,128)(2,1)S(1)}, bf16[256,2048]{1,0:T(8,128)(2,1)S(1)}, u32[]{:S(2)}, u32[]{:S(2)}) collective-permute-start(bf16[256,2048]{1,0:T(8,128)(2,1)S(1)} %bitcast_convert_fusion), channel_id=1, source_target_pairs={{0,3},{1,2},{2,1},{3,0},{4,7},{5,6},{6,5},{7,4},{8,11},{9,10},{10,... | collective-permute-start | bytes 3145736 | tf_op jit(solution)/shard_map/ppermute | solution.py:325
  244.4 4.4 copy-start.1
  248.8 11.9 %copy-start = (bf16[1024,1408]{1,0:T(8,128)(2,1)}, bf16[1024,1408]{1,0:T(8,128)(2,1)S(1)}, u32[]{:S(2)}) copy-start(bf16[1024,1408]{1,0:T(8,128)(2,1)S(1)} %multiply_convert_fusion.2.refs_1_) | copy-start | bytes 8650756
  325.9 141.3 %reduce-scatter.6.cloned.1.call-start = ((), (), s32[]{:S(2)}) async-start(), calls=%async_computation.7 | async-start | bytes 6488064 | tf_op jit(solution)/shard_map/reduce_scatter | solution.py:1329
  326.5 209.1 %reduce-scatter.10.cloned.1.call-start = ((), (), s32[]{:S(2)}) async-start(), calls=%async_computation.9 | async-start | bytes 6488064 | tf_op jit(solution)/shard_map/reduce_scatter | solution.py:1329
  327.1 231.5 %reduce-scatter.12.cloned.1.call-start = ((), (), s32[]{:S(2)}) async-start(), calls=%async_computation.10 | async-start | bytes 2359296 | tf_op jit(solution)/shard_map/reduce_scatter | solution.py:1329
  412.9 184.6 %reduce-scatter.14.cloned.1.call-start = ((), (), s32[]{:S(2)}) async-start(), calls=%async_computation.11 | async-start | bytes 2949120 | tf_op jit(solution)/shard_map/reduce_scatter | solution.py:1329
  413.7 52.2 %copy-start.6 = (f32[1,2048]{1,0:T(1,128)S(1)}, f32[1,2048]{1,0:T(1,128)}, u32[]{:S(2)}) copy-start(f32[1,2048]{1,0:T(1,128)} %get-tuple-element.76) | copy-start | bytes 24580
  622.7 7.5 %copy-start.3 = (f32[256,2048]{1,0:T(8,128)S(1)}, f32[256,2048]{1,0:T(8,128)}, u32[]{:S(2)}) copy-start(f32[256,2048]{1,0:T(8,128)} %get-tuple-element.68) | copy-start | bytes 6291460
  630.2 2.3 copy-start.4
  630.2 3.7 copy-start.5
Sparse Core Ops, SparseCore 0:
  70.9 111.7 all-gather.2
  184.9 58.6 all-gather.4
  326.0 64.2 reduce-scatter.7
  392.5 63.2 reduce-scatter.5
  457.9 63.9 reduce-scatter.9
  524.1 34.5 reduce-scatter.11
  560.9 36.4 reduce-scatter.13

commit v3 on v2

--- a/solution.py
+++ b/solution.py
@@ -460,8 +460,8 @@
     own_ref[half:] += far_ref[1].astype(wide)
 
 
-def share_own(all_ref, half, sems, before):
-    copies = gather_copies(all_ref.at[0], all_ref, half, sems, len(before))
+def share_own(own_ref, all_ref, half, sems, before):
+    copies = gather_copies(own_ref, all_ref, half, sems, len(before))
     for copy in copies[:4]:
         copy.start()
     copies[0].wait_recv()
@@ -475,11 +475,12 @@
 
 
 def enter_kernel(
-    count, normed_ref, spots_ref, shard_ref, out_shard_ref,
-    all_ref, rows_ref, out_ref, table_ref,
-    held_ref, send_sems, recv_sems, spot_send, spot_recv, item_up, item_down, item_side, item_recv, local_sem,
+    count, current_ref, gain_ref, spots_ref, shard_ref, out_shard_ref, gate_up_ref, down_ref,
+    all_ref, rows_ref, out_ref, table_ref, gate_up_part_ref, down_part_ref, scale_ref,
+    normed_ref, held_ref, part_ref, held_down,
+    send_sems, recv_sems, spot_send, spot_recv, item_up, item_down, item_side, item_recv, local_sem,
 ):
-    part, _ = normed_ref.shape
+    part, _ = current_ref.shape
     heads = H // count
     pieces = heads + 2
     items = pieces + lax.axis_size("fsdp")
@@ -506,6 +507,83 @@
     greetings = count + (chip > 0).astype(jnp.int32) + (chip < chips - 1).astype(jnp.int32)
     pl.semaphore_wait(barrier, greetings)
 
+    part_rows = part_ref.shape[0]
+    take = pltpu.make_async_copy(
+        gate_up_ref.at[pl.ds(pl.multiple_of(index * part_rows, part_rows), part_rows)], part_ref, local_sem.at[items + 1]
+    )
+    take.start()
+    take_down = pltpu.make_async_copy(down_ref, held_down, local_sem.at[items + 3])
+    take_down.start()
+
+    def qkv_item(item):
+        block = jnp.where(
+            item < heads, index * heads + item, jnp.where(item == heads, H + index, H + KVH + index)
+        )
+        source = shard_ref.at[pl.ds(pl.multiple_of(block % per_shard * HD, HD), HD)]
+        return block // per_shard, source, rows_ref.at[pl.ds(pl.multiple_of(item * HD, HD), HD)], item
+
+    def out_item(item):
+        source = out_shard_ref.at[:, pl.ds(pl.multiple_of(index * columns, columns), columns)]
+        target = out_ref.at[pl.ds(pl.multiple_of(item * out_rows, out_rows), out_rows)]
+        return item, source, target, item + pieces
+
+    kinds = ((qkv_item, pieces), (out_item, items - pieces))
+
+    def item_copy(source, target, slot, sem, peer):
+        return pltpu.make_async_remote_copy(
+            src_ref=source,
+            dst_ref=target,
+            send_sem=sem.at[slot],
+            recv_sem=item_recv.at[slot],
+            device_id=fsdp_peer(peer),
+            device_id_type=MESH,
+        )
+
+    def pass_on(source, target, slot, owner_chip, act):
+        @pl.when((chip >= owner_chip) & (chip < chips - 1))
+        def _():
+            act(item_copy(source, target, slot, item_up, place + 2))
+
+        @pl.when((chip <= owner_chip) & (chip > 0))
+        def _():
+            act(item_copy(source, target, slot, item_down, place - 2))
+
+        act(item_copy(source, target, slot, item_side, place ^ 1))
+
+    def send_own(item_of):
+        def body(item, carry):
+            owner, source, target, slot = item_of(item)
+
+            @pl.when(place == owner)
+            def _():
+                pass_on(source, target, slot, owner // 2, lambda copy: copy.start())
+                pltpu.make_async_copy(source, target, local_sem.at[slot]).start()
+
+            return carry
+
+        return body
+
+    def pass_far(item_of, distance):
+        def body(item, carry):
+            owner, _, target, slot = item_of(item)
+            owner_chip = owner // 2
+            apart = jnp.where(chip > owner_chip, chip - owner_chip, owner_chip - chip)
+
+            @pl.when((apart == distance) & (core == owner % 2))
+            def _():
+                item_copy(target, target, slot, item_side, place ^ 1).wait_recv()
+                pass_on(target, target, slot, owner_chip, lambda copy: copy.start())
+
+            return carry
+
+        return body
+
+    for item_of, number in kinds:
+        lax.fori_loop(0, number, send_own(item_of), 0)
+    current = current_ref[...]
+    scale = lax.rsqrt(jnp.mean(current * current, 1, keepdims=True) + EPS)
+    scale_ref[...] = jnp.broadcast_to(scale, scale_ref.shape)
+    normed_ref[...] = (current * scale * gain_ref[...]).astype(jnp.bfloat16)
     copies = gather_copies(normed_ref, all_ref, part // 2, sems)
     for copy in copies[:4]:
         copy.start()
@@ -518,72 +596,6 @@
         copy.start()
     own = pltpu.make_async_copy(normed_ref, all_ref.at[0], local_sem.at[items])
     own.start()
-
-    def qkv_item(item):
-        block = jnp.where(
-            item < heads, index * heads + item, jnp.where(item == heads, H + index, H + KVH + index)
-        )
-        source = shard_ref.at[pl.ds(pl.multiple_of(block % per_shard * HD, HD), HD)]
-        return block // per_shard, source, rows_ref.at[pl.ds(pl.multiple_of(item * HD, HD), HD)], item
-
-    def out_item(item):
-        source = out_shard_ref.at[:, pl.ds(pl.multiple_of(index * columns, columns), columns)]
-        target = out_ref.at[pl.ds(pl.multiple_of(item * out_rows, out_rows), out_rows)]
-        return item, source, target, item + pieces
-
-    kinds = ((qkv_item, pieces), (out_item, items - pieces))
-
-    def item_copy(source, target, slot, sem, peer):
-        return pltpu.make_async_remote_copy(
-            src_ref=source,
-            dst_ref=target,
-            send_sem=sem.at[slot],
-            recv_sem=item_recv.at[slot],
-            device_id=fsdp_peer(peer),
-            device_id_type=MESH,
-        )
-
-    def pass_on(source, target, slot, owner_chip, act):
-        @pl.when((chip >= owner_chip) & (chip < chips - 1))
-        def _():
-            act(item_copy(source, target, slot, item_up, place + 2))
-
-        @pl.when((chip <= owner_chip) & (chip > 0))
-        def _():
-            act(item_copy(source, target, slot, item_down, place - 2))
-
-        act(item_copy(source, target, slot, item_side, place ^ 1))
-
-    def send_own(item_of):
-        def body(item, carry):
-            owner, source, target, slot = item_of(item)
-
-            @pl.when(place == owner)
-            def _():
-                pass_on(source, target, slot, owner // 2, lambda copy: copy.start())
-                pltpu.make_async_copy(source, target, local_sem.at[slot]).start()
-
-            return carry
-
-        return body
-
-    def pass_far(item_of, distance):
-        def body(item, carry):
-            owner, _, target, slot = item_of(item)
-            owner_chip = owner // 2
-            apart = jnp.where(chip > owner_chip, chip - owner_chip, owner_chip - chip)
-
-            @pl.when((apart == distance) & (core == owner % 2))
-            def _():
-                item_copy(target, target, slot, item_side, place ^ 1).wait_recv()
-                pass_on(target, target, slot, owner_chip, lambda copy: copy.start())
-
-            return carry
-
-        return body
-
-    for item_of, number in kinds:
-        lax.fori_loop(0, number, send_own(item_of), 0)
     for distance in range(1, chips):
         for item_of, number in kinds:
             lax.fori_loop(0, number, pass_far(item_of, distance), 0)
@@ -592,6 +604,23 @@
                 copies[4].start()
                 copies[1].wait_recv()
                 copies[5].start()
+
+    take.wait()
+    put = pltpu.make_async_copy(part_ref, gate_up_part_ref, local_sem.at[items + 2])
+    put.start()
+    take_down.wait()
+    columns_here = part_rows
+    for device in range(count):
+
+        @pl.when(index == device)
+        def _():
+            down_part_ref[...] = jnp.concatenate(
+                [
+                    held_down[:, start + device * columns_here : start + (device + 1) * columns_here]
+                    for start in range(0, held_down.shape[1], count * columns_here)
+                ],
+                1,
+            )
 
     for copy in spot_copies:
         copy.wait()
@@ -628,32 +657,41 @@
     for item_of, number in kinds:
         lax.fori_loop(0, number, finish(item_of), 0)
     own.wait()
+    put.wait()
     for copy in copies[2:]:
         copy.wait_recv()
     for copy in copies:
         copy.wait_send()
 
 
-def enter(normed, spots, shard, out_shard, count):
-    part, width = normed.shape
+def enter(current, gain, spots, shard, out_shard, gate_up, down, count):
+    part, width = current.shape
     length = part * count
     heads = H // count
     pieces = heads + 2
     items = pieces + lax.axis_size("fsdp")
     vmem = pl.BlockSpec(memory_space=pltpu.VMEM)
     spots = jnp.broadcast_to(spots.astype(jnp.float32)[None], (8, part))
-    gathered, rows, out_cols, table = pl.pallas_call(
+    whole = pl.BlockSpec(memory_space=pl.ANY)
+    part_shape = (gate_up.shape[0] // count, width)
+    gathered, rows, out_cols, table, gate_up_part, down_part, scale = pl.pallas_call(
         lambda *refs: enter_kernel(count, *refs),
         out_shape=(
             jax.ShapeDtypeStruct((count, part, width), jnp.bfloat16),
             jax.ShapeDtypeStruct((pieces * HD, width), jnp.bfloat16),
             jax.ShapeDtypeStruct((out_shard.shape[0] * (items - pieces), heads * HD), jnp.bfloat16),
             jax.ShapeDtypeStruct((length, HD), jnp.float32),
+            jax.ShapeDtypeStruct(part_shape, gate_up.dtype),
+            jax.ShapeDtypeStruct((down.shape[0], down.shape[1] // count), down.dtype),
+            jax.ShapeDtypeStruct((part, 128), jnp.float32),
         ),
-        in_specs=[vmem] * 4,
-        out_specs=[vmem] * 4,
+        in_specs=[vmem] * 5 + [whole] * 2,
+        out_specs=[whole] + [vmem] * 3 + [whole] + [vmem] * 2,
         scratch_shapes=[
+            pltpu.VMEM((part, width), jnp.bfloat16),
             pltpu.VMEM((count, 8, part), jnp.float32),
+            pltpu.VMEM(part_shape, gate_up.dtype),
+            pltpu.VMEM(down.shape, down.dtype),
             pltpu.SemaphoreType.DMA((6,)),
             pltpu.SemaphoreType.DMA((6,)),
             pltpu.SemaphoreType.DMA((count - 1,)),
@@ -662,12 +700,12 @@
             pltpu.SemaphoreType.DMA((items,)),
             pltpu.SemaphoreType.DMA((items,)),
             pltpu.SemaphoreType.DMA((items,)),
-            pltpu.SemaphoreType.DMA((items + 1,)),
+            pltpu.SemaphoreType.DMA((items + 4,)),
         ],
         compiler_params=pltpu.CompilerParams(collective_id=1, has_side_effects=True, vmem_limit_bytes=LIMIT),
         name="enter",
-    )(normed, spots, shard, out_shard)
-    return gathered.reshape(length, width), rows, out_cols, table
+    )(current, gain, spots, shard, out_shard, gate_up, down)
+    return gathered.reshape(length, width), rows, out_cols, table, gate_up_part, down_part, scale
 
 
 def qkv_kernel(index_ref, normed_ref, weight_ref, table_ref, q_ref, k_ref, v_ref):
@@ -715,7 +753,7 @@
 def attend_kernel(
     count, q_ref, k_ref, v_ref, weight_ref, current_ref, gain_ref,
     attn_ref, lse_ref, middle_ref, scale_ref, all_ref,
-    held_ref, sent_ref, side_ref, below_ref, far_ref, send_sems, recv_sems,
+    held_ref, sent_ref, side_ref, below_ref, far_ref, two_ref, send_sems, recv_sems, own_sem,
 ):
     heads, _, _ = q_ref.shape
     part, _ = current_ref.shape
@@ -769,8 +807,11 @@
     middle = middle_ref[...]
     scale = lax.rsqrt(jnp.mean(middle * middle, 1, keepdims=True) + EPS)
     scale_ref[...] = jnp.broadcast_to(scale, scale_ref.shape)
-    all_ref[0] = (middle * scale * gain_ref[...]).astype(jnp.bfloat16)
-    share_own(all_ref, half, sems, sums)
+    two_ref[...] = (middle * scale * gain_ref[...]).astype(jnp.bfloat16)
+    own = pltpu.make_async_copy(two_ref, all_ref.at[0], own_sem)
+    share_own(two_ref, all_ref, half, sems, sums)
+    own.start()
+    own.wait()
 
 
 def attend(queries, keys_in, values_in, weight, current, gain, count):
@@ -787,15 +828,17 @@
             jax.ShapeDtypeStruct((count, part, width), jnp.bfloat16),
         ),
         in_specs=[vmem] * 6,
-        out_specs=[vmem] * 5,
+        out_specs=[vmem] * 4 + [pl.BlockSpec(memory_space=pl.ANY)],
         scratch_shapes=[
             pltpu.VMEM((heads, part, HD), jnp.bfloat16),
             pltpu.VMEM((count, part, width), jnp.bfloat16),
             pltpu.VMEM((2, part // 2, width), jnp.bfloat16),
             pltpu.VMEM((2, part // 2, width), jnp.bfloat16),
             pltpu.VMEM((2, part // 2, width), jnp.bfloat16),
+            pltpu.VMEM((part, width), jnp.bfloat16),
             pltpu.SemaphoreType.DMA((12,)),
             pltpu.SemaphoreType.DMA((12,)),
+            pltpu.SemaphoreType.DMA,
         ],
         compiler_params=pltpu.CompilerParams(collective_id=2, has_side_effects=True, vmem_limit_bytes=LIMIT),
         name="attend",
@@ -833,9 +876,10 @@
 
 
 def attend_back_kernel(
-    count, q_ref, k_ref, v_ref, attn_ref, lse_ref, dy_ref, weight_ref, table_ref, pick_ref, down_ref, middle_ref,
-    out_ref, turned_ref, term_ref, result_ref,
-    do_ref, delta_ref, dq_ref, dk_ref, dv_ref, side_ref, below_ref, far_ref, passed_ref, send_sems, recv_sems,
+    count, q_ref, k_ref, v_ref, attn_ref, lse_ref, dy_ref, weight_ref, table_ref, pick_ref, passed_ref, base_ref, shard_ref,
+    out_ref, turned_ref, term_ref, result_ref, slot_ref,
+    do_ref, delta_ref, dq_ref, dk_ref, dv_ref, far_ref, held_dy, held_base, held_pick,
+    send_sems, recv_sems, load_sems,
 ):
     heads, length, _ = q_ref.shape
     part = length // count
@@ -843,10 +887,28 @@
     index = lax.axis_index("seq")
     greet([seq_peer(1), seq_peer(2)])
     half = part // 2
-    sums = sum_copies(down_ref, side_ref, below_ref, far_ref, half, (send_sems, recv_sems), passed_ref)
-    for copy in sums[:4]:
+    sems = (send_sems, recv_sems)
+    sums = [
+        remote(passed_ref.at[0], far_ref.at[0], sems, 6, seq_peer(2)),
+        remote(passed_ref.at[1], far_ref.at[1], sems, 7, seq_peer(1)),
+    ]
+    group = gather_copies(shard_ref, slot_ref, upper_half(shard_ref.shape[0]), sems)
+    share_start([group])
+    for copy in sums:
         copy.start()
-    result_ref[...] = middle_ref[...] + down_ref[0].astype(wide)
+
+    def load_dy(step):
+        rows = pl.ds(pl.multiple_of(step * part, part), part)
+        return pltpu.make_async_copy(dy_ref.at[rows], held_dy.at[rows], load_sems.at[step])
+
+    loads = [
+        pltpu.make_async_copy(base_ref, held_base, load_sems.at[count]),
+        pltpu.make_async_copy(pick_ref, held_pick, load_sems.at[count + 1]),
+    ]
+    for here in range(count):
+        load_dy(here ^ index).start()
+    for load in loads:
+        load.start()
     dk_ref[...] = jnp.zeros_like(dk_ref)
     dv_ref[...] = jnp.zeros_like(dv_ref)
     owner = lax.broadcasted_iota(jnp.int32, (heads, heads * HD), 1) // HD
@@ -860,7 +922,8 @@
     def one_part(here, carry):
         spot = here ^ index
         rows_here = pl.ds(pl.multiple_of(spot * part, part), part)
-        dattn = matmul(dy_ref[rows_here, :], weight_ref[...], 1, 0).astype(jnp.bfloat16)
+        load_dy(spot).wait()
+        dattn = matmul(held_dy[rows_here, :], weight_ref[...], 1, 0).astype(jnp.bfloat16)
         product = dattn.astype(wide) * attn_ref[rows_here, :].astype(wide)
         delta_ref[...] = lax.dot_general(
             same, product, (((1,), (1,)), ((), ())), precision=lax.Precision.HIGHEST, preferred_element_type=wide
@@ -896,12 +959,7 @@
 
         @pl.when(here == 1)
         def _():
-            sums[0].wait_recv()
-            passed_ref[0] = (down_ref[2, :half].astype(wide) + side_ref[1].astype(wide)).astype(jnp.bfloat16)
-            sums[4].start()
-            sums[1].wait_recv()
-            passed_ref[1] = (down_ref[1, half:].astype(wide) + below_ref[1].astype(wide)).astype(jnp.bfloat16)
-            sums[5].start()
+            share_on(group)
 
         return carry
 
@@ -912,7 +970,9 @@
         both = jnp.concatenate([dk_ref[rows_block], dv_ref[rows_block]], 1).astype(jnp.bfloat16).astype(wide)
         both = unturn(both, *spread_tables(table_ref[rows_there, :], 0, True))
         out_ref[rows_there, heads * HD :] = both.astype(jnp.bfloat16)
-    chosen = matmul(pick_ref[...], out_ref[...], 1, 1).astype(jnp.bfloat16)
+    for load in loads:
+        load.wait()
+    chosen = matmul(held_pick[...], out_ref[...], 1, 1).astype(jnp.bfloat16)
     size = turned_ref.shape[1]
     for block in range(count):
         turned_ref[block] = chosen[block * size : (block + 1) * size]
@@ -920,20 +980,24 @@
 
     def one_tile(number, carry):
         columns = pl.ds(pl.multiple_of(number * tile, tile), tile)
-        term_ref[columns, :] = matmul(dy_ref[:, columns], attn_ref[...], 0, 0).astype(jnp.bfloat16)
+        term_ref[columns, :] = matmul(held_dy[:, columns], attn_ref[...], 0, 0).astype(jnp.bfloat16)
         return carry
 
-    lax.fori_loop(0, dy_ref.shape[1] // tile, one_tile, 0)
-    end_sums(sums, side_ref, below_ref, far_ref, result_ref, half)
+    lax.fori_loop(0, held_dy.shape[1] // tile, one_tile, 0)
+    for copy in sums:
+        copy.wait_recv()
+    result_ref[:half] = held_base[:half] + far_ref[0].astype(wide)
+    result_ref[half:] = held_base[half:] + far_ref[1].astype(wide)
+    share_end([group])
     for copy in sums:
         copy.wait_send()
 
 
-def attend_back(queries, keys_in, values_in, attn, lse, dy, weight, table, pick, down, middle, count):
+def attend_back(queries, keys_in, values_in, attn, lse, dy, weight, table, pick, passed, base, shard, count):
     heads, length, _ = queries.shape
-    part, width = middle.shape
+    part, width = base.shape
     columns = (heads + 2) * HD
-    vmem = pl.BlockSpec(memory_space=pltpu.VMEM)
+    vmem, whole = pl.BlockSpec(memory_space=pltpu.VMEM), pl.BlockSpec(memory_space=pl.ANY)
     return pl.pallas_call(
         lambda *refs: attend_back_kernel(count, *refs),
         out_shape=[
@@ -941,9 +1005,10 @@
             jax.ShapeDtypeStruct((count, columns // count, length), jnp.bfloat16),
             jax.ShapeDtypeStruct((width, heads * HD), jnp.bfloat16),
             jax.ShapeDtypeStruct((part, width), jnp.float32),
+            jax.ShapeDtypeStruct((count,) + shard.shape, shard.dtype),
         ],
-        in_specs=[vmem] * 11,
-        out_specs=[vmem] * 4,
+        in_specs=[vmem] * 5 + [whole] + [vmem] * 2 + [whole] * 4,
+        out_specs=[vmem] * 4 + [whole],
         scratch_shapes=[
             pltpu.VMEM((heads, part, HD), jnp.bfloat16),
             pltpu.VMEM((heads, part), jnp.float32),
@@ -951,17 +1016,19 @@
             pltpu.VMEM((length, HD), jnp.float32),
             pltpu.VMEM((length, HD), jnp.float32),
         ]
-        + [pltpu.VMEM((2, part // 2, width), jnp.bfloat16)] * 4
-        + [pltpu.SemaphoreType.DMA((6,)), pltpu.SemaphoreType.DMA((6,))],
+        + [pltpu.VMEM((2, part // 2, width), jnp.bfloat16)]
+        + [pltpu.VMEM(dy.shape, dy.dtype), pltpu.VMEM(base.shape, base.dtype), pltpu.VMEM(pick.shape, pick.dtype)]
+        + [pltpu.SemaphoreType.DMA((8,)), pltpu.SemaphoreType.DMA((8,)), pltpu.SemaphoreType.DMA((count + 2,))],
         compiler_params=pltpu.CompilerParams(collective_id=4, has_side_effects=True, vmem_limit_bytes=LIMIT),
         name="attend_back",
-    )(queries, keys_in, values_in, attn, lse, dy, weight, table, pick, down, middle)
+    )(queries, keys_in, values_in, attn, lse, dy, weight, table, pick, passed, base, shard)
 
 
 def leave_kernel(
-    count, grads_ref, weight_ref, flowing_ref, first_ref, scale_ref, gain_ref, turned_ref, normed_ref,
+    count, grads_ref, weight_ref, flowing_in, first_in, scale_ref, gain_ref, turned_ref, normed_in,
     own_ref, gain_out_ref, term_ref,
-    sent_ref, side_ref, below_ref, far_ref, slot_ref, whole_ref, send_sems, recv_sems, swap_send, swap_recv,
+    sent_ref, side_ref, below_ref, far_ref, slot_ref, whole_ref, normed_ref, flowing_ref, first_ref,
+    send_sems, recv_sems, swap_send, swap_recv, load_sems,
 ):
     part, _ = flowing_ref.shape
     half = part // 2
@@ -976,7 +1043,19 @@
     ]
     for copy in swaps:
         copy.start()
-    slot_ref[0] = turned_ref[index]
+    loads = [
+        pltpu.make_async_copy(source, target, load_sems.at[number])
+        for number, (source, target) in enumerate(
+            (
+                (turned_ref.at[index], slot_ref.at[0]),
+                (normed_in, normed_ref),
+                (flowing_in, flowing_ref),
+                (first_in, first_ref),
+            )
+        )
+    ]
+    for load in loads:
+        load.start()
     sums = sum_copies(sent_ref, side_ref, below_ref, far_ref, half, (send_sems, recv_sems))
 
     def one_part(turn, carry):
@@ -987,6 +1066,8 @@
         return carry
 
     lax.fori_loop(0, count, one_part, 0)
+    for load in loads:
+        load.wait()
     for step in range(count):
         if step:
             swaps[step - 1].wait_recv()
@@ -1011,7 +1092,7 @@
 
 def leave(grads, weight, flowing, first, scale, gain, turned, normed, count):
     part, width = flowing.shape
-    vmem = pl.BlockSpec(memory_space=pltpu.VMEM)
+    vmem, whole = pl.BlockSpec(memory_space=pltpu.VMEM), pl.BlockSpec(memory_space=pl.ANY)
     size, length = turned.shape[1:]
     own, gain_term, term = pl.pallas_call(
         lambda *refs: leave_kernel(count, *refs),
@@ -1020,7 +1101,7 @@
             jax.ShapeDtypeStruct((1, width), jnp.float32),
             jax.ShapeDtypeStruct((size * count, width), jnp.bfloat16),
         ),
-        in_specs=[vmem] * 8,
+        in_specs=[vmem] * 2 + [whole] * 2 + [vmem] * 2 + [whole] * 2,
         out_specs=[vmem] * 3,
         scratch_shapes=[
             pltpu.VMEM((count, part, width), jnp.bfloat16),
@@ -1029,10 +1110,14 @@
             pltpu.VMEM((2, part // 2, width), jnp.bfloat16),
             pltpu.VMEM((count, size, length), jnp.bfloat16),
             pltpu.VMEM((count * size, length), jnp.bfloat16),
+            pltpu.VMEM(normed.shape, jnp.bfloat16),
+            pltpu.VMEM((part, width), jnp.float32),
+            pltpu.VMEM((part, width), jnp.float32),
             pltpu.SemaphoreType.DMA((6,)),
             pltpu.SemaphoreType.DMA((6,)),
             pltpu.SemaphoreType.DMA((count - 1,)),
             pltpu.SemaphoreType.DMA((count - 1,)),
+            pltpu.SemaphoreType.DMA((4,)),
         ],
         compiler_params=pltpu.CompilerParams(collective_id=5, has_side_effects=True, vmem_limit_bytes=LIMIT),
         name="leave",
@@ -1057,19 +1142,20 @@
         gather_copies(shard, slot, upper_half(shard.shape[0]), (send_sems, recv_sems), 6 * spot)
         for spot, (shard, slot) in enumerate(zip(shards, slots))
     ]
-    share_start(copies)
     if fsdp:
         total_ref[...] = term_ref[...]
     tells = []
     for step, peer in enumerate(steps):
+        if step == 2:
+            share_start(copies)
         told_ref[step] = total_ref[...]
         tell = remote(told_ref.at[step], heard_ref.at[step], (sum_send, sum_recv), step, peer)
         tell.start()
         tell.wait_recv()
         total_ref[...] += heard_ref[step]
         tells.append(tell)
-    for shard, slot in zip(shards, slots):
-        slot[0] = shard[...]
+    if not fsdp:
+        share_start(copies)
     for group in copies:
         share_on(group)
     share_end(copies)
@@ -1090,8 +1176,8 @@
         lambda *refs: share_kernel(len(shards), fsdp, *refs),
         out_shape=[jax.ShapeDtypeStruct((count,) + shard.shape, shard.dtype) for shard in shards]
         + [jax.ShapeDtypeStruct(value.shape, value.dtype) for value in extra],
-        in_specs=[vmem] * (len(shards) + len(extra)),
-        out_specs=[vmem] * (len(shards) + len(extra)),
+        in_specs=[pl.BlockSpec(memory_space=pl.ANY)] * len(shards) + [vmem] * len(extra),
+        out_specs=[pl.BlockSpec(memory_space=pl.ANY)] * len(shards) + [vmem] * len(extra),
         scratch_shapes=scratch,
         compiler_params=pltpu.CompilerParams(
             collective_id=name, has_side_effects=True, vmem_limit_bytes=LIMIT
@@ -1100,44 +1186,65 @@
     )(*shards, *extra)
 
 
-def join_rows_kernel(index_ref, *refs):
-    out_ref = refs[-1]
-    out_ref[...] = jnp.concatenate([ref[0] for ref in refs[:-1]], 1).astype(jnp.float32)
-
-
-def join_rows(index, slots, count):
+def join_rows_kernel(number, index_ref, *refs):
+    owns, slots, out_ref = refs[:number], refs[number : 2 * number], refs[-1]
+    mine = pl.program_id(0) == index_ref[0]
+
+    @pl.when(mine)
+    def _():
+        out_ref[...] = jnp.concatenate([ref[...] for ref in owns], 1).astype(jnp.float32)
+
+    @pl.when(jnp.logical_not(mine))
+    def _():
+        out_ref[...] = jnp.concatenate([ref[0] for ref in slots], 1).astype(jnp.float32)
+
+
+def join_rows(index, owns, slots, count):
     rows = slots[0].shape[1]
     width = sum(slot.shape[2] for slot in slots)
     return pl.pallas_call(
-        join_rows_kernel,
+        lambda *refs: join_rows_kernel(len(owns), *refs),
         out_shape=jax.ShapeDtypeStruct((rows * count, width), jnp.float32),
         grid_spec=pltpu.PrefetchScalarGridSpec(
             num_scalar_prefetch=1,
             grid=(count,),
-            in_specs=[pl.BlockSpec((1,) + slot.shape[1:], lambda i, s: (i ^ s[0], 0, 0)) for slot in slots],
+            in_specs=[pl.BlockSpec(own.shape, lambda i, s: (0, 0)) for own in owns]
+            + [pl.BlockSpec((1,) + slot.shape[1:], lambda i, s: (i ^ s[0], 0, 0)) for slot in slots],
             out_specs=pl.BlockSpec((rows, width), lambda i, s: (i, 0)),
         ),
         compiler_params=pltpu.CompilerParams(vmem_limit_bytes=LIMIT),
         name="join_rows",
-    )(index, *slots)
-
-
-def join_pieces_kernel(count, row_piece, column_piece, index_ref, slot_ref, out_ref):
+    )(index, *owns, *slots)
+
+
+def join_pieces_kernel(count, row_piece, column_piece, index_ref, own_ref, *refs):
+    slot_refs, out_ref = refs[:-1], refs[-1]
     index = index_ref[0]
-    _, rows, columns = slot_ref.shape
+    rows, columns = own_ref.shape
+
     for device in range(count):
-        values = slot_ref[device ^ index].astype(jnp.float32)
-        for top in range(0, rows, row_piece):
-            for left in range(0, columns, column_piece):
-                down = top * count + device * row_piece if row_piece < rows else top
-                across = left * count + device * column_piece if row_piece == rows else left
-                out_ref[down : down + row_piece, across : across + column_piece] = values[
-                    top : top + row_piece, left : left + column_piece
-                ]
-
-
-def join_pieces(index, slots, row_piece, column_piece):
-    count, rows, columns = slots.shape
+
+        def place_pieces(values):
+            values = values.astype(jnp.float32)
+            for top in range(0, rows, row_piece):
+                for left in range(0, columns, column_piece):
+                    down = top * count + device * row_piece if row_piece < rows else top
+                    across = left * count + device * column_piece if row_piece == rows else left
+                    out_ref[down : down + row_piece, across : across + column_piece] = values[
+                        top : top + row_piece, left : left + column_piece
+                    ]
+
+        if len(slot_refs) == 1:
+            values = slot_refs[0][device ^ index]
+        else:
+            values = own_ref[...]
+            for step, ref in enumerate(slot_refs):
+                values = jnp.where(device ^ index == step + 1, ref[...], values)
+        place_pieces(jnp.where(device == index, own_ref[...], values))
+
+
+def join_pieces(index, own, slots, count, row_piece, column_piece):
+    rows, columns = own.shape
     shape = (rows * count, columns) if row_piece < rows else (rows, columns * count)
     return pl.pallas_call(
         lambda *refs: join_pieces_kernel(count, row_piece, column_piece, *refs),
@@ -1145,24 +1252,61 @@
         grid_spec=pltpu.PrefetchScalarGridSpec(
             num_scalar_prefetch=1,
             grid=(1,),
-            in_specs=[pl.BlockSpec(slots.shape, lambda i, s: (0, 0, 0))],
+            in_specs=[pl.BlockSpec(own.shape, lambda i, s: (0, 0))]
+            + [pl.BlockSpec(slot.shape, lambda i, s, n=slot.ndim: (0,) * n) for slot in slots],
             out_specs=pl.BlockSpec(shape, lambda i, s: (0, 0)),
         ),
         compiler_params=pltpu.CompilerParams(vmem_limit_bytes=LIMIT),
         name="join_pieces",
-    )(index, slots)
+    )(index, own, *slots)
 
 
 def norm_back_kernel(
-    count, grads_ref, weight_ref, flowing_ref, middle_ref, scale_ref, gain_ref, inputs_ref,
-    own_ref, gain_out_ref, dy_ref, left_ref, right_ref,
-    sent_ref, side_ref, below_ref, far_ref, stage_ref, send_sems, recv_sems, store_sems,
+    count, grads_ref, weight_ref, flowing_in, middle_in, scale_ref, gain_ref, inputs_ref,
+    own_ref, gain_out_ref, dy_ref, term_ref,
+    sent_ref, side_ref, below_ref, far_ref, stage_ref, held_grads, held_weight, held_inputs, flowing_ref, middle_ref,
+    send_sems, recv_sems, store_sems, load_sems,
 ):
     part, width = flowing_ref.shape
     half = part // 2
     sems = (send_sems, recv_sems)
+    units = grads_ref.shape[1]
+    tile = stage_ref.shape[1]
+    tiles = units // tile
+    cuts = [tiles * number // 4 * tile for number in range(5)]
+    last = pl.ds((count - 1) * part, part)
+    rest = pl.ds(0, (count - 1) * part)
+    load_last = pltpu.make_async_copy(grads_ref.at[last], held_grads.at[last], load_sems.at[0])
+    load_last.start()
+    load_weight = []
+    for number in range(4):
+        rows = pl.ds(cuts[number], cuts[number + 1] - cuts[number])
+        load = pltpu.make_async_copy(weight_ref.at[rows], held_weight.at[rows], load_sems.at[1 + number])
+        load.start()
+        load_weight.append(load)
+    load_rest = pltpu.make_async_copy(grads_ref.at[rest], held_grads.at[rest], load_sems.at[5])
+    load_rest.start()
+    load_inputs = pltpu.make_async_copy(inputs_ref, held_inputs, load_sems.at[6])
+    load_inputs.start()
+    load_ends = [
+        pltpu.make_async_copy(flowing_in, flowing_ref, load_sems.at[7]),
+        pltpu.make_async_copy(middle_in, middle_ref, load_sems.at[8]),
+    ]
+    for load in load_ends:
+        load.start()
+    grads_ref, weight_ref, inputs_ref = held_grads, held_weight, held_inputs
+    load_last.wait()
+    partial = jnp.zeros((part, width), jnp.float32)
+    for number in range(4):
+        load_weight[number].wait()
+        rows = slice(cuts[number], cuts[number + 1])
+        partial += matmul(grads_ref[last, rows], weight_ref[rows, :], 1, 0)
+    sent_ref[count - 1] = partial.astype(jnp.bfloat16)
     greet([seq_peer(1), seq_peer(2)])
     sums = sum_copies(sent_ref, side_ref, below_ref, far_ref, half, sems)
+    sums[0].start()
+    sums[1].start()
+    load_rest.wait()
 
     def one_part(turn, carry):
         step = count - 1 - turn
@@ -1171,33 +1315,23 @@
         pass_sums(turn, step, partial, sums, sent_ref, side_ref, below_ref, own_ref, half)
         return carry
 
-    lax.fori_loop(0, count, one_part, 0)
-
-    tile = stage_ref.shape[1]
-    tiles = grads_ref.shape[1] // tile
-
-    def stores(number):
-        slot = number % 2
+    lax.fori_loop(1, count, one_part, 0)
+    load_inputs.wait()
+    for load in load_ends:
+        load.wait()
+
+    def store(number):
         rows = pl.ds(pl.multiple_of(number * tile, tile), tile)
-        return [
-            pltpu.make_async_copy(
-                stage_ref.at[slot, :, pl.ds(place * (width // 2), width // 2)],
-                target.at[rows],
-                store_sems.at[place, slot],
-            )
-            for place, target in enumerate((left_ref, right_ref))
-        ]
+        return pltpu.make_async_copy(stage_ref.at[number % 2], term_ref.at[rows], store_sems.at[number % 2])
 
     def one_tile(number, carry):
         @pl.when(number >= 2)
         def _():
-            for store in stores(number - 2):
-                store.wait()
+            store(number - 2).wait()
 
         columns = pl.ds(pl.multiple_of(number * tile, tile), tile)
         stage_ref[number % 2] = matmul(grads_ref[:, columns], inputs_ref[...], 0, 0).astype(jnp.bfloat16)
-        for store in stores(number):
-            store.start()
+        store(number).start()
         return carry
 
     lax.fori_loop(0, tiles, one_tile, 0)
@@ -1210,8 +1344,7 @@
     own_ref[...] = flowing_ref[...] + scale * (inner - unit * jnp.mean(inner * unit, 1, keepdims=True))
     dy_ref[...] = own_ref[...].astype(jnp.bfloat16)
     for number in range(tiles - 2, tiles):
-        for store in stores(number):
-            store.wait()
+        store(number).wait()
     for copy in sums:
         copy.wait_send()
 
@@ -1221,68 +1354,94 @@
     units = grads.shape[1]
     tile = 2 * 128
     vmem = pl.BlockSpec(memory_space=pltpu.VMEM)
-    own, gain_term, dy, left, right = pl.pallas_call(
+    own, gain_term, dy, term = pl.pallas_call(
         lambda *refs: norm_back_kernel(count, *refs),
         out_shape=(
             jax.ShapeDtypeStruct((part, width), jnp.float32),
             jax.ShapeDtypeStruct((1, width), jnp.float32),
             jax.ShapeDtypeStruct((part, width), jnp.bfloat16),
-            jax.ShapeDtypeStruct((units, width // 2), jnp.bfloat16),
-            jax.ShapeDtypeStruct((units, width // 2), jnp.bfloat16),
+            jax.ShapeDtypeStruct((units, width), jnp.bfloat16),
         ),
-        in_specs=[vmem] * 7,
-        out_specs=[vmem] * 3 + [pl.BlockSpec(memory_space=pl.ANY)] * 2,
+        in_specs=[pl.BlockSpec(memory_space=pl.ANY)] * 4 + [vmem] * 2 + [pl.BlockSpec(memory_space=pl.ANY)],
+        out_specs=[vmem] * 3 + [pl.BlockSpec(memory_space=pl.ANY)],
         scratch_shapes=[
             pltpu.VMEM((count, part, width), jnp.bfloat16),
             pltpu.VMEM((2, part // 2, width), jnp.bfloat16),
             pltpu.VMEM((2, part // 2, width), jnp.bfloat16),
             pltpu.VMEM((2, part // 2, width), jnp.bfloat16),
             pltpu.VMEM((2, tile, width), jnp.bfloat16),
+            pltpu.VMEM(grads.shape, jnp.bfloat16),
+            pltpu.VMEM(weight.shape, jnp.bfloat16),
+            pltpu.VMEM(inputs.shape, jnp.bfloat16),
+            pltpu.VMEM((part, width), jnp.float32),
+            pltpu.VMEM((part, width), jnp.float32),
             pltpu.SemaphoreType.DMA((6,)),
             pltpu.SemaphoreType.DMA((6,)),
-            pltpu.SemaphoreType.DMA((2, 2)),
+            pltpu.SemaphoreType.DMA((2,)),
+            pltpu.SemaphoreType.DMA((9,)),
         ],
         compiler_params=pltpu.CompilerParams(collective_id=3, has_side_effects=True, vmem_limit_bytes=LIMIT),
         name="norm_back",
     )(grads, weight, flowing, middle, scale, gain, inputs)
-    return own, gain_term[0], dy, left, right
-
-
-def share_dy_kernel(count, dy_ref, act_ref, weight_ref, all_ref, down_ref, send_sems, recv_sems):
+    return own, gain_term[0], dy, term
+
+
+def share_dy_kernel(
+    dy_ref, down_ref, side_ref, below_ref, middle_ref, all_ref, base_ref, passed_ref,
+    piece_ref, send_sems, recv_sems, load_sems,
+):
     part = dy_ref.shape[0]
+    half = part // 2
+    wide = jnp.float32
+    top, bottom = pl.ds(0, half), pl.ds(half, half)
+    loads = [
+        pltpu.make_async_copy(down_ref.at[0], piece_ref.at[0], load_sems.at[0]),
+        pltpu.make_async_copy(down_ref.at[2].at[top], piece_ref.at[1].at[top], load_sems.at[1]),
+        pltpu.make_async_copy(down_ref.at[1].at[bottom], piece_ref.at[1].at[bottom], load_sems.at[2]),
+        pltpu.make_async_copy(dy_ref, all_ref.at[0], load_sems.at[3]),
+    ]
     greet([seq_peer(1), seq_peer(2)])
-    group = gather_copies(dy_ref, all_ref, part // 2, (send_sems, recv_sems))
+    group = gather_copies(dy_ref, all_ref, half, (send_sems, recv_sems))
     share_start([group])
-    all_ref[0] = dy_ref[...]
-
-    def one_part(step, carry):
-        rows = pl.ds(pl.multiple_of(step * part, part), part)
-        down_ref[step] = matmul(act_ref[rows, :], weight_ref[...], 1, 1).astype(jnp.bfloat16)
-        return carry
-
-    lax.fori_loop(0, count, one_part, 0)
+    for load in loads:
+        load.start()
+    for load in loads:
+        load.wait()
+    base_ref[...] = middle_ref[...] + piece_ref[0].astype(wide)
+    base_ref[:half] += side_ref[0].astype(wide)
+    base_ref[half:] += below_ref[0].astype(wide)
+    passed_ref[0] = (piece_ref[1, :half].astype(wide) + side_ref[1].astype(wide)).astype(jnp.bfloat16)
+    passed_ref[1] = (piece_ref[1, half:].astype(wide) + below_ref[1].astype(wide)).astype(jnp.bfloat16)
     share_on(group)
     share_end([group])
 
 
-def share_dy(dy, act, weight, count):
+def share_dy(dy, down, side, below, middle, count):
     part, width = dy.shape
-    vmem = pl.BlockSpec(memory_space=pltpu.VMEM)
-    gathered, down = pl.pallas_call(
-        lambda *refs: share_dy_kernel(count, *refs),
-        out_shape=[jax.ShapeDtypeStruct((count, part, width), jnp.bfloat16)] * 2,
-        in_specs=[vmem] * 3,
-        out_specs=[vmem] * 2,
-        scratch_shapes=[pltpu.SemaphoreType.DMA((6,)), pltpu.SemaphoreType.DMA((6,))],
+    vmem, whole = pl.BlockSpec(memory_space=pltpu.VMEM), pl.BlockSpec(memory_space=pl.ANY)
+    gathered, base, passed = pl.pallas_call(
+        lambda *refs: share_dy_kernel(*refs),
+        out_shape=[
+            jax.ShapeDtypeStruct((count, part, width), jnp.bfloat16),
+            jax.ShapeDtypeStruct((part, width), jnp.float32),
+            jax.ShapeDtypeStruct((2, part // 2, width), jnp.bfloat16),
+        ],
+        in_specs=[vmem, whole, vmem, vmem, vmem],
+        out_specs=[whole, vmem, vmem],
+        scratch_shapes=[
+            pltpu.VMEM((2, part, width), jnp.bfloat16),
+            pltpu.SemaphoreType.DMA((6,)),
+            pltpu.SemaphoreType.DMA((6,)),
+            pltpu.SemaphoreType.DMA((4,)),
+        ],
         compiler_params=pltpu.CompilerParams(collective_id=8, has_side_effects=True, vmem_limit_bytes=LIMIT),
         name="share_dy",
-    )(dy, act, weight)
-    return gathered.reshape(part * count, width), down
+    )(dy, down, side, below, middle)
+    return gathered.reshape(part * count, width), base, passed
 
 
 def fast_body(hidden, positions, gains, w_qkv, w_out, w_gate_up, w_down, cotangent):
     count = lax.axis_size("seq")
-    fsdp = lax.axis_size("fsdp")
     index = lax.axis_index("seq")
     place = index.astype(jnp.int32).reshape(1)
     current = hidden[0]
@@ -1295,31 +1454,21 @@
     group = math.gcd(rows, HD)
     chunk = group // count
     per_head = HD // group
-    normed, scale_one = normalize(current, gain[0])
-    scale_one = jnp.broadcast_to(scale_one, (part_len, 128))
-    normed_all, qkv_rows, out_cols, table = enter(normed, positions[0], w_qkv[0], w_out[0], count)
-    normed_all, gate_up_shard = after((normed_all, w_gate_up[0]))
+    normed_all, qkv_rows, out_cols, table, gate_up_part, down_part, scale_one = enter(
+        current, gain[:1], positions[0], w_qkv[0], w_out[0], w_gate_up[0], w_down[0], count
+    )
     gu_rows = w_gate_up.shape[1] // count
-    gate_up = lax.all_gather(
-        lax.dynamic_slice_in_dim(gate_up_shard, index * gu_rows, gu_rows, 0), "fsdp", axis=0, tiled=True
-    )
+    gate_up = lax.all_gather(gate_up_part, "fsdp", axis=0, tiled=True)
     units = FF // count
     down_rows = w_down.shape[1]
-    down_cols = lax.all_gather(
-        lax.dynamic_index_in_dim(
-            w_down[0].reshape(down_rows, fsdp // 2, count, gu_rows), index, 2, keepdims=False
-        ).reshape(down_rows, units),
-        "fsdp",
-        axis=0,
-        tiled=True,
-    )
 
     queries, keys_in, values_in = project_qkv(place, normed_all, qkv_rows, table, count)
     attn_flat, log_total, middle, scale_two, normed_two_all = attend(
         queries, keys_in, values_in, out_cols, current, gain[1:], count
     )
     flowing = cotangent[0]
-    normed_two_all, dm_sent = after((normed_two_all, flowing.astype(jnp.bfloat16)))
+    normed_two_all, dm_sent, down_part = after((normed_two_all, flowing.astype(jnp.bfloat16), down_part))
+    down_cols = lax.all_gather(down_part, "fsdp", axis=0, tiled=True)
     dm_all = jnp.concatenate([dm_sent] + [neighbour(dm_sent, step) for step in range(1, count)], 0)
     both = matmul(normed_two_all, gate_up, 1, 1)
     gate_part, up_part = both[:, :units], both[:, units:]
@@ -1329,41 +1478,46 @@
         return lax.psum_scatter(grad.astype(jnp.bfloat16), "fsdp", scatter_dimension=0, tiled=True)
 
     term_down = matmul(dm_all, activated, 0, 0).astype(jnp.bfloat16)
-    dm_all, term_down = after((dm_all, term_down))
+    dm_all, activated, term_down = after((dm_all, activated, term_down))
     grad_down = owned(term_down)
+    down_sent = matmul(activated, down_cols, 1, 1).astype(jnp.bfloat16)
+    down_sent = down_sent.reshape(count, part_len, width)
+    dm_all, down_sent = after((dm_all, down_sent))
+    half = part_len // 2
+    from_side = neighbour(jnp.stack([down_sent[1, :half], down_sent[3, :half]]), 1)
+    from_below = neighbour(jnp.stack([down_sent[2, half:], down_sent[3, half:]]), 2)
     dact = matmul(dm_all, down_cols, 1, 0)
     sigma = jax.nn.sigmoid(gate_part)
     dgate = dact * up_part * sigma * (1.0 + gate_part * (1.0 - sigma))
     dup = dact * gate_part * sigma
     dgu = jnp.concatenate([dgate, dup], 1).astype(jnp.bfloat16)
-    dmiddle, gain_two, dy, *terms_gate_up = norm_back(
+    dmiddle, gain_two, dy, term_gate_up = norm_back(
         dgu, gate_up, flowing, middle, scale_two, gain[1:], normed_two_all, count
     )
-    grads_gate_up = [owned(terms_gate_up[0]), owned(terms_gate_up[1])]
-    dy_all, down_sent = share_dy(dy, activated, down_cols, count)
+    grad_gate_up = owned(term_gate_up)
+    dy_all, base, passed = share_dy(dy, down_sent, from_side, from_below, middle, count)
     pieces = heads + 2
     picked = np.arange(pieces * HD).reshape(pieces * per_head, count, chunk).transpose(1, 0, 2).reshape(-1)
     pick = jnp.asarray(picked[:, None] == np.arange(pieces * HD)[None, :], jnp.bfloat16)
-    djoint, djoint_turned, term_out, result = attend_back(
-        queries, keys_in, values_in, attn_flat, log_total, dy_all, out_cols, table, pick, down_sent, middle, count
+    djoint, djoint_turned, term_out, result, down_slots = attend_back(
+        queries, keys_in, values_in, attn_flat, log_total, dy_all, out_cols, table, pick, passed, base, grad_down,
+        count,
     )
     grad_out = owned(term_out)
     grad_hidden, gain_one, term_qkv = leave(
         djoint, qkv_rows, dmiddle, current, scale_one, gain[:1], djoint_turned, normed_all, count
     )
     grad_qkv = owned(term_qkv)
-    down_slots, gate_up_slots, gain_total = share(
-        6, (grad_down, grads_gate_up[0]), count, jnp.stack([gain_one, gain_two])
-    )
-    grad_gate_up_b, gate_up_slots = after((grads_gate_up[1], gate_up_slots))
-    gate_up_slots_b, out_slots = share(7, (grad_gate_up_b, grad_out), count)
-    gate_up_slots_b, grad_qkv = after((gate_up_slots_b, grad_qkv))
-    (qkv_slots,) = share(9, (grad_qkv,), count)
+    gate_up_slots, gain_total = share(6, (grad_gate_up,), count, jnp.stack([gain_one, gain_two]))
+    grad_out, gate_up_slots = after((grad_out, gate_up_slots))
+    (out_slots,) = share(7, (grad_out,), count)
+    gate_up_slots, grad_qkv, down_slots, out_slots = after((gate_up_slots, grad_qkv, down_slots, out_slots))
+    qkv_slots = [neighbour(grad_qkv, step) for step in range(1, count)]
     gain_total = gain_total[None]
-    down_shard = join_pieces(place, down_slots, down_rows, gu_rows)
-    gate_up_shard = join_rows(place, (gate_up_slots, gate_up_slots_b), count)
-    out_shard = join_pieces(place, out_slots, down_rows, heads * HD)
-    qkv_shard = join_pieces(place, qkv_slots, chunk, width)
+    down_shard = join_pieces(place, grad_down, (down_slots,), count, down_rows, gu_rows)
+    gate_up_shard = join_rows(place, (grad_gate_up,), (gate_up_slots,), count)
+    out_shard = join_pieces(place, grad_out, (out_slots,), count, down_rows, heads * HD)
+    qkv_shard = join_pieces(place, grad_qkv, qkv_slots, count, chunk, width)
     return (
         result[None],
         grad_hidden[None],

time: 650 us -> 586 us (0.902)
  Pallas kernels: 476 us -> 415 us
  waiting for transfers between devices: 69.8 us -> 61.5 us
  matrix products: 43.6 us -> 51.8 us
    pallas_call x3 -> x2, Pallas kernels: 118 us -> 72.4 us  [share(): pl.pallas_call(lambda *refs: share_kernel(len(shards), fsdp, *refs), out_...]
    reduce_scatter x5 -> x4, waiting for transfers between devices: 26.4 us -> 0.07 us  [owned(): lax.psum_scatter(grad.astype(jnp.bfloat16), 'fsdp', scatter_dimension=0,...]
    ppermute x3 -> x8, waiting for transfers between devices: 42.3 us -> 61.3 us  [neighbour(): return lax.ppermute(values, 'seq', [(i, i ^ step) for i in range(count)])]
    dot_general x3 -> x4, matrix products: 43.6 us -> 51.8 us  [matmul(): lax.dot_general(left, right, (((left_dim,), (right_dim,)), ((), ())), pre...]
    unnamed x21 -> x30, local copies, waits for them, and re-layouts: 13.1 us -> 12.8 us
  transfers between devices with their start and end apart: 10 -> 14, of which waited for: 4 -> 4; matrix products, arithmetic and copies ran while one was open for 7% -> 11% of each run, Pallas kernels for 53% -> 62%
where the time goes in v3:
time: 586 us; the launch traced here: 578 us
  Pallas kernels  415 us (71%)
  waiting for transfers between devices  61.5 us (10%)
  matrix products  51.8 us (9%)
  local copies, waits for them, and re-layouts  18.4 us (3%)
  between operations  14.5 us (2%)
  starting transfers between devices  9.85 us (2%)
  other arithmetic  6.95 us (1%)
    pallas_call x1, Pallas kernels, attend(): pl.pallas_call(lambda *refs: attend_kernel(count, *refs), out_shape=(jax....  90.1 us
    pallas_call x2, Pallas kernels, share(): pl.pallas_call(lambda *refs: share_kernel(len(shards), fsdp, *refs), out_...  72.4 us
    ppermute x8, waiting for transfers between devices, neighbour(): return lax.ppermute(values, 'seq', [(i, i ^ step) for i in range(count)])  61.3 us
    pallas_call x1, Pallas kernels, enter(): pl.pallas_call(lambda *refs: enter_kernel(count, *refs), out_shape=(jax.S...  52.8 us
    dot_general x4, matrix products, matmul(): lax.dot_general(left, right, (((left_dim,), (right_dim,)), ((), ())), pre...  51.8 us
    pallas_call x1, Pallas kernels, leave(): pl.pallas_call(lambda *refs: leave_kernel(count, *refs), out_shape=(jax.S...  50.8 us
    pallas_call x1, Pallas kernels, norm_back(): pl.pallas_call(lambda *refs: norm_back_kernel(count, *refs), out_shape=(j...  43.7 us
    pallas_call x1, Pallas kernels, attend_back(): pl.pallas_call(lambda *refs: attend_back_kernel(count, *refs), out_shape=...  41.2 us
  transfers between devices with their start and end apart: 14, of which 4 were waited for; matrix products, arithmetic and copies ran while one was open for 11% of the time, Pallas kernels for 62%

profile of v3, /device:TPU:0, one launch (start us, length us, event | category | flops | bytes accessed | tf_op | source)
XLA Modules:
  0.0 578.4 jit_solution(8497831654545527204)
XLA Ops:
  7.9 1.4 slice_bitcast_fusion
  9.9 52.8 %enter.1 = (bf16[4,256,2048]{2,1,0:T(8,128)(2,1)}, bf16[640,2048]{1,0:T(8,128)(2,1)}, bf16[2048,512]{1,0:T(8,128)(2,1)}, f32[1024,64]{1,0:T(8,128)}, bf16[352,20...) custom-call(f32[256,2048]{1,0:T(8,128)} %bitcast.32, f32[1,2048]{1,0:T(1,128)} %get-tuple-element.104.refs_1_.refs_5_, ...), custom_call_target="tpu_custom_call" | custom-call | tf_op jit(solution)/shard_map/enter/pallas_call | solution.py:677
  62.8 9.1 %project_qkv.1 = (bf16[8,1024,64]{2,1,0:T(8,128)(2,1)}, bf16[1024,64]{1,0:T(8,128)(2,1)}, bf16[1024,64]{1,0:T(8,128)(2,1)}) custom-call(s32[1]{0:T(128)} %bitcast.index_ref.refs_0_, bf16[1024,2048]{1,0:T(8,128)(2,1)} %bitcast.35, bf16[640,2048]{1,0:T(8,128)(2,1)} %get-tuple-element.54.weight_ref.refs_1_, f32[1024,64]{1,0:T(8,128)} %get-tuple-element.55.table_ref.refs_7_), custom_call_target="tpu_custom_call" | custom-call | tf_op jit(solution)/shard_map/project_qkv/pallas_call | solution.py:727
  71.9 90.1 %attend.1 = (bf16[1024,512]{1,0:T(8,128)(2,1)}, f32[8,1024]{1,0:T(8,128)}, f32[256,2048]{1,0:T(8,128)}, f32[256,128]{1,0:T(8,128)}, bf16[4,256,2048]{2,1,0:T(8,128)(2,1)}) custom-call(bf16[8,1024,64]{2,1,0:T(8,128)(2,1)} %get-tuple-element.56.refs_0_, bf16[1024,64]{1,0:T(8,128)(2,1)} %get-tuple-element.57.refs_1_, ...), custom_call_target="tpu_custom_call" | custom-call | tf_op jit(solution)/shard_map/attend/pallas_call | solution.py:821
  162.4 1.8 collective-permute-start
  164.5 1.5 collective-permute-start.2
  167.0 21.5 %collective-permute-done = bf16[256,2048]{1,0:T(8,128)(2,1)S(1)} collective-permute-done((bf16[256,2048]{1,0:T(8,128)(2,1)S(1)}, bf16[256,2048]{1,0:T(8,128)(2,1)S(1)}, u32[]{:S(2)}, u32[]{:S(2)}) %collective-permute-start) | collective-permute-done | bytes 1048608 | tf_op jit(solution)/shard_map/ppermute | solution.py:325
  189.6 20.8 %collective-permute-done.1 = bf16[256,2048]{1,0:T(8,128)(2,1)S(1)} collective-permute-done((bf16[256,2048]{1,0:T(8,128)(2,1)S(1)}, bf16[256,2048]{1,0:T(8,128)(2,1)S(1)}, u32[]{:S(2)}, u32[]{:S(2)}) %collective-permute-start.1) | collective-permute-done | bytes 1048608 | tf_op jit(solution)/shard_map/ppermute | solution.py:325
  212.4 17.3 %fusion.1 = f32[1024,2816]{1,0:T(8,128)S(1)} fusion(bf16[1024,2048]{1,0:T(8,128)(2,1)} %bitcast.44, bf16[2816,2048]{1,0:T(8,128)(2,1)} %all-gather.3.cloned.1.call-done.refs_1_), kind=kOutput, calls=%fused_computation.17 | convolution fusion | flops 11811160064 | bytes 27262976 | tf_op jit(solution)/shard_map/dot_general | solution.py:329
  229.7 1.8 multiply_convert_fusion.2
  231.5 2.6 copy-done
  234.2 10.9 %convolution_convert_fusion = bf16[2048,1408]{1,0:T(8,128)(2,1)} fusion(bf16[1024,2048]{1,0:T(8,128)(2,1)} %constant_dynamic-update-slice_fusion, bf16[1024,1408]{1,0:T(8,128)(2,1)S(1)} %multiply_convert_fusion.2), kind=kOutput, calls=%fused_computation | convolution fusion | flops 5908463616 | bytes 12845056 | tf_op jit(solution)/shard_map/dot_general | solution.py:329
  245.4 11.0 %convolution_convert_fusion.1 = bf16[1024,2048]{1,0:T(8,128)(2,1)} fusion(bf16[1024,1408]{1,0:T(8,128)(2,1)S(1)} %multiply_convert_fusion.2, bf16[2048,1408]{1,0:T(8,128)(2,1)} %all-gather.5.cloned.1.call-done), kind=kOutput, calls=%fused_computation.6 | convolution fusion | flops 5907677184 | bytes 12845056 | tf_op jit(solution)/shard_map/dot_general | solution.py:329
  256.4 12.5 %multiply_convert_fusion.1 = (bf16[1024,1408]{1,0:T(8,128)(2,1)S(1)}, bf16[1024,1408]{1,0:T(8,128)(2,1)S(1)}) fusion(f32[1024,2816]{1,0:T(8,128)} %copy-done, bf16[1024,2048]{1,0:T(8,128)(2,1)} %constant_dynamic-update-slice_fusion, bf16[2048,1408]{1,0:T(8,128)(2,1)S(1)} %copy-done.11), kind=kOutput, calls=%fused_computation.3 | convolution fusion | flops 5924323328 | bytes 27262976 | tf_op jit(solution)/shard_map/dot_general | solution.py:329
  268.9 2.9 pad_maximum_fusion.refs_0_
  271.9 43.7 %norm_back.1 = (f32[256,2048]{1,0:T(8,128)}, f32[1,2048]{1,0:T(1,128)}, bf16[256,2048]{1,0:T(8,128)(2,1)}, bf16[2816,2048]{1,0:T(8,128)(2,1)}) custom-call(bf16[1024,2816]{1,0:T(8,128)(2,1)} %pad_maximum_fusion.refs_0_, bf16[2816,2048]{1,0:T(8,128)(2,1)} %all-gather.3.cloned.1.call-done.refs_1_, f32[256,2048]{1,0:T(8,128)} %bitcast.41, ...), custom_call_target="tpu_custom_call" | custom-call | tf_op jit(solution)/shard_map/norm_back/pallas_call | solution.py:1357
  318.7 1.7 collective-permute-start.4
  320.4 18.9 %collective-permute-done.3.refs_2_ = bf16[2,128,2048]{2,1,0:T(8,128)(2,1)S(1)} collective-permute-done((bf16[2,128,2048]{2,1,0:T(8,128)(2,1)S(1)}, bf16[2,128,2048]{2,1,0:T(8,128)(2,1)S(1)}, u32[]{:S(2)}, u32[]{:S(2)}) %collective-permute-start.3) | collective-permute-done | bytes 1048608 | tf_op jit(solution)/shard_map/ppermute | solution.py:325
  340.7 36.2 %share_dy.1 = (bf16[4,256,2048]{2,1,0:T(8,128)(2,1)}, f32[256,2048]{1,0:T(8,128)}, bf16[2,128,2048]{2,1,0:T(8,128)(2,1)}) custom-call(bf16[256,2048]{1,0:T(8,128)(2,1)} %get-tuple-element.73.refs_0_, bf16[4,256,2048]{2,1,0:T(8,128)(2,1)} %bitcast.40, bf16[2,128,2048]{2,1,0:T(8,128)(2,1)} %copy-done.4, bf16[2,128,2048]{2,1,0:T(8,128)(2,1)} %copy-done.5, ...), custom_call_target="tpu_custom_call" | custom-call | tf_op jit(solution)/shard_map/share_dy/pallas_call | solution.py:1422
  376.9 41.2 %attend_back.1 = (bf16[1024,640]{1,0:T(8,128)(2,1)}, bf16[4,160,1024]{2,1,0:T(8,128)(2,1)}, bf16[2048,512]{1,0:T(8,128)(2,1)}, f32[256,2048]{1,0:T(8,128)}, bf16[4,256,1408]{2,1,0:T(8,128)(2,1)}) custom-call(bf16[8,1024,64]{2,1,0:T(8,128)(2,1)} %get-tuple-element.56.refs_0_, bf16[1024,64]{1,0:T(8,128)(2,1)} %get-tuple-element.57.refs_1_, ...), custom_call_target="tpu_custom_call" | custom-call | tf_op jit(solution)/shard_map/attend_back/pallas_call | solution.py:1001
  418.2 50.8 %leave.1 = (f32[256,2048]{1,0:T(8,128)}, f32[1,2048]{1,0:T(1,128)}, bf16[640,2048]{1,0:T(8,128)(2,1)}) custom-call(bf16[1024,640]{1,0:T(8,128)(2,1)} %get-tuple-element.80.refs_0_, bf16[640,2048]{1,0:T(8,128)(2,1)} %get-tuple-element.54.weight_ref.refs_1_, f32[256,2048]{1,0:T(8,128)} %get-tuple-element.81.refs_2_, f32[256,2048]{1,0:T(8,128)} %bitcast.34, ...), custom_call_target="tpu_custom_call" | custom-call | tf_op jit(solution)/shard_map/leave/pallas_call | solution.py:1097
  469.1 1.3 pad_maximum_fusion.2.refs_1_
  470.4 58.5 %share.2 = (bf16[4,352,2048]{2,1,0:T(8,128)(2,1)}, f32[2,2048]{1,0:T(2,128)}) custom-call(bf16[352,2048]{1,0:T(8,128)(2,1)} %reduce-scatter.7.cloned.1.call-done.refs_0_.refs_1_, f32[2,2048]{1,0:T(2,128)} %pad_maximum_fusion.2.refs_1_), custom_call_target="tpu_custom_call" | custom-call | tf_op jit(solution)/shard_map/share/pallas_call | solution.py:1175
  528.9 13.9 %share.3.refs_2_ = bf16[4,256,512]{2,1,0:T(8,128)(2,1)} custom-call(bf16[256,512]{1,0:T(8,128)(2,1)} %reduce-scatter.9.cloned.1.call-done.refs_0_.refs_1_), custom_call_target="tpu_custom_call" | custom-call | tf_op jit(solution)/shard_map/share/pallas_call | solution.py:1175
  542.9 1.5 collective-permute-start.7
  544.4 2.0 collective-permute-start.6
  546.5 2.8 join_pieces.4
  549.2 5.4 join_pieces.5
  554.6 7.9 %join_rows.1 = f32[1408,2048]{1,0:T(8,128)} custom-call(s32[1]{0:T(128)} %bitcast.index_ref.refs_0_, bf16[352,2048]{1,0:T(8,128)(2,1)} %reduce-scatter.7.cloned.1.call-done.refs_0_.refs_1_, bf16[4,352,2048]{2,1,0:T(8,128)(2,1)} %get-tuple-element.97.refs_2_), custom_call_target="tpu_custom_call" | custom-call | tf_op jit(solution)/shard_map/join_rows/pallas_call | solution.py:1205
  564.1 3.0 join_pieces.3
  567.1 1.3 copy.22
  569.5 1.3 copy.23
  (60 shorter events, 14.2 us)
Async XLA Ops:
  7.2 205.2 %all-gather.3.cloned.1.call-start = ((), (), s32[]{:S(2)}) async-start(), calls=%async_computation.4 | async-start | bytes 12976128 | tf_op jit(solution)/shard_map/all_gather | solution.py:1461
  62.8 182.6 %all-gather.5.cloned.1.call-start = ((), (), s32[]{:S(2)}) async-start(), calls=%async_computation.5 | async-start | bytes 6488064 | tf_op jit(solution)/shard_map/all_gather | solution.py:1471
  71.9 90.1 %copy-start.1 = (f32[1,256,2048]{2,1,0:T(8,128)S(1)}, f32[1,256,2048]{2,1,0:T(8,128)}, u32[]{:S(2)}) copy-start(f32[1,256,2048]{2,1,0:T(8,128)} %param.16) | copy-start | bytes 6291460
  162.2 214.7 %reduce-scatter.5.cloned.1.call-start = ((), (), s32[]{:S(2)}) async-start(), calls=%async_computation.6 | async-start | bytes 6488064 | tf_op jit(solution)/shard_map/reduce_scatter | solution.py:1478
  162.4 26.1 %collective-permute-start = (bf16[256,2048]{1,0:T(8,128)(2,1)S(1)}, bf16[256,2048]{1,0:T(8,128)(2,1)S(1)}, u32[]{:S(2)}, u32[]{:S(2)}) collective-permute-start(bf16[256,2048]{1,0:T(8,128)(2,1)S(1)} %bitcast_convert_fusion), channel_id=1, source_target_pairs={{0,1},{1,0},{2,3},{3,2},{4,5},{5,4},{6,7},{7,6},{8,9},{9,8},{10,11... | collective-permute-start | bytes 3145736 | tf_op jit(solution)/shard_map/ppermute | solution.py:325
  164.2 46.1 %collective-permute-start.1 = (bf16[256,2048]{1,0:T(8,128)(2,1)S(1)}, bf16[256,2048]{1,0:T(8,128)(2,1)S(1)}, u32[]{:S(2)}, u32[]{:S(2)}) collective-permute-start(bf16[256,2048]{1,0:T(8,128)(2,1)S(1)} %bitcast_convert_fusion), channel_id=1, source_target_pairs={{0,2},{1,3},{2,0},{3,1},{4,6},{5,7},{6,4},{7,5},{8,10},{9,11},{10,... | collective-permute-start | bytes 3145736 | tf_op jit(solution)/shard_map/ppermute | solution.py:325
  164.5 46.8 %collective-permute-start.2 = (bf16[256,2048]{1,0:T(8,128)(2,1)S(1)}, bf16[256,2048]{1,0:T(8,128)(2,1)S(1)}, u32[]{:S(2)}, u32[]{:S(2)}) collective-permute-start(bf16[256,2048]{1,0:T(8,128)(2,1)S(1)} %bitcast_convert_fusion), channel_id=1, source_target_pairs={{0,3},{1,2},{2,1},{3,0},{4,7},{5,6},{6,5},{7,4},{8,11},{9,10},{10,... | collective-permute-start | bytes 3145736 | tf_op jit(solution)/shard_map/ppermute | solution.py:325
  229.7 4.4 copy-start
  245.1 225.4 %reduce-scatter.7.cloned.1.call-start = ((), (), s32[]{:S(2)}) async-start(), calls=%async_computation.7 | async-start | bytes 12976128 | tf_op jit(solution)/shard_map/reduce_scatter | solution.py:1478
  245.4 11.0 %copy-start.11 = (bf16[2048,1408]{1,0:T(8,128)(2,1)S(1)}, bf16[2048,1408]{1,0:T(8,128)(2,1)}, u32[]{:S(2)}) copy-start(bf16[2048,1408]{1,0:T(8,128)(2,1)} %all-gather.5.cloned.1.call-done) | copy-start | bytes 17301508
  315.6 213.3 %reduce-scatter.9.cloned.1.call-start = ((), (), s32[]{:S(2)}) async-start(), calls=%async_computation.8 | async-start | bytes 2359296 | tf_op jit(solution)/shard_map/reduce_scatter | solution.py:1478
  318.3 21.0 %collective-permute-start.3 = (bf16[2,128,2048]{2,1,0:T(8,128)(2,1)S(1)}, bf16[2,128,2048]{2,1,0:T(8,128)(2,1)S(1)}, u32[]{:S(2)}, u32[]{:S(2)}) collective-permute-start(bf16[2,128,2048]{2,1,0:T(8,128)(2,1)S(1)} %pad_maximum_fusion.1), channel_id=1, source_target_pairs={{0,1},{1,0},{2,3},{3,2},{4,5},{5,4},{6,7},{7,6},{8,9},{9,8},{10,11... | collective-permute-start | bytes 3145736 | tf_op jit(solution)/shard_map/ppermute | solution.py:325
  318.7 20.8 %collective-permute-start.4 = (bf16[2,128,2048]{2,1,0:T(8,128)(2,1)S(1)}, bf16[2,128,2048]{2,1,0:T(8,128)(2,1)S(1)}, u32[]{:S(2)}, u32[]{:S(2)}) collective-permute-start(bf16[2,128,2048]{2,1,0:T(8,128)(2,1)S(1)} %stack.10), channel_id=1, source_target_pairs={{0,2},{1,3},{2,0},{3,1},{4,6},{5,7},{6,4},{7,5},{8,10},{9,11},{10,... | collective-permute-start | bytes 3145736 | tf_op jit(solution)/shard_map/ppermute | solution.py:325
  339.4 1.0 copy-start.4
  339.5 1.2 copy-start.5
  418.2 124.7 %reduce-scatter.11.cloned.1.call-start = ((), (), s32[]{:S(2)}) async-start(), calls=%async_computation.9 | async-start | bytes 2949120 | tf_op jit(solution)/shard_map/reduce_scatter | solution.py:1478
  418.2 50.9 %copy-start.10 = (f32[1,2048]{1,0:T(1,128)S(1)}, f32[1,2048]{1,0:T(1,128)}, u32[]{:S(2)}) copy-start(f32[1,2048]{1,0:T(1,128)} %get-tuple-element.87) | copy-start | bytes 24580
  542.9 19.6 %collective-permute-start.7 = (bf16[80,2048]{1,0:T(8,128)(2,1)}, bf16[80,2048]{1,0:T(8,128)(2,1)S(1)}, u32[]{:S(2)}, u32[]{:S(2)}) collective-permute-start(bf16[80,2048]{1,0:T(8,128)(2,1)} %reduce-scatter.11.cloned.1.call-done.refs_1_), channel_id=1, source_target_pairs={{0,3},{1,2},{2,1},{3,0},{4,7},{5,6},{6,5},{7,4},{8,11},{9,10},{10,... | collective-permute-start | bytes 983048 | tf_op jit(solution)/shard_map/ppermute | solution.py:325
  544.4 18.1 %collective-permute-start.6 = (bf16[80,2048]{1,0:T(8,128)(2,1)}, bf16[80,2048]{1,0:T(8,128)(2,1)S(1)}, u32[]{:S(2)}, u32[]{:S(2)}) collective-permute-start(bf16[80,2048]{1,0:T(8,128)(2,1)} %reduce-scatter.11.cloned.1.call-done.refs_1_), channel_id=1, source_target_pairs={{0,2},{1,3},{2,0},{3,1},{4,6},{5,7},{6,4},{7,5},{8,10},{9,11},{10,... | collective-permute-start | bytes 983048 | tf_op jit(solution)/shard_map/ppermute | solution.py:325
  546.5 16.1 %collective-permute-start.5 = (bf16[80,2048]{1,0:T(8,128)(2,1)}, bf16[80,2048]{1,0:T(8,128)(2,1)S(1)}, u32[]{:S(2)}, u32[]{:S(2)}) collective-permute-start(bf16[80,2048]{1,0:T(8,128)(2,1)} %reduce-scatter.11.cloned.1.call-done.refs_1_), channel_id=1, source_target_pairs={{0,1},{1,0},{2,3},{3,2},{4,5},{5,4},{6,7},{7,6},{8,9},{9,8},{10,11... | collective-permute-start | bytes 983048 | tf_op jit(solution)/shard_map/ppermute | solution.py:325
  562.5 4.6 copy-start.2
  562.5 0.7 copy-start.6
  562.5 0.8 copy-start.7
  563.4 0.7 copy-start.8
  567.1 2.3 copy-start.3
  567.1 3.7 copy-start.9
Sparse Core Ops, SparseCore 0:
  62.9 112.4 all-gather.2
  177.0 58.6 all-gather.4
  245.2 63.9 reduce-scatter.4
  315.7 118.3 reduce-scatter.6
  436.2 34.5 reduce-scatter.8
  473.0 37.3 reduce-scatter.10

commit v4 on v3

--- a/solution.py
+++ b/solution.py
@@ -876,9 +876,9 @@
 
 
 def attend_back_kernel(
-    count, q_ref, k_ref, v_ref, attn_ref, lse_ref, dy_ref, weight_ref, table_ref, pick_ref, passed_ref, base_ref, shard_ref,
-    out_ref, turned_ref, term_ref, result_ref, slot_ref,
-    do_ref, delta_ref, dq_ref, dk_ref, dv_ref, far_ref, held_dy, held_base, held_pick,
+    count, q_ref, k_ref, v_ref, attn_ref, lse_ref, dy_ref, weight_ref, table_ref, pick_ref, passed_ref, shard_ref,
+    out_ref, turned_ref, term_ref, far_ref, slot_ref,
+    do_ref, delta_ref, dq_ref, dk_ref, dv_ref, held_dy, held_pick,
     send_sems, recv_sems, load_sems,
 ):
     heads, length, _ = q_ref.shape
@@ -886,7 +886,6 @@
     wide = jnp.float32
     index = lax.axis_index("seq")
     greet([seq_peer(1), seq_peer(2)])
-    half = part // 2
     sems = (send_sems, recv_sems)
     sums = [
         remote(passed_ref.at[0], far_ref.at[0], sems, 6, seq_peer(2)),
@@ -901,14 +900,10 @@
         rows = pl.ds(pl.multiple_of(step * part, part), part)
         return pltpu.make_async_copy(dy_ref.at[rows], held_dy.at[rows], load_sems.at[step])
 
-    loads = [
-        pltpu.make_async_copy(base_ref, held_base, load_sems.at[count]),
-        pltpu.make_async_copy(pick_ref, held_pick, load_sems.at[count + 1]),
-    ]
+    load = pltpu.make_async_copy(pick_ref, held_pick, load_sems.at[count])
     for here in range(count):
         load_dy(here ^ index).start()
-    for load in loads:
-        load.start()
+    load.start()
     dk_ref[...] = jnp.zeros_like(dk_ref)
     dv_ref[...] = jnp.zeros_like(dv_ref)
     owner = lax.broadcasted_iota(jnp.int32, (heads, heads * HD), 1) // HD
@@ -970,8 +965,7 @@
         both = jnp.concatenate([dk_ref[rows_block], dv_ref[rows_block]], 1).astype(jnp.bfloat16).astype(wide)
         both = unturn(both, *spread_tables(table_ref[rows_there, :], 0, True))
         out_ref[rows_there, heads * HD :] = both.astype(jnp.bfloat16)
-    for load in loads:
-        load.wait()
+    load.wait()
     chosen = matmul(held_pick[...], out_ref[...], 1, 1).astype(jnp.bfloat16)
     size = turned_ref.shape[1]
     for block in range(count):
@@ -986,16 +980,14 @@
     lax.fori_loop(0, held_dy.shape[1] // tile, one_tile, 0)
     for copy in sums:
         copy.wait_recv()
-    result_ref[:half] = held_base[:half] + far_ref[0].astype(wide)
-    result_ref[half:] = held_base[half:] + far_ref[1].astype(wide)
     share_end([group])
     for copy in sums:
         copy.wait_send()
 
 
-def attend_back(queries, keys_in, values_in, attn, lse, dy, weight, table, pick, passed, base, shard, count):
+def attend_back(queries, keys_in, values_in, attn, lse, dy, weight, table, pick, passed, shard, count):
     heads, length, _ = queries.shape
-    part, width = base.shape
+    part, width = length // count, dy.shape[1]
     columns = (heads + 2) * HD
     vmem, whole = pl.BlockSpec(memory_space=pltpu.VMEM), pl.BlockSpec(memory_space=pl.ANY)
     return pl.pallas_call(
@@ -1004,11 +996,11 @@
             jax.ShapeDtypeStruct((length, columns), jnp.bfloat16),
             jax.ShapeDtypeStruct((count, columns // count, length), jnp.bfloat16),
             jax.ShapeDtypeStruct((width, heads * HD), jnp.bfloat16),
-            jax.ShapeDtypeStruct((part, width), jnp.float32),
+            jax.ShapeDtypeStruct((2, part // 2, width), jnp.bfloat16),
             jax.ShapeDtypeStruct((count,) + shard.shape, shard.dtype),
         ],
-        in_specs=[vmem] * 5 + [whole] + [vmem] * 2 + [whole] * 4,
-        out_specs=[vmem] * 4 + [whole],
+        in_specs=[vmem] * 5 + [whole] + [vmem] * 2 + [whole] * 3,
+        out_specs=[vmem] * 3 + [whole] * 2,
         scratch_shapes=[
             pltpu.VMEM((heads, part, HD), jnp.bfloat16),
             pltpu.VMEM((heads, part), jnp.float32),
@@ -1016,27 +1008,29 @@
             pltpu.VMEM((length, HD), jnp.float32),
             pltpu.VMEM((length, HD), jnp.float32),
         ]
-        + [pltpu.VMEM((2, part // 2, width), jnp.bfloat16)]
-        + [pltpu.VMEM(dy.shape, dy.dtype), pltpu.VMEM(base.shape, base.dtype), pltpu.VMEM(pick.shape, pick.dtype)]
-        + [pltpu.SemaphoreType.DMA((8,)), pltpu.SemaphoreType.DMA((8,)), pltpu.SemaphoreType.DMA((count + 2,))],
+        + [pltpu.VMEM(dy.shape, dy.dtype), pltpu.VMEM(pick.shape, pick.dtype)]
+        + [pltpu.SemaphoreType.DMA((8,)), pltpu.SemaphoreType.DMA((8,)), pltpu.SemaphoreType.DMA((count + 1,))],
         compiler_params=pltpu.CompilerParams(collective_id=4, has_side_effects=True, vmem_limit_bytes=LIMIT),
         name="attend_back",
-    )(queries, keys_in, values_in, attn, lse, dy, weight, table, pick, passed, base, shard)
+    )(queries, keys_in, values_in, attn, lse, dy, weight, table, pick, passed, shard)
 
 
 def leave_kernel(
-    count, grads_ref, weight_ref, flowing_in, first_in, scale_ref, gain_ref, turned_ref, normed_in,
-    own_ref, gain_out_ref, term_ref,
-    sent_ref, side_ref, below_ref, far_ref, slot_ref, whole_ref, normed_ref, flowing_ref, first_ref,
-    send_sems, recv_sems, swap_send, swap_recv, load_sems,
+    count, grads_ref, weight_ref, first_in, scale_ref, gain_ref, other_ref, turned_ref, normed_in,
+    own_ref, total_ref, term_ref,
+    sent_ref, side_ref, below_ref, far_ref, slot_ref, whole_ref, normed_ref, first_ref,
+    told_ref, heard_ref, send_sems, recv_sems, swap_send, swap_recv, load_sems, sum_send, sum_recv,
 ):
-    part, _ = flowing_ref.shape
+    part, _ = first_ref.shape
     half = part // 2
     size = turned_ref.shape[1]
     heads = H // count
     chunk = size // (heads + 2)
     index = lax.axis_index("seq")
-    greet([seq_peer(step) for step in range(1, count)])
+    place = lax.axis_index("fsdp")
+    peers = [seq_peer(step) for step in range(1, count)]
+    fsdp_peers = [fsdp_peer(place ^ (1 << bit)) for bit in range(lax.axis_size("fsdp").bit_length() - 1)]
+    greet(peers + fsdp_peers)
     swaps = [
         remote(turned_ref.at[index ^ step], slot_ref.at[step], (swap_send, swap_recv), step - 1, seq_peer(step))
         for step in range(1, count)
@@ -1049,25 +1043,44 @@
             (
                 (turned_ref.at[index], slot_ref.at[0]),
                 (normed_in, normed_ref),
-                (flowing_in, flowing_ref),
                 (first_in, first_ref),
             )
         )
     ]
     for load in loads:
         load.start()
+    total_ref[0:1] = jnp.zeros_like(other_ref)
+    total_ref[1:2] = other_ref[...]
+    loads[1].wait()
     sums = sum_copies(sent_ref, side_ref, below_ref, far_ref, half, (send_sems, recv_sems))
 
     def one_part(turn, carry):
         step = count - 1 - turn
         rows_step = pl.ds(pl.multiple_of(step * part, part), part)
         partial = matmul(grads_ref[rows_step, :], weight_ref[...], 1, 0)
+        total_ref[0:1] += jnp.sum(partial * normed_ref[rows_step, :].astype(jnp.float32), 0, keepdims=True)
         pass_sums(turn, step, partial, sums, sent_ref, side_ref, below_ref, own_ref, half)
         return carry
 
     lax.fori_loop(0, count, one_part, 0)
-    for load in loads:
-        load.wait()
+    loads[0].wait()
+    loads[2].wait()
+    total_ref[0:1] = total_ref[0:1] / gain_ref[...]
+    tells = []
+    for step, peer in enumerate(fsdp_peers):
+        told_ref[step] = total_ref[...]
+        tell = remote(told_ref.at[step], heard_ref.at[step], (sum_send, sum_recv), step, peer)
+        tell.start()
+        tell.wait_recv()
+        total_ref[...] += heard_ref[step]
+        tells.append(tell)
+    first = len(tells)
+    told_ref[first] = total_ref[...]
+    for step, peer in enumerate(peers):
+        tells.append(
+            remote(told_ref.at[first], heard_ref.at[first + step], (sum_send, sum_recv), first + step, peer)
+        )
+        tells[-1].start()
     for step in range(count):
         if step:
             swaps[step - 1].wait_recv()
@@ -1083,25 +1096,28 @@
     end_sums(sums, side_ref, below_ref, far_ref, own_ref, half)
     unit = first_ref[...] * scale_ref[:, :1]
     grads = own_ref[...]
-    gain_out_ref[...] = jnp.sum(grads * unit, 0, keepdims=True)
     inner = grads * gain_ref[...]
-    own_ref[...] = flowing_ref[...] + scale_ref[:, :1] * (inner - unit * jnp.mean(inner * unit, 1, keepdims=True))
-    for copy in sums + swaps:
+    own_ref[...] = scale_ref[:, :1] * (inner - unit * jnp.mean(inner * unit, 1, keepdims=True))
+    for step in range(len(peers)):
+        tells[first + step].wait_recv()
+        total_ref[...] += heard_ref[first + step]
+    for copy in sums + swaps + tells:
         copy.wait_send()
 
 
-def leave(grads, weight, flowing, first, scale, gain, turned, normed, count):
-    part, width = flowing.shape
+def leave(grads, weight, first, scale, gain, other, turned, normed, count):
+    part, width = first.shape
     vmem, whole = pl.BlockSpec(memory_space=pltpu.VMEM), pl.BlockSpec(memory_space=pl.ANY)
     size, length = turned.shape[1:]
-    own, gain_term, term = pl.pallas_call(
+    steps = lax.axis_size("fsdp").bit_length() - 1 + count - 1
+    own, total, term = pl.pallas_call(
         lambda *refs: leave_kernel(count, *refs),
         out_shape=(
             jax.ShapeDtypeStruct((part, width), jnp.float32),
-            jax.ShapeDtypeStruct((1, width), jnp.float32),
+            jax.ShapeDtypeStruct((2, width), jnp.float32),
             jax.ShapeDtypeStruct((size * count, width), jnp.bfloat16),
         ),
-        in_specs=[vmem] * 2 + [whole] * 2 + [vmem] * 2 + [whole] * 2,
+        in_specs=[vmem] * 2 + [whole] + [vmem] * 3 + [whole] * 2,
         out_specs=[vmem] * 3,
         scratch_shapes=[
             pltpu.VMEM((count, part, width), jnp.bfloat16),
@@ -1112,135 +1128,73 @@
             pltpu.VMEM((count * size, length), jnp.bfloat16),
             pltpu.VMEM(normed.shape, jnp.bfloat16),
             pltpu.VMEM((part, width), jnp.float32),
-            pltpu.VMEM((part, width), jnp.float32),
+            pltpu.VMEM((steps, 2, width), jnp.float32),
+            pltpu.VMEM((steps, 2, width), jnp.float32),
             pltpu.SemaphoreType.DMA((6,)),
             pltpu.SemaphoreType.DMA((6,)),
             pltpu.SemaphoreType.DMA((count - 1,)),
             pltpu.SemaphoreType.DMA((count - 1,)),
-            pltpu.SemaphoreType.DMA((4,)),
+            pltpu.SemaphoreType.DMA((3,)),
+            pltpu.SemaphoreType.DMA((steps,)),
+            pltpu.SemaphoreType.DMA((steps,)),
         ],
         compiler_params=pltpu.CompilerParams(collective_id=5, has_side_effects=True, vmem_limit_bytes=LIMIT),
         name="leave",
-    )(grads, weight, flowing, first, scale, gain, turned, normed)
-    return own, gain_term[0], term
-
-
-def share_kernel(number, fsdp, *refs):
-    extra = 1 if fsdp else 0
-    shards, slots = refs[:number], refs[number + extra : 2 * number + extra]
-    send_sems, recv_sems = refs[2 * number + 2 * extra : 2 * number + 2 * extra + 2]
-    peers = [seq_peer(1), seq_peer(2)]
-    steps = []
-    if fsdp:
-        term_ref, total_ref = refs[number], refs[2 * number + 1]
-        heard_ref, told_ref, sum_send, sum_recv = refs[2 * number + 4 :]
-        place = lax.axis_index("fsdp")
-        steps = [seq_peer(1), seq_peer(2)] + [fsdp_peer(place ^ (1 << bit)) for bit in range(fsdp.bit_length() - 1)]
-        peers += steps[2:]
-    greet(peers)
-    copies = [
-        gather_copies(shard, slot, upper_half(shard.shape[0]), (send_sems, recv_sems), 6 * spot)
-        for spot, (shard, slot) in enumerate(zip(shards, slots))
-    ]
-    if fsdp:
-        total_ref[...] = term_ref[...]
-    tells = []
-    for step, peer in enumerate(steps):
-        if step == 2:
-            share_start(copies)
-        told_ref[step] = total_ref[...]
-        tell = remote(told_ref.at[step], heard_ref.at[step], (sum_send, sum_recv), step, peer)
-        tell.start()
-        tell.wait_recv()
-        total_ref[...] += heard_ref[step]
-        tells.append(tell)
-    if not fsdp:
-        share_start(copies)
-    for group in copies:
-        share_on(group)
-    share_end(copies)
-    for tell in tells:
-        tell.wait_send()
-
-
-def share(name, shards, count, term=None):
-    vmem = pl.BlockSpec(memory_space=pltpu.VMEM)
-    fsdp = lax.axis_size("fsdp") if term is not None else 0
-    extra = [] if term is None else [term]
-    scratch = [pltpu.SemaphoreType.DMA((6 * len(shards),)) for _ in range(2)]
-    if fsdp:
-        steps = fsdp.bit_length() + 1
-        scratch += [pltpu.VMEM((steps,) + term.shape, term.dtype) for _ in range(2)]
-        scratch += [pltpu.SemaphoreType.DMA((steps,)) for _ in range(2)]
+    )(grads, weight, first, scale, gain, other, turned, normed)
+    return own, total, term
+
+
+def join_rows_kernel(index_ref, own_ref, side_ref, below_ref, top_ref, bottom_ref, out_ref):
+    step = pl.program_id(0) ^ index_ref[0]
+    half = top_ref.shape[0]
+    for number, ref in enumerate((own_ref, side_ref, below_ref)):
+
+        @pl.when(step == number)
+        def _():
+            out_ref[...] = ref[...].astype(jnp.float32)
+
+    @pl.when(step == 3)
+    def _():
+        out_ref[:half] = top_ref[...].astype(jnp.float32)
+        out_ref[half:] = bottom_ref[...].astype(jnp.float32)
+
+
+def join_rows(index, own, side, below, top, bottom, count):
+    rows, width = own.shape
+    parts = (own, side, below, top, bottom)
     return pl.pallas_call(
-        lambda *refs: share_kernel(len(shards), fsdp, *refs),
-        out_shape=[jax.ShapeDtypeStruct((count,) + shard.shape, shard.dtype) for shard in shards]
-        + [jax.ShapeDtypeStruct(value.shape, value.dtype) for value in extra],
-        in_specs=[pl.BlockSpec(memory_space=pl.ANY)] * len(shards) + [vmem] * len(extra),
-        out_specs=[pl.BlockSpec(memory_space=pl.ANY)] * len(shards) + [vmem] * len(extra),
-        scratch_shapes=scratch,
-        compiler_params=pltpu.CompilerParams(
-            collective_id=name, has_side_effects=True, vmem_limit_bytes=LIMIT
-        ),
-        name="share",
-    )(*shards, *extra)
-
-
-def join_rows_kernel(number, index_ref, *refs):
-    owns, slots, out_ref = refs[:number], refs[number : 2 * number], refs[-1]
-    mine = pl.program_id(0) == index_ref[0]
-
-    @pl.when(mine)
-    def _():
-        out_ref[...] = jnp.concatenate([ref[...] for ref in owns], 1).astype(jnp.float32)
-
-    @pl.when(jnp.logical_not(mine))
-    def _():
-        out_ref[...] = jnp.concatenate([ref[0] for ref in slots], 1).astype(jnp.float32)
-
-
-def join_rows(index, owns, slots, count):
-    rows = slots[0].shape[1]
-    width = sum(slot.shape[2] for slot in slots)
-    return pl.pallas_call(
-        lambda *refs: join_rows_kernel(len(owns), *refs),
+        join_rows_kernel,
         out_shape=jax.ShapeDtypeStruct((rows * count, width), jnp.float32),
         grid_spec=pltpu.PrefetchScalarGridSpec(
             num_scalar_prefetch=1,
             grid=(count,),
-            in_specs=[pl.BlockSpec(own.shape, lambda i, s: (0, 0)) for own in owns]
-            + [pl.BlockSpec((1,) + slot.shape[1:], lambda i, s: (i ^ s[0], 0, 0)) for slot in slots],
+            in_specs=[pl.BlockSpec(part.shape, lambda i, s: (0, 0)) for part in parts],
             out_specs=pl.BlockSpec((rows, width), lambda i, s: (i, 0)),
         ),
         compiler_params=pltpu.CompilerParams(vmem_limit_bytes=LIMIT),
         name="join_rows",
-    )(index, *owns, *slots)
+    )(index, *parts)
 
 
 def join_pieces_kernel(count, row_piece, column_piece, index_ref, own_ref, *refs):
     slot_refs, out_ref = refs[:-1], refs[-1]
     index = index_ref[0]
     rows, columns = own_ref.shape
-
     for device in range(count):
-
-        def place_pieces(values):
-            values = values.astype(jnp.float32)
-            for top in range(0, rows, row_piece):
-                for left in range(0, columns, column_piece):
-                    down = top * count + device * row_piece if row_piece < rows else top
-                    across = left * count + device * column_piece if row_piece == rows else left
-                    out_ref[down : down + row_piece, across : across + column_piece] = values[
-                        top : top + row_piece, left : left + column_piece
-                    ]
-
         if len(slot_refs) == 1:
             values = slot_refs[0][device ^ index]
         else:
             values = own_ref[...]
             for step, ref in enumerate(slot_refs):
                 values = jnp.where(device ^ index == step + 1, ref[...], values)
-        place_pieces(jnp.where(device == index, own_ref[...], values))
+        values = jnp.where(device == index, own_ref[...], values).astype(jnp.float32)
+        for top in range(0, rows, row_piece):
+            for left in range(0, columns, column_piece):
+                down = top * count + device * row_piece if row_piece < rows else top
+                across = left * count + device * column_piece if row_piece == rows else left
+                out_ref[down : down + row_piece, across : across + column_piece] = values[
+                    top : top + row_piece, left : left + column_piece
+                ]
 
 
 def join_pieces(index, own, slots, count, row_piece, column_piece):
@@ -1261,8 +1215,28 @@
     )(index, own, *slots)
 
 
+def last_sums_kernel(base_ref, passed_ref, flowing_ref, piece_ref, result_ref, grad_ref):
+    result_ref[...] = base_ref[...] + passed_ref[...].astype(jnp.float32)
+    grad_ref[...] = flowing_ref[...] + piece_ref[...]
+
+
+def last_sums(base, passed, flowing, piece):
+    rows, width = base.shape
+    tile = rows // 4
+    block = pl.BlockSpec((tile, width), lambda i: (i, 0))
+    return pl.pallas_call(
+        last_sums_kernel,
+        out_shape=[jax.ShapeDtypeStruct((rows, width), jnp.float32)] * 2,
+        grid=(4,),
+        in_specs=[block] * 4,
+        out_specs=[block] * 2,
+        compiler_params=pltpu.CompilerParams(vmem_limit_bytes=LIMIT),
+        name="last_sums",
+    )(base, passed, flowing, piece)
+
+
 def norm_back_kernel(
-    count, grads_ref, weight_ref, flowing_in, middle_in, scale_ref, gain_ref, inputs_ref,
+    count, left_in, right_in, weight_ref, flowing_in, middle_in, scale_ref, gain_ref, inputs_ref,
     own_ref, gain_out_ref, dy_ref, term_ref,
     sent_ref, side_ref, below_ref, far_ref, stage_ref, held_grads, held_weight, held_inputs, flowing_ref, middle_ref,
     send_sems, recv_sems, store_sems, load_sems,
@@ -1270,22 +1244,34 @@
     part, width = flowing_ref.shape
     half = part // 2
     sems = (send_sems, recv_sems)
-    units = grads_ref.shape[1]
+    units = held_grads.shape[1]
     tile = stage_ref.shape[1]
     tiles = units // tile
     cuts = [tiles * number // 4 * tile for number in range(5)]
     last = pl.ds((count - 1) * part, part)
     rest = pl.ds(0, (count - 1) * part)
-    load_last = pltpu.make_async_copy(grads_ref.at[last], held_grads.at[last], load_sems.at[0])
-    load_last.start()
+
+    def load_grads(rows, number):
+        return [
+            pltpu.make_async_copy(
+                source.at[rows],
+                held_grads.at[rows, pl.ds(place * (units // 2), units // 2)],
+                load_sems.at[number + place],
+            )
+            for place, source in enumerate((left_in, right_in))
+        ]
+
+    load_last, load_rest = load_grads(last, 9), load_grads(rest, 11)
+    for load in load_last:
+        load.start()
     load_weight = []
     for number in range(4):
         rows = pl.ds(cuts[number], cuts[number + 1] - cuts[number])
-        load = pltpu.make_async_copy(weight_ref.at[rows], held_weight.at[rows], load_sems.at[1 + number])
+        load = pltpu.make_async_copy(weight_ref.at[rows], held_weight.at[rows], load_sems.at[number])
         load.start()
         load_weight.append(load)
-    load_rest = pltpu.make_async_copy(grads_ref.at[rest], held_grads.at[rest], load_sems.at[5])
-    load_rest.start()
+    for load in load_rest:
+        load.start()
     load_inputs = pltpu.make_async_copy(inputs_ref, held_inputs, load_sems.at[6])
     load_inputs.start()
     load_ends = [
@@ -1295,7 +1281,8 @@
     for load in load_ends:
         load.start()
     grads_ref, weight_ref, inputs_ref = held_grads, held_weight, held_inputs
-    load_last.wait()
+    for load in load_last:
+        load.wait()
     partial = jnp.zeros((part, width), jnp.float32)
     for number in range(4):
         load_weight[number].wait()
@@ -1306,7 +1293,8 @@
     sums = sum_copies(sent_ref, side_ref, below_ref, far_ref, half, sems)
     sums[0].start()
     sums[1].start()
-    load_rest.wait()
+    for load in load_rest:
+        load.wait()
 
     def one_part(turn, carry):
         step = count - 1 - turn
@@ -1349,9 +1337,9 @@
         copy.wait_send()
 
 
-def norm_back(grads, weight, flowing, middle, scale, gain, inputs, count):
+def norm_back(left, right, weight, flowing, middle, scale, gain, inputs, count):
     part, width = flowing.shape
-    units = grads.shape[1]
+    units = left.shape[1] + right.shape[1]
     tile = 2 * 128
     vmem = pl.BlockSpec(memory_space=pltpu.VMEM)
     own, gain_term, dy, term = pl.pallas_call(
@@ -1362,7 +1350,7 @@
             jax.ShapeDtypeStruct((part, width), jnp.bfloat16),
             jax.ShapeDtypeStruct((units, width), jnp.bfloat16),
         ),
-        in_specs=[pl.BlockSpec(memory_space=pl.ANY)] * 4 + [vmem] * 2 + [pl.BlockSpec(memory_space=pl.ANY)],
+        in_specs=[pl.BlockSpec(memory_space=pl.ANY)] * 5 + [vmem] * 2 + [pl.BlockSpec(memory_space=pl.ANY)],
         out_specs=[vmem] * 3 + [pl.BlockSpec(memory_space=pl.ANY)],
         scratch_shapes=[
             pltpu.VMEM((count, part, width), jnp.bfloat16),
@@ -1370,7 +1358,7 @@
             pltpu.VMEM((2, part // 2, width), jnp.bfloat16),
             pltpu.VMEM((2, part // 2, width), jnp.bfloat16),
             pltpu.VMEM((2, tile, width), jnp.bfloat16),
-            pltpu.VMEM(grads.shape, jnp.bfloat16),
+            pltpu.VMEM((part * count, units), jnp.bfloat16),
             pltpu.VMEM(weight.shape, jnp.bfloat16),
             pltpu.VMEM(inputs.shape, jnp.bfloat16),
             pltpu.VMEM((part, width), jnp.float32),
@@ -1378,11 +1366,11 @@
             pltpu.SemaphoreType.DMA((6,)),
             pltpu.SemaphoreType.DMA((6,)),
             pltpu.SemaphoreType.DMA((2,)),
-            pltpu.SemaphoreType.DMA((9,)),
+            pltpu.SemaphoreType.DMA((13,)),
         ],
         compiler_params=pltpu.CompilerParams(collective_id=3, has_side_effects=True, vmem_limit_bytes=LIMIT),
         name="norm_back",
-    )(grads, weight, flowing, middle, scale, gain, inputs)
+    )(left, right, weight, flowing, middle, scale, gain, inputs)
     return own, gain_term[0], dy, term
 
 
@@ -1490,34 +1478,38 @@
     sigma = jax.nn.sigmoid(gate_part)
     dgate = dact * up_part * sigma * (1.0 + gate_part * (1.0 - sigma))
     dup = dact * gate_part * sigma
-    dgu = jnp.concatenate([dgate, dup], 1).astype(jnp.bfloat16)
+    dgate, dup = dgate.astype(jnp.bfloat16), dup.astype(jnp.bfloat16)
     dmiddle, gain_two, dy, term_gate_up = norm_back(
-        dgu, gate_up, flowing, middle, scale_two, gain[1:], normed_two_all, count
+        dgate, dup, gate_up, flowing, middle, scale_two, gain[1:], normed_two_all, count
     )
     grad_gate_up = owned(term_gate_up)
     dy_all, base, passed = share_dy(dy, down_sent, from_side, from_below, middle, count)
     pieces = heads + 2
     picked = np.arange(pieces * HD).reshape(pieces * per_head, count, chunk).transpose(1, 0, 2).reshape(-1)
     pick = jnp.asarray(picked[:, None] == np.arange(pieces * HD)[None, :], jnp.bfloat16)
-    djoint, djoint_turned, term_out, result, down_slots = attend_back(
-        queries, keys_in, values_in, attn_flat, log_total, dy_all, out_cols, table, pick, passed, base, grad_down,
-        count,
+    djoint, djoint_turned, term_out, passed_on, down_slots = attend_back(
+        queries, keys_in, values_in, attn_flat, log_total, dy_all, out_cols, table, pick, passed, grad_down, count
     )
     grad_out = owned(term_out)
-    grad_hidden, gain_one, term_qkv = leave(
-        djoint, qkv_rows, dmiddle, current, scale_one, gain[:1], djoint_turned, normed_all, count
+    grad_piece, gain_total, term_qkv = leave(
+        djoint, qkv_rows, current, scale_one, gain[:1], gain_two[None], djoint_turned, normed_all, count
     )
     grad_qkv = owned(term_qkv)
-    gate_up_slots, gain_total = share(6, (grad_gate_up,), count, jnp.stack([gain_one, gain_two]))
-    grad_out, gate_up_slots = after((grad_out, gate_up_slots))
-    (out_slots,) = share(7, (grad_out,), count)
-    gate_up_slots, grad_qkv, down_slots, out_slots = after((gate_up_slots, grad_qkv, down_slots, out_slots))
+    grad_gate_up, grad_piece = after((grad_gate_up, grad_piece))
+    half = upper_half(gu_rows)
+    side = neighbour(grad_gate_up, 1)
+    below = neighbour(grad_gate_up, 2)
+    far_top = neighbour(side[:half], 2)
+    far_bottom = neighbour(below[half:], 1)
+    down_shard = join_pieces(place, grad_down, (down_slots,), count, down_rows, gu_rows)
+    result, grad_hidden = last_sums(base, passed_on.reshape(part_len, width), dmiddle, grad_piece)
+    out_slots = [neighbour(grad_out, step) for step in range(1, count)]
+    grad_qkv, out_slots = after((grad_qkv, out_slots))
     qkv_slots = [neighbour(grad_qkv, step) for step in range(1, count)]
+    gate_up_shard = join_rows(place, grad_gate_up, side, below, far_top, far_bottom, count)
+    out_shard = join_pieces(place, grad_out, out_slots, count, down_rows, heads * HD)
+    qkv_shard = join_pieces(place, grad_qkv, qkv_slots, count, chunk, width)
     gain_total = gain_total[None]
-    down_shard = join_pieces(place, grad_down, (down_slots,), count, down_rows, gu_rows)
-    gate_up_shard = join_rows(place, (grad_gate_up,), (gate_up_slots,), count)
-    out_shard = join_pieces(place, grad_out, (out_slots,), count, down_rows, heads * HD)
-    qkv_shard = join_pieces(place, grad_qkv, qkv_slots, count, chunk, width)
     return (
         result[None],
         grad_hidden[None],

time: 586 us -> 581 us (level)
  Pallas kernels: 415 us -> 352 us
  waiting for transfers between devices: 61.5 us -> 116 us
  starting transfers between devices: 9.85 us -> 17.5 us
    pallas_call x3 -> x2, Pallas kernels: 80.3 us -> 12.6 us  [the longest x1 7.2 us: join_rows(): pl.pallas_call(join_rows_kernel, out_shape=jax.ShapeDtypeStruct((rows * c...]
    ppermute x8 -> x15, waiting for transfers between devices: 61.3 us -> 116 us  [neighbour(): return lax.ppermute(values, 'seq', [(i, i ^ step) for i in range(count)])]
    ppermute x8 -> x15, starting transfers between devices: 9.22 us -> 16.9 us  [neighbour(): return lax.ppermute(values, 'seq', [(i, i ^ step) for i in range(count)])]
    unnamed x30 -> x26, local copies, waits for them, and re-layouts: 12.8 us -> 9.27 us
  transfers between devices with their start and end apart: 14 -> 21, of which waited for: 4 -> 8; matrix products, arithmetic and copies ran while one was open for 11% -> 11% of each run, Pallas kernels for 62% -> 51%
where the time goes in v4:
time: 581 us; the launch traced here: 573 us
  Pallas kernels  352 us (61%)
  waiting for transfers between devices  116 us (20%)
  matrix products  53.3 us (9%)
  starting transfers between devices  17.5 us (3%)
  local copies, waits for them, and re-layouts  16.8 us (3%)
  between operations  14.5 us (2%)
    ppermute x15, waiting for transfers between devices, neighbour(): return lax.ppermute(values, 'seq', [(i, i ^ step) for i in range(count)])  116 us
    pallas_call x1, Pallas kernels, attend(): pl.pallas_call(lambda *refs: attend_kernel(count, *refs), out_shape=(jax....  90 us
    pallas_call x1, Pallas kernels, leave(): pl.pallas_call(lambda *refs: leave_kernel(count, *refs), out_shape=(jax.S...  56.1 us
    dot_general x4, matrix products, matmul(): lax.dot_general(left, right, (((left_dim,), (right_dim,)), ((), ())), pre...  53.3 us
    pallas_call x1, Pallas kernels, enter(): pl.pallas_call(lambda *refs: enter_kernel(count, *refs), out_shape=(jax.S...  52.9 us
    pallas_call x1, Pallas kernels, norm_back(): pl.pallas_call(lambda *refs: norm_back_kernel(count, *refs), out_shape=(j...  43.8 us
    pallas_call x1, Pallas kernels, attend_back(): pl.pallas_call(lambda *refs: attend_back_kernel(count, *refs), out_shape=...  40.3 us
    pallas_call x1, Pallas kernels, share_dy(): pl.pallas_call(lambda *refs: share_dy_kernel(*refs), out_shape=[jax.Shape...  36 us
  transfers between devices with their start and end apart: 21, of which 8 were waited for; matrix products, arithmetic and copies ran while one was open for 11% of the time, Pallas kernels for 51%

profile of v4, /device:TPU:0, one launch (start us, length us, event | category | flops | bytes accessed | tf_op | source)
XLA Modules:
  0.0 572.7 jit_solution(10186600866735810410)
XLA Ops:
  7.9 1.4 slice_bitcast_fusion
  9.9 52.9 %enter.1 = (bf16[4,256,2048]{2,1,0:T(8,128)(2,1)}, bf16[640,2048]{1,0:T(8,128)(2,1)}, bf16[2048,512]{1,0:T(8,128)(2,1)}, f32[1024,64]{1,0:T(8,128)}, bf16[352,20...) custom-call(f32[256,2048]{1,0:T(8,128)} %bitcast.33, f32[1,2048]{1,0:T(1,128)} %get-tuple-element.104.refs_1_.refs_4_, ...), custom_call_target="tpu_custom_call" | custom-call | tf_op jit(solution)/shard_map/enter/pallas_call | solution.py:677
  62.9 9.1 %project_qkv.1 = (bf16[8,1024,64]{2,1,0:T(8,128)(2,1)}, bf16[1024,64]{1,0:T(8,128)(2,1)}, bf16[1024,64]{1,0:T(8,128)(2,1)}) custom-call(s32[1]{0:T(128)} %bitcast.index_ref.refs_0_, bf16[1024,2048]{1,0:T(8,128)(2,1)} %bitcast.36, bf16[640,2048]{1,0:T(8,128)(2,1)} %get-tuple-element.54.weight_ref.refs_1_, f32[1024,64]{1,0:T(8,128)} %get-tuple-element.55.table_ref.refs_7_), custom_call_target="tpu_custom_call" | custom-call | tf_op jit(solution)/shard_map/project_qkv/pallas_call | solution.py:727
  72.0 90.0 %attend.1 = (bf16[1024,512]{1,0:T(8,128)(2,1)}, f32[8,1024]{1,0:T(8,128)}, f32[256,2048]{1,0:T(8,128)}, f32[256,128]{1,0:T(8,128)}, bf16[4,256,2048]{2,1,0:T(8,128)(2,1)}) custom-call(bf16[8,1024,64]{2,1,0:T(8,128)(2,1)} %get-tuple-element.56.refs_0_, bf16[1024,64]{1,0:T(8,128)(2,1)} %get-tuple-element.57.refs_1_, ...), custom_call_target="tpu_custom_call" | custom-call | tf_op jit(solution)/shard_map/attend/pallas_call | solution.py:821
  162.5 1.8 collective-permute-start
  164.6 1.5 collective-permute-start.2
  167.1 21.5 %collective-permute-done = bf16[256,2048]{1,0:T(8,128)(2,1)S(1)} collective-permute-done((bf16[256,2048]{1,0:T(8,128)(2,1)S(1)}, bf16[256,2048]{1,0:T(8,128)(2,1)S(1)}, u32[]{:S(2)}, u32[]{:S(2)}) %collective-permute-start) | collective-permute-done | bytes 1048608 | tf_op jit(solution)/shard_map/ppermute | solution.py:325
  189.7 20.7 %collective-permute-done.1 = bf16[256,2048]{1,0:T(8,128)(2,1)S(1)} collective-permute-done((bf16[256,2048]{1,0:T(8,128)(2,1)S(1)}, bf16[256,2048]{1,0:T(8,128)(2,1)S(1)}, u32[]{:S(2)}, u32[]{:S(2)}) %collective-permute-start.1) | collective-permute-done | bytes 1048608 | tf_op jit(solution)/shard_map/ppermute | solution.py:325
  212.6 17.3 %fusion.1 = f32[1024,2816]{1,0:T(8,128)S(1)} fusion(bf16[1024,2048]{1,0:T(8,128)(2,1)} %bitcast.46, bf16[2816,2048]{1,0:T(8,128)(2,1)} %all-gather.3.cloned.1.call-done.refs_2_), kind=kOutput, calls=%fused_computation.15 | convolution fusion | flops 11811160064 | bytes 27262976 | tf_op jit(solution)/shard_map/dot_general | solution.py:329
  229.9 1.8 multiply_convert_fusion.2
  231.7 2.6 copy-done
  234.3 10.8 %convolution_convert_fusion = bf16[2048,1408]{1,0:T(8,128)(2,1)} fusion(bf16[1024,2048]{1,0:T(8,128)(2,1)} %constant_dynamic-update-slice_fusion, bf16[1024,1408]{1,0:T(8,128)(2,1)S(1)} %multiply_convert_fusion.2), kind=kOutput, calls=%fused_computation | convolution fusion | flops 5908463616 | bytes 12845056 | tf_op jit(solution)/shard_map/dot_general | solution.py:329
  245.5 11.0 %convolution_convert_fusion.1 = bf16[1024,2048]{1,0:T(8,128)(2,1)} fusion(bf16[1024,1408]{1,0:T(8,128)(2,1)S(1)} %multiply_convert_fusion.2, bf16[2048,1408]{1,0:T(8,128)(2,1)} %all-gather.5.cloned.1.call-done), kind=kOutput, calls=%fused_computation.5 | convolution fusion | flops 5907677184 | bytes 12845056 | tf_op jit(solution)/shard_map/dot_general | solution.py:329
  256.5 14.1 %multiply_convert_fusion = (bf16[1024,1408]{1,0:T(8,128)(2,1)}, bf16[1024,1408]{1,0:T(8,128)(2,1)}) fusion(f32[1024,2816]{1,0:T(8,128)} %copy-done, bf16[1024,2048]{1,0:T(8,128)(2,1)} %constant_dynamic-update-slice_fusion, bf16[2048,1408]{1,0:T(8,128)(2,1)S(1)} %copy-done.10), kind=kOutput, calls=%fused_computation.1 | convolution fusion | flops 5924323328 | bytes 27262976 | tf_op jit(solution)/shard_map/dot_general | solution.py:329
  270.6 43.8 %norm_back.1 = (f32[256,2048]{1,0:T(8,128)}, f32[1,2048]{1,0:T(1,128)}, bf16[256,2048]{1,0:T(8,128)(2,1)}, bf16[2816,2048]{1,0:T(8,128)(2,1)}) custom-call(bf16[1024,1408]{1,0:T(8,128)(2,1)} %get-tuple-element.100.refs_0_, bf16[1024,1408]{1,0:T(8,128)(2,1)} %get-tuple-element.99.refs_1_, bf16[2816,2048]{1,0:T(8,128)(2,1)} %all-gather.3.cloned.1.call-done.refs_2_, ...), custom_call_target="tpu_custom_call" | custom-call | tf_op jit(solution)/shard_map/norm_back/pallas_call | solution.py:1345
  317.6 1.7 collective-permute-start.4
  319.3 18.9 %collective-permute-done.3.refs_2_ = bf16[2,128,2048]{2,1,0:T(8,128)(2,1)S(1)} collective-permute-done((bf16[2,128,2048]{2,1,0:T(8,128)(2,1)S(1)}, bf16[2,128,2048]{2,1,0:T(8,128)(2,1)S(1)}, u32[]{:S(2)}, u32[]{:S(2)}) %collective-permute-start.3) | collective-permute-done | bytes 1048608 | tf_op jit(solution)/shard_map/ppermute | solution.py:325
  339.5 36.0 %share_dy.1 = (bf16[4,256,2048]{2,1,0:T(8,128)(2,1)}, f32[256,2048]{1,0:T(8,128)}, bf16[2,128,2048]{2,1,0:T(8,128)(2,1)}) custom-call(bf16[256,2048]{1,0:T(8,128)(2,1)} %get-tuple-element.71.refs_0_, bf16[4,256,2048]{2,1,0:T(8,128)(2,1)} %bitcast.41, bf16[2,128,2048]{2,1,0:T(8,128)(2,1)} %copy-done.4, bf16[2,128,2048]{2,1,0:T(8,128)(2,1)} %copy-done.5, ...), custom_call_target="tpu_custom_call" | custom-call | tf_op jit(solution)/shard_map/share_dy/pallas_call | solution.py:1410
  375.6 40.3 %attend_back.1 = (bf16[1024,640]{1,0:T(8,128)(2,1)}, bf16[4,160,1024]{2,1,0:T(8,128)(2,1)}, bf16[2048,512]{1,0:T(8,128)(2,1)}, bf16[2,128,2048]{2,1,0:T(8,128)(2,1)}, bf16[4,256,1408]{2,1,0:T(8,128)(2,1)}) custom-call(bf16[8,1024,64]{2,1,0:T(8,128)(2,1)} %get-tuple-element.56.refs_0_, bf16[1024,64]{1,0:T(8,128)(2,1)} %get-tuple-element.57.refs_1_, ...), custom_call_target="tpu_custom_call" | custom-call | tf_op jit(solution)/shard_map/attend_back/pallas_call | solution.py:993
  416.0 56.1 %leave.1 = (f32[256,2048]{1,0:T(8,128)}, f32[2,2048]{1,0:T(2,128)}, bf16[640,2048]{1,0:T(8,128)(2,1)}) custom-call(bf16[1024,640]{1,0:T(8,128)(2,1)} %get-tuple-element.82.refs_0_, bf16[640,2048]{1,0:T(8,128)(2,1)} %get-tuple-element.54.weight_ref.refs_1_, f32[256,2048]{1,0:T(8,128)} %bitcast.35, f32[256,128]{1,0:T(8,128)} %get-tuple-element.83.refs_3_, ...), custom_call_target="tpu_custom_call" | custom-call | tf_op jit(solution)/shard_map/leave/pallas_call | solution.py:1113
  474.2 28.5 %collective-permute-done.12.below_ref = bf16[352,2048]{1,0:T(8,128)(2,1)S(1)} collective-permute-done((bf16[352,2048]{1,0:T(8,128)(2,1)}, bf16[352,2048]{1,0:T(8,128)(2,1)S(1)}, u32[]{:S(2)}, u32[]{:S(2)}) %collective-permute-start.12) | collective-permute-done | bytes 1441824 | tf_op jit(solution)/shard_map/ppermute | solution.py:325
  503.7 1.4 collective-permute-start.14
  508.2 1.4 collective-permute-start.6
  510.4 17.6 %collective-permute-done.7.refs_4_ = bf16[256,512]{1,0:T(8,128)(2,1)} collective-permute-done((bf16[256,512]{1,0:T(8,128)(2,1)}, bf16[256,512]{1,0:T(8,128)(2,1)}, u32[]{:S(2)}, u32[]{:S(2)}) %collective-permute-start.7) | collective-permute-done | bytes 262176 | tf_op jit(solution)/shard_map/ppermute | solution.py:325
  528.0 8.2 %collective-permute-done.6.refs_3_ = bf16[256,512]{1,0:T(8,128)(2,1)} collective-permute-done((bf16[256,512]{1,0:T(8,128)(2,1)}, bf16[256,512]{1,0:T(8,128)(2,1)}, u32[]{:S(2)}, u32[]{:S(2)}) %collective-permute-start.6) | collective-permute-done | bytes 262176 | tf_op jit(solution)/shard_map/ppermute | solution.py:325
  536.2 1.5 collective-permute-start.10
  538.0 1.7 collective-permute-start.8
  539.7 5.4 join_pieces.5
  545.1 2.7 join_pieces.4
  549.4 3.0 join_pieces.3
  552.5 5.4 last_sums.1
  557.9 7.2 %join_rows.1 = f32[1408,2048]{1,0:T(8,128)} custom-call(s32[1]{0:T(128)} %bitcast.index_ref.refs_0_, bf16[352,2048]{1,0:T(8,128)(2,1)} %reduce-scatter.7.cloned.1.call-done.own_ref, bf16[352,2048]{1,0:T(8,128)(2,1)} %copy-done.3, bf16[352,2048]{1,0:T(8,128)(2,1)} %copy-done.2, bf16[176,2048]{1,0:T(8,128)(2,1)} %collective-permute-done.13.top_ref, ...), custom_call_target="tpu_custom_call" | custom-call | tf_op jit(solution)/shard_map/join_rows/pallas_call | solution.py:1165
  (69 shorter events, 20.5 us)
Async XLA Ops:
  7.2 205.4 %all-gather.3.cloned.1.call-start = ((), (), s32[]{:S(2)}) async-start(), calls=%async_computation.4 | async-start | bytes 12976128 | tf_op jit(solution)/shard_map/all_gather | solution.py:1449
  62.9 182.6 %all-gather.5.cloned.1.call-start = ((), (), s32[]{:S(2)}) async-start(), calls=%async_computation.5 | async-start | bytes 6488064 | tf_op jit(solution)/shard_map/all_gather | solution.py:1459
  72.0 90.0 %copy-start.1 = (f32[1,256,2048]{2,1,0:T(8,128)S(1)}, f32[1,256,2048]{2,1,0:T(8,128)}, u32[]{:S(2)}) copy-start(f32[1,256,2048]{2,1,0:T(8,128)} %param.16) | copy-start | bytes 6291460
  162.3 213.3 %reduce-scatter.5.cloned.1.call-start = ((), (), s32[]{:S(2)}) async-start(), calls=%async_computation.6 | async-start | bytes 6488064 | tf_op jit(solution)/shard_map/reduce_scatter | solution.py:1466
  162.5 26.1 %collective-permute-start = (bf16[256,2048]{1,0:T(8,128)(2,1)S(1)}, bf16[256,2048]{1,0:T(8,128)(2,1)S(1)}, u32[]{:S(2)}, u32[]{:S(2)}) collective-permute-start(bf16[256,2048]{1,0:T(8,128)(2,1)S(1)} %bitcast_convert_fusion), channel_id=1, source_target_pairs={{0,1},{1,0},{2,3},{3,2},{4,5},{5,4},{6,7},{7,6},{8,9},{9,8},{10,11... | collective-permute-start | bytes 3145736 | tf_op jit(solution)/shard_map/ppermute | solution.py:325
  164.3 46.1 %collective-permute-start.1 = (bf16[256,2048]{1,0:T(8,128)(2,1)S(1)}, bf16[256,2048]{1,0:T(8,128)(2,1)S(1)}, u32[]{:S(2)}, u32[]{:S(2)}) collective-permute-start(bf16[256,2048]{1,0:T(8,128)(2,1)S(1)} %bitcast_convert_fusion), channel_id=1, source_target_pairs={{0,2},{1,3},{2,0},{3,1},{4,6},{5,7},{6,4},{7,5},{8,10},{9,11},{10,... | collective-permute-start | bytes 3145736 | tf_op jit(solution)/shard_map/ppermute | solution.py:325
  164.6 47.0 %collective-permute-start.2 = (bf16[256,2048]{1,0:T(8,128)(2,1)S(1)}, bf16[256,2048]{1,0:T(8,128)(2,1)S(1)}, u32[]{:S(2)}, u32[]{:S(2)}) collective-permute-start(bf16[256,2048]{1,0:T(8,128)(2,1)S(1)} %bitcast_convert_fusion), channel_id=1, source_target_pairs={{0,3},{1,2},{2,1},{3,0},{4,7},{5,6},{6,5},{7,4},{8,11},{9,10},{10,... | collective-permute-start | bytes 3145736 | tf_op jit(solution)/shard_map/ppermute | solution.py:325
  229.9 4.4 copy-start
  245.2 227.0 %reduce-scatter.7.cloned.1.call-start = ((), (), s32[]{:S(2)}) async-start(), calls=%async_computation.7 | async-start | bytes 12976128 | tf_op jit(solution)/shard_map/reduce_scatter | solution.py:1466
  245.5 11.1 %copy-start.10 = (bf16[2048,1408]{1,0:T(8,128)(2,1)S(1)}, bf16[2048,1408]{1,0:T(8,128)(2,1)}, u32[]{:S(2)}) copy-start(bf16[2048,1408]{1,0:T(8,128)(2,1)} %all-gather.5.cloned.1.call-done) | copy-start | bytes 17301508
  314.4 192.4 %reduce-scatter.11.cloned.1.call-start = ((), (), s32[]{:S(2)}) async-start(), calls=%async_computation.9 | async-start | bytes 2359296 | tf_op jit(solution)/shard_map/reduce_scatter | solution.py:1466
  317.2 21.0 %collective-permute-start.3 = (bf16[2,128,2048]{2,1,0:T(8,128)(2,1)S(1)}, bf16[2,128,2048]{2,1,0:T(8,128)(2,1)S(1)}, u32[]{:S(2)}, u32[]{:S(2)}) collective-permute-start(bf16[2,128,2048]{2,1,0:T(8,128)(2,1)S(1)} %pad_maximum_fusion), channel_id=1, source_target_pairs={{0,1},{1,0},{2,3},{3,2},{4,5},{5,4},{6,7},{7,6},{8,9},{9,8},{10,11... | collective-permute-start | bytes 3145736 | tf_op jit(solution)/shard_map/ppermute | solution.py:325
  317.6 20.7 %collective-permute-start.4 = (bf16[2,128,2048]{2,1,0:T(8,128)(2,1)S(1)}, bf16[2,128,2048]{2,1,0:T(8,128)(2,1)S(1)}, u32[]{:S(2)}, u32[]{:S(2)}) collective-permute-start(bf16[2,128,2048]{2,1,0:T(8,128)(2,1)S(1)} %stack.7), channel_id=1, source_target_pairs={{0,2},{1,3},{2,0},{3,1},{4,6},{5,7},{6,4},{7,5},{8,10},{9,11},{10,... | collective-permute-start | bytes 3145736 | tf_op jit(solution)/shard_map/ppermute | solution.py:325
  338.2 1.0 copy-start.4
  338.3 1.2 copy-start.5
  415.9 120.3 %reduce-scatter.9.cloned.1.call-start = ((), (), s32[]{:S(2)}) async-start(), calls=%async_computation.8 | async-start | bytes 2949120 | tf_op jit(solution)/shard_map/reduce_scatter | solution.py:1466
  472.2 30.6 %collective-permute-start.12 = (bf16[352,2048]{1,0:T(8,128)(2,1)}, bf16[352,2048]{1,0:T(8,128)(2,1)S(1)}, u32[]{:S(2)}, u32[]{:S(2)}) collective-permute-start(bf16[352,2048]{1,0:T(8,128)(2,1)} %reduce-scatter.7.cloned.1.call-done.own_ref), channel_id=1, source_target_pairs={{0,2},{1,3},{2,0},{3,1},{4,6},{5,7},{6,4},{7,5},{8,10},{9,11},{10,... | collective-permute-start | bytes 4325384 | tf_op jit(solution)/shard_map/ppermute | solution.py:325
  473.3 31.9 %collective-permute-start.11 = (bf16[352,2048]{1,0:T(8,128)(2,1)}, bf16[352,2048]{1,0:T(8,128)(2,1)S(1)}, u32[]{:S(2)}, u32[]{:S(2)}) collective-permute-start(bf16[352,2048]{1,0:T(8,128)(2,1)} %reduce-scatter.7.cloned.1.call-done.own_ref), channel_id=1, source_target_pairs={{0,1},{1,0},{2,3},{3,2},{4,5},{5,4},{6,7},{7,6},{8,9},{9,8},{10,11... | collective-permute-start | bytes 4325384 | tf_op jit(solution)/shard_map/ppermute | solution.py:325
  502.7 42.4 %copy-start.2 = (bf16[352,2048]{1,0:T(8,128)(2,1)}, bf16[352,2048]{1,0:T(8,128)(2,1)S(1)}, u32[]{:S(2)}) copy-start(bf16[352,2048]{1,0:T(8,128)(2,1)S(1)} %collective-permute-done.12.below_ref) | copy-start | bytes 4325380
  503.7 54.1 %collective-permute-start.14 = (bf16[176,2048]{1,0:T(8,128)(2,1)}, bf16[176,2048]{1,0:T(8,128)(2,1)}, u32[]{:S(2)}, u32[]{:S(2)}) collective-permute-start(bf16[176,2048]{1,0:T(8,128)(2,1)} %slice.48), channel_id=1, source_target_pairs={{0,1},{1,0},{2,3},{3,2},{4,5},{5,4},{6,7},{7,6},{8,9},{9,8},{10,11... | collective-permute-start | bytes 2162696 | tf_op jit(solution)/shard_map/ppermute | solution.py:325
  505.2 40.0 %copy-start.3 = (bf16[352,2048]{1,0:T(8,128)(2,1)}, bf16[352,2048]{1,0:T(8,128)(2,1)S(1)}, u32[]{:S(2)}) copy-start(bf16[352,2048]{1,0:T(8,128)(2,1)S(1)} %collective-permute-done.11.side_ref) | copy-start | bytes 4325380
  506.1 51.8 %collective-permute-start.13 = (bf16[176,2048]{1,0:T(8,128)(2,1)}, bf16[176,2048]{1,0:T(8,128)(2,1)}, u32[]{:S(2)}, u32[]{:S(2)}) collective-permute-start(bf16[176,2048]{1,0:T(8,128)(2,1)} %slice.47), channel_id=1, source_target_pairs={{0,2},{1,3},{2,0},{3,1},{4,6},{5,7},{6,4},{7,5},{8,10},{9,11},{10,... | collective-permute-start | bytes 2162696 | tf_op jit(solution)/shard_map/ppermute | solution.py:325
  506.9 21.1 %collective-permute-start.7 = (bf16[256,512]{1,0:T(8,128)(2,1)}, bf16[256,512]{1,0:T(8,128)(2,1)}, u32[]{:S(2)}, u32[]{:S(2)}) collective-permute-start(bf16[256,512]{1,0:T(8,128)(2,1)} %reduce-scatter.11.cloned.1.call-done.refs_1_), channel_id=1, source_target_pairs={{0,3},{1,2},{2,1},{3,0},{4,7},{5,6},{6,5},{7,4},{8,11},{9,10},{10,... | collective-permute-start | bytes 786440 | tf_op jit(solution)/shard_map/ppermute | solution.py:325
  508.2 28.0 %collective-permute-start.6 = (bf16[256,512]{1,0:T(8,128)(2,1)}, bf16[256,512]{1,0:T(8,128)(2,1)}, u32[]{:S(2)}, u32[]{:S(2)}) collective-permute-start(bf16[256,512]{1,0:T(8,128)(2,1)} %reduce-scatter.11.cloned.1.call-done.refs_1_), channel_id=1, source_target_pairs={{0,2},{1,3},{2,0},{3,1},{4,6},{5,7},{6,4},{7,5},{8,10},{9,11},{10,... | collective-permute-start | bytes 786440 | tf_op jit(solution)/shard_map/ppermute | solution.py:325
  509.6 26.6 %collective-permute-start.5 = (bf16[256,512]{1,0:T(8,128)(2,1)}, bf16[256,512]{1,0:T(8,128)(2,1)}, u32[]{:S(2)}, u32[]{:S(2)}) collective-permute-start(bf16[256,512]{1,0:T(8,128)(2,1)} %reduce-scatter.11.cloned.1.call-done.refs_1_), channel_id=1, source_target_pairs={{0,1},{1,0},{2,3},{3,2},{4,5},{5,4},{6,7},{7,6},{8,9},{9,8},{10,11... | collective-permute-start | bytes 786440 | tf_op jit(solution)/shard_map/ppermute | solution.py:325
  536.2 11.6 %collective-permute-start.10 = (bf16[80,2048]{1,0:T(8,128)(2,1)}, bf16[80,2048]{1,0:T(8,128)(2,1)S(1)}, u32[]{:S(2)}, u32[]{:S(2)}) collective-permute-start(bf16[80,2048]{1,0:T(8,128)(2,1)} %reduce-scatter.9.cloned.1.call-done.refs_1_), channel_id=1, source_target_pairs={{0,3},{1,2},{2,1},{3,0},{4,7},{5,6},{6,5},{7,4},{8,11},{9,10},{10,... | collective-permute-start | bytes 983048 | tf_op jit(solution)/shard_map/ppermute | solution.py:325
  537.7 10.2 %collective-permute-start.9 = (bf16[80,2048]{1,0:T(8,128)(2,1)}, bf16[80,2048]{1,0:T(8,128)(2,1)S(1)}, u32[]{:S(2)}, u32[]{:S(2)}) collective-permute-start(bf16[80,2048]{1,0:T(8,128)(2,1)} %reduce-scatter.9.cloned.1.call-done.refs_1_), channel_id=1, source_target_pairs={{0,2},{1,3},{2,0},{3,1},{4,6},{5,7},{6,4},{7,5},{8,10},{9,11},{10,... | collective-permute-start | bytes 983048 | tf_op jit(solution)/shard_map/ppermute | solution.py:325
  538.0 9.9 %collective-permute-start.8 = (bf16[80,2048]{1,0:T(8,128)(2,1)}, bf16[80,2048]{1,0:T(8,128)(2,1)S(1)}, u32[]{:S(2)}, u32[]{:S(2)}) collective-permute-start(bf16[80,2048]{1,0:T(8,128)(2,1)} %reduce-scatter.9.cloned.1.call-done.refs_1_), channel_id=1, source_target_pairs={{0,1},{1,0},{2,3},{3,2},{4,5},{5,4},{6,7},{7,6},{8,9},{9,8},{10,11... | collective-permute-start | bytes 983048 | tf_op jit(solution)/shard_map/ppermute | solution.py:325
  547.8 0.7 copy-start.6
  547.9 0.8 copy-start.7
  548.7 0.7 copy-start.8
  557.9 7.2 %copy-start.9 = (f32[2,2048]{1,0:T(2,128)S(1)}, f32[2,2048]{1,0:T(2,128)}, u32[]{:S(2)}) copy-start(f32[2,2048]{1,0:T(2,128)} %get-tuple-element.90) | copy-start | bytes 49156
Sparse Core Ops, SparseCore 0:
  63.0 112.4 all-gather.2
  177.1 58.6 all-gather.4
  245.3 63.8 reduce-scatter.4
  314.6 118.3 reduce-scatter.6
  435.1 34.6 reduce-scatter.10
  472.3 37.6 reduce-scatter.8

commit v5 on v4

--- a/solution.py
+++ b/solution.py
@@ -1236,77 +1236,129 @@
 
 
 def norm_back_kernel(
-    count, left_in, right_in, weight_ref, flowing_in, middle_in, scale_ref, gain_ref, inputs_ref,
-    own_ref, gain_out_ref, dy_ref, term_ref,
-    sent_ref, side_ref, below_ref, far_ref, stage_ref, held_grads, held_weight, held_inputs, flowing_ref, middle_ref,
-    send_sems, recv_sems, store_sems, load_sems,
+    count, act_in, down_in, dm_in, gates_in, weight_in, flowing_in, middle_in, inputs_in, scale_ref, gain_ref,
+    own_ref, gain_out_ref, dy_ref, term_ref, product_ref, from_side_ref, from_below_ref,
+    act_ref, down_ref, dm_ref, gates_ref, grads_ref, weight_ref, flowing_ref, middle_ref, inputs_ref,
+    held_ref, sent_ref, side_ref, below_ref, far_ref, stage_ref,
+    send_sems, recv_sems, load_sems, part_sems, store_sems, product_sems,
 ):
-    part, width = flowing_ref.shape
+    part, _ = flowing_in.shape
     half = part // 2
+    wide, narrow = jnp.float32, jnp.bfloat16
+    units = down_ref.shape[1]
     sems = (send_sems, recv_sems)
-    units = held_grads.shape[1]
-    tile = stage_ref.shape[1]
-    tiles = units // tile
-    cuts = [tiles * number // 4 * tile for number in range(5)]
-    last = pl.ds((count - 1) * part, part)
-    rest = pl.ds(0, (count - 1) * part)
-
-    def load_grads(rows, number):
+
+    def load(source, target, number):
+        copy = pltpu.make_async_copy(source, target, load_sems.at[number])
+        copy.start()
+        return copy
+
+    def load_parts(turn):
+        rows = pl.ds(pl.multiple_of((count - 1 - turn) * part, part), part)
+        slot = turn % 2
         return [
-            pltpu.make_async_copy(
-                source.at[rows],
-                held_grads.at[rows, pl.ds(place * (units // 2), units // 2)],
-                load_sems.at[number + place],
-            )
-            for place, source in enumerate((left_in, right_in))
+            pltpu.make_async_copy(dm_in.at[rows], dm_ref.at[slot], part_sems.at[0, slot]),
+            pltpu.make_async_copy(gates_in.at[rows], gates_ref.at[slot], part_sems.at[1, slot]),
         ]
 
-    load_last, load_rest = load_grads(last, 9), load_grads(rest, 11)
-    for load in load_last:
-        load.start()
-    load_weight = []
-    for number in range(4):
-        rows = pl.ds(cuts[number], cuts[number + 1] - cuts[number])
-        load = pltpu.make_async_copy(weight_ref.at[rows], held_weight.at[rows], load_sems.at[number])
-        load.start()
-        load_weight.append(load)
-    for load in load_rest:
-        load.start()
-    load_inputs = pltpu.make_async_copy(inputs_ref, held_inputs, load_sems.at[6])
-    load_inputs.start()
-    load_ends = [
-        pltpu.make_async_copy(flowing_in, flowing_ref, load_sems.at[7]),
-        pltpu.make_async_copy(middle_in, middle_ref, load_sems.at[8]),
+    firsts = [load(act_in, act_ref, 0), load(down_in, down_ref, 1)]
+    for copy in load_parts(0):
+        copy.start()
+    load_weight = load(weight_in, weight_ref, 2)
+    for copy in load_parts(1):
+        copy.start()
+    lasts = [load(inputs_in, inputs_ref, 3), load(flowing_in, flowing_ref, 4), load(middle_in, middle_ref, 5)]
+    greet([seq_peer(1), seq_peer(2)])
+    top, bottom = pl.ds(0, half), pl.ds(half, half)
+    firsts_sums = [
+        remote(held_ref.at[3].at[top], from_side_ref.at[1], sems, 6, seq_peer(1)),
+        remote(held_ref.at[3].at[bottom], from_below_ref.at[1], sems, 7, seq_peer(2)),
+        remote(held_ref.at[2].at[bottom], from_below_ref.at[0], sems, 8, seq_peer(2)),
+        remote(held_ref.at[1].at[top], from_side_ref.at[0], sems, 9, seq_peer(1)),
     ]
-    for load in load_ends:
-        load.start()
-    grads_ref, weight_ref, inputs_ref = held_grads, held_weight, held_inputs
-    for load in load_last:
-        load.wait()
-    partial = jnp.zeros((part, width), jnp.float32)
-    for number in range(4):
-        load_weight[number].wait()
-        rows = slice(cuts[number], cuts[number + 1])
-        partial += matmul(grads_ref[last, rows], weight_ref[rows, :], 1, 0)
-    sent_ref[count - 1] = partial.astype(jnp.bfloat16)
-    greet([seq_peer(1), seq_peer(2)])
     sums = sum_copies(sent_ref, side_ref, below_ref, far_ref, half, sems)
-    sums[0].start()
-    sums[1].start()
-    for load in load_rest:
-        load.wait()
+    for copy in firsts:
+        copy.wait()
+
+    def down_part(turn, carry):
+        step = count - 1 - turn
+        rows = pl.ds(pl.multiple_of(step * part, part), part)
+        held_ref[step] = matmul(act_ref[rows, :], down_ref[...], 1, 1).astype(narrow)
+
+        @pl.when(turn == 0)
+        def _():
+            firsts_sums[0].start()
+            firsts_sums[1].start()
+
+        @pl.when(turn == 1)
+        def _():
+            firsts_sums[2].start()
+
+        @pl.when(turn == 2)
+        def _():
+            firsts_sums[3].start()
+
+        return carry
+
+    lax.fori_loop(0, count, down_part, 0)
+    product = pltpu.make_async_copy(held_ref, product_ref, product_sems.at[0])
+    product.start()
+    load_weight.wait()
 
     def one_part(turn, carry):
         step = count - 1 - turn
-        rows_step = pl.ds(pl.multiple_of(step * part, part), part)
-        partial = matmul(grads_ref[rows_step, :], weight_ref[...], 1, 0)
-        pass_sums(turn, step, partial, sums, sent_ref, side_ref, below_ref, own_ref, half)
+        slot = turn % 2
+        rows = pl.ds(pl.multiple_of(step * part, part), part)
+        for copy in load_parts(turn):
+            copy.wait()
+        dact = matmul(dm_ref[slot], down_ref[...], 1, 0)
+        gate = gates_ref[slot, :, :units].astype(wide)
+        up = gates_ref[slot, :, units:].astype(wide)
+        sigma = jax.nn.sigmoid(gate)
+        grads_ref[rows, :units] = (dact * up * sigma * (1.0 + gate * (1.0 - sigma))).astype(narrow)
+        grads_ref[rows, units:] = (dact * gate * sigma).astype(narrow)
+
+        @pl.when(turn < count - 2)
+        def _():
+            for copy in load_parts(turn + 2):
+                copy.start()
+
+        partial = matmul(grads_ref[rows, :], weight_ref[...], 1, 0)
+
+        @pl.when(turn == count - 1)
+        def _():
+            own_ref[...] = partial
+
+        @pl.when(turn < count - 1)
+        def _():
+            sent_ref[step] = partial.astype(narrow)
+
+        @pl.when(turn == 0)
+        def _():
+            sums[0].start()
+            sums[1].start()
+
+        @pl.when(turn == 1)
+        def _():
+            sums[2].start()
+
+        @pl.when(turn == 2)
+        def _():
+            sums[3].start()
+
         return carry
 
-    lax.fori_loop(1, count, one_part, 0)
-    load_inputs.wait()
-    for load in load_ends:
-        load.wait()
+    lax.fori_loop(0, count, one_part, 0)
+    sums[0].wait_recv()
+    sent_ref[2, :half] = (sent_ref[2, :half].astype(wide) + side_ref[1].astype(wide)).astype(narrow)
+    sums[4].start()
+    sums[1].wait_recv()
+    sent_ref[1, half:] = (sent_ref[1, half:].astype(wide) + below_ref[1].astype(wide)).astype(narrow)
+    sums[5].start()
+    for copy in lasts:
+        copy.wait()
+    tile = stage_ref.shape[1]
+    tiles = grads_ref.shape[1] // tile
 
     def store(number):
         rows = pl.ds(pl.multiple_of(number * tile, tile), tile)
@@ -1318,7 +1370,7 @@
             store(number - 2).wait()
 
         columns = pl.ds(pl.multiple_of(number * tile, tile), tile)
-        stage_ref[number % 2] = matmul(grads_ref[:, columns], inputs_ref[...], 0, 0).astype(jnp.bfloat16)
+        stage_ref[number % 2] = matmul(grads_ref[:, columns], inputs_ref[...], 0, 0).astype(narrow)
         store(number).start()
         return carry
 
@@ -1330,48 +1382,63 @@
     gain_out_ref[...] = jnp.sum(grads * unit, 0, keepdims=True)
     inner = grads * gain_ref[...]
     own_ref[...] = flowing_ref[...] + scale * (inner - unit * jnp.mean(inner * unit, 1, keepdims=True))
-    dy_ref[...] = own_ref[...].astype(jnp.bfloat16)
+    dy_ref[...] = own_ref[...].astype(narrow)
     for number in range(tiles - 2, tiles):
         store(number).wait()
-    for copy in sums:
+    product.wait()
+    for copy in firsts_sums:
+        copy.wait_recv()
+    for copy in sums + firsts_sums:
         copy.wait_send()
 
 
-def norm_back(left, right, weight, flowing, middle, scale, gain, inputs, count):
+def norm_back(act, down, dm, gates, weight, flowing, middle, inputs, scale, gain, count):
     part, width = flowing.shape
-    units = left.shape[1] + right.shape[1]
+    units = gates.shape[1]
     tile = 2 * 128
-    vmem = pl.BlockSpec(memory_space=pltpu.VMEM)
-    own, gain_term, dy, term = pl.pallas_call(
+    vmem, whole = pl.BlockSpec(memory_space=pltpu.VMEM), pl.BlockSpec(memory_space=pl.ANY)
+    narrow, wide = jnp.bfloat16, jnp.float32
+    pair = (2, part // 2, width)
+    own, gain_term, dy, term, product, from_side, from_below = pl.pallas_call(
         lambda *refs: norm_back_kernel(count, *refs),
         out_shape=(
-            jax.ShapeDtypeStruct((part, width), jnp.float32),
-            jax.ShapeDtypeStruct((1, width), jnp.float32),
-            jax.ShapeDtypeStruct((part, width), jnp.bfloat16),
-            jax.ShapeDtypeStruct((units, width), jnp.bfloat16),
+            jax.ShapeDtypeStruct((part, width), wide),
+            jax.ShapeDtypeStruct((1, width), wide),
+            jax.ShapeDtypeStruct((part, width), narrow),
+            jax.ShapeDtypeStruct((units, width), narrow),
+            jax.ShapeDtypeStruct((count, part, width), narrow),
+            jax.ShapeDtypeStruct(pair, narrow),
+            jax.ShapeDtypeStruct(pair, narrow),
         ),
-        in_specs=[pl.BlockSpec(memory_space=pl.ANY)] * 5 + [vmem] * 2 + [pl.BlockSpec(memory_space=pl.ANY)],
-        out_specs=[vmem] * 3 + [pl.BlockSpec(memory_space=pl.ANY)],
+        in_specs=[whole] * 8 + [vmem] * 2,
+        out_specs=[vmem] * 3 + [whole] * 4,
         scratch_shapes=[
-            pltpu.VMEM((count, part, width), jnp.bfloat16),
-            pltpu.VMEM((2, part // 2, width), jnp.bfloat16),
-            pltpu.VMEM((2, part // 2, width), jnp.bfloat16),
-            pltpu.VMEM((2, part // 2, width), jnp.bfloat16),
-            pltpu.VMEM((2, tile, width), jnp.bfloat16),
-            pltpu.VMEM((part * count, units), jnp.bfloat16),
-            pltpu.VMEM(weight.shape, jnp.bfloat16),
-            pltpu.VMEM(inputs.shape, jnp.bfloat16),
-            pltpu.VMEM((part, width), jnp.float32),
-            pltpu.VMEM((part, width), jnp.float32),
+            pltpu.VMEM(act.shape, narrow),
+            pltpu.VMEM(down.shape, narrow),
+            pltpu.VMEM((2, part, width), narrow),
+            pltpu.VMEM((2, part, units), narrow),
+            pltpu.VMEM((part * count, units), narrow),
+            pltpu.VMEM(weight.shape, narrow),
+            pltpu.VMEM((part, width), wide),
+            pltpu.VMEM((part, width), wide),
+            pltpu.VMEM(inputs.shape, narrow),
+            pltpu.VMEM((count, part, width), narrow),
+            pltpu.VMEM((count, part, width), narrow),
+            pltpu.VMEM(pair, narrow),
+            pltpu.VMEM(pair, narrow),
+            pltpu.VMEM(pair, narrow),
+            pltpu.VMEM((2, tile, width), narrow),
+            pltpu.SemaphoreType.DMA((10,)),
+            pltpu.SemaphoreType.DMA((10,)),
             pltpu.SemaphoreType.DMA((6,)),
-            pltpu.SemaphoreType.DMA((6,)),
+            pltpu.SemaphoreType.DMA((2, 2)),
             pltpu.SemaphoreType.DMA((2,)),
-            pltpu.SemaphoreType.DMA((13,)),
+            pltpu.SemaphoreType.DMA((1,)),
         ],
-        compiler_params=pltpu.CompilerParams(collective_id=3, has_side_effects=True, vmem_limit_bytes=LIMIT),
+        compiler_params=pltpu.CompilerParams(collective_id=3, has_side_effects=True, vmem_limit_bytes=67043328),
         name="norm_back",
-    )(left, right, weight, flowing, middle, scale, gain, inputs)
-    return own, gain_term[0], dy, term
+    )(act, down, dm, gates, weight, flowing, middle, inputs, scale, gain)
+    return own, gain_term[0], dy, term, product, from_side, from_below
 
 
 def share_dy_kernel(
@@ -1459,8 +1526,8 @@
     down_cols = lax.all_gather(down_part, "fsdp", axis=0, tiled=True)
     dm_all = jnp.concatenate([dm_sent] + [neighbour(dm_sent, step) for step in range(1, count)], 0)
     both = matmul(normed_two_all, gate_up, 1, 1)
-    gate_part, up_part = both[:, :units], both[:, units:]
-    activated = (jax.nn.silu(gate_part) * up_part).astype(jnp.bfloat16)
+    gates = both.astype(jnp.bfloat16)
+    activated = (jax.nn.silu(both[:, :units]) * both[:, units:]).astype(jnp.bfloat16)
 
     def owned(grad):
         return lax.psum_scatter(grad.astype(jnp.bfloat16), "fsdp", scatter_dimension=0, tiled=True)
@@ -1468,19 +1535,8 @@
     term_down = matmul(dm_all, activated, 0, 0).astype(jnp.bfloat16)
     dm_all, activated, term_down = after((dm_all, activated, term_down))
     grad_down = owned(term_down)
-    down_sent = matmul(activated, down_cols, 1, 1).astype(jnp.bfloat16)
-    down_sent = down_sent.reshape(count, part_len, width)
-    dm_all, down_sent = after((dm_all, down_sent))
-    half = part_len // 2
-    from_side = neighbour(jnp.stack([down_sent[1, :half], down_sent[3, :half]]), 1)
-    from_below = neighbour(jnp.stack([down_sent[2, half:], down_sent[3, half:]]), 2)
-    dact = matmul(dm_all, down_cols, 1, 0)
-    sigma = jax.nn.sigmoid(gate_part)
-    dgate = dact * up_part * sigma * (1.0 + gate_part * (1.0 - sigma))
-    dup = dact * gate_part * sigma
-    dgate, dup = dgate.astype(jnp.bfloat16), dup.astype(jnp.bfloat16)
-    dmiddle, gain_two, dy, term_gate_up = norm_back(
-        dgate, dup, gate_up, flowing, middle, scale_two, gain[1:], normed_two_all, count
+    dmiddle, gain_two, dy, term_gate_up, down_sent, from_side, from_below = norm_back(
+        activated, down_cols, dm_all, gates, gate_up, flowing, middle, normed_two_all, scale_two, gain[1:], count
     )
     grad_gate_up = owned(term_gate_up)
     dy_all, base, passed = share_dy(dy, down_sent, from_side, from_below, middle, count)

time: 581 us -> 558 us (0.960)
  matrix products: 53.3 us -> 30.8 us
  Pallas kernels: 352 us -> 374 us
  waiting for transfers between devices: 116 us -> 96.9 us
    dot_general x4 -> x2, matrix products: 53.3 us -> 30.8 us  [matmul(): lax.dot_general(left, right, (((left_dim,), (right_dim,)), ((), ())), pre...]
    pallas_call x1, Pallas kernels: 43.8 us -> 64 us  [norm_back(): pl.pallas_call(lambda *refs: norm_back_kernel(count, *refs), out_shape=(j...]
    ppermute x15 -> x13, waiting for transfers between devices: 116 us -> 96.8 us  [neighbour(): return lax.ppermute(values, 'seq', [(i, i ^ step) for i in range(count)])]
    ppermute x15 -> x13, starting transfers between devices: 16.9 us -> 14.4 us  [neighbour(): return lax.ppermute(values, 'seq', [(i, i ^ step) for i in range(count)])]
  transfers between devices with their start and end apart: 21 -> 19, of which waited for: 8 -> 6; matrix products, arithmetic and copies ran while one was open for 11% -> 8% of each run, Pallas kernels for 51% -> 57%
where the time goes in v5:
time: 558 us; the launch traced here: 550 us
  Pallas kernels  374 us (67%)
  waiting for transfers between devices  96.9 us (17%)
  matrix products  30.8 us (6%)
  starting transfers between devices  15.8 us (3%)
  between operations  14.5 us (3%)
  local copies, waits for them, and re-layouts  11.9 us (2%)
  other arithmetic  6.05 us (1%)
    ppermute x13, waiting for transfers between devices, neighbour(): return lax.ppermute(values, 'seq', [(i, i ^ step) for i in range(count)])  96.8 us
    pallas_call x1, Pallas kernels, attend(): pl.pallas_call(lambda *refs: attend_kernel(count, *refs), out_shape=(jax....  90 us
    pallas_call x1, Pallas kernels, norm_back(): pl.pallas_call(lambda *refs: norm_back_kernel(count, *refs), out_shape=(j...  64 us
    pallas_call x1, Pallas kernels, leave(): pl.pallas_call(lambda *refs: leave_kernel(count, *refs), out_shape=(jax.S...  56.2 us
    pallas_call x1, Pallas kernels, enter(): pl.pallas_call(lambda *refs: enter_kernel(count, *refs), out_shape=(jax.S...  52.9 us
    pallas_call x1, Pallas kernels, attend_back(): pl.pallas_call(lambda *refs: attend_back_kernel(count, *refs), out_shape=...  41.2 us
    pallas_call x1, Pallas kernels, share_dy(): pl.pallas_call(lambda *refs: share_dy_kernel(*refs), out_shape=[jax.Shape...  37.2 us
    dot_general x2, matrix products, matmul(): lax.dot_general(left, right, (((left_dim,), (right_dim,)), ((), ())), pre...  30.8 us
  transfers between devices with their start and end apart: 19, of which 6 were waited for; matrix products, arithmetic and copies ran while one was open for 8% of the time, Pallas kernels for 57%

profile of v5, /device:TPU:0, one launch (start us, length us, event | category | flops | bytes accessed | tf_op | source)
XLA Modules:
  0.0 550.4 jit_solution(6739464703177889508)
XLA Ops:
  7.9 1.4 slice_bitcast_fusion
  9.9 52.9 %enter.1 = (bf16[4,256,2048]{2,1,0:T(8,128)(2,1)}, bf16[640,2048]{1,0:T(8,128)(2,1)}, bf16[2048,512]{1,0:T(8,128)(2,1)}, f32[1024,64]{1,0:T(8,128)}, bf16[352,20...) custom-call(f32[256,2048]{1,0:T(8,128)} %bitcast.28, f32[1,2048]{1,0:T(1,128)} %get-tuple-element.102.refs_1_.refs_4_, ...), custom_call_target="tpu_custom_call" | custom-call | tf_op jit(solution)/shard_map/enter/pallas_call | solution.py:677
  62.8 9.1 %project_qkv.1 = (bf16[8,1024,64]{2,1,0:T(8,128)(2,1)}, bf16[1024,64]{1,0:T(8,128)(2,1)}, bf16[1024,64]{1,0:T(8,128)(2,1)}) custom-call(s32[1]{0:T(128)} %bitcast.index_ref.refs_0_, bf16[1024,2048]{1,0:T(8,128)(2,1)} %bitcast.31, bf16[640,2048]{1,0:T(8,128)(2,1)} %get-tuple-element.55.weight_ref.refs_1_, f32[1024,64]{1,0:T(8,128)} %get-tuple-element.56.table_ref.refs_7_), custom_call_target="tpu_custom_call" | custom-call | tf_op jit(solution)/shard_map/project_qkv/pallas_call | solution.py:727
  72.0 90.0 %attend.1 = (bf16[1024,512]{1,0:T(8,128)(2,1)}, f32[8,1024]{1,0:T(8,128)}, f32[256,2048]{1,0:T(8,128)}, f32[256,128]{1,0:T(8,128)}, bf16[4,256,2048]{2,1,0:T(8,128)(2,1)}) custom-call(bf16[8,1024,64]{2,1,0:T(8,128)(2,1)} %get-tuple-element.57.refs_0_, bf16[1024,64]{1,0:T(8,128)(2,1)} %get-tuple-element.58.refs_1_, ...), custom_call_target="tpu_custom_call" | custom-call | tf_op jit(solution)/shard_map/attend/pallas_call | solution.py:821
  162.8 1.8 collective-permute-start
  164.9 1.5 collective-permute-start.2
  167.4 21.5 %collective-permute-done = bf16[256,2048]{1,0:T(8,128)(2,1)S(1)} collective-permute-done((bf16[256,2048]{1,0:T(8,128)(2,1)S(1)}, bf16[256,2048]{1,0:T(8,128)(2,1)S(1)}, u32[]{:S(2)}, u32[]{:S(2)}) %collective-permute-start) | collective-permute-done | bytes 1048608 | tf_op jit(solution)/shard_map/ppermute | solution.py:325
  188.9 1.1 constant_dynamic-update-slice_fusion.2
  190.0 20.8 %collective-permute-done.1 = bf16[256,2048]{1,0:T(8,128)(2,1)S(1)} collective-permute-done((bf16[256,2048]{1,0:T(8,128)(2,1)S(1)}, bf16[256,2048]{1,0:T(8,128)(2,1)S(1)}, u32[]{:S(2)}, u32[]{:S(2)}) %collective-permute-start.1) | collective-permute-done | bytes 1048608 | tf_op jit(solution)/shard_map/ppermute | solution.py:325
  212.8 20.0 %fusion.1 = (bf16[1024,2816]{1,0:T(8,128)(2,1)}, f32[1024,2816]{1,0:T(8,128)}) fusion(bf16[1024,2048]{1,0:T(8,128)(2,1)} %bitcast.38, bf16[2816,2048]{1,0:T(8,128)(2,1)} %all-gather.3.cloned.1.call-done.refs_4_), kind=kOutput, calls=%fused_computation.10 | convolution fusion | flops 11814043648 | bytes 33030144 | tf_op jit(solution)/shard_map/dot_general | solution.py:329
  232.8 5.2 fusion.refs_0_
  238.1 1.6 copy-done
  239.6 10.8 %convolution_convert_fusion = bf16[2048,1408]{1,0:T(8,128)(2,1)} fusion(bf16[1024,2048]{1,0:T(8,128)(2,1)} %constant_dynamic-update-slice_fusion.refs_2_, bf16[1024,1408]{1,0:T(8,128)(2,1)S(1)} %fusion.refs_0_), kind=kOutput, calls=%fused_computation | convolution fusion | flops 5908463616 | bytes 12845056 | tf_op jit(solution)/shard_map/dot_general | solution.py:329
  250.7 64.0 %norm_back.1 = (f32[256,2048]{1,0:T(8,128)}, f32[1,2048]{1,0:T(1,128)}, bf16[256,2048]{1,0:T(8,128)(2,1)}, bf16[2816,2048]{1,0:T(8,128)(2,1)}, bf16[4,256,2048]{...) custom-call(bf16[1024,1408]{1,0:T(8,128)(2,1)} %copy-done, ...), custom_call_target="tpu_custom_call" | custom-call | tf_op jit(solution)/shard_map/norm_back/pallas_call | solution.py:1402
  315.0 37.2 %share_dy.1 = (bf16[4,256,2048]{2,1,0:T(8,128)(2,1)}, f32[256,2048]{1,0:T(8,128)}, bf16[2,128,2048]{2,1,0:T(8,128)(2,1)}) custom-call(bf16[256,2048]{1,0:T(8,128)(2,1)} %get-tuple-element.71.refs_0_, bf16[4,256,2048]{2,1,0:T(8,128)(2,1)} %get-tuple-element.72.refs_1_, bf16[2,128,2048]{2,1,0:T(8,128)(2,1)} %get-tuple-element.73.refs_2_, ...), custom_call_target="tpu_custom_call" | custom-call | tf_op jit(solution)/shard_map/share_dy/pallas_call | solution.py:1477
  352.3 41.2 %attend_back.1 = (bf16[1024,640]{1,0:T(8,128)(2,1)}, bf16[4,160,1024]{2,1,0:T(8,128)(2,1)}, bf16[2048,512]{1,0:T(8,128)(2,1)}, bf16[2,128,2048]{2,1,0:T(8,128)(2,1)}, bf16[4,256,1408]{2,1,0:T(8,128)(2,1)}) custom-call(bf16[8,1024,64]{2,1,0:T(8,128)(2,1)} %get-tuple-element.57.refs_0_, bf16[1024,64]{1,0:T(8,128)(2,1)} %get-tuple-element.58.refs_1_, ...), custom_call_target="tpu_custom_call" | custom-call | tf_op jit(solution)/shard_map/attend_back/pallas_call | solution.py:993
  393.8 56.2 %leave.1 = (f32[256,2048]{1,0:T(8,128)}, f32[2,2048]{1,0:T(2,128)}, bf16[640,2048]{1,0:T(8,128)(2,1)}) custom-call(bf16[1024,640]{1,0:T(8,128)(2,1)} %get-tuple-element.84.refs_0_, bf16[640,2048]{1,0:T(8,128)(2,1)} %get-tuple-element.55.weight_ref.refs_1_, f32[256,2048]{1,0:T(8,128)} %bitcast.30, f32[256,128]{1,0:T(8,128)} %get-tuple-element.85.refs_3_, ...), custom_call_target="tpu_custom_call" | custom-call | tf_op jit(solution)/shard_map/leave/pallas_call | solution.py:1113
  450.0 1.1 collective-permute-start.10
  451.1 1.1 collective-permute-start.9
  452.1 30.2 %collective-permute-done.10.below_ref = bf16[352,2048]{1,0:T(8,128)(2,1)S(1)} collective-permute-done((bf16[352,2048]{1,0:T(8,128)(2,1)}, bf16[352,2048]{1,0:T(8,128)(2,1)S(1)}, u32[]{:S(2)}, u32[]{:S(2)}) %collective-permute-start.10) | collective-permute-done | bytes 1441824 | tf_op jit(solution)/shard_map/ppermute | solution.py:325
  484.9 1.2 collective-permute-start.11
  486.1 1.7 collective-permute-start.5
  489.6 18.3 %collective-permute-done.5.refs_4_ = bf16[256,512]{1,0:T(8,128)(2,1)} collective-permute-done((bf16[256,512]{1,0:T(8,128)(2,1)}, bf16[256,512]{1,0:T(8,128)(2,1)}, u32[]{:S(2)}, u32[]{:S(2)}) %collective-permute-start.5) | collective-permute-done | bytes 262176 | tf_op jit(solution)/shard_map/ppermute | solution.py:325
  507.9 3.7 collective-permute-done.4.refs_3_
  511.6 1.8 collective-permute-start.8
  513.4 1.5 collective-permute-start.7
  515.1 5.4 join_pieces.5
  520.5 2.7 join_pieces.4
  523.2 2.3 collective-permute-done.7.refs_3_
  527.0 3.0 join_pieces.3
  530.0 5.4 last_sums.1
  535.5 7.2 %join_rows.1 = f32[1408,2048]{1,0:T(8,128)} custom-call(s32[1]{0:T(128)} %bitcast.index_ref.refs_0_, bf16[352,2048]{1,0:T(8,128)(2,1)} %reduce-scatter.7.cloned.1.call-done.own_ref, bf16[352,2048]{1,0:T(8,128)(2,1)} %copy-done.3, bf16[352,2048]{1,0:T(8,128)(2,1)} %copy-done.2, bf16[176,2048]{1,0:T(8,128)(2,1)} %collective-permute-done.11.top_ref, ...), custom_call_target="tpu_custom_call" | custom-call | tf_op jit(solution)/shard_map/join_rows/pallas_call | solution.py:1165
  (54 shorter events, 13.0 us)
Async XLA Ops:
  7.2 205.7 %all-gather.3.cloned.1.call-start = ((), (), s32[]{:S(2)}) async-start(), calls=%async_computation.4 | async-start | bytes 12976128 | tf_op jit(solution)/shard_map/all_gather | solution.py:1516
  62.8 187.9 %all-gather.5.cloned.1.call-start = ((), (), s32[]{:S(2)}) async-start(), calls=%async_computation.5 | async-start | bytes 6488064 | tf_op jit(solution)/shard_map/all_gather | solution.py:1526
  72.0 90.0 %copy-start.1 = (f32[1,256,2048]{2,1,0:T(8,128)S(1)}, f32[1,256,2048]{2,1,0:T(8,128)}, u32[]{:S(2)}) copy-start(f32[1,256,2048]{2,1,0:T(8,128)} %param.16) | copy-start | bytes 6291460
  162.2 190.1 %reduce-scatter.5.cloned.1.call-start = ((), (), s32[]{:S(2)}) async-start(), calls=%async_computation.6 | async-start | bytes 6488064 | tf_op jit(solution)/shard_map/reduce_scatter | solution.py:1533
  162.8 26.1 %collective-permute-start = (bf16[256,2048]{1,0:T(8,128)(2,1)S(1)}, bf16[256,2048]{1,0:T(8,128)(2,1)S(1)}, u32[]{:S(2)}, u32[]{:S(2)}) collective-permute-start(bf16[256,2048]{1,0:T(8,128)(2,1)S(1)} %bitcast_convert_fusion), channel_id=1, source_target_pairs={{0,1},{1,0},{2,3},{3,2},{4,5},{5,4},{6,7},{7,6},{8,9},{9,8},{10,11... | collective-permute-start | bytes 3145736 | tf_op jit(solution)/shard_map/ppermute | solution.py:325
  164.6 46.1 %collective-permute-start.1 = (bf16[256,2048]{1,0:T(8,128)(2,1)S(1)}, bf16[256,2048]{1,0:T(8,128)(2,1)S(1)}, u32[]{:S(2)}, u32[]{:S(2)}) collective-permute-start(bf16[256,2048]{1,0:T(8,128)(2,1)S(1)} %bitcast_convert_fusion), channel_id=1, source_target_pairs={{0,2},{1,3},{2,0},{3,1},{4,6},{5,7},{6,4},{7,5},{8,10},{9,11},{10,... | collective-permute-start | bytes 3145736 | tf_op jit(solution)/shard_map/ppermute | solution.py:325
  164.9 46.9 %collective-permute-start.2 = (bf16[256,2048]{1,0:T(8,128)(2,1)S(1)}, bf16[256,2048]{1,0:T(8,128)(2,1)S(1)}, u32[]{:S(2)}, u32[]{:S(2)}) collective-permute-start(bf16[256,2048]{1,0:T(8,128)(2,1)S(1)} %bitcast_convert_fusion), channel_id=1, source_target_pairs={{0,3},{1,2},{2,1},{3,0},{4,7},{5,6},{6,5},{7,4},{8,11},{9,10},{10,... | collective-permute-start | bytes 3145736 | tf_op jit(solution)/shard_map/ppermute | solution.py:325
  238.1 1.6 copy-start
  250.5 199.5 %reduce-scatter.7.cloned.1.call-start = ((), (), s32[]{:S(2)}) async-start(), calls=%async_computation.7 | async-start | bytes 12976128 | tf_op jit(solution)/shard_map/reduce_scatter | solution.py:1533
  314.7 171.3 %reduce-scatter.11.cloned.1.call-start = ((), (), s32[]{:S(2)}) async-start(), calls=%async_computation.9 | async-start | bytes 2359296 | tf_op jit(solution)/shard_map/reduce_scatter | solution.py:1533
  393.5 118.1 %reduce-scatter.9.cloned.1.call-start = ((), (), s32[]{:S(2)}) async-start(), calls=%async_computation.8 | async-start | bytes 2949120 | tf_op jit(solution)/shard_map/reduce_scatter | solution.py:1533
  450.0 32.3 %collective-permute-start.10 = (bf16[352,2048]{1,0:T(8,128)(2,1)}, bf16[352,2048]{1,0:T(8,128)(2,1)S(1)}, u32[]{:S(2)}, u32[]{:S(2)}) collective-permute-start(bf16[352,2048]{1,0:T(8,128)(2,1)} %reduce-scatter.7.cloned.1.call-done.own_ref), channel_id=1, source_target_pairs={{0,2},{1,3},{2,0},{3,1},{4,6},{5,7},{6,4},{7,5},{8,10},{9,11},{10,... | collective-permute-start | bytes 4325384 | tf_op jit(solution)/shard_map/ppermute | solution.py:325
  451.1 32.8 %collective-permute-start.9 = (bf16[352,2048]{1,0:T(8,128)(2,1)}, bf16[352,2048]{1,0:T(8,128)(2,1)S(1)}, u32[]{:S(2)}, u32[]{:S(2)}) collective-permute-start(bf16[352,2048]{1,0:T(8,128)(2,1)} %reduce-scatter.7.cloned.1.call-done.own_ref), channel_id=1, source_target_pairs={{0,1},{1,0},{2,3},{3,2},{4,5},{5,4},{6,7},{7,6},{8,9},{9,8},{10,11... | collective-permute-start | bytes 4325384 | tf_op jit(solution)/shard_map/ppermute | solution.py:325
  482.3 38.2 %copy-start.2 = (bf16[352,2048]{1,0:T(8,128)(2,1)}, bf16[352,2048]{1,0:T(8,128)(2,1)S(1)}, u32[]{:S(2)}) copy-start(bf16[352,2048]{1,0:T(8,128)(2,1)S(1)} %collective-permute-done.10.below_ref) | copy-start | bytes 4325380
  483.3 52.1 %collective-permute-start.12 = (bf16[176,2048]{1,0:T(8,128)(2,1)}, bf16[176,2048]{1,0:T(8,128)(2,1)}, u32[]{:S(2)}, u32[]{:S(2)}) collective-permute-start(bf16[176,2048]{1,0:T(8,128)(2,1)} %slice.37), channel_id=1, source_target_pairs={{0,1},{1,0},{2,3},{3,2},{4,5},{5,4},{6,7},{7,6},{8,9},{9,8},{10,11... | collective-permute-start | bytes 2162696 | tf_op jit(solution)/shard_map/ppermute | solution.py:325
  483.9 36.6 %copy-start.3 = (bf16[352,2048]{1,0:T(8,128)(2,1)}, bf16[352,2048]{1,0:T(8,128)(2,1)S(1)}, u32[]{:S(2)}) copy-start(bf16[352,2048]{1,0:T(8,128)(2,1)S(1)} %collective-permute-done.9.side_ref) | copy-start | bytes 4325380
  484.9 50.6 %collective-permute-start.11 = (bf16[176,2048]{1,0:T(8,128)(2,1)}, bf16[176,2048]{1,0:T(8,128)(2,1)}, u32[]{:S(2)}, u32[]{:S(2)}) collective-permute-start(bf16[176,2048]{1,0:T(8,128)(2,1)} %slice.36), channel_id=1, source_target_pairs={{0,2},{1,3},{2,0},{3,1},{4,6},{5,7},{6,4},{7,5},{8,10},{9,11},{10,... | collective-permute-start | bytes 2162696 | tf_op jit(solution)/shard_map/ppermute | solution.py:325
  486.1 21.8 %collective-permute-start.5 = (bf16[256,512]{1,0:T(8,128)(2,1)}, bf16[256,512]{1,0:T(8,128)(2,1)}, u32[]{:S(2)}, u32[]{:S(2)}) collective-permute-start(bf16[256,512]{1,0:T(8,128)(2,1)} %reduce-scatter.11.cloned.1.call-done.refs_1_), channel_id=1, source_target_pairs={{0,3},{1,2},{2,1},{3,0},{4,7},{5,6},{6,5},{7,4},{8,11},{9,10},{10,... | collective-permute-start | bytes 786440 | tf_op jit(solution)/shard_map/ppermute | solution.py:325
  487.8 23.8 %collective-permute-start.4 = (bf16[256,512]{1,0:T(8,128)(2,1)}, bf16[256,512]{1,0:T(8,128)(2,1)}, u32[]{:S(2)}, u32[]{:S(2)}) collective-permute-start(bf16[256,512]{1,0:T(8,128)(2,1)} %reduce-scatter.11.cloned.1.call-done.refs_1_), channel_id=1, source_target_pairs={{0,2},{1,3},{2,0},{3,1},{4,6},{5,7},{6,4},{7,5},{8,10},{9,11},{10,... | collective-permute-start | bytes 786440 | tf_op jit(solution)/shard_map/ppermute | solution.py:325
  488.6 23.0 %collective-permute-start.3 = (bf16[256,512]{1,0:T(8,128)(2,1)}, bf16[256,512]{1,0:T(8,128)(2,1)}, u32[]{:S(2)}, u32[]{:S(2)}) collective-permute-start(bf16[256,512]{1,0:T(8,128)(2,1)} %reduce-scatter.11.cloned.1.call-done.refs_1_), channel_id=1, source_target_pairs={{0,1},{1,0},{2,3},{3,2},{4,5},{5,4},{6,7},{7,6},{8,9},{9,8},{10,11... | collective-permute-start | bytes 786440 | tf_op jit(solution)/shard_map/ppermute | solution.py:325
  511.6 11.6 %collective-permute-start.8 = (bf16[80,2048]{1,0:T(8,128)(2,1)}, bf16[80,2048]{1,0:T(8,128)(2,1)S(1)}, u32[]{:S(2)}, u32[]{:S(2)}) collective-permute-start(bf16[80,2048]{1,0:T(8,128)(2,1)} %reduce-scatter.9.cloned.1.call-done.refs_1_), channel_id=1, source_target_pairs={{0,3},{1,2},{2,1},{3,0},{4,7},{5,6},{6,5},{7,4},{8,11},{9,10},{10,... | collective-permute-start | bytes 983048 | tf_op jit(solution)/shard_map/ppermute | solution.py:325
  513.4 12.1 %collective-permute-start.7 = (bf16[80,2048]{1,0:T(8,128)(2,1)}, bf16[80,2048]{1,0:T(8,128)(2,1)S(1)}, u32[]{:S(2)}, u32[]{:S(2)}) collective-permute-start(bf16[80,2048]{1,0:T(8,128)(2,1)} %reduce-scatter.9.cloned.1.call-done.refs_1_), channel_id=1, source_target_pairs={{0,2},{1,3},{2,0},{3,1},{4,6},{5,7},{6,4},{7,5},{8,10},{9,11},{10,... | collective-permute-start | bytes 983048 | tf_op jit(solution)/shard_map/ppermute | solution.py:325
  514.9 10.6 %collective-permute-start.6 = (bf16[80,2048]{1,0:T(8,128)(2,1)}, bf16[80,2048]{1,0:T(8,128)(2,1)S(1)}, u32[]{:S(2)}, u32[]{:S(2)}) collective-permute-start(bf16[80,2048]{1,0:T(8,128)(2,1)} %reduce-scatter.9.cloned.1.call-done.refs_1_), channel_id=1, source_target_pairs={{0,1},{1,0},{2,3},{3,2},{4,5},{5,4},{6,7},{7,6},{8,9},{9,8},{10,11... | collective-permute-start | bytes 983048 | tf_op jit(solution)/shard_map/ppermute | solution.py:325
  523.2 2.3 copy-start.4
  525.5 0.7 copy-start.5
  526.2 0.7 copy-start.6
  535.4 7.2 %copy-start.7 = (f32[2,2048]{1,0:T(2,128)S(1)}, f32[2,2048]{1,0:T(2,128)}, u32[]{:S(2)}) copy-start(f32[2,2048]{1,0:T(2,128)} %get-tuple-element.92) | copy-start | bytes 49156
Sparse Core Ops, SparseCore 0:
  62.9 112.4 all-gather.2
  177.0 58.6 all-gather.4
  250.6 63.7 reduce-scatter.4
  316.5 118.0 reduce-scatter.6
  436.8 34.8 reduce-scatter.10
  473.9 36.2 reduce-scatter.8

commit v6 on v5

--- a/solution.py
+++ b/solution.py
@@ -475,9 +475,9 @@
 
 
 def enter_kernel(
-    count, current_ref, gain_ref, spots_ref, shard_ref, out_shard_ref, gate_up_ref, down_ref,
+    count, current_in, gain_ref, positions_ref, shard_ref, out_shard_ref, gate_up_ref, down_ref,
     all_ref, rows_ref, out_ref, table_ref, gate_up_part_ref, down_part_ref, scale_ref,
-    normed_ref, held_ref, part_ref, held_down,
+    current_ref, normed_ref, spots_ref, held_ref, part_ref, held_down,
     send_sems, recv_sems, spot_send, spot_recv, item_up, item_down, item_side, item_recv, local_sem,
 ):
     part, _ = current_ref.shape
@@ -492,6 +492,8 @@
     chip, core = place // 2, place % 2
     sems = (send_sems, recv_sems)
 
+    take_current = pltpu.make_async_copy(current_in, current_ref, local_sem.at[items + 4])
+    take_current.start()
     barrier = pltpu.get_barrier_semaphore()
     for peer in [seq_peer(step) for step in range(1, count)] + [fsdp_peer(place ^ 1)]:
         pl.semaphore_signal(barrier, inc=1, device_id=peer, device_id_type=MESH)
@@ -580,6 +582,7 @@
 
     for item_of, number in kinds:
         lax.fori_loop(0, number, send_own(item_of), 0)
+    take_current.wait()
     current = current_ref[...]
     scale = lax.rsqrt(jnp.mean(current * current, 1, keepdims=True) + EPS)
     scale_ref[...] = jnp.broadcast_to(scale, scale_ref.shape)
@@ -587,6 +590,7 @@
     copies = gather_copies(normed_ref, all_ref, part // 2, sems)
     for copy in copies[:4]:
         copy.start()
+    spots_ref[...] = jnp.broadcast_to(positions_ref[...].astype(jnp.float32), spots_ref.shape)
     held_ref[0] = spots_ref[...]
     spot_copies = [
         remote(spots_ref, held_ref.at[step], (spot_send, spot_recv), step - 1, seq_peer(step))
@@ -664,14 +668,13 @@
         copy.wait_send()
 
 
-def enter(current, gain, spots, shard, out_shard, gate_up, down, count):
+def enter(current, gain, positions, shard, out_shard, gate_up, down, count):
     part, width = current.shape
     length = part * count
     heads = H // count
     pieces = heads + 2
     items = pieces + lax.axis_size("fsdp")
     vmem = pl.BlockSpec(memory_space=pltpu.VMEM)
-    spots = jnp.broadcast_to(spots.astype(jnp.float32)[None], (8, part))
     whole = pl.BlockSpec(memory_space=pl.ANY)
     part_shape = (gate_up.shape[0] // count, width)
     gathered, rows, out_cols, table, gate_up_part, down_part, scale = pl.pallas_call(
@@ -685,10 +688,12 @@
             jax.ShapeDtypeStruct((down.shape[0], down.shape[1] // count), down.dtype),
             jax.ShapeDtypeStruct((part, 128), jnp.float32),
         ),
-        in_specs=[vmem] * 5 + [whole] * 2,
+        in_specs=[whole] + [vmem] * 2 + [whole] * 4,
         out_specs=[whole] + [vmem] * 3 + [whole] + [vmem] * 2,
         scratch_shapes=[
+            pltpu.VMEM((part, width), jnp.float32),
             pltpu.VMEM((part, width), jnp.bfloat16),
+            pltpu.VMEM((8, part), jnp.float32),
             pltpu.VMEM((count, 8, part), jnp.float32),
             pltpu.VMEM(part_shape, gate_up.dtype),
             pltpu.VMEM(down.shape, down.dtype),
@@ -700,11 +705,11 @@
             pltpu.SemaphoreType.DMA((items,)),
             pltpu.SemaphoreType.DMA((items,)),
             pltpu.SemaphoreType.DMA((items,)),
-            pltpu.SemaphoreType.DMA((items + 4,)),
+            pltpu.SemaphoreType.DMA((items + 5,)),
         ],
         compiler_params=pltpu.CompilerParams(collective_id=1, has_side_effects=True, vmem_limit_bytes=LIMIT),
         name="enter",
-    )(current, gain, spots, shard, out_shard, gate_up, down)
+    )(current, gain, positions, shard, out_shard, gate_up, down)
     return gathered.reshape(length, width), rows, out_cols, table, gate_up_part, down_part, scale
 
 
@@ -876,15 +881,18 @@
 
 
 def attend_back_kernel(
-    count, q_ref, k_ref, v_ref, attn_ref, lse_ref, dy_ref, weight_ref, table_ref, pick_ref, passed_ref, shard_ref,
+    count, q_in, k_in, v_in, attn_in, lse_in, dy_ref, weight_in, table_in, pick_ref, passed_ref, shard_ref,
     out_ref, turned_ref, term_ref, far_ref, slot_ref,
+    q_ref, k_ref, v_ref, attn_ref, lse_ref, weight_ref, table_ref,
     do_ref, delta_ref, dq_ref, dk_ref, dv_ref, held_dy, held_pick,
     send_sems, recv_sems, load_sems,
 ):
-    heads, length, _ = q_ref.shape
+    heads, length, _ = q_in.shape
     part = length // count
     wide = jnp.float32
     index = lax.axis_index("seq")
+    load_weight = pltpu.make_async_copy(weight_in, weight_ref, load_sems.at[count + 1])
+    load_weight.start()
     greet([seq_peer(1), seq_peer(2)])
     sems = (send_sems, recv_sems)
     sums = [
@@ -901,9 +909,20 @@
         return pltpu.make_async_copy(dy_ref.at[rows], held_dy.at[rows], load_sems.at[step])
 
     load = pltpu.make_async_copy(pick_ref, held_pick, load_sems.at[count])
-    for here in range(count):
+    sources, targets = (attn_in, q_in, k_in, v_in, lse_in, table_in), (attn_ref, q_ref, k_ref, v_ref, lse_ref, table_ref)
+    loads = [
+        pltpu.make_async_copy(source, target, load_sems.at[count + 2 + number])
+        for number, (source, target) in enumerate(zip(sources, targets))
+    ]
+    load_dy(index).start()
+    for copy in loads:
+        copy.start()
+    for here in range(1, count):
         load_dy(here ^ index).start()
     load.start()
+    load_weight.wait()
+    for copy in loads:
+        copy.wait()
     dk_ref[...] = jnp.zeros_like(dk_ref)
     dv_ref[...] = jnp.zeros_like(dv_ref)
     owner = lax.broadcasted_iota(jnp.int32, (heads, heads * HD), 1) // HD
@@ -999,9 +1018,12 @@
             jax.ShapeDtypeStruct((2, part // 2, width), jnp.bfloat16),
             jax.ShapeDtypeStruct((count,) + shard.shape, shard.dtype),
         ],
-        in_specs=[vmem] * 5 + [whole] + [vmem] * 2 + [whole] * 3,
+        in_specs=[whole] * 11,
         out_specs=[vmem] * 3 + [whole] * 2,
         scratch_shapes=[
+            pltpu.VMEM(value.shape, value.dtype) for value in (queries, keys_in, values_in, attn, lse, weight, table)
+        ]
+        + [
             pltpu.VMEM((heads, part, HD), jnp.bfloat16),
             pltpu.VMEM((heads, part), jnp.float32),
             pltpu.VMEM((heads, part, HD), jnp.bfloat16),
@@ -1009,16 +1031,16 @@
             pltpu.VMEM((length, HD), jnp.float32),
         ]
         + [pltpu.VMEM(dy.shape, dy.dtype), pltpu.VMEM(pick.shape, pick.dtype)]
-        + [pltpu.SemaphoreType.DMA((8,)), pltpu.SemaphoreType.DMA((8,)), pltpu.SemaphoreType.DMA((count + 1,))],
+        + [pltpu.SemaphoreType.DMA((8,)), pltpu.SemaphoreType.DMA((8,)), pltpu.SemaphoreType.DMA((count + 8,))],
         compiler_params=pltpu.CompilerParams(collective_id=4, has_side_effects=True, vmem_limit_bytes=LIMIT),
         name="attend_back",
     )(queries, keys_in, values_in, attn, lse, dy, weight, table, pick, passed, shard)
 
 
 def leave_kernel(
-    count, grads_ref, weight_ref, first_in, scale_ref, gain_ref, other_ref, turned_ref, normed_in,
+    count, grads_in, weight_in, first_in, scale_ref, gain_ref, other_ref, turned_ref, normed_in,
     own_ref, total_ref, term_ref,
-    sent_ref, side_ref, below_ref, far_ref, slot_ref, whole_ref, normed_ref, first_ref,
+    sent_ref, side_ref, below_ref, far_ref, slot_ref, whole_ref, normed_ref, first_ref, grads_ref, weight_ref,
     told_ref, heard_ref, send_sems, recv_sems, swap_send, swap_recv, load_sems, sum_send, sum_recv,
 ):
     part, _ = first_ref.shape
@@ -1044,14 +1066,17 @@
                 (turned_ref.at[index], slot_ref.at[0]),
                 (normed_in, normed_ref),
                 (first_in, first_ref),
+                (grads_in, grads_ref),
+                (weight_in, weight_ref),
             )
         )
     ]
-    for load in loads:
-        load.start()
+    for number in (3, 4, 1, 0, 2):
+        loads[number].start()
     total_ref[0:1] = jnp.zeros_like(other_ref)
     total_ref[1:2] = other_ref[...]
-    loads[1].wait()
+    for number in (3, 4, 1):
+        loads[number].wait()
     sums = sum_copies(sent_ref, side_ref, below_ref, far_ref, half, (send_sems, recv_sems))
 
     def one_part(turn, carry):
@@ -1117,7 +1142,7 @@
             jax.ShapeDtypeStruct((2, width), jnp.float32),
             jax.ShapeDtypeStruct((size * count, width), jnp.bfloat16),
         ),
-        in_specs=[vmem] * 2 + [whole] + [vmem] * 3 + [whole] * 2,
+        in_specs=[whole] * 3 + [vmem] * 3 + [whole] * 2,
         out_specs=[vmem] * 3,
         scratch_shapes=[
             pltpu.VMEM((count, part, width), jnp.bfloat16),
@@ -1128,13 +1153,15 @@
             pltpu.VMEM((count * size, length), jnp.bfloat16),
             pltpu.VMEM(normed.shape, jnp.bfloat16),
             pltpu.VMEM((part, width), jnp.float32),
+            pltpu.VMEM(grads.shape, grads.dtype),
+            pltpu.VMEM(weight.shape, weight.dtype),
             pltpu.VMEM((steps, 2, width), jnp.float32),
             pltpu.VMEM((steps, 2, width), jnp.float32),
             pltpu.SemaphoreType.DMA((6,)),
             pltpu.SemaphoreType.DMA((6,)),
             pltpu.SemaphoreType.DMA((count - 1,)),
             pltpu.SemaphoreType.DMA((count - 1,)),
-            pltpu.SemaphoreType.DMA((3,)),
+            pltpu.SemaphoreType.DMA((5,)),
             pltpu.SemaphoreType.DMA((steps,)),
             pltpu.SemaphoreType.DMA((steps,)),
         ],
@@ -1442,8 +1469,8 @@
 
 
 def share_dy_kernel(
-    dy_ref, down_ref, side_ref, below_ref, middle_ref, all_ref, base_ref, passed_ref,
-    piece_ref, send_sems, recv_sems, load_sems,
+    dy_ref, down_ref, side_in, below_in, middle_in, all_ref, base_ref, passed_ref,
+    piece_ref, side_ref, below_ref, send_sems, recv_sems, load_sems,
 ):
     part = dy_ref.shape[0]
     half = part // 2
@@ -1454,6 +1481,9 @@
         pltpu.make_async_copy(down_ref.at[2].at[top], piece_ref.at[1].at[top], load_sems.at[1]),
         pltpu.make_async_copy(down_ref.at[1].at[bottom], piece_ref.at[1].at[bottom], load_sems.at[2]),
         pltpu.make_async_copy(dy_ref, all_ref.at[0], load_sems.at[3]),
+        pltpu.make_async_copy(side_in, side_ref, load_sems.at[4]),
+        pltpu.make_async_copy(below_in, below_ref, load_sems.at[5]),
+        pltpu.make_async_copy(middle_in, base_ref, load_sems.at[6]),
     ]
     greet([seq_peer(1), seq_peer(2)])
     group = gather_copies(dy_ref, all_ref, half, (send_sems, recv_sems))
@@ -1462,7 +1492,7 @@
         load.start()
     for load in loads:
         load.wait()
-    base_ref[...] = middle_ref[...] + piece_ref[0].astype(wide)
+    base_ref[...] += piece_ref[0].astype(wide)
     base_ref[:half] += side_ref[0].astype(wide)
     base_ref[half:] += below_ref[0].astype(wide)
     passed_ref[0] = (piece_ref[1, :half].astype(wide) + side_ref[1].astype(wide)).astype(jnp.bfloat16)
@@ -1481,13 +1511,15 @@
             jax.ShapeDtypeStruct((part, width), jnp.float32),
             jax.ShapeDtypeStruct((2, part // 2, width), jnp.bfloat16),
         ],
-        in_specs=[vmem, whole, vmem, vmem, vmem],
+        in_specs=[vmem] + [whole] * 4,
         out_specs=[whole, vmem, vmem],
         scratch_shapes=[
             pltpu.VMEM((2, part, width), jnp.bfloat16),
+            pltpu.VMEM((2, part // 2, width), jnp.bfloat16),
+            pltpu.VMEM((2, part // 2, width), jnp.bfloat16),
             pltpu.SemaphoreType.DMA((6,)),
             pltpu.SemaphoreType.DMA((6,)),
-            pltpu.SemaphoreType.DMA((4,)),
+            pltpu.SemaphoreType.DMA((7,)),
         ],
         compiler_params=pltpu.CompilerParams(collective_id=8, has_side_effects=True, vmem_limit_bytes=LIMIT),
         name="share_dy",
@@ -1510,7 +1542,7 @@
     chunk = group // count
     per_head = HD // group
     normed_all, qkv_rows, out_cols, table, gate_up_part, down_part, scale_one = enter(
-        current, gain[:1], positions[0], w_qkv[0], w_out[0], w_gate_up[0], w_down[0], count
+        current, gain[:1], positions, w_qkv[0], w_out[0], w_gate_up[0], w_down[0], count
     )
     gu_rows = w_gate_up.shape[1] // count
     gate_up = lax.all_gather(gate_up_part, "fsdp", axis=0, tiled=True)

time: 558 us -> 556 us (level)
  transfers between devices with their start and end apart: 19 -> 19, of which waited for: 6 -> 9; matrix products, arithmetic and copies ran while one was open for 8% -> 8% of each run, Pallas kernels for 57% -> 57%
where the time goes in v6:
time: 556 us; the launch traced here: 548 us
  Pallas kernels  369 us (66%)
  waiting for transfers between devices  102 us (18%)
  matrix products  30.8 us (6%)
  starting transfers between devices  15.6 us (3%)
  between operations  14.5 us (3%)
  local copies, waits for them, and re-layouts  11.2 us (2%)
    ppermute x13, waiting for transfers between devices, neighbour(): return lax.ppermute(values, 'seq', [(i, i ^ step) for i in range(count)])  98.7 us
    pallas_call x1, Pallas kernels, attend(): pl.pallas_call(lambda *refs: attend_kernel(count, *refs), out_shape=(jax....  90.2 us
    pallas_call x1, Pallas kernels, norm_back(): pl.pallas_call(lambda *refs: norm_back_kernel(count, *refs), out_shape=(j...  64.1 us
    pallas_call x1, Pallas kernels, leave(): pl.pallas_call(lambda *refs: leave_kernel(count, *refs), out_shape=(jax.S...  55 us
    pallas_call x1, Pallas kernels, enter(): pl.pallas_call(lambda *refs: enter_kernel(count, *refs), out_shape=(jax.S...  51.5 us
    pallas_call x1, Pallas kernels, attend_back(): pl.pallas_call(lambda *refs: attend_back_kernel(count, *refs), out_shape=...  39.2 us
    pallas_call x1, Pallas kernels, share_dy(): pl.pallas_call(lambda *refs: share_dy_kernel(*refs), out_shape=[jax.Shape...  36 us
    dot_general x2, matrix products, matmul(): lax.dot_general(left, right, (((left_dim,), (right_dim,)), ((), ())), pre...  30.8 us
  transfers between devices with their start and end apart: 19, of which 9 were waited for; matrix products, arithmetic and copies ran while one was open for 8% of the time, Pallas kernels for 57%

profile of v6, /device:TPU:0, one launch (start us, length us, event | category | flops | bytes accessed | tf_op | source)
XLA Modules:
  0.0 548.1 jit_solution(16801378603205166777)
XLA Ops:
  7.2 1.4 slice_bitcast_fusion
  8.6 51.5 %enter.1 = (bf16[4,256,2048]{2,1,0:T(8,128)(2,1)}, bf16[640,2048]{1,0:T(8,128)(2,1)}, bf16[2048,512]{1,0:T(8,128)(2,1)}, f32[1024,64]{1,0:T(8,128)}, bf16[352,20...) custom-call(f32[256,2048]{1,0:T(8,128)} %bitcast.27, f32[1,2048]{1,0:T(1,128)} %get-tuple-element.102.refs_1_.refs_4_, ...), custom_call_target="tpu_custom_call" | custom-call | tf_op jit(solution)/shard_map/enter/pallas_call | solution.py:680
  60.2 9.1 %project_qkv.1 = (bf16[8,1024,64]{2,1,0:T(8,128)(2,1)}, bf16[1024,64]{1,0:T(8,128)(2,1)}, bf16[1024,64]{1,0:T(8,128)(2,1)}) custom-call(s32[1]{0:T(128)} %bitcast.index_ref.refs_0_, bf16[1024,2048]{1,0:T(8,128)(2,1)} %bitcast.30, bf16[640,2048]{1,0:T(8,128)(2,1)} %get-tuple-element.55.weight_ref.refs_1_, f32[1024,64]{1,0:T(8,128)} %get-tuple-element.56.table_ref.refs_7_), custom_call_target="tpu_custom_call" | custom-call | tf_op jit(solution)/shard_map/project_qkv/pallas_call | solution.py:732
  69.3 90.2 %attend.1 = (bf16[1024,512]{1,0:T(8,128)(2,1)}, f32[8,1024]{1,0:T(8,128)}, f32[256,2048]{1,0:T(8,128)}, f32[256,128]{1,0:T(8,128)}, bf16[4,256,2048]{2,1,0:T(8,128)(2,1)}) custom-call(bf16[8,1024,64]{2,1,0:T(8,128)(2,1)} %get-tuple-element.57.refs_0_, bf16[1024,64]{1,0:T(8,128)(2,1)} %get-tuple-element.58.refs_1_, ...), custom_call_target="tpu_custom_call" | custom-call | tf_op jit(solution)/shard_map/attend/pallas_call | solution.py:826
  160.3 2.0 collective-permute-start
  162.4 1.5 collective-permute-start.2
  163.8 1.0 constant_dynamic-update-slice_fusion.3
  164.9 21.5 %collective-permute-done = bf16[256,2048]{1,0:T(8,128)(2,1)S(1)} collective-permute-done((bf16[256,2048]{1,0:T(8,128)(2,1)S(1)}, bf16[256,2048]{1,0:T(8,128)(2,1)S(1)}, u32[]{:S(2)}, u32[]{:S(2)}) %collective-permute-start) | collective-permute-done | bytes 1048608 | tf_op jit(solution)/shard_map/ppermute | solution.py:325
  186.4 1.1 constant_dynamic-update-slice_fusion.2
  187.5 20.9 %collective-permute-done.1 = bf16[256,2048]{1,0:T(8,128)(2,1)S(1)} collective-permute-done((bf16[256,2048]{1,0:T(8,128)(2,1)S(1)}, bf16[256,2048]{1,0:T(8,128)(2,1)S(1)}, u32[]{:S(2)}, u32[]{:S(2)}) %collective-permute-start.1) | collective-permute-done | bytes 1048608 | tf_op jit(solution)/shard_map/ppermute | solution.py:325
  208.4 1.1 constant_dynamic-update-slice_fusion.1
  210.5 20.0 %fusion.1 = (bf16[1024,2816]{1,0:T(8,128)(2,1)}, f32[1024,2816]{1,0:T(8,128)}) fusion(bf16[1024,2048]{1,0:T(8,128)(2,1)} %bitcast.37, bf16[2816,2048]{1,0:T(8,128)(2,1)} %all-gather.3.cloned.1.call-done.refs_4_), kind=kOutput, calls=%fused_computation.10 | convolution fusion | flops 11814043648 | bytes 33030144 | tf_op jit(solution)/shard_map/dot_general | solution.py:329
  230.5 5.2 fusion.refs_0_
  235.7 1.6 copy-done
  237.3 10.8 %convolution_convert_fusion = bf16[2048,1408]{1,0:T(8,128)(2,1)} fusion(bf16[1024,2048]{1,0:T(8,128)(2,1)} %constant_dynamic-update-slice_fusion.refs_2_, bf16[1024,1408]{1,0:T(8,128)(2,1)S(1)} %fusion.refs_0_), kind=kOutput, calls=%fused_computation | convolution fusion | flops 5908463616 | bytes 12845056 | tf_op jit(solution)/shard_map/dot_general | solution.py:329
  248.4 64.1 %norm_back.1 = (f32[256,2048]{1,0:T(8,128)}, f32[1,2048]{1,0:T(1,128)}, bf16[256,2048]{1,0:T(8,128)(2,1)}, bf16[2816,2048]{1,0:T(8,128)(2,1)}, bf16[4,256,2048]{...) custom-call(bf16[1024,1408]{1,0:T(8,128)(2,1)} %copy-done, ...), custom_call_target="tpu_custom_call" | custom-call | tf_op jit(solution)/shard_map/norm_back/pallas_call | solution.py:1429
  312.8 36.0 %share_dy.1 = (bf16[4,256,2048]{2,1,0:T(8,128)(2,1)}, f32[256,2048]{1,0:T(8,128)}, bf16[2,128,2048]{2,1,0:T(8,128)(2,1)}) custom-call(bf16[256,2048]{1,0:T(8,128)(2,1)} %get-tuple-element.71.refs_0_, bf16[4,256,2048]{2,1,0:T(8,128)(2,1)} %get-tuple-element.72.refs_1_, bf16[2,128,2048]{2,1,0:T(8,128)(2,1)} %get-tuple-element.73.refs_2_, ...), custom_call_target="tpu_custom_call" | custom-call | tf_op jit(solution)/shard_map/share_dy/pallas_call | solution.py:1507
  348.8 39.2 %attend_back.1 = (bf16[1024,640]{1,0:T(8,128)(2,1)}, bf16[4,160,1024]{2,1,0:T(8,128)(2,1)}, bf16[2048,512]{1,0:T(8,128)(2,1)}, bf16[2,128,2048]{2,1,0:T(8,128)(2,1)}, bf16[4,256,1408]{2,1,0:T(8,128)(2,1)}) custom-call(bf16[8,1024,64]{2,1,0:T(8,128)(2,1)} %get-tuple-element.57.refs_0_, bf16[1024,64]{1,0:T(8,128)(2,1)} %get-tuple-element.58.refs_1_, ...), custom_call_target="tpu_custom_call" | custom-call | tf_op jit(solution)/shard_map/attend_back/pallas_call | solution.py:1012
  388.4 55.0 %leave.1 = (f32[256,2048]{1,0:T(8,128)}, f32[2,2048]{1,0:T(2,128)}, bf16[640,2048]{1,0:T(8,128)(2,1)}) custom-call(bf16[1024,640]{1,0:T(8,128)(2,1)} %get-tuple-element.84.refs_0_, bf16[640,2048]{1,0:T(8,128)(2,1)} %get-tuple-element.55.weight_ref.refs_1_, f32[256,2048]{1,0:T(8,128)} %bitcast.29, f32[256,128]{1,0:T(8,128)} %get-tuple-element.85.refs_3_, ...), custom_call_target="tpu_custom_call" | custom-call | tf_op jit(solution)/shard_map/leave/pallas_call | solution.py:1138
  445.5 30.1 %collective-permute-done.10.below_ref = bf16[352,2048]{1,0:T(8,128)(2,1)S(1)} collective-permute-done((bf16[352,2048]{1,0:T(8,128)(2,1)}, bf16[352,2048]{1,0:T(8,128)(2,1)S(1)}, u32[]{:S(2)}, u32[]{:S(2)}) %collective-permute-start.10) | collective-permute-done | bytes 1441824 | tf_op jit(solution)/shard_map/ppermute | solution.py:325
  475.6 1.0 slice.37
  479.3 1.8 collective-permute-start.5
  482.8 18.4 %collective-permute-done.5.refs_4_ = bf16[256,512]{1,0:T(8,128)(2,1)} collective-permute-done((bf16[256,512]{1,0:T(8,128)(2,1)}, bf16[256,512]{1,0:T(8,128)(2,1)}, u32[]{:S(2)}, u32[]{:S(2)}) %collective-permute-start.5) | collective-permute-done | bytes 262176 | tf_op jit(solution)/shard_map/ppermute | solution.py:325
  501.2 4.0 collective-permute-done.4.refs_3_
  505.2 2.8 reduce-scatter.9.cloned.1.call-done.refs_1_
  508.0 2.4 collective-permute-start.8
  511.5 5.4 join_pieces.5
  516.9 2.7 join_pieces.4
  519.7 3.5 collective-permute-done.7.refs_3_
  524.7 3.0 join_pieces.3
  527.7 5.4 last_sums.1
  533.2 7.2 %join_rows.1 = f32[1408,2048]{1,0:T(8,128)} custom-call(s32[1]{0:T(128)} %bitcast.index_ref.refs_0_, bf16[352,2048]{1,0:T(8,128)(2,1)} %reduce-scatter.7.cloned.1.call-done.own_ref, bf16[352,2048]{1,0:T(8,128)(2,1)} %copy-done.3, bf16[352,2048]{1,0:T(8,128)(2,1)} %copy-done.2, bf16[176,2048]{1,0:T(8,128)(2,1)} %collective-permute-done.11.top_ref, ...), custom_call_target="tpu_custom_call" | custom-call | tf_op jit(solution)/shard_map/join_rows/pallas_call | solution.py:1192
  (52 shorter events, 12.5 us)
Async XLA Ops:
  7.2 203.3 %all-gather.3.cloned.1.call-start = ((), (), s32[]{:S(2)}) async-start(), calls=%async_computation.4 | async-start | bytes 12976128 | tf_op jit(solution)/shard_map/all_gather | solution.py:1548
  60.1 188.2 %all-gather.5.cloned.1.call-start = ((), (), s32[]{:S(2)}) async-start(), calls=%async_computation.5 | async-start | bytes 6488064 | tf_op jit(solution)/shard_map/all_gather | solution.py:1558
  69.3 90.2 %copy-start.1 = (f32[1,256,2048]{2,1,0:T(8,128)S(1)}, f32[1,256,2048]{2,1,0:T(8,128)}, u32[]{:S(2)}) copy-start(f32[1,256,2048]{2,1,0:T(8,128)} %param.16) | copy-start | bytes 6291460
  159.7 189.1 %reduce-scatter.5.cloned.1.call-start = ((), (), s32[]{:S(2)}) async-start(), calls=%async_computation.6 | async-start | bytes 6488064 | tf_op jit(solution)/shard_map/reduce_scatter | solution.py:1565
  160.3 26.1 %collective-permute-start = (bf16[256,2048]{1,0:T(8,128)(2,1)S(1)}, bf16[256,2048]{1,0:T(8,128)(2,1)S(1)}, u32[]{:S(2)}, u32[]{:S(2)}) collective-permute-start(bf16[256,2048]{1,0:T(8,128)(2,1)S(1)} %bitcast_convert_fusion), channel_id=1, source_target_pairs={{0,1},{1,0},{2,3},{3,2},{4,5},{5,4},{6,7},{7,6},{8,9},{9,8},{10,11... | collective-permute-start | bytes 3145736 | tf_op jit(solution)/shard_map/ppermute | solution.py:325
  162.3 46.1 %collective-permute-start.1 = (bf16[256,2048]{1,0:T(8,128)(2,1)S(1)}, bf16[256,2048]{1,0:T(8,128)(2,1)S(1)}, u32[]{:S(2)}, u32[]{:S(2)}) collective-permute-start(bf16[256,2048]{1,0:T(8,128)(2,1)S(1)} %bitcast_convert_fusion), channel_id=1, source_target_pairs={{0,2},{1,3},{2,0},{3,1},{4,6},{5,7},{6,4},{7,5},{8,10},{9,11},{10,... | collective-permute-start | bytes 3145736 | tf_op jit(solution)/shard_map/ppermute | solution.py:325
  162.4 47.1 %collective-permute-start.2 = (bf16[256,2048]{1,0:T(8,128)(2,1)S(1)}, bf16[256,2048]{1,0:T(8,128)(2,1)S(1)}, u32[]{:S(2)}, u32[]{:S(2)}) collective-permute-start(bf16[256,2048]{1,0:T(8,128)(2,1)S(1)} %bitcast_convert_fusion), channel_id=1, source_target_pairs={{0,3},{1,2},{2,1},{3,0},{4,7},{5,6},{6,5},{7,4},{8,11},{9,10},{10,... | collective-permute-start | bytes 3145736 | tf_op jit(solution)/shard_map/ppermute | solution.py:325
  235.7 1.6 copy-start
  248.1 195.3 %reduce-scatter.7.cloned.1.call-start = ((), (), s32[]{:S(2)}) async-start(), calls=%async_computation.7 | async-start | bytes 12976128 | tf_op jit(solution)/shard_map/reduce_scatter | solution.py:1565
  312.5 166.8 %reduce-scatter.11.cloned.1.call-start = ((), (), s32[]{:S(2)}) async-start(), calls=%async_computation.9 | async-start | bytes 2359296 | tf_op jit(solution)/shard_map/reduce_scatter | solution.py:1565
  388.1 119.9 %reduce-scatter.9.cloned.1.call-start = ((), (), s32[]{:S(2)}) async-start(), calls=%async_computation.8 | async-start | bytes 2949120 | tf_op jit(solution)/shard_map/reduce_scatter | solution.py:1565
  443.5 32.1 %collective-permute-start.10 = (bf16[352,2048]{1,0:T(8,128)(2,1)}, bf16[352,2048]{1,0:T(8,128)(2,1)S(1)}, u32[]{:S(2)}, u32[]{:S(2)}) collective-permute-start(bf16[352,2048]{1,0:T(8,128)(2,1)} %reduce-scatter.7.cloned.1.call-done.own_ref), channel_id=1, source_target_pairs={{0,2},{1,3},{2,0},{3,1},{4,6},{5,7},{6,4},{7,5},{8,10},{9,11},{10,... | collective-permute-start | bytes 4325384 | tf_op jit(solution)/shard_map/ppermute | solution.py:325
  444.5 33.1 %collective-permute-start.9 = (bf16[352,2048]{1,0:T(8,128)(2,1)}, bf16[352,2048]{1,0:T(8,128)(2,1)S(1)}, u32[]{:S(2)}, u32[]{:S(2)}) collective-permute-start(bf16[352,2048]{1,0:T(8,128)(2,1)} %reduce-scatter.7.cloned.1.call-done.own_ref), channel_id=1, source_target_pairs={{0,1},{1,0},{2,3},{3,2},{4,5},{5,4},{6,7},{7,6},{8,9},{9,8},{10,11... | collective-permute-start | bytes 4325384 | tf_op jit(solution)/shard_map/ppermute | solution.py:325
  475.6 41.3 %copy-start.2 = (bf16[352,2048]{1,0:T(8,128)(2,1)}, bf16[352,2048]{1,0:T(8,128)(2,1)S(1)}, u32[]{:S(2)}) copy-start(bf16[352,2048]{1,0:T(8,128)(2,1)S(1)} %collective-permute-done.10.below_ref) | copy-start | bytes 4325380
  476.6 56.5 %collective-permute-start.12 = (bf16[176,2048]{1,0:T(8,128)(2,1)}, bf16[176,2048]{1,0:T(8,128)(2,1)}, u32[]{:S(2)}, u32[]{:S(2)}) collective-permute-start(bf16[176,2048]{1,0:T(8,128)(2,1)} %slice.37), channel_id=1, source_target_pairs={{0,1},{1,0},{2,3},{3,2},{4,5},{5,4},{6,7},{7,6},{8,9},{9,8},{10,11... | collective-permute-start | bytes 2162696 | tf_op jit(solution)/shard_map/ppermute | solution.py:325
  477.5 39.4 %copy-start.3 = (bf16[352,2048]{1,0:T(8,128)(2,1)}, bf16[352,2048]{1,0:T(8,128)(2,1)S(1)}, u32[]{:S(2)}) copy-start(bf16[352,2048]{1,0:T(8,128)(2,1)S(1)} %collective-permute-done.9.side_ref) | copy-start | bytes 4325380
  478.5 54.6 %collective-permute-start.11 = (bf16[176,2048]{1,0:T(8,128)(2,1)}, bf16[176,2048]{1,0:T(8,128)(2,1)}, u32[]{:S(2)}, u32[]{:S(2)}) collective-permute-start(bf16[176,2048]{1,0:T(8,128)(2,1)} %slice.36), channel_id=1, source_target_pairs={{0,2},{1,3},{2,0},{3,1},{4,6},{5,7},{6,4},{7,5},{8,10},{9,11},{10,... | collective-permute-start | bytes 2162696 | tf_op jit(solution)/shard_map/ppermute | solution.py:325
  479.3 21.9 %collective-permute-start.5 = (bf16[256,512]{1,0:T(8,128)(2,1)}, bf16[256,512]{1,0:T(8,128)(2,1)}, u32[]{:S(2)}, u32[]{:S(2)}) collective-permute-start(bf16[256,512]{1,0:T(8,128)(2,1)} %reduce-scatter.11.cloned.1.call-done.refs_1_), channel_id=1, source_target_pairs={{0,3},{1,2},{2,1},{3,0},{4,7},{5,6},{6,5},{7,4},{8,11},{9,10},{10,... | collective-permute-start | bytes 786440 | tf_op jit(solution)/shard_map/ppermute | solution.py:325
  481.1 24.1 %collective-permute-start.4 = (bf16[256,512]{1,0:T(8,128)(2,1)}, bf16[256,512]{1,0:T(8,128)(2,1)}, u32[]{:S(2)}, u32[]{:S(2)}) collective-permute-start(bf16[256,512]{1,0:T(8,128)(2,1)} %reduce-scatter.11.cloned.1.call-done.refs_1_), channel_id=1, source_target_pairs={{0,2},{1,3},{2,0},{3,1},{4,6},{5,7},{6,4},{7,5},{8,10},{9,11},{10,... | collective-permute-start | bytes 786440 | tf_op jit(solution)/shard_map/ppermute | solution.py:325
  481.9 23.3 %collective-permute-start.3 = (bf16[256,512]{1,0:T(8,128)(2,1)}, bf16[256,512]{1,0:T(8,128)(2,1)}, u32[]{:S(2)}, u32[]{:S(2)}) collective-permute-start(bf16[256,512]{1,0:T(8,128)(2,1)} %reduce-scatter.11.cloned.1.call-done.refs_1_), channel_id=1, source_target_pairs={{0,1},{1,0},{2,3},{3,2},{4,5},{5,4},{6,7},{7,6},{8,9},{9,8},{10,11... | collective-permute-start | bytes 786440 | tf_op jit(solution)/shard_map/ppermute | solution.py:325
  508.0 11.7 %collective-permute-start.8 = (bf16[80,2048]{1,0:T(8,128)(2,1)}, bf16[80,2048]{1,0:T(8,128)(2,1)S(1)}, u32[]{:S(2)}, u32[]{:S(2)}) collective-permute-start(bf16[80,2048]{1,0:T(8,128)(2,1)} %reduce-scatter.9.cloned.1.call-done.refs_1_), channel_id=1, source_target_pairs={{0,3},{1,2},{2,1},{3,0},{4,7},{5,6},{6,5},{7,4},{8,11},{9,10},{10,... | collective-permute-start | bytes 983048 | tf_op jit(solution)/shard_map/ppermute | solution.py:325
  510.4 12.9 %collective-permute-start.7 = (bf16[80,2048]{1,0:T(8,128)(2,1)}, bf16[80,2048]{1,0:T(8,128)(2,1)S(1)}, u32[]{:S(2)}, u32[]{:S(2)}) collective-permute-start(bf16[80,2048]{1,0:T(8,128)(2,1)} %reduce-scatter.9.cloned.1.call-done.refs_1_), channel_id=1, source_target_pairs={{0,2},{1,3},{2,0},{3,1},{4,6},{5,7},{6,4},{7,5},{8,10},{9,11},{10,... | collective-permute-start | bytes 983048 | tf_op jit(solution)/shard_map/ppermute | solution.py:325
  510.9 12.4 %collective-permute-start.6 = (bf16[80,2048]{1,0:T(8,128)(2,1)}, bf16[80,2048]{1,0:T(8,128)(2,1)S(1)}, u32[]{:S(2)}, u32[]{:S(2)}) collective-permute-start(bf16[80,2048]{1,0:T(8,128)(2,1)} %reduce-scatter.9.cloned.1.call-done.refs_1_), channel_id=1, source_target_pairs={{0,1},{1,0},{2,3},{3,2},{4,5},{5,4},{6,7},{7,6},{8,9},{9,8},{10,11... | collective-permute-start | bytes 983048 | tf_op jit(solution)/shard_map/ppermute | solution.py:325
  519.7 3.6 copy-start.4
  523.2 0.7 copy-start.5
  523.9 0.7 copy-start.6
  533.1 7.2 %copy-start.7 = (f32[2,2048]{1,0:T(2,128)S(1)}, f32[2,2048]{1,0:T(2,128)}, u32[]{:S(2)}) copy-start(f32[2,2048]{1,0:T(2,128)} %get-tuple-element.92) | copy-start | bytes 49156
Sparse Core Ops, SparseCore 0:
  60.3 112.7 all-gather.2
  174.7 58.6 all-gather.4
  248.2 63.8 reduce-scatter.4
  314.3 118.3 reduce-scatter.6
  434.8 34.5 reduce-scatter.10
  471.6 36.3 reduce-scatter.8

commit v7 on v6

--- a/solution.py
+++ b/solution.py
@@ -1262,6 +1262,241 @@
     )(base, passed, flowing, piece)
 
 
+def greet_chain(count):
+    place = lax.axis_index("fsdp")
+    chips = lax.axis_size("fsdp") // 2
+    chip = place // 2
+    barrier = pltpu.get_barrier_semaphore()
+    for peer in [seq_peer(step) for step in range(1, count)] + [fsdp_peer(place ^ 1)]:
+        pl.semaphore_signal(barrier, inc=1, device_id=peer, device_id_type=MESH)
+
+    @pl.when(chip > 0)
+    def _():
+        pl.semaphore_signal(barrier, inc=1, device_id=fsdp_peer(place - 2), device_id_type=MESH)
+
+    @pl.when(chip < chips - 1)
+    def _():
+        pl.semaphore_signal(barrier, inc=1, device_id=fsdp_peer(place + 2), device_id_type=MESH)
+
+    greetings = count + (chip > 0).astype(jnp.int32) + (chip < chips - 1).astype(jnp.int32)
+    pl.semaphore_wait(barrier, greetings)
+
+
+def weight_chain(item_of, number, sems):
+    item_up, item_down, item_side, item_recv, local_sem = sems
+    place = lax.axis_index("fsdp")
+    chips = lax.axis_size("fsdp") // 2
+    chip, core = place // 2, place % 2
+
+    def item_copy(source, target, slot, sem, peer):
+        return pltpu.make_async_remote_copy(
+            src_ref=source,
+            dst_ref=target,
+            send_sem=sem.at[slot],
+            recv_sem=item_recv.at[slot],
+            device_id=fsdp_peer(peer),
+            device_id_type=MESH,
+        )
+
+    def pass_on(source, target, slot, owner_chip, act):
+        @pl.when((chip >= owner_chip) & (chip < chips - 1))
+        def _():
+            act(item_copy(source, target, slot, item_up, place + 2))
+
+        @pl.when((chip <= owner_chip) & (chip > 0))
+        def _():
+            act(item_copy(source, target, slot, item_down, place - 2))
+
+        act(item_copy(source, target, slot, item_side, place ^ 1))
+
+    def send_own():
+        def body(item, carry):
+            owner, source, target, slot = item_of(item)
+
+            @pl.when(place == owner)
+            def _():
+                pass_on(source, target, slot, owner // 2, lambda copy: copy.start())
+                pltpu.make_async_copy(source, target, local_sem.at[slot]).start()
+
+            return carry
+
+        lax.fori_loop(0, number, body, 0)
+
+    def pass_far(distance):
+        def body(item, carry):
+            owner, _, target, slot = item_of(item)
+            owner_chip = owner // 2
+            apart = jnp.where(chip > owner_chip, chip - owner_chip, owner_chip - chip)
+
+            @pl.when((apart == distance) & (core == owner % 2))
+            def _():
+                item_copy(target, target, slot, item_side, place ^ 1).wait_recv()
+                pass_on(target, target, slot, owner_chip, lambda copy: copy.start())
+
+            return carry
+
+        lax.fori_loop(0, number, body, 0)
+
+    def finish():
+        def body(item, carry):
+            owner, source, target, slot = item_of(item)
+
+            @pl.when(core != owner % 2)
+            def _():
+                item_copy(target, target, slot, item_side, place ^ 1).wait_recv()
+
+            @pl.when(place == owner)
+            def _():
+                pltpu.make_async_copy(source, target, local_sem.at[slot]).wait()
+
+            @pl.when(core == owner % 2)
+            def _():
+                pass_on(target, target, slot, owner // 2, lambda copy: copy.wait_send())
+
+            return carry
+
+        lax.fori_loop(0, number, body, 0)
+
+    return send_own, pass_far, finish
+
+
+def feed_kernel(
+    count, normed_in, weight_in, dm_in, down_part_ref,
+    gates_out, act_out, dm_out, term_out, down_ref,
+    normed_ref, weight_ref, gates_ref, act_ref, dm_ref, term_ref,
+    send_sems, recv_sems, load_sems, item_up, item_down, item_side, item_recv, local_sem,
+    gates_sems, act_sems, dm_sem, term_sems,
+):
+    part, width = dm_in.shape
+    units = act_ref.shape[1]
+    chips = lax.axis_size("fsdp") // 2
+    narrow = jnp.bfloat16
+    load_weight = pltpu.make_async_copy(weight_in, weight_ref, load_sems.at[0])
+    load_normed = pltpu.make_async_copy(normed_in, normed_ref, load_sems.at[1])
+    load_weight.start()
+    load_normed.start()
+    greet_chain(count)
+    down_rows = down_part_ref.shape[0]
+
+    def down_item(item):
+        target = down_ref.at[pl.ds(pl.multiple_of(item * down_rows, down_rows), down_rows)]
+        return item, down_part_ref, target, item
+
+    send_own, pass_far, finish = weight_chain(
+        down_item, 2 * chips, (item_up, item_down, item_side, item_recv, local_sem)
+    )
+    send_own()
+    group = gather_copies(dm_in, dm_ref, part // 2, (send_sems, recv_sems))
+    share_start([group])
+    dm_ref[0] = dm_in[...]
+    load_normed.wait()
+    load_weight.wait()
+
+    def store_gates(step):
+        rows = pl.ds(pl.multiple_of(step * part, part), part)
+        return pltpu.make_async_copy(gates_ref.at[step % 2], gates_out.at[rows], gates_sems.at[step % 2])
+
+    def store_act(step):
+        rows = pl.ds(pl.multiple_of(step * part, part), part)
+        return pltpu.make_async_copy(act_ref.at[rows], act_out.at[rows], act_sems.at[step])
+
+    def one_part(step, carry):
+        rows = pl.ds(pl.multiple_of(step * part, part), part)
+        both = matmul(normed_ref[rows, :], weight_ref[...], 1, 1)
+
+        @pl.when(step >= 2)
+        def _():
+            store_gates(step - 2).wait()
+
+        gates_ref[step % 2] = both.astype(narrow)
+        gate = both[:, :units]
+        act_ref[rows, :] = (gate * jax.nn.sigmoid(gate) * both[:, units:]).astype(narrow)
+        store_gates(step).start()
+        store_act(step).start()
+
+        @pl.when(step == count - 2)
+        def _():
+            share_on(group)
+            pass_far(1)
+
+        return carry
+
+    lax.fori_loop(0, count, one_part, 0)
+    pass_far(2)
+    share_end([group])
+    keep_dm = pltpu.make_async_copy(dm_ref, dm_out, dm_sem)
+    keep_dm.start()
+    tile = 2 * 128
+    tiles = width // tile
+
+    def store_term(number):
+        rows = pl.ds(pl.multiple_of(number * tile, tile), tile)
+        return pltpu.make_async_copy(term_ref.at[number % 2], term_out.at[rows], term_sems.at[number % 2])
+
+    def one_tile(number, carry):
+        @pl.when(number >= 2)
+        def _():
+            store_term(number - 2).wait()
+
+        columns = pl.ds(pl.multiple_of(number * tile, tile), tile)
+        upstream = dm_ref[:, :, columns].reshape(part * count, tile)
+        term_ref[number % 2] = matmul(upstream, act_ref[...], 0, 0).astype(narrow)
+        store_term(number).start()
+        return carry
+
+    lax.fori_loop(0, tiles, one_tile, 0)
+    for distance in range(3, chips):
+        pass_far(distance)
+    for step in range(count - 2, count):
+        store_gates(step).wait()
+    for step in range(count):
+        store_act(step).wait()
+    keep_dm.wait()
+    for number in range(tiles - 2, tiles):
+        store_term(number).wait()
+    finish()
+
+
+def feed(normed, weight, dm, down_part, count):
+    part, width = dm.shape
+    length, units = part * count, down_part.shape[1]
+    items = lax.axis_size("fsdp")
+    vmem, whole = pl.BlockSpec(memory_space=pltpu.VMEM), pl.BlockSpec(memory_space=pl.ANY)
+    gates, act, dm_all, term, down_cols = pl.pallas_call(
+        lambda *refs: feed_kernel(count, *refs),
+        out_shape=[
+            jax.ShapeDtypeStruct((length, 2 * units), jnp.bfloat16),
+            jax.ShapeDtypeStruct((length, units), jnp.bfloat16),
+            jax.ShapeDtypeStruct((count, part, width), jnp.bfloat16),
+            jax.ShapeDtypeStruct((width, units), jnp.bfloat16),
+            jax.ShapeDtypeStruct((items * down_part.shape[0], units), jnp.bfloat16),
+        ],
+        in_specs=[whole] * 2 + [vmem] + [whole],
+        out_specs=[whole] * 5,
+        scratch_shapes=[
+            pltpu.VMEM(normed.shape, normed.dtype),
+            pltpu.VMEM(weight.shape, weight.dtype),
+            pltpu.VMEM((2, part, 2 * units), jnp.bfloat16),
+            pltpu.VMEM((length, units), jnp.bfloat16),
+            pltpu.VMEM((count, part, width), jnp.bfloat16),
+            pltpu.VMEM((2, 2 * 128, units), jnp.bfloat16),
+            pltpu.SemaphoreType.DMA((6,)),
+            pltpu.SemaphoreType.DMA((6,)),
+            pltpu.SemaphoreType.DMA((2,)),
+        ]
+        + [pltpu.SemaphoreType.DMA((items,))] * 5
+        + [
+            pltpu.SemaphoreType.DMA((2,)),
+            pltpu.SemaphoreType.DMA((count,)),
+            pltpu.SemaphoreType.DMA,
+            pltpu.SemaphoreType.DMA((2,)),
+        ],
+        compiler_params=pltpu.CompilerParams(collective_id=9, has_side_effects=True, vmem_limit_bytes=LIMIT),
+        name="feed",
+    )(normed, weight, dm, down_part)
+    return gates, act, dm_all.reshape(length, width), term, down_cols
+
+
 def norm_back_kernel(
     count, act_in, down_in, dm_in, gates_in, weight_in, flowing_in, middle_in, inputs_in, scale_ref, gain_ref,
     own_ref, gain_out_ref, dy_ref, term_ref, product_ref, from_side_ref, from_below_ref,
@@ -1546,7 +1781,6 @@
     )
     gu_rows = w_gate_up.shape[1] // count
     gate_up = lax.all_gather(gate_up_part, "fsdp", axis=0, tiled=True)
-    units = FF // count
     down_rows = w_down.shape[1]
 
     queries, keys_in, values_in = project_qkv(place, normed_all, qkv_rows, table, count)
@@ -1554,18 +1788,13 @@
         queries, keys_in, values_in, out_cols, current, gain[1:], count
     )
     flowing = cotangent[0]
-    normed_two_all, dm_sent, down_part = after((normed_two_all, flowing.astype(jnp.bfloat16), down_part))
-    down_cols = lax.all_gather(down_part, "fsdp", axis=0, tiled=True)
-    dm_all = jnp.concatenate([dm_sent] + [neighbour(dm_sent, step) for step in range(1, count)], 0)
-    both = matmul(normed_two_all, gate_up, 1, 1)
-    gates = both.astype(jnp.bfloat16)
-    activated = (jax.nn.silu(both[:, :units]) * both[:, units:]).astype(jnp.bfloat16)
+    gates, activated, dm_all, term_down, down_cols = feed(
+        normed_two_all, gate_up, flowing.astype(jnp.bfloat16), down_part, count
+    )
 
     def owned(grad):
         return lax.psum_scatter(grad.astype(jnp.bfloat16), "fsdp", scatter_dimension=0, tiled=True)
 
-    term_down = matmul(dm_all, activated, 0, 0).astype(jnp.bfloat16)
-    dm_all, activated, term_down = after((dm_all, activated, term_down))
     grad_down = owned(term_down)
     dmiddle, gain_two, dy, term_gate_up, down_sent, from_side, from_below = norm_back(
         activated, down_cols, dm_all, gates, gate_up, flowing, middle, normed_two_all, scale_two, gain[1:], count

time: 556 us -> 541 us (0.973)
  Pallas kernels: 369 us -> 433 us
  waiting for transfers between devices: 102 us -> 68.7 us
  matrix products: 30.8 us -> 0 us
  local copies, waits for them, and re-layouts: 11.2 us -> 5.38 us
    pallas_call x0 -> x1, Pallas kernels: none -> 56.4 us  [feed(): pl.pallas_call(lambda *refs: feed_kernel(count, *refs), out_shape=[jax.Sh...]
    ppermute x13 -> x10, waiting for transfers between devices: 98.7 us -> 56.2 us  [neighbour(): return lax.ppermute(values, 'seq', [(i, i ^ step) for i in range(count)])]
    dot_general x2 -> x0, matrix products: 30.8 us -> none  [matmul(): lax.dot_general(left, right, (((left_dim,), (right_dim,)), ((), ())), pre...]
    all_gather x1, waiting for transfers between devices: 0.01 us -> 12.4 us  [fast_body(): gate_up = lax.all_gather(gate_up_part, 'fsdp', axis=0, tiled=True)]
    ppermute x13 -> x10, starting transfers between devices: 14.2 us -> 10.1 us  [neighbour(): return lax.ppermute(values, 'seq', [(i, i ^ step) for i in range(count)])]
  transfers between devices with their start and end apart: 19 -> 15, of which waited for: 9 -> 5; matrix products, arithmetic and copies ran while one was open for 8% -> 1% of each run, Pallas kernels for 57% -> 60%
where the time goes in v7:
time: 541 us; the launch traced here: 533 us
  Pallas kernels  433 us (80%)
  waiting for transfers between devices  68.7 us (13%)
  between operations  14.1 us (3%)
  starting transfers between devices  10.7 us (2%)
    pallas_call x1, Pallas kernels, attend(): pl.pallas_call(lambda *refs: attend_kernel(count, *refs), out_shape=(jax....  90.2 us
    pallas_call x1, Pallas kernels, norm_back(): pl.pallas_call(lambda *refs: norm_back_kernel(count, *refs), out_shape=(j...  68.3 us
    pallas_call x1, Pallas kernels, feed(): pl.pallas_call(lambda *refs: feed_kernel(count, *refs), out_shape=[jax.Sh...  56.4 us
    ppermute x10, waiting for transfers between devices, neighbour(): return lax.ppermute(values, 'seq', [(i, i ^ step) for i in range(count)])  56.2 us
    pallas_call x1, Pallas kernels, leave(): pl.pallas_call(lambda *refs: leave_kernel(count, *refs), out_shape=(jax.S...  55.2 us
    pallas_call x1, Pallas kernels, enter(): pl.pallas_call(lambda *refs: enter_kernel(count, *refs), out_shape=(jax.S...  51.5 us
    pallas_call x1, Pallas kernels, share_dy(): pl.pallas_call(lambda *refs: share_dy_kernel(*refs), out_shape=[jax.Shape...  39.3 us
    pallas_call x1, Pallas kernels, attend_back(): pl.pallas_call(lambda *refs: attend_back_kernel(count, *refs), out_shape=...  39.2 us
  transfers between devices with their start and end apart: 15, of which 5 were waited for; matrix products, arithmetic and copies ran while one was open for 1% of the time, Pallas kernels for 60%

profile of v7, /device:TPU:0, one launch (start us, length us, event | category | flops | bytes accessed | tf_op | source)
XLA Modules:
  0.0 533.0 jit_solution(4565568170932065929)
XLA Ops:
  7.2 1.4 slice_bitcast_fusion
  8.6 51.5 %enter.1 = (bf16[4,256,2048]{2,1,0:T(8,128)(2,1)}, bf16[640,2048]{1,0:T(8,128)(2,1)}, bf16[2048,512]{1,0:T(8,128)(2,1)}, f32[1024,64]{1,0:T(8,128)}, bf16[352,20...) custom-call(f32[256,2048]{1,0:T(8,128)} %bitcast.24, f32[1,2048]{1,0:T(1,128)} %get-tuple-element.100.refs_1_.refs_4_, ...), custom_call_target="tpu_custom_call" | custom-call | tf_op jit(solution)/shard_map/enter/pallas_call | solution.py:680
  60.2 9.1 %project_qkv.1 = (bf16[8,1024,64]{2,1,0:T(8,128)(2,1)}, bf16[1024,64]{1,0:T(8,128)(2,1)}, bf16[1024,64]{1,0:T(8,128)(2,1)}) custom-call(s32[1]{0:T(128)} %bitcast.index_ref.refs_0_, bf16[1024,2048]{1,0:T(8,128)(2,1)} %bitcast.27, bf16[640,2048]{1,0:T(8,128)(2,1)} %get-tuple-element.54.weight_ref.refs_1_, f32[1024,64]{1,0:T(8,128)} %get-tuple-element.55.table_ref.refs_7_), custom_call_target="tpu_custom_call" | custom-call | tf_op jit(solution)/shard_map/project_qkv/pallas_call | solution.py:732
  69.3 90.2 %attend.1 = (bf16[1024,512]{1,0:T(8,128)(2,1)}, f32[8,1024]{1,0:T(8,128)}, f32[256,2048]{1,0:T(8,128)}, f32[256,128]{1,0:T(8,128)}, bf16[4,256,2048]{2,1,0:T(8,128)(2,1)}) custom-call(bf16[8,1024,64]{2,1,0:T(8,128)(2,1)} %get-tuple-element.56.refs_0_, bf16[1024,64]{1,0:T(8,128)(2,1)} %get-tuple-element.57.refs_1_, ...), custom_call_target="tpu_custom_call" | custom-call | tf_op jit(solution)/shard_map/attend/pallas_call | solution.py:826
  159.5 1.1 bitcast_convert_fusion.refs_2_
  160.6 12.4 %all-gather.2.cloned.1.call-done.refs_1_.refs_4_ = bf16[2816,2048]{1,0:T(8,128)(2,1)} async-done(((bf16[352,2048]{1,0:T(8,128)(2,1)}), bf16[2816,2048]{1,0:T(8,128)(2,1)}) %all-gather.2.cloned.1.call-update) | async-done | bytes 11534352 | tf_op jit(solution)/shard_map/all_gather | solution.py:1783
  173.1 56.4 %feed.1 = (bf16[1024,2816]{1,0:T(8,128)(2,1)}, bf16[1024,1408]{1,0:T(8,128)(2,1)}, bf16[4,256,2048]{2,1,0:T(8,128)(2,1)}, bf16[2048,1408]{1,0:T(8,128)(2,1)}, bf16[2048,1408]{1,0:T(8,128)(2,1)}) custom-call(bf16[1024,2048]{1,0:T(8,128)(2,1)} %bitcast.29, bf16[2816,2048]{1,0:T(8,128)(2,1)} %all-gather.2.cloned.1.call-done.refs_1_.refs_4_, ...), custom_call_target="tpu_custom_call" | custom-call | tf_op jit(solution)/shard_map/feed/pallas_call | solution.py:1465
  229.5 68.3 %norm_back.1 = (f32[256,2048]{1,0:T(8,128)}, f32[1,2048]{1,0:T(1,128)}, bf16[256,2048]{1,0:T(8,128)(2,1)}, bf16[2816,2048]{1,0:T(8,128)(2,1)}, bf16[4,256,2048]{...) custom-call(bf16[1024,1408]{1,0:T(8,128)(2,1)} %get-tuple-element.63.refs_0_, ...), custom_call_target="tpu_custom_call" | custom-call | tf_op jit(solution)/shard_map/norm_back/pallas_call | solution.py:1664
  298.1 39.3 %share_dy.1 = (bf16[4,256,2048]{2,1,0:T(8,128)(2,1)}, f32[256,2048]{1,0:T(8,128)}, bf16[2,128,2048]{2,1,0:T(8,128)(2,1)}) custom-call(bf16[256,2048]{1,0:T(8,128)(2,1)} %get-tuple-element.69.refs_0_, bf16[4,256,2048]{2,1,0:T(8,128)(2,1)} %get-tuple-element.70.refs_1_, bf16[2,128,2048]{2,1,0:T(8,128)(2,1)} %get-tuple-element.71.refs_2_, ...), custom_call_target="tpu_custom_call" | custom-call | tf_op jit(solution)/shard_map/share_dy/pallas_call | solution.py:1742
  337.4 39.2 %attend_back.1 = (bf16[1024,640]{1,0:T(8,128)(2,1)}, bf16[4,160,1024]{2,1,0:T(8,128)(2,1)}, bf16[2048,512]{1,0:T(8,128)(2,1)}, bf16[2,128,2048]{2,1,0:T(8,128)(2,1)}, bf16[4,256,1408]{2,1,0:T(8,128)(2,1)}) custom-call(bf16[8,1024,64]{2,1,0:T(8,128)(2,1)} %get-tuple-element.56.refs_0_, bf16[1024,64]{1,0:T(8,128)(2,1)} %get-tuple-element.57.refs_1_, ...), custom_call_target="tpu_custom_call" | custom-call | tf_op jit(solution)/shard_map/attend_back/pallas_call | solution.py:1012
  376.8 55.2 %leave.1 = (f32[256,2048]{1,0:T(8,128)}, f32[2,2048]{1,0:T(2,128)}, bf16[640,2048]{1,0:T(8,128)(2,1)}) custom-call(bf16[1024,640]{1,0:T(8,128)(2,1)} %get-tuple-element.82.refs_0_, bf16[640,2048]{1,0:T(8,128)(2,1)} %get-tuple-element.54.weight_ref.refs_1_, f32[256,2048]{1,0:T(8,128)} %bitcast.26, f32[256,128]{1,0:T(8,128)} %get-tuple-element.83.refs_3_, ...), custom_call_target="tpu_custom_call" | custom-call | tf_op jit(solution)/shard_map/leave/pallas_call | solution.py:1138
  432.1 1.0 collective-permute-start.7
  433.1 1.0 collective-permute-start.6
  434.0 30.6 %collective-permute-done.7.below_ref = bf16[352,2048]{1,0:T(8,128)(2,1)S(1)} collective-permute-done((bf16[352,2048]{1,0:T(8,128)(2,1)}, bf16[352,2048]{1,0:T(8,128)(2,1)S(1)}, u32[]{:S(2)}, u32[]{:S(2)}) %collective-permute-start.7) | collective-permute-done | bytes 1441824 | tf_op jit(solution)/shard_map/ppermute | solution.py:325
  464.6 1.0 slice.27
  465.6 0.7 collective-permute-start.9
  466.3 1.0 slice.26
  467.8 2.3 collective-permute-start.2
  470.0 0.7 collective-permute-start.1
  471.3 19.1 %collective-permute-done.2.refs_4_ = bf16[256,512]{1,0:T(8,128)(2,1)} collective-permute-done((bf16[256,512]{1,0:T(8,128)(2,1)}, bf16[256,512]{1,0:T(8,128)(2,1)}, u32[]{:S(2)}, u32[]{:S(2)}) %collective-permute-start.2) | collective-permute-done | bytes 262176 | tf_op jit(solution)/shard_map/ppermute | solution.py:325
  490.3 3.9 collective-permute-done.1.refs_3_
  494.2 1.5 collective-permute-start.5
  495.8 1.7 collective-permute-start.4
  497.7 5.4 %join_pieces.5 = f32[256,5632]{1,0:T(8,128)} custom-call(s32[1]{0:T(128)} %bitcast.index_ref.refs_0_, bf16[256,1408]{1,0:T(8,128)(2,1)} %reduce-scatter.5.cloned.1.call-done.refs_10_.refs_1_, bf16[4,256,1408]{2,1,0:T(8,128)(2,1)} %get-tuple-element.98.refs_2_), custom_call_target="tpu_custom_call" | custom-call | tf_op jit(solution)/shard_map/join_pieces/pallas_call | solution.py:1230
  503.1 2.7 join_pieces.4
  505.9 2.6 collective-permute-done.4.refs_3_
  508.5 0.7 copy-done.4
  509.2 0.7 copy-done.5
  510.0 3.0 join_pieces.3
  513.0 5.4 %last_sums.1 = (f32[256,2048]{1,0:T(8,128)}, f32[256,2048]{1,0:T(8,128)}) custom-call(f32[256,2048]{1,0:T(8,128)} %get-tuple-element.73.base_ref, bf16[256,2048]{1,0:T(8,128)(2,1)} %bitcast.42, f32[256,2048]{1,0:T(8,128)} %get-tuple-element.80.flowing_ref, f32[256,2048]{1,0:T(8,128)} %get-tuple-element.87.piece_ref), custom_call_target="tpu_custom_call" | custom-call | tf_op jit(solution)/shard_map/last_sums/pallas_call | solution.py:1254
  518.4 7.2 %join_rows.1 = f32[1408,2048]{1,0:T(8,128)} custom-call(s32[1]{0:T(128)} %bitcast.index_ref.refs_0_, bf16[352,2048]{1,0:T(8,128)(2,1)} %reduce-scatter.7.cloned.1.call-done.own_ref, bf16[352,2048]{1,0:T(8,128)(2,1)} %copy-done.2, bf16[352,2048]{1,0:T(8,128)(2,1)} %copy-done.1, bf16[176,2048]{1,0:T(8,128)(2,1)} %collective-permute-done.8.top_ref, ...), custom_call_target="tpu_custom_call" | custom-call | tf_op jit(solution)/shard_map/join_rows/pallas_call | solution.py:1192
  525.6 0.6 copy.17
  (35 shorter events, 2.0 us)
Async XLA Ops:
  7.2 165.9 %all-gather.2.cloned.1.call-start = ((), (), s32[]{:S(2)}) async-start(), calls=%async_computation.4 | async-start | bytes 12976128 | tf_op jit(solution)/shard_map/all_gather | solution.py:1783
  60.1 277.2 %reduce-scatter.5.cloned.1.call-start = ((), (), s32[]{:S(2)}) async-start(), calls=%async_computation.5 | async-start | bytes 6488064 | tf_op jit(solution)/shard_map/reduce_scatter | solution.py:1796
  69.3 90.2 %copy-start = (f32[1,256,2048]{2,1,0:T(8,128)S(1)}, f32[1,256,2048]{2,1,0:T(8,128)}, u32[]{:S(2)}) copy-start(f32[1,256,2048]{2,1,0:T(8,128)} %param.16) | copy-start | bytes 6291460
  229.5 202.6 %reduce-scatter.7.cloned.1.call-start = ((), (), s32[]{:S(2)}) async-start(), calls=%async_computation.6 | async-start | bytes 12976128 | tf_op jit(solution)/shard_map/reduce_scatter | solution.py:1796
  297.8 169.9 %reduce-scatter.11.cloned.1.call-start = ((), (), s32[]{:S(2)}) async-start(), calls=%async_computation.8 | async-start | bytes 2359296 | tf_op jit(solution)/shard_map/reduce_scatter | solution.py:1796
  376.5 117.7 %reduce-scatter.9.cloned.1.call-start = ((), (), s32[]{:S(2)}) async-start(), calls=%async_computation.7 | async-start | bytes 2949120 | tf_op jit(solution)/shard_map/reduce_scatter | solution.py:1796
  432.1 32.5 %collective-permute-start.7 = (bf16[352,2048]{1,0:T(8,128)(2,1)}, bf16[352,2048]{1,0:T(8,128)(2,1)S(1)}, u32[]{:S(2)}, u32[]{:S(2)}) collective-permute-start(bf16[352,2048]{1,0:T(8,128)(2,1)} %reduce-scatter.7.cloned.1.call-done.own_ref), channel_id=1, source_target_pairs={{0,2},{1,3},{2,0},{3,1},{4,6},{5,7},{6,4},{7,5},{8,10},{9,11},{10,... | collective-permute-start | bytes 4325384 | tf_op jit(solution)/shard_map/ppermute | solution.py:325
  433.1 33.2 %collective-permute-start.6 = (bf16[352,2048]{1,0:T(8,128)(2,1)}, bf16[352,2048]{1,0:T(8,128)(2,1)S(1)}, u32[]{:S(2)}, u32[]{:S(2)}) collective-permute-start(bf16[352,2048]{1,0:T(8,128)(2,1)} %reduce-scatter.7.cloned.1.call-done.own_ref), channel_id=1, source_target_pairs={{0,1},{1,0},{2,3},{3,2},{4,5},{5,4},{6,7},{7,6},{8,9},{9,8},{10,11... | collective-permute-start | bytes 4325384 | tf_op jit(solution)/shard_map/ppermute | solution.py:325
  464.6 38.5 %copy-start.1 = (bf16[352,2048]{1,0:T(8,128)(2,1)}, bf16[352,2048]{1,0:T(8,128)(2,1)S(1)}, u32[]{:S(2)}) copy-start(bf16[352,2048]{1,0:T(8,128)(2,1)S(1)} %collective-permute-done.7.below_ref) | copy-start | bytes 4325380
  465.6 52.9 %collective-permute-start.9 = (bf16[176,2048]{1,0:T(8,128)(2,1)}, bf16[176,2048]{1,0:T(8,128)(2,1)}, u32[]{:S(2)}, u32[]{:S(2)}) collective-permute-start(bf16[176,2048]{1,0:T(8,128)(2,1)} %slice.27), channel_id=1, source_target_pairs={{0,1},{1,0},{2,3},{3,2},{4,5},{5,4},{6,7},{7,6},{8,9},{9,8},{10,11... | collective-permute-start | bytes 2162696 | tf_op jit(solution)/shard_map/ppermute | solution.py:325
  466.3 36.8 %copy-start.2 = (bf16[352,2048]{1,0:T(8,128)(2,1)}, bf16[352,2048]{1,0:T(8,128)(2,1)S(1)}, u32[]{:S(2)}) copy-start(bf16[352,2048]{1,0:T(8,128)(2,1)S(1)} %collective-permute-done.6.side_ref) | copy-start | bytes 4325380
  467.3 51.2 %collective-permute-start.8 = (bf16[176,2048]{1,0:T(8,128)(2,1)}, bf16[176,2048]{1,0:T(8,128)(2,1)}, u32[]{:S(2)}, u32[]{:S(2)}) collective-permute-start(bf16[176,2048]{1,0:T(8,128)(2,1)} %slice.26), channel_id=1, source_target_pairs={{0,2},{1,3},{2,0},{3,1},{4,6},{5,7},{6,4},{7,5},{8,10},{9,11},{10,... | collective-permute-start | bytes 2162696 | tf_op jit(solution)/shard_map/ppermute | solution.py:325
  467.8 22.6 %collective-permute-start.2 = (bf16[256,512]{1,0:T(8,128)(2,1)}, bf16[256,512]{1,0:T(8,128)(2,1)}, u32[]{:S(2)}, u32[]{:S(2)}) collective-permute-start(bf16[256,512]{1,0:T(8,128)(2,1)} %reduce-scatter.11.cloned.1.call-done.refs_1_), channel_id=1, source_target_pairs={{0,3},{1,2},{2,1},{3,0},{4,7},{5,6},{6,5},{7,4},{8,11},{9,10},{10,... | collective-permute-start | bytes 786440 | tf_op jit(solution)/shard_map/ppermute | solution.py:325
  470.0 24.2 %collective-permute-start.1 = (bf16[256,512]{1,0:T(8,128)(2,1)}, bf16[256,512]{1,0:T(8,128)(2,1)}, u32[]{:S(2)}, u32[]{:S(2)}) collective-permute-start(bf16[256,512]{1,0:T(8,128)(2,1)} %reduce-scatter.11.cloned.1.call-done.refs_1_), channel_id=1, source_target_pairs={{0,2},{1,3},{2,0},{3,1},{4,6},{5,7},{6,4},{7,5},{8,10},{9,11},{10,... | collective-permute-start | bytes 786440 | tf_op jit(solution)/shard_map/ppermute | solution.py:325
  470.8 23.5 %collective-permute-start = (bf16[256,512]{1,0:T(8,128)(2,1)}, bf16[256,512]{1,0:T(8,128)(2,1)}, u32[]{:S(2)}, u32[]{:S(2)}) collective-permute-start(bf16[256,512]{1,0:T(8,128)(2,1)} %reduce-scatter.11.cloned.1.call-done.refs_1_), channel_id=1, source_target_pairs={{0,1},{1,0},{2,3},{3,2},{4,5},{5,4},{6,7},{7,6},{8,9},{9,8},{10,11... | collective-permute-start | bytes 786440 | tf_op jit(solution)/shard_map/ppermute | solution.py:325
  494.2 11.6 %collective-permute-start.5 = (bf16[80,2048]{1,0:T(8,128)(2,1)}, bf16[80,2048]{1,0:T(8,128)(2,1)S(1)}, u32[]{:S(2)}, u32[]{:S(2)}) collective-permute-start(bf16[80,2048]{1,0:T(8,128)(2,1)} %reduce-scatter.9.cloned.1.call-done.refs_1_), channel_id=1, source_target_pairs={{0,3},{1,2},{2,1},{3,0},{4,7},{5,6},{6,5},{7,4},{8,11},{9,10},{10,... | collective-permute-start | bytes 983048 | tf_op jit(solution)/shard_map/ppermute | solution.py:325
  495.8 12.8 %collective-permute-start.4 = (bf16[80,2048]{1,0:T(8,128)(2,1)}, bf16[80,2048]{1,0:T(8,128)(2,1)S(1)}, u32[]{:S(2)}, u32[]{:S(2)}) collective-permute-start(bf16[80,2048]{1,0:T(8,128)(2,1)} %reduce-scatter.9.cloned.1.call-done.refs_1_), channel_id=1, source_target_pairs={{0,2},{1,3},{2,0},{3,1},{4,6},{5,7},{6,4},{7,5},{8,10},{9,11},{10,... | collective-permute-start | bytes 983048 | tf_op jit(solution)/shard_map/ppermute | solution.py:325
  497.5 11.0 %collective-permute-start.3 = (bf16[80,2048]{1,0:T(8,128)(2,1)}, bf16[80,2048]{1,0:T(8,128)(2,1)S(1)}, u32[]{:S(2)}, u32[]{:S(2)}) collective-permute-start(bf16[80,2048]{1,0:T(8,128)(2,1)} %reduce-scatter.9.cloned.1.call-done.refs_1_), channel_id=1, source_target_pairs={{0,1},{1,0},{2,3},{3,2},{4,5},{5,4},{6,7},{7,6},{8,9},{9,8},{10,11... | collective-permute-start | bytes 983048 | tf_op jit(solution)/shard_map/ppermute | solution.py:325
  505.9 2.6 copy-start.3
  508.5 0.7 copy-start.4
  509.2 0.7 copy-start.5
  518.4 7.2 %copy-start.6 = (f32[2,2048]{1,0:T(2,128)S(1)}, f32[2,2048]{1,0:T(2,128)}, u32[]{:S(2)}) copy-start(f32[2,2048]{1,0:T(2,128)} %get-tuple-element.90) | copy-start | bytes 49156
Sparse Core Ops, SparseCore 0:
  60.3 112.7 all-gather.1
  229.6 64.1 reduce-scatter.4
  298.0 118.6 reduce-scatter.6
  418.8 34.4 reduce-scatter.10
  455.5 36.5 reduce-scatter.8

commit v8 on v7

--- a/solution.py
+++ b/solution.py
@@ -586,7 +586,7 @@
     current = current_ref[...]
     scale = lax.rsqrt(jnp.mean(current * current, 1, keepdims=True) + EPS)
     scale_ref[...] = jnp.broadcast_to(scale, scale_ref.shape)
-    normed_ref[...] = (current * scale * gain_ref[...]).astype(jnp.bfloat16)
+    normed_ref[...] = (current * scale * gain_ref[:1]).astype(jnp.bfloat16)
     copies = gather_copies(normed_ref, all_ref, part // 2, sems)
     for copy in copies[:4]:
         copy.start()
@@ -689,7 +689,7 @@
             jax.ShapeDtypeStruct((part, 128), jnp.float32),
         ),
         in_specs=[whole] + [vmem] * 2 + [whole] * 4,
-        out_specs=[whole] + [vmem] * 3 + [whole] + [vmem] * 2,
+        out_specs=[whole] * 3 + [vmem, whole] + [vmem] * 2,
         scratch_shapes=[
             pltpu.VMEM((part, width), jnp.float32),
             pltpu.VMEM((part, width), jnp.bfloat16),
@@ -812,7 +812,7 @@
     middle = middle_ref[...]
     scale = lax.rsqrt(jnp.mean(middle * middle, 1, keepdims=True) + EPS)
     scale_ref[...] = jnp.broadcast_to(scale, scale_ref.shape)
-    two_ref[...] = (middle * scale * gain_ref[...]).astype(jnp.bfloat16)
+    two_ref[...] = (middle * scale * gain_ref[1:2]).astype(jnp.bfloat16)
     own = pltpu.make_async_copy(two_ref, all_ref.at[0], own_sem)
     share_own(two_ref, all_ref, half, sems, sums)
     own.start()
@@ -1090,7 +1090,7 @@
     lax.fori_loop(0, count, one_part, 0)
     loads[0].wait()
     loads[2].wait()
-    total_ref[0:1] = total_ref[0:1] / gain_ref[...]
+    total_ref[0:1] = total_ref[0:1] / gain_ref[:1]
     tells = []
     for step, peer in enumerate(fsdp_peers):
         told_ref[step] = total_ref[...]
@@ -1121,7 +1121,7 @@
     end_sums(sums, side_ref, below_ref, far_ref, own_ref, half)
     unit = first_ref[...] * scale_ref[:, :1]
     grads = own_ref[...]
-    inner = grads * gain_ref[...]
+    inner = grads * gain_ref[:1]
     own_ref[...] = scale_ref[:, :1] * (inner - unit * jnp.mean(inner * unit, 1, keepdims=True))
     for step in range(len(peers)):
         tells[first + step].wait_recv()
@@ -1642,7 +1642,7 @@
     unit = middle_ref[...] * scale
     grads = own_ref[...]
     gain_out_ref[...] = jnp.sum(grads * unit, 0, keepdims=True)
-    inner = grads * gain_ref[...]
+    inner = grads * gain_ref[1:2]
     own_ref[...] = flowing_ref[...] + scale * (inner - unit * jnp.mean(inner * unit, 1, keepdims=True))
     dy_ref[...] = own_ref[...].astype(narrow)
     for number in range(tiles - 2, tiles):
@@ -1777,7 +1777,7 @@
     chunk = group // count
     per_head = HD // group
     normed_all, qkv_rows, out_cols, table, gate_up_part, down_part, scale_one = enter(
-        current, gain[:1], positions, w_qkv[0], w_out[0], w_gate_up[0], w_down[0], count
+        current, gain, positions, w_qkv[0], w_out[0], w_gate_up[0], w_down[0], count
     )
     gu_rows = w_gate_up.shape[1] // count
     gate_up = lax.all_gather(gate_up_part, "fsdp", axis=0, tiled=True)
@@ -1785,7 +1785,7 @@
 
     queries, keys_in, values_in = project_qkv(place, normed_all, qkv_rows, table, count)
     attn_flat, log_total, middle, scale_two, normed_two_all = attend(
-        queries, keys_in, values_in, out_cols, current, gain[1:], count
+        queries, keys_in, values_in, out_cols, current, gain, count
     )
     flowing = cotangent[0]
     gates, activated, dm_all, term_down, down_cols = feed(
@@ -1797,7 +1797,7 @@
 
     grad_down = owned(term_down)
     dmiddle, gain_two, dy, term_gate_up, down_sent, from_side, from_below = norm_back(
-        activated, down_cols, dm_all, gates, gate_up, flowing, middle, normed_two_all, scale_two, gain[1:], count
+        activated, down_cols, dm_all, gates, gate_up, flowing, middle, normed_two_all, scale_two, gain, count
     )
     grad_gate_up = owned(term_gate_up)
     dy_all, base, passed = share_dy(dy, down_sent, from_side, from_below, middle, count)
@@ -1809,7 +1809,7 @@
     )
     grad_out = owned(term_out)
     grad_piece, gain_total, term_qkv = leave(
-        djoint, qkv_rows, current, scale_one, gain[:1], gain_two[None], djoint_turned, normed_all, count
+        djoint, qkv_rows, current, scale_one, gain, gain_two[None], djoint_turned, normed_all, count
     )
     grad_qkv = owned(term_qkv)
     grad_gate_up, grad_piece = after((grad_gate_up, grad_piece))

time: 541 us -> 538 us (level)
  transfers between devices with their start and end apart: 15 -> 15, of which waited for: 5 -> 5; matrix products, arithmetic and copies ran while one was open for 1% -> 1% of each run, Pallas kernels for 60% -> 59%
where the time goes in v8:
time: 538 us; the launch traced here: 531 us
  Pallas kernels  432 us (80%)
  waiting for transfers between devices  68.6 us (13%)
  between operations  14.1 us (3%)
  starting transfers between devices  10.7 us (2%)
    pallas_call x1, Pallas kernels, attend(): pl.pallas_call(lambda *refs: attend_kernel(count, *refs), out_shape=(jax....  85.3 us
    pallas_call x1, Pallas kernels, norm_back(): pl.pallas_call(lambda *refs: norm_back_kernel(count, *refs), out_shape=(j...  68.3 us
    pallas_call x1, Pallas kernels, feed(): pl.pallas_call(lambda *refs: feed_kernel(count, *refs), out_shape=[jax.Sh...  56.4 us
    ppermute x10, waiting for transfers between devices, neighbour(): return lax.ppermute(values, 'seq', [(i, i ^ step) for i in range(count)])  56.2 us
    pallas_call x1, Pallas kernels, enter(): pl.pallas_call(lambda *refs: enter_kernel(count, *refs), out_shape=(jax.S...  55.5 us
    pallas_call x1, Pallas kernels, leave(): pl.pallas_call(lambda *refs: leave_kernel(count, *refs), out_shape=(jax.S...  55.3 us
    pallas_call x1, Pallas kernels, share_dy(): pl.pallas_call(lambda *refs: share_dy_kernel(*refs), out_shape=[jax.Shape...  39.3 us
    pallas_call x1, Pallas kernels, attend_back(): pl.pallas_call(lambda *refs: attend_back_kernel(count, *refs), out_shape=...  39.1 us
  transfers between devices with their start and end apart: 15, of which 5 were waited for; matrix products, arithmetic and copies ran while one was open for 1% of the time, Pallas kernels for 59%

profile of v8, /device:TPU:0, one launch (start us, length us, event | category | flops | bytes accessed | tf_op | source)
XLA Modules:
  0.0 530.6 jit_solution(16377159194803340239)
XLA Ops:
  7.2 55.5 %enter.1 = (bf16[4,256,2048]{2,1,0:T(8,128)(2,1)}, bf16[640,2048]{1,0:T(8,128)(2,1)}, bf16[2048,512]{1,0:T(8,128)(2,1)}, f32[1024,64]{1,0:T(8,128)}, bf16[352,20...) custom-call(f32[256,2048]{1,0:T(8,128)} %bitcast.21, f32[2,2048]{1,0:T(2,128)} %bitcast.40, ...), custom_call_target="tpu_custom_call" | custom-call | tf_op jit(solution)/shard_map/enter/pallas_call | solution.py:680
  62.8 9.2 %project_qkv.1 = (bf16[8,1024,64]{2,1,0:T(8,128)(2,1)}, bf16[1024,64]{1,0:T(8,128)(2,1)}, bf16[1024,64]{1,0:T(8,128)(2,1)}) custom-call(s32[1]{0:T(128)} %bitcast.index_ref.refs_0_, bf16[1024,2048]{1,0:T(8,128)(2,1)} %bitcast.24, bf16[640,2048]{1,0:T(8,128)(2,1)} %get-tuple-element.54.weight_ref.refs_1_, f32[1024,64]{1,0:T(8,128)} %get-tuple-element.55.table_ref.refs_7_), custom_call_target="tpu_custom_call" | custom-call | tf_op jit(solution)/shard_map/project_qkv/pallas_call | solution.py:732
  72.0 85.3 %attend.1 = (bf16[1024,512]{1,0:T(8,128)(2,1)}, f32[8,1024]{1,0:T(8,128)}, f32[256,2048]{1,0:T(8,128)}, f32[256,128]{1,0:T(8,128)}, bf16[4,256,2048]{2,1,0:T(8,128)(2,1)}) custom-call(bf16[8,1024,64]{2,1,0:T(8,128)(2,1)} %get-tuple-element.56.refs_0_, bf16[1024,64]{1,0:T(8,128)(2,1)} %get-tuple-element.57.refs_1_, ...), custom_call_target="tpu_custom_call" | custom-call | tf_op jit(solution)/shard_map/attend/pallas_call | solution.py:826
  157.4 1.1 bitcast_convert_fusion.refs_2_
  158.5 12.2 %all-gather.2.cloned.1.call-done.refs_1_.refs_4_ = bf16[2816,2048]{1,0:T(8,128)(2,1)} async-done(((bf16[352,2048]{1,0:T(8,128)(2,1)}), bf16[2816,2048]{1,0:T(8,128)(2,1)}) %all-gather.2.cloned.1.call-update) | async-done | bytes 11534352 | tf_op jit(solution)/shard_map/all_gather | solution.py:1783
  170.7 56.4 %feed.1 = (bf16[1024,2816]{1,0:T(8,128)(2,1)}, bf16[1024,1408]{1,0:T(8,128)(2,1)}, bf16[4,256,2048]{2,1,0:T(8,128)(2,1)}, bf16[2048,1408]{1,0:T(8,128)(2,1)}, bf16[2048,1408]{1,0:T(8,128)(2,1)}) custom-call(bf16[1024,2048]{1,0:T(8,128)(2,1)} %bitcast.26, bf16[2816,2048]{1,0:T(8,128)(2,1)} %all-gather.2.cloned.1.call-done.refs_1_.refs_4_, ...), custom_call_target="tpu_custom_call" | custom-call | tf_op jit(solution)/shard_map/feed/pallas_call | solution.py:1465
  227.1 68.3 %norm_back.1 = (f32[256,2048]{1,0:T(8,128)}, f32[1,2048]{1,0:T(1,128)}, bf16[256,2048]{1,0:T(8,128)(2,1)}, bf16[2816,2048]{1,0:T(8,128)(2,1)}, bf16[4,256,2048]{...) custom-call(bf16[1024,1408]{1,0:T(8,128)(2,1)} %get-tuple-element.63.refs_0_, ...), custom_call_target="tpu_custom_call" | custom-call | tf_op jit(solution)/shard_map/norm_back/pallas_call | solution.py:1664
  295.7 39.3 %share_dy.1 = (bf16[4,256,2048]{2,1,0:T(8,128)(2,1)}, f32[256,2048]{1,0:T(8,128)}, bf16[2,128,2048]{2,1,0:T(8,128)(2,1)}) custom-call(bf16[256,2048]{1,0:T(8,128)(2,1)} %get-tuple-element.69.refs_0_, bf16[4,256,2048]{2,1,0:T(8,128)(2,1)} %get-tuple-element.70.refs_1_, bf16[2,128,2048]{2,1,0:T(8,128)(2,1)} %get-tuple-element.71.refs_2_, ...), custom_call_target="tpu_custom_call" | custom-call | tf_op jit(solution)/shard_map/share_dy/pallas_call | solution.py:1742
  335.0 39.1 %attend_back.1 = (bf16[1024,640]{1,0:T(8,128)(2,1)}, bf16[4,160,1024]{2,1,0:T(8,128)(2,1)}, bf16[2048,512]{1,0:T(8,128)(2,1)}, bf16[2,128,2048]{2,1,0:T(8,128)(2,1)}, bf16[4,256,1408]{2,1,0:T(8,128)(2,1)}) custom-call(bf16[8,1024,64]{2,1,0:T(8,128)(2,1)} %get-tuple-element.56.refs_0_, bf16[1024,64]{1,0:T(8,128)(2,1)} %get-tuple-element.57.refs_1_, ...), custom_call_target="tpu_custom_call" | custom-call | tf_op jit(solution)/shard_map/attend_back/pallas_call | solution.py:1012
  374.4 55.3 %leave.1 = (f32[256,2048]{1,0:T(8,128)}, f32[2,2048]{1,0:T(2,128)}, bf16[640,2048]{1,0:T(8,128)(2,1)}) custom-call(bf16[1024,640]{1,0:T(8,128)(2,1)} %get-tuple-element.82.refs_0_, bf16[640,2048]{1,0:T(8,128)(2,1)} %get-tuple-element.54.weight_ref.refs_1_, f32[256,2048]{1,0:T(8,128)} %bitcast.23, f32[256,128]{1,0:T(8,128)} %get-tuple-element.83.refs_3_, ...), custom_call_target="tpu_custom_call" | custom-call | tf_op jit(solution)/shard_map/leave/pallas_call | solution.py:1138
  429.7 1.0 collective-permute-start.7
  430.7 1.0 collective-permute-start.6
  431.6 30.6 %collective-permute-done.7.below_ref = bf16[352,2048]{1,0:T(8,128)(2,1)S(1)} collective-permute-done((bf16[352,2048]{1,0:T(8,128)(2,1)}, bf16[352,2048]{1,0:T(8,128)(2,1)S(1)}, u32[]{:S(2)}, u32[]{:S(2)}) %collective-permute-start.7) | collective-permute-done | bytes 1441824 | tf_op jit(solution)/shard_map/ppermute | solution.py:325
  462.2 1.0 slice.9
  463.2 0.7 collective-permute-start.9
  463.9 1.0 slice.8
  465.4 2.3 collective-permute-start.2
  467.6 0.7 collective-permute-start.1
  468.4 0.5 collective-permute-start
  468.9 19.1 %collective-permute-done.2.refs_4_ = bf16[256,512]{1,0:T(8,128)(2,1)} collective-permute-done((bf16[256,512]{1,0:T(8,128)(2,1)}, bf16[256,512]{1,0:T(8,128)(2,1)}, u32[]{:S(2)}, u32[]{:S(2)}) %collective-permute-start.2) | collective-permute-done | bytes 262176 | tf_op jit(solution)/shard_map/ppermute | solution.py:325
  487.9 3.9 collective-permute-done.1.refs_3_
  491.9 1.5 collective-permute-start.5
  493.4 1.7 collective-permute-start.4
  495.4 5.4 %join_pieces.5 = f32[256,5632]{1,0:T(8,128)} custom-call(s32[1]{0:T(128)} %bitcast.index_ref.refs_0_, bf16[256,1408]{1,0:T(8,128)(2,1)} %reduce-scatter.5.cloned.1.call-done.refs_10_.refs_1_, bf16[4,256,1408]{2,1,0:T(8,128)(2,1)} %get-tuple-element.98.refs_2_), custom_call_target="tpu_custom_call" | custom-call | tf_op jit(solution)/shard_map/join_pieces/pallas_call | solution.py:1230
  500.8 2.7 join_pieces.4
  503.5 2.6 collective-permute-done.4.refs_3_
  506.1 0.7 copy-done.4
  506.9 0.7 copy-done.5
  507.6 3.0 join_pieces.3
  510.6 5.4 %last_sums.1 = (f32[256,2048]{1,0:T(8,128)}, f32[256,2048]{1,0:T(8,128)}) custom-call(f32[256,2048]{1,0:T(8,128)} %get-tuple-element.73.base_ref, bf16[256,2048]{1,0:T(8,128)(2,1)} %bitcast.38, f32[256,2048]{1,0:T(8,128)} %get-tuple-element.80.flowing_ref, f32[256,2048]{1,0:T(8,128)} %get-tuple-element.87.piece_ref), custom_call_target="tpu_custom_call" | custom-call | tf_op jit(solution)/shard_map/last_sums/pallas_call | solution.py:1254
  516.1 7.2 %join_rows.1 = f32[1408,2048]{1,0:T(8,128)} custom-call(s32[1]{0:T(128)} %bitcast.index_ref.refs_0_, bf16[352,2048]{1,0:T(8,128)(2,1)} %reduce-scatter.7.cloned.1.call-done.own_ref, bf16[352,2048]{1,0:T(8,128)(2,1)} %copy-done.2, bf16[352,2048]{1,0:T(8,128)(2,1)} %copy-done.1, bf16[176,2048]{1,0:T(8,128)(2,1)} %collective-permute-done.8.top_ref, ...), custom_call_target="tpu_custom_call" | custom-call | tf_op jit(solution)/shard_map/join_rows/pallas_call | solution.py:1192
  523.3 0.6 copy.17
  (34 shorter events, 1.5 us)
Async XLA Ops:
  7.2 163.5 %all-gather.2.cloned.1.call-start = ((), (), s32[]{:S(2)}) async-start(), calls=%async_computation.4 | async-start | bytes 12976128 | tf_op jit(solution)/shard_map/all_gather | solution.py:1783
  62.8 272.2 %reduce-scatter.5.cloned.1.call-start = ((), (), s32[]{:S(2)}) async-start(), calls=%async_computation.5 | async-start | bytes 6488064 | tf_op jit(solution)/shard_map/reduce_scatter | solution.py:1796
  72.0 85.3 %copy-start = (f32[1,256,2048]{2,1,0:T(8,128)S(1)}, f32[1,256,2048]{2,1,0:T(8,128)}, u32[]{:S(2)}) copy-start(f32[1,256,2048]{2,1,0:T(8,128)} %param.16) | copy-start | bytes 6291460
  227.1 202.6 %reduce-scatter.7.cloned.1.call-start = ((), (), s32[]{:S(2)}) async-start(), calls=%async_computation.6 | async-start | bytes 12976128 | tf_op jit(solution)/shard_map/reduce_scatter | solution.py:1796
  295.4 169.9 %reduce-scatter.11.cloned.1.call-start = ((), (), s32[]{:S(2)}) async-start(), calls=%async_computation.8 | async-start | bytes 2359296 | tf_op jit(solution)/shard_map/reduce_scatter | solution.py:1796
  374.1 117.7 %reduce-scatter.9.cloned.1.call-start = ((), (), s32[]{:S(2)}) async-start(), calls=%async_computation.7 | async-start | bytes 2949120 | tf_op jit(solution)/shard_map/reduce_scatter | solution.py:1796
  429.7 32.5 %collective-permute-start.7 = (bf16[352,2048]{1,0:T(8,128)(2,1)}, bf16[352,2048]{1,0:T(8,128)(2,1)S(1)}, u32[]{:S(2)}, u32[]{:S(2)}) collective-permute-start(bf16[352,2048]{1,0:T(8,128)(2,1)} %reduce-scatter.7.cloned.1.call-done.own_ref), channel_id=1, source_target_pairs={{0,2},{1,3},{2,0},{3,1},{4,6},{5,7},{6,4},{7,5},{8,10},{9,11},{10,... | collective-permute-start | bytes 4325384 | tf_op jit(solution)/shard_map/ppermute | solution.py:325
  430.7 33.2 %collective-permute-start.6 = (bf16[352,2048]{1,0:T(8,128)(2,1)}, bf16[352,2048]{1,0:T(8,128)(2,1)S(1)}, u32[]{:S(2)}, u32[]{:S(2)}) collective-permute-start(bf16[352,2048]{1,0:T(8,128)(2,1)} %reduce-scatter.7.cloned.1.call-done.own_ref), channel_id=1, source_target_pairs={{0,1},{1,0},{2,3},{3,2},{4,5},{5,4},{6,7},{7,6},{8,9},{9,8},{10,11... | collective-permute-start | bytes 4325384 | tf_op jit(solution)/shard_map/ppermute | solution.py:325
  462.2 38.5 %copy-start.1 = (bf16[352,2048]{1,0:T(8,128)(2,1)}, bf16[352,2048]{1,0:T(8,128)(2,1)S(1)}, u32[]{:S(2)}) copy-start(bf16[352,2048]{1,0:T(8,128)(2,1)S(1)} %collective-permute-done.7.below_ref) | copy-start | bytes 4325380
  463.2 52.9 %collective-permute-start.9 = (bf16[176,2048]{1,0:T(8,128)(2,1)}, bf16[176,2048]{1,0:T(8,128)(2,1)}, u32[]{:S(2)}, u32[]{:S(2)}) collective-permute-start(bf16[176,2048]{1,0:T(8,128)(2,1)} %slice.9), channel_id=1, source_target_pairs={{0,1},{1,0},{2,3},{3,2},{4,5},{5,4},{6,7},{7,6},{8,9},{9,8},{10,11... | collective-permute-start | bytes 2162696 | tf_op jit(solution)/shard_map/ppermute | solution.py:325
  463.9 36.8 %copy-start.2 = (bf16[352,2048]{1,0:T(8,128)(2,1)}, bf16[352,2048]{1,0:T(8,128)(2,1)S(1)}, u32[]{:S(2)}) copy-start(bf16[352,2048]{1,0:T(8,128)(2,1)S(1)} %collective-permute-done.6.side_ref) | copy-start | bytes 4325380
  464.9 51.2 %collective-permute-start.8 = (bf16[176,2048]{1,0:T(8,128)(2,1)}, bf16[176,2048]{1,0:T(8,128)(2,1)}, u32[]{:S(2)}, u32[]{:S(2)}) collective-permute-start(bf16[176,2048]{1,0:T(8,128)(2,1)} %slice.8), channel_id=1, source_target_pairs={{0,2},{1,3},{2,0},{3,1},{4,6},{5,7},{6,4},{7,5},{8,10},{9,11},{10,... | collective-permute-start | bytes 2162696 | tf_op jit(solution)/shard_map/ppermute | solution.py:325
  465.4 22.6 %collective-permute-start.2 = (bf16[256,512]{1,0:T(8,128)(2,1)}, bf16[256,512]{1,0:T(8,128)(2,1)}, u32[]{:S(2)}, u32[]{:S(2)}) collective-permute-start(bf16[256,512]{1,0:T(8,128)(2,1)} %reduce-scatter.11.cloned.1.call-done.refs_1_), channel_id=1, source_target_pairs={{0,3},{1,2},{2,1},{3,0},{4,7},{5,6},{6,5},{7,4},{8,11},{9,10},{10,... | collective-permute-start | bytes 786440 | tf_op jit(solution)/shard_map/ppermute | solution.py:325
  467.6 24.2 %collective-permute-start.1 = (bf16[256,512]{1,0:T(8,128)(2,1)}, bf16[256,512]{1,0:T(8,128)(2,1)}, u32[]{:S(2)}, u32[]{:S(2)}) collective-permute-start(bf16[256,512]{1,0:T(8,128)(2,1)} %reduce-scatter.11.cloned.1.call-done.refs_1_), channel_id=1, source_target_pairs={{0,2},{1,3},{2,0},{3,1},{4,6},{5,7},{6,4},{7,5},{8,10},{9,11},{10,... | collective-permute-start | bytes 786440 | tf_op jit(solution)/shard_map/ppermute | solution.py:325
  468.4 23.5 %collective-permute-start = (bf16[256,512]{1,0:T(8,128)(2,1)}, bf16[256,512]{1,0:T(8,128)(2,1)}, u32[]{:S(2)}, u32[]{:S(2)}) collective-permute-start(bf16[256,512]{1,0:T(8,128)(2,1)} %reduce-scatter.11.cloned.1.call-done.refs_1_), channel_id=1, source_target_pairs={{0,1},{1,0},{2,3},{3,2},{4,5},{5,4},{6,7},{7,6},{8,9},{9,8},{10,11... | collective-permute-start | bytes 786440 | tf_op jit(solution)/shard_map/ppermute | solution.py:325
  491.9 11.6 %collective-permute-start.5 = (bf16[80,2048]{1,0:T(8,128)(2,1)}, bf16[80,2048]{1,0:T(8,128)(2,1)S(1)}, u32[]{:S(2)}, u32[]{:S(2)}) collective-permute-start(bf16[80,2048]{1,0:T(8,128)(2,1)} %reduce-scatter.9.cloned.1.call-done.refs_1_), channel_id=1, source_target_pairs={{0,3},{1,2},{2,1},{3,0},{4,7},{5,6},{6,5},{7,4},{8,11},{9,10},{10,... | collective-permute-start | bytes 983048 | tf_op jit(solution)/shard_map/ppermute | solution.py:325
  493.4 12.8 %collective-permute-start.4 = (bf16[80,2048]{1,0:T(8,128)(2,1)}, bf16[80,2048]{1,0:T(8,128)(2,1)S(1)}, u32[]{:S(2)}, u32[]{:S(2)}) collective-permute-start(bf16[80,2048]{1,0:T(8,128)(2,1)} %reduce-scatter.9.cloned.1.call-done.refs_1_), channel_id=1, source_target_pairs={{0,2},{1,3},{2,0},{3,1},{4,6},{5,7},{6,4},{7,5},{8,10},{9,11},{10,... | collective-permute-start | bytes 983048 | tf_op jit(solution)/shard_map/ppermute | solution.py:325
  495.1 11.0 %collective-permute-start.3 = (bf16[80,2048]{1,0:T(8,128)(2,1)}, bf16[80,2048]{1,0:T(8,128)(2,1)S(1)}, u32[]{:S(2)}, u32[]{:S(2)}) collective-permute-start(bf16[80,2048]{1,0:T(8,128)(2,1)} %reduce-scatter.9.cloned.1.call-done.refs_1_), channel_id=1, source_target_pairs={{0,1},{1,0},{2,3},{3,2},{4,5},{5,4},{6,7},{7,6},{8,9},{9,8},{10,11... | collective-permute-start | bytes 983048 | tf_op jit(solution)/shard_map/ppermute | solution.py:325
  503.5 2.6 copy-start.3
  506.1 0.7 copy-start.4
  506.9 0.7 copy-start.5
  516.1 7.2 %copy-start.6 = (f32[2,2048]{1,0:T(2,128)S(1)}, f32[2,2048]{1,0:T(2,128)}, u32[]{:S(2)}) copy-start(f32[2,2048]{1,0:T(2,128)} %get-tuple-element.90) | copy-start | bytes 49156
Sparse Core Ops, SparseCore 0:
  62.9 107.7 all-gather.1
  227.2 64.1 reduce-scatter.4
  295.6 118.6 reduce-scatter.6
  416.4 34.4 reduce-scatter.10
  453.0 36.5 reduce-scatter.8
